TPU v7x, 32 devices: a whole 2x2x4 slice. The times are simulated.
32 devices in a mesh: dp: 4 (over z), row: 4 (over y, core), col: 2 (over x).
Axes of the slice: x: 2, y: 2, z: 4, core: 2. Of those that a mesh axis runs over, the one named last changes fastest.
Arguments:
- inputs: bfloat16 [16384, 1024], P(('dp', 'col'), 'row'), may hold values from -6 to 6
- gain_first: float32 [1024], P('row'), may hold values from 0.5 to 1.5
- shift_first: float32 [1024], P('row'), may hold values from -1 to 1
- w_query: bfloat16 [1024, 1024], P('row', 'col'), may hold values from -0.1875 to 0.1875
- w_key: bfloat16 [1024, 1024], P('row', 'col'), may hold values from -0.1875 to 0.1875
- w_value: bfloat16 [1024, 1024], P('row', 'col'), may hold values from -0.1875 to 0.1875
- w_output: bfloat16 [1024, 1024], P('col', 'row'), may hold values from -1.5 to 1.5
- gain_second: float32 [1024], P('row'), may hold values from 0.5 to 1.5
- shift_second: float32 [1024], P('row'), may hold values from -1 to 1
- w_up: bfloat16 [1024, 4096], P('row', 'col'), may hold values from -0.1875 to 0.1875
- bias_up: float32 [4096], P('col'), may hold values from -1.5 to 1.5
- w_down: bfloat16 [4096, 1024], P('col', 'row'), may hold values from -0.09375 to 0.09375
- bias_down: float32 [1024], P('row'), may hold values from -2.5 to 2.5
- segments: int32 [16, 1024], P(('dp', 'row')), may hold values from 0 to 4, as said below
- random_blocks: int32 [16, 16, 3], P('col'), may hold values from 0 to 15
- global_blocks: int32 [2], replicated, may hold values from 0 to 15, as said below
- cotangent: bfloat16 [16384, 1024], P(('dp', 'col'), 'row'), may hold values from -6 to 6
Outputs:
- layer_out: bfloat16 [16384, 1024], P(('dp', 'col'), 'row')
- grad_inputs: float32 [16384, 1024], P(('dp', 'col'), 'row')
- grad_gain_first: float32 [1024], P('row')
- grad_shift_first: float32 [1024], P('row')
- grad_w_query: float32 [1024, 1024], P('row', 'col')
- grad_w_key: float32 [1024, 1024], P('row', 'col')
- grad_w_value: float32 [1024, 1024], P('row', 'col')
- grad_w_output: float32 [1024, 1024], P('col', 'row')
- grad_gain_second: float32 [1024], P('row')
- grad_shift_second: float32 [1024], P('row')
- grad_w_up: float32 [1024, 4096], P('row', 'col')
- grad_bias_up: float32 [4096], P('col')
- grad_w_down: float32 [4096, 1024], P('col', 'row')
- grad_bias_down: float32 [1024], P('row')
Inputs may be any that keep to these rules, and one draw needn't show every extreme that they name: `segments`: each sequence of 1024 tokens holds four documents labelled 1, 2, 3, 4 in order, then 1 to 64 padding tokens labelled 0; each of the first three documents has 100 to 300 tokens. `global_blocks`: distinct block positions; one of them is the last block, 15.
All inputs are finite; a program needn't handle non-finite values.
Results may differ from a plain program's by a relative error of at most 0.015.
Values may be sent and summed in bfloat16 or wider, within the bound.
No kernel may reach another device: no remote copies, remote signals or barrier semaphores. Data moves between devices by JAX's collectives and lax.ppermute only.
A program may use at most 256 MiB of HBM per device.

v0:
```python
import math

import jax
import jax.numpy as jnp
from jax import lax
from jax.sharding import PartitionSpec as P

D = 1024
HD = 64
BLK = 64
NB = 16


EPS = 1e-05


def product(picked, weight, flipped):
    if flipped:
        return lax.dot_general(
            picked, weight, (((1,), (1,)), ((), ())), preferred_element_type=jnp.float32
        )
    return jnp.dot(picked, weight, preferred_element_type=jnp.float32)


def to_columns(moving, weight, flipped):
    gathered = lax.all_gather(moving, "col", axis=0, tiled=True)
    row_count = gathered.shape[0] // lax.axis_size("row")

    def term_rows(first_row, how_many):
        return product(gathered, weight, flipped)

    result = lax.psum_scatter(
        term_rows(jnp.int32(0), lax.axis_size("row") * row_count),
        "row",
        scatter_dimension=0,
        tiled=True,
    )
    return (result, gathered)


def to_rows(moving, weight, flipped):
    gathered = lax.all_gather(moving, "row", axis=0, tiled=True)
    row_count = gathered.shape[0] // lax.axis_size("col")

    def term_rows(first_row, how_many):
        return product(gathered, weight, flipped)

    return (
        lax.psum_scatter(
            term_rows(jnp.int32(0), lax.axis_size("col") * row_count),
            "col",
            scatter_dimension=0,
            tiled=True,
        ),
        gathered,
    )


def norm_sums(first_sum, second_sum):
    return lax.psum((first_sum, second_sum), "row")


def norm_forward(moving, gain_row, shift_row):
    totals, squares = norm_sums(jnp.sum(moving, axis=1), jnp.sum(moving * moving, axis=1))
    center = totals / D
    spread = squares / D - center * center
    inverse = lax.rsqrt(spread + EPS)
    normed = (moving - center[:, None]) * inverse[:, None]
    return (normed * gain_row + shift_row, normed, inverse)


def norm_backward(upstream, normed, inverse, gain_row):
    scaled = upstream * gain_row
    first_sum, second_sum = norm_sums(jnp.sum(scaled, axis=1), jnp.sum(scaled * normed, axis=1))
    return inverse[:, None] * (scaled - first_sum[:, None] / D - normed * (second_sum[:, None] / D))


def head_masks(random_blocks, global_blocks):
    block_ids = jnp.arange(NB, dtype=jnp.int32)
    nearby = jnp.abs(block_ids[:, None] - block_ids[None, :]) <= 1
    chosen = jnp.any(random_blocks[:, :, :, None] == block_ids[None, None, None, :], axis=2)
    marked = jnp.any(global_blocks[:, None] == block_ids[None, :], axis=0)
    block_table = nearby[None] | chosen | marked[None, None, :] | marked[None, :, None]
    return jnp.repeat(jnp.repeat(block_table, BLK, axis=1), BLK, axis=2)


def seq_logits(seq_queries, seq_keys, labels, pattern):
    same_doc = (labels[:, None] == labels[None, :]) & (labels[None, :] != 0)
    raw_scores = jnp.einsum(
        "qhd,khd->hqk", seq_queries, seq_keys, preferred_element_type=jnp.float32
    )
    return jnp.where(pattern & same_doc[None], raw_scores * (1.0 / math.sqrt(HD)), -1000000000.0)


def attend_forward(queries, key_block, value_block, segments, pattern):

    def one_seq(pieces):
        seq_queries, seq_keys, seq_values, labels = pieces
        logits = seq_logits(seq_queries, seq_keys, labels, pattern)
        row_peak = jnp.max(logits, axis=2, keepdims=True)
        exp_terms = jnp.exp(logits - row_peak)
        row_total = jnp.sum(exp_terms, axis=2, keepdims=True)
        softmax = (exp_terms / row_total).astype(jnp.bfloat16)
        attended = jnp.einsum(
            "hqk,khd->qhd", softmax, seq_values, preferred_element_type=jnp.float32
        )
        live_rows = (labels != 0).astype(jnp.float32)
        return (attended * live_rows[:, None, None], (row_peak + jnp.log(row_total))[:, :, 0])

    return lax.map(one_seq, (queries, key_block, value_block, segments))


def attend_backward(queries, key_block, value_block, segments, pattern, grad_heads, log_total):

    def one_seq(pieces):
        seq_queries, seq_keys, seq_values, labels, seq_grads, seq_log = pieces
        logits = seq_logits(seq_queries, seq_keys, labels, pattern)
        softmax = jnp.exp(logits - seq_log[:, :, None])
        grad_probs = jnp.einsum(
            "qhd,khd->hqk", seq_grads, seq_values, preferred_element_type=jnp.float32
        )
        grad_values = jnp.einsum(
            "hqk,qhd->khd",
            softmax.astype(jnp.bfloat16),
            seq_grads,
            preferred_element_type=jnp.float32,
        )
        inner_sum = jnp.sum(softmax * grad_probs, axis=2, keepdims=True)
        grad_raw = (softmax * (grad_probs - inner_sum) * (1.0 / math.sqrt(HD))).astype(jnp.bfloat16)
        grad_queries = jnp.einsum(
            "hqk,khd->qhd", grad_raw, seq_keys, preferred_element_type=jnp.float32
        )
        grad_keys = jnp.einsum(
            "hqk,qhd->khd", grad_raw, seq_queries, preferred_element_type=jnp.float32
        )
        return (grad_queries, grad_keys, grad_values)

    return lax.map(one_seq, (queries, key_block, value_block, segments, grad_heads, log_total))


def gelu_tanh(values):
    return jax.nn.gelu(values, approximate=True)


def weight_grad(left, right):
    return lax.dot_general(
        left, right, (((0,), (0,)), ((), ())), preferred_element_type=jnp.float32
    )


def body(
    inputs,
    gain_first,
    shift_first,
    w_query,
    w_key,
    w_value,
    w_output,
    gain_second,
    shift_second,
    w_up,
    bias_up,
    w_down,
    bias_down,
    segments,
    random_blocks,
    global_blocks,
    cotangent,
):
    seq_count, seq_len = segments.shape
    head_width = w_query.shape[1]
    heads_here = random_blocks.shape[0]
    seq_shape = (seq_count, seq_len, heads_here, HD)
    pattern = head_masks(random_blocks, global_blocks)
    live_tokens = (segments != 0).reshape(-1)
    x_first = inputs.astype(jnp.float32)
    first_full, normed_one, inverse_one = norm_forward(x_first, gain_first, shift_first)
    first_low = first_full.astype(jnp.bfloat16)
    stacked = jnp.concatenate((w_query, w_key, w_value), axis=1)
    projected, first_all = to_columns(first_low, stacked, False)
    proj_low = projected.astype(jnp.bfloat16)
    queries = proj_low[:, :head_width].reshape(seq_shape)
    key_block = proj_low[:, head_width : 2 * head_width].reshape(seq_shape)
    value_block = proj_low[:, 2 * head_width :].reshape(seq_shape)
    heads_out, log_total = attend_forward(queries, key_block, value_block, segments, pattern)
    heads_low = heads_out.reshape(-1, head_width).astype(jnp.bfloat16)
    mixed_out, heads_all = to_rows(heads_low, w_output, False)
    residual = x_first + mixed_out
    second_full, normed_two, inverse_two = norm_forward(residual, gain_second, shift_second)
    second_low = second_full.astype(jnp.bfloat16)
    upward, second_all = to_columns(second_low, w_up, False)
    upward = upward + bias_up
    hidden_low = gelu_tanh(upward).astype(jnp.bfloat16)
    downward, hidden_all = to_rows(hidden_low, w_down, False)
    layer_out = (residual + (downward + bias_down)).astype(jnp.bfloat16)
    grad_hidden, cotangent_all = to_columns(cotangent, w_down, True)
    activated, pull_back = jax.vjp(gelu_tanh, upward)
    grad_upward = pull_back(grad_hidden)[0].astype(jnp.bfloat16)
    grad_second, grad_upward_all = to_rows(grad_upward, w_up, True)
    grad_residual = cotangent.astype(jnp.float32) + norm_backward(
        grad_second, normed_two, inverse_two, gain_second
    )
    grad_mixed = grad_residual.astype(jnp.bfloat16)
    grad_heads, grad_mixed_all = to_columns(grad_mixed, w_output, True)
    grad_heads = jnp.where(live_tokens[:, None], grad_heads, 0.0).astype(jnp.bfloat16)
    grad_queries, grad_keys, grad_values = attend_backward(
        queries, key_block, value_block, segments, pattern, grad_heads.reshape(seq_shape), log_total
    )
    grad_proj = jnp.concatenate(
        (
            grad_queries.reshape(-1, head_width),
            grad_keys.reshape(-1, head_width),
            grad_values.reshape(-1, head_width),
        ),
        axis=1,
    ).astype(jnp.bfloat16)
    grad_first, grad_proj_all = to_rows(grad_proj, stacked, True)
    grad_inputs = grad_residual + norm_backward(grad_first, normed_one, inverse_one, gain_first)
    grad_stacked = weight_grad(first_all, grad_proj_all)
    grad_out_weight = weight_grad(heads_all, grad_mixed_all)
    grad_up_weight = weight_grad(second_all, grad_upward_all)
    grad_down_weight = weight_grad(hidden_all, cotangent_all)
    grad_up_bias = jnp.sum(grad_upward_all, axis=0, dtype=jnp.float32)
    grad_down_bias = jnp.sum(cotangent_all, axis=0, dtype=jnp.float32)
    gain_terms = lax.psum(
        (
            jnp.sum(grad_first * normed_one, axis=0),
            jnp.sum(grad_first, axis=0),
            jnp.sum(grad_second * normed_two, axis=0),
            jnp.sum(grad_second, axis=0),
        ),
        ("dp", "col"),
    )
    summed = (
        lax.psum(grad_stacked.astype(jnp.bfloat16), "dp").astype(jnp.float32),
        lax.psum(grad_out_weight.astype(jnp.bfloat16), "dp").astype(jnp.float32),
        lax.psum(grad_up_weight.astype(jnp.bfloat16), "dp").astype(jnp.float32),
        lax.psum(grad_down_weight.astype(jnp.bfloat16), "dp").astype(jnp.float32),
        lax.psum(grad_up_bias.astype(jnp.bfloat16), "dp").astype(jnp.float32),
        lax.psum(grad_down_bias.astype(jnp.bfloat16), "dp").astype(jnp.float32),
    )
    return (
        layer_out,
        grad_inputs,
        gain_terms[0],
        gain_terms[1],
        summed[0][:, :head_width],
        summed[0][:, head_width : 2 * head_width],
        summed[0][:, 2 * head_width :],
        summed[1],
        gain_terms[2],
        gain_terms[3],
        summed[2],
        summed[4],
        summed[3],
        summed[5],
    )


def solution(mesh):
    placed = (
        P(("dp", "col"), "row"),
        P("row"),
        P("row"),
        P("row", "col"),
        P("row", "col"),
        P("row", "col"),
        P("col", "row"),
        P("row"),
        P("row"),
        P("row", "col"),
        P("col"),
        P("col", "row"),
        P("row"),
        P(("dp", "row"), None),
        P("col", None, None),
        P(),
        P(("dp", "col"), "row"),
    )
    return jax.shard_map(
        body,
        mesh=mesh,
        in_specs=placed,
        out_specs=(
            P(("dp", "col"), "row"),
            P(("dp", "col"), "row"),
            P("row"),
            P("row"),
            P("row", "col"),
            P("row", "col"),
            P("row", "col"),
            P("col", "row"),
            P("row"),
            P("row"),
            P("row", "col"),
            P("col"),
            P("col", "row"),
            P("row"),
        ),
        check_vma=False,
    )
```

profile of v0, /device:TPU:0, one launch (start us, length us, event | category | flops | bytes accessed | tf_op | source)
XLA Modules:
  0.0 1793.3 jit_solution(9766734146856281676)
XLA Ops:
  7.3 2.0 convert_reduce_fusion
  9.2 12.7 all-reduce.4
  22.6 2.5 fusion.36
  25.3 33.4 %all-gather.9.cloned.1.call-done = bf16[4096,256]{1,0:T(8,128)(2,1)} async-done(((bf16[2048,256]{1,0:T(8,128)(2,1)}), bf16[4096,256]{1,0:T(8,128)(2,1)}) %all-gather.9.cloned.1.call-update) | async-done | bytes 2097168 | tf_op jit(solution)/shard_map/all_gather | solution.py:26
  58.7 11.8 fusion.66
  72.4 1.8 compare_and_fusion
  74.2 178.4 %reduce-scatter.9.cloned.1.call-done = f32[1024,1536]{1,0:T(8,128)} async-done(((f32[4096,1536]{1,0:T(8,128)}), f32[1024,1536]{1,0:T(8,128)}) %reduce-scatter.9.cloned.1.call-update) | async-done | bytes 6291472 | tf_op jit(solution)/shard_map/reduce_scatter | solution.py:32
  252.6 3.2 convert_element_type.96
  255.7 1.3 fusion.63
  257.0 2.3 copy.57
  259.3 1.3 copy.56
  261.1 16.7 fusion.65
  277.8 13.0 fusion.2
  290.8 14.6 multiply_convert_fusion.2
  305.5 34.5 %all-gather.11.cloned.1.call-done = bf16[4096,512]{0,1:T(8,128)(2,1)} async-done(((bf16[1024,512]{0,1:T(8,128)(2,1)}), bf16[4096,512]{0,1:T(8,128)(2,1)}) %all-gather.11.cloned.1.call-update) | async-done | bytes 4194320 | tf_op jit(solution)/shard_map/all_gather | solution.py:42
  340.1 5.5 fusion.67
  346.3 53.9 %reduce-scatter.11.cloned.1.call-done = f32[2048,256]{1,0:T(8,128)} async-done(((f32[4096,256]{1,0:T(8,128)}), f32[2048,256]{1,0:T(8,128)}) %reduce-scatter.11.cloned.1.call-update) | async-done | bytes 2097168 | tf_op jit(solution)/shard_map/reduce_scatter | solution.py:49
  400.2 2.5 fusion.61
  402.7 11.0 all-reduce.3
  413.6 1.5 add_convert_fusion.1
  415.2 19.5 %all-gather.17.cloned.1.call-done = bf16[4096,256]{1,0:T(8,128)(2,1)} async-done(((bf16[2048,256]{1,0:T(8,128)(2,1)}), bf16[4096,256]{1,0:T(8,128)(2,1)}) %all-gather.17.cloned.1.call-update) | async-done | bytes 2097168 | tf_op jit(solution)/shard_map/all_gather | solution.py:26
  434.7 18.6 %fusion.70 = f32[4096,2048]{1,0:T(8,128)} fusion(bf16[4096,256]{1,0:T(8,128)(2,1)} %all-gather.17.cloned.1.call-done, bf16[2048,256]{1,0:T(8,128)(2,1)} %param.28), kind=kOutput, calls=%fused_computation.97 | convolution fusion | flops 4294967296 | bytes 36700160 | tf_op jit(solution)/shard_map/dot_general | solution.py:19
  453.3 16.5 all-gather.13.cloned.1.call-done
  469.8 20.5 %fusion.68 = f32[4096,2048]{1,0:T(8,128)} fusion(bf16[4096,256]{1,0:T(8,128)(2,1)} %all-gather.13.cloned.1.call-done, bf16[256,2048]{1,0:T(8,128)(2,1)S(1)} %copy-done), kind=kOutput, calls=%fused_computation.95 | convolution fusion | flops 4294967296 | bytes 36700160 | tf_op jit(solution)/shard_map/dot_general | solution.py:22
  490.4 214.3 %reduce-scatter.17.cloned.1.call-done = f32[1024,2048]{1,0:T(8,128)} async-done(((f32[4096,2048]{1,0:T(8,128)}), f32[1024,2048]{1,0:T(8,128)}) %reduce-scatter.17.cloned.1.call-update) | async-done | bytes 8388624 | tf_op jit(solution)/shard_map/reduce_scatter | solution.py:32
  704.7 234.9 %reduce-scatter.13.cloned.1.call-done = f32[1024,2048]{1,0:T(8,128)} async-done(((f32[4096,2048]{1,0:T(8,128)}), f32[1024,2048]{1,0:T(8,128)}) %reduce-scatter.13.cloned.1.call-update) | async-done | bytes 8388624 | tf_op jit(solution)/shard_map/reduce_scatter | solution.py:32
  939.7 13.0 fusion.17
  953.7 105.0 %all-gather.19.cloned.1.call-done = bf16[4096,2048]{1,0:T(8,128)(2,1)} async-done(((bf16[1024,2048]{1,0:T(8,128)(2,1)}), bf16[4096,2048]{1,0:T(8,128)(2,1)}) %all-gather.19.cloned.1.call-update) | async-done | bytes 16777232 | tf_op jit(solution)/shard_map/all_gather | solution.py:42
  1058.8 10.3 fusion.71
  1069.2 96.9 %all-gather.15.cloned.1.call-done = bf16[4096,2048]{1,0:T(8,128)(2,1)} async-done(((bf16[1024,2048]{1,0:T(8,128)(2,1)}), bf16[4096,2048]{1,0:T(8,128)(2,1)}) %all-gather.15.cloned.1.call-update) | async-done | bytes 16777232 | tf_op jit(solution)/shard_map/all_gather | solution.py:42
  1166.1 10.1 fusion.69
  1176.3 46.5 %reduce-scatter.19.cloned.1.call-done = f32[2048,256]{1,0:T(8,128)} async-done(((f32[4096,256]{1,0:T(8,128)}), f32[2048,256]{1,0:T(8,128)}) %reduce-scatter.19.cloned.1.call-update) | async-done | bytes 2097168 | tf_op jit(solution)/shard_map/reduce_scatter | solution.py:49
  1222.8 2.5 multiply_reduce_fusion.1
  1225.3 11.1 all-reduce.2
  1236.5 42.9 %reduce-scatter.15.cloned.1.call-done = f32[2048,256]{1,0:T(8,128)} async-done(((f32[4096,256]{1,0:T(8,128)}), f32[2048,256]{1,0:T(8,128)}) %reduce-scatter.15.cloned.1.call-update) | async-done | bytes 2097168 | tf_op jit(solution)/shard_map/reduce_scatter | solution.py:49
  1279.4 5.8 fusion.62
  1285.3 33.2 %all-gather.21.cloned.1.call-done = bf16[4096,256]{1,0:T(8,128)(2,1)} async-done(((bf16[2048,256]{1,0:T(8,128)(2,1)}), bf16[4096,256]{1,0:T(8,128)(2,1)}) %all-gather.21.cloned.1.call-update) | async-done | bytes 2097168 | tf_op jit(solution)/shard_map/all_gather | solution.py:26
  1318.5 6.1 fusion.72
  1324.8 71.3 %reduce-scatter.21.cloned.1.call-done = f32[1024,512]{1,0:T(8,128)} async-done(((f32[4096,512]{1,0:T(8,128)}), f32[1024,512]{1,0:T(8,128)}) %reduce-scatter.21.cloned.1.call-update) | async-done | bytes 2097168 | tf_op jit(solution)/shard_map/reduce_scatter | solution.py:32
  1396.1 1.8 select_convert_fusion
  1398.5 31.5 %fusion.43 = bf16[8,64,1024]{2,1,0:T(8,128)(2,1)} fusion(bf16[1024,8,64]{0,2,1:T(8,128)(2,1)S(1)} %bitcast.68, f32[8,1024,1024]{1,2,0:T(8,128)} %get-tuple-element.118, f32[8,1024]{1,0:T(8,128)S(1)} %log_add_fusion, bf16[1024,8,64]{0,2,1:T(8,128)(2,1)S(1)} %bitcast.63, bf16[1024,8,64]{0,2,1:T(8,128)(2,1)} %bitcast.72), kind=kOutput, calls=%fused_computation.61 | convolution fusion | flops 3280479232 | bytes 37781504 | tf_op jit(solution)/shard_map/while/body/eval_jaxpr/hqk,khd->qhd/dot_general | solution.py:130
  1430.0 33.5 %fusion.48 = bf16[8,64,1024]{2,1,0:T(8,128)(2,1)} fusion(bf16[1024,8,64]{0,2,1:T(8,128)(2,1)S(1)} %bitcast.70, f32[8,1024,1024]{1,2,0:T(8,128)} %get-tuple-element.118, f32[8,1024]{1,0:T(8,128)S(1)} %log_add_fusion, bf16[1024,8,64]{0,2,1:T(8,128)(2,1)S(1)} %bitcast.64, bf16[1024,8,64]{0,2,1:T(8,128)(2,1)} %bitcast.73), kind=kOutput, calls=%fused_computation.62 | convolution fusion | flops 3280479232 | bytes 37781504 | tf_op jit(solution)/shard_map/while/body/eval_jaxpr/hqk,qhd->khd/dot_general | solution.py:133
  1463.5 13.5 fusion.53
  1477.0 2.9 pad_maximum_fusion
  1480.2 12.8 convolution_convert_fusion
  1493.0 10.3 convolution_convert_fusion.1
  1503.3 2.0 convolution_convert_fusion.3
  1505.3 56.8 %all-gather.23.cloned.1.call-done = bf16[4096,1536]{0,1:T(8,128)(2,1)} async-done(((bf16[1024,1536]{0,1:T(8,128)(2,1)}), bf16[4096,1536]{0,1:T(8,128)(2,1)}) %all-gather.23.cloned.1.call-update) | async-done | bytes 12582928 | tf_op jit(solution)/shard_map/all_gather | solution.py:42
  1562.1 7.5 convolution_convert_fusion.2
  1570.0 10.2 fusion.73
  1580.2 1.6 copy-done.4
  1582.3 9.8 reduce_sum.166
  1592.1 12.6 all-reduce.5
  1605.3 0.6 convert_element_type.117
  1605.9 85.5 %all-reduce.9.cloned.1.call-done = (bf16[256,1536]{1,0:T(8,128)(2,1)}, bf16[512,256]{1,0:T(8,128)(2,1)}, bf16[256,2048]{1,0:T(8,128)(2,1)}, bf16[2048,256]{1,0:T(8,128)(2,1)}) async-done(((bf16[256,1536]{1,0:T(8,128)(2,1)}, bf16[512,256]{1,0:T(8,128)(2,1)}, bf16[256,2048]{1,0:T(8,128)(2,1)}, bf16[2048,256]{1,0:T(8,128)(2,1)}), (bf16[256,1536]{1,0:T(8,128)(2,1)}, bf16[512,256]{1,0:T(8,128)(2,1)}, ...) | async-done | bytes 3145744 | tf_op jit(solution)/shard_map/psum | solution.py:235
  1691.4 1.9 convert_element_type.114
  1693.3 2.9 convert_element_type.116
  1696.2 1.5 convert_element_type.119
  1697.7 1.2 fusion.64
  1698.9 48.1 %reduce-scatter.23.cloned.1.call-done = f32[2048,256]{1,0:T(8,128)} async-done(((f32[4096,256]{1,0:T(8,128)}), f32[2048,256]{1,0:T(8,128)}) %reduce-scatter.23.cloned.1.call-update) | async-done | bytes 2097168 | tf_op jit(solution)/shard_map/reduce_scatter | solution.py:49
  1747.0 2.7 fusion.41
  1749.7 10.7 all-reduce.1
  1760.5 21.0 %all-reduce = (f32[256]{0:T(256)}, f32[256]{0:T(256)}, f32[256]{0:T(256)}, f32[256]{0:T(256)}) all-reduce(f32[256]{0:T(256)S(1)} %get-tuple-element.62, f32[256]{0:T(256)S(1)} %get-tuple-element.78, f32[256]{0:T(256)S(1)} %get-tuple-element.60, f32[256]{0:T(256)S(1)} %get-tuple-element.77), channel_id=1, replica_groups=mesh['dp'=4,'row'=4,'col'=2] {'dp','col'}, use_global_device_ids=true, to_apply=%region_30.31 | all-reduce | flops 1024 | bytes 8192 | tf_op jit(solution)/shard_map/psum | solution.py:225
  1781.5 5.0 fusion.40
  (128 shorter events, 7.9 us)
Async XLA Ops:
  7.2 462.6 %copy-start = (bf16[256,2048]{1,0:T(8,128)(2,1)S(1)}, bf16[256,2048]{1,0:T(8,128)(2,1)}, u32[]{:S(2)}) copy-start(bf16[256,2048]{1,0:T(8,128)(2,1)} %param.26) | copy-start | bytes 3145732
  7.2 18.0 %copy-start.19 = (bf16[256,512]{1,0:T(8,128)(2,1)S(1)}, bf16[256,512]{1,0:T(8,128)(2,1)}, u32[]{:S(2)}) copy-start(bf16[256,512]{1,0:T(8,128)(2,1)} %param.20) | copy-start | bytes 786436
  7.2 18.0 %copy-start.20 = (bf16[256,512]{1,0:T(8,128)(2,1)S(1)}, bf16[256,512]{1,0:T(8,128)(2,1)}, u32[]{:S(2)}) copy-start(bf16[256,512]{1,0:T(8,128)(2,1)} %param.21) | copy-start | bytes 786436
  7.2 18.1 %copy-start.21 = (bf16[256,512]{1,0:T(8,128)(2,1)S(1)}, bf16[256,512]{1,0:T(8,128)(2,1)}, u32[]{:S(2)}) copy-start(bf16[256,512]{1,0:T(8,128)(2,1)} %param.22) | copy-start | bytes 786436
  7.2 51.5 %all-gather.9.cloned.1.call-start = ((), (), s32[]{:S(2)}) async-start(), calls=%async_computation.8 | async-start | bytes 3145728 | tf_op jit(solution)/shard_map/all_gather | solution.py:26
  22.0 0.6 copy-start.22
  22.0 0.6 copy-start.24
  25.1 227.4 %reduce-scatter.9.cloned.1.call-start = ((), (), s32[]{:S(2)}) async-start(), calls=%async_computation.9 | async-start | bytes 31457280 | tf_op jit(solution)/shard_map/reduce_scatter | solution.py:32
  25.3 45.1 %copy-start.12 = (bf16[256,1536]{1,0:T(8,128)(2,1)}, bf16[256,1536]{1,0:T(8,128)(2,1)S(1)}, u32[]{:S(2)}) copy-start(bf16[256,1536]{1,0:T(8,128)(2,1)S(1)} %constant_dynamic-update-slice_fusion) | copy-start | bytes 2359300
  70.4 0.7 copy-start.27
  70.4 0.7 copy-start.35
  70.4 1.9 copy-start.26
  70.5 269.6 %all-gather.11.cloned.1.call-start = ((), (), s32[]{:S(2)}) async-start(), calls=%async_computation.10 | async-start | bytes 5242880 | tf_op jit(solution)/shard_map/all_gather | solution.py:42
  72.4 180.2 %copy-start.29 = (pred[1024]{0:T(1024)(128)(4,1)}, pred[1024]{0:T(1024)(128)(4,1)S(1)}, u32[]{:S(2)}) copy-start(pred[1024]{0:T(1024)(128)(4,1)S(1)} %compare_reduce_fusion) | copy-start | bytes 3076
  261.1 29.7 %copy-start.17 = (bf16[1024,512]{0,1:T(8,128)(2,1)}, bf16[1024,512]{0,1:T(8,128)(2,1)S(1)}, u32[]{:S(2)}) copy-start(bf16[1024,512]{0,1:T(8,128)(2,1)S(1)} %copy.53) | copy-start | bytes 3145732
  290.8 49.3 %copy-start.16 = (bf16[512,256]{1,0:T(8,128)(2,1)S(1)}, bf16[512,256]{1,0:T(8,128)(2,1)}, u32[]{:S(2)}) copy-start(bf16[512,256]{1,0:T(8,128)(2,1)} %param.23) | copy-start | bytes 786436
  305.5 94.7 %reduce-scatter.11.cloned.1.call-start = ((), (), s32[]{:S(2)}) async-start(), calls=%async_computation.11 | async-start | bytes 6291456 | tf_op jit(solution)/shard_map/reduce_scatter | solution.py:49
  345.6 68.0 %copy-start.28 = (f32[256]{0:T(256)S(1)}, f32[256]{0:T(256)}, u32[]{:S(2)}) copy-start(f32[256]{0:T(256)} %param.24) | copy-start | bytes 3076
  345.6 68.0 %copy-start.33 = (f32[256]{0:T(256)S(1)}, f32[256]{0:T(256)}, u32[]{:S(2)}) copy-start(f32[256]{0:T(256)} %param.25) | copy-start | bytes 3076
  345.7 89.0 %all-gather.17.cloned.1.call-start = ((), (), s32[]{:S(2)}) async-start(), calls=%async_computation.16 | async-start | bytes 3145728 | tf_op jit(solution)/shard_map/all_gather | solution.py:26
  346.2 123.5 %all-gather.13.cloned.1.call-start = ((), (), s32[]{:S(2)}) async-start(), calls=%async_computation.12 | async-start | bytes 3145728 | tf_op jit(solution)/shard_map/all_gather | solution.py:26
  415.2 289.6 %reduce-scatter.17.cloned.1.call-start = ((), (), s32[]{:S(2)}) async-start(), calls=%async_computation.17 | async-start | bytes 41943040 | tf_op jit(solution)/shard_map/reduce_scatter | solution.py:32
  453.3 486.4 %reduce-scatter.13.cloned.1.call-start = ((), (), s32[]{:S(2)}) async-start(), calls=%async_computation.13 | async-start | bytes 41943040 | tf_op jit(solution)/shard_map/reduce_scatter | solution.py:32
  490.3 449.4 %copy-start.32 = (f32[2048]{0:T(1024)S(1)}, f32[2048]{0:T(1024)}, u32[]{:S(2)}) copy-start(f32[2048]{0:T(1024)} %param.27) | copy-start | bytes 24580
  490.3 568.4 %all-gather.19.cloned.1.call-start = ((), (), s32[]{:S(2)}) async-start(), calls=%async_computation.18 | async-start | bytes 20971520 | tf_op jit(solution)/shard_map/all_gather | solution.py:42
  952.7 213.4 %all-gather.15.cloned.1.call-start = ((), (), s32[]{:S(2)}) async-start(), calls=%async_computation.14 | async-start | bytes 20971520 | tf_op jit(solution)/shard_map/all_gather | solution.py:42
  953.3 269.5 %reduce-scatter.19.cloned.1.call-start = ((), (), s32[]{:S(2)}) async-start(), calls=%async_computation.19 | async-start | bytes 6291456 | tf_op jit(solution)/shard_map/reduce_scatter | solution.py:49
  1069.1 97.0 %copy-start.14 = (bf16[2048,256]{1,0:T(8,128)(2,1)S(1)}, bf16[2048,256]{1,0:T(8,128)(2,1)}, u32[]{:S(2)}) copy-start(bf16[2048,256]{1,0:T(8,128)(2,1)} %param.28) | copy-start | bytes 3145732
  1069.1 210.2 %reduce-scatter.15.cloned.1.call-start = ((), (), s32[]{:S(2)}) async-start(), calls=%async_computation.15 | async-start | bytes 6291456 | tf_op jit(solution)/shard_map/reduce_scatter | solution.py:49
  1176.2 103.2 %copy-start.6 = (bf16[2048,256]{1,0:T(8,128)(2,1)S(1)}, bf16[2048,256]{1,0:T(8,128)(2,1)}, u32[]{:S(2)}) copy-start(bf16[2048,256]{1,0:T(8,128)(2,1)} %param.33) | copy-start | bytes 3145732
  1176.2 103.2 %copy-start.34 = (f32[256]{0:T(256)S(1)}, f32[256]{0:T(256)}, u32[]{:S(2)}) copy-start(f32[256]{0:T(256)} %param.29) | copy-start | bytes 3076
  1176.2 142.3 %all-gather.21.cloned.1.call-start = ((), (), s32[]{:S(2)}) async-start(), calls=%async_computation.20 | async-start | bytes 3145728 | tf_op jit(solution)/shard_map/all_gather | solution.py:26
  1285.2 110.9 %reduce-scatter.21.cloned.1.call-start = ((), (), s32[]{:S(2)}) async-start(), calls=%async_computation.21 | async-start | bytes 10485760 | tf_op jit(solution)/shard_map/reduce_scatter | solution.py:32
  1324.5 71.6 %copy-start.30 = (pred[1024]{0:T(1024)(128)(4,1)S(1)}, pred[1024]{0:T(1024)(128)(4,1)}, u32[]{:S(2)}) copy-start(pred[1024]{0:T(1024)(128)(4,1)} %copy-done.29) | copy-start | bytes 3076
  1324.6 73.9 %copy-start.7 = (bf16[1024,512]{0,1:T(8,128)(2,1)S(1)}, bf16[1024,512]{0,1:T(8,128)(2,1)}, u32[]{:S(2)}) copy-start(bf16[1024,512]{0,1:T(8,128)(2,1)} %copy.57) | copy-start | bytes 3145732
  1324.6 237.5 %all-gather.23.cloned.1.call-start = ((), (), s32[]{:S(2)}) async-start(), calls=%async_computation.22 | async-start | bytes 15728640 | tf_op jit(solution)/shard_map/all_gather | solution.py:42
  1398.5 31.5 %copy-start.8 = (bf16[1024,512]{0,1:T(8,128)(2,1)S(1)}, bf16[1024,512]{0,1:T(8,128)(2,1)}, u32[]{:S(2)}) copy-start(bf16[1024,512]{0,1:T(8,128)(2,1)} %copy.56) | copy-start | bytes 3145732
  1463.5 13.5 copy-start.18
  1479.9 13.1 copy-start.3
  1479.9 211.5 %all-reduce.9.cloned.1.call-start = ((), (), s32[]{:S(2)}) async-start(), calls=%async_computation.24 | async-start | bytes 6291456 | tf_op jit(solution)/shard_map/psum | solution.py:235
  1493.0 10.3 copy-start.5
  1493.0 10.3 copy-start.10
  1503.3 58.8 %copy-start.9 = (bf16[4096,256]{1,0:T(8,128)(2,1)S(1)}, bf16[4096,256]{1,0:T(8,128)(2,1)}, u32[]{:S(2)}) copy-start(bf16[4096,256]{1,0:T(8,128)(2,1)} %all-gather.9.cloned.1.call-done) | copy-start | bytes 6291460
  1505.3 64.6 %copy-start.13 = (bf16[256,1536]{1,0:T(8,128)(2,1)S(1)}, bf16[256,1536]{1,0:T(8,128)(2,1)}, u32[]{:S(2)}) copy-start(bf16[256,1536]{1,0:T(8,128)(2,1)} %copy-done.12) | copy-start | bytes 2359300
  1569.6 177.3 %reduce-scatter.23.cloned.1.call-start = ((), (), s32[]{:S(2)}) async-start(), calls=%async_computation.23 | async-start | bytes 6291456 | tf_op jit(solution)/shard_map/reduce_scatter | solution.py:49
  1580.2 1.6 copy-start.4
  1691.4 4.8 copy-start.15
  1691.4 6.3 copy-start.11
  1693.3 53.7 %copy-start.2 = (bf16[2048,256]{1,0:T(8,128)(2,1)S(1)}, bf16[2048,256]{1,0:T(8,128)(2,1)}, u32[]{:S(2)}) copy-start(bf16[2048,256]{1,0:T(8,128)(2,1)} %param.17) | copy-start | bytes 3145732
  1693.3 53.7 %copy-start.23 = (f32[2048]{0:T(1024)S(1)}, f32[2048]{0:T(1024)}, u32[]{:S(2)}) copy-start(f32[2048]{0:T(1024)} %copy-done.22) | copy-start | bytes 24580
  1693.3 53.7 %copy-start.25 = (f32[2048]{0:T(1024)S(1)}, f32[2048]{0:T(1024)}, u32[]{:S(2)}) copy-start(f32[2048]{0:T(1024)} %copy-done.24) | copy-start | bytes 24580
  1693.3 53.7 %copy-start.31 = (f32[256]{0:T(256)S(1)}, f32[256]{0:T(256)}, u32[]{:S(2)}) copy-start(f32[256]{0:T(256)} %param.18) | copy-start | bytes 3076
  1747.0 39.5 %copy-start.1 = (bf16[256,2048]{1,0:T(8,128)(2,1)S(1)}, bf16[256,2048]{1,0:T(8,128)(2,1)}, u32[]{:S(2)}) copy-start(bf16[256,2048]{1,0:T(8,128)(2,1)} %param.26) | copy-start | bytes 3145732
Sparse Core Ops, SparseCore 0:
  25.3 33.3 all-gather.8
  70.6 181.9 reduce-scatter.8
  305.6 34.4 all-gather.10
  345.8 54.3 reduce-scatter.10
  401.6 33.0 all-gather.16
  436.7 33.0 all-gather.12
  472.4 232.3 reduce-scatter.16
  707.3 232.3 reduce-scatter.12
  952.8 105.9 all-gather.18
  1060.2 105.8 all-gather.14
  1168.4 54.3 reduce-scatter.18
  1225.0 54.3 reduce-scatter.14
  1285.4 33.0 all-gather.20
  1324.7 71.3 reduce-scatter.20
  1480.0 82.0 all-gather.22
  1569.8 121.6 all-reduce.8
  1693.6 53.3 reduce-scatter.22
where the time goes:
time: 1800 us; the launch traced here: 1790 us
  waiting for transfers between devices  1370 us (76%)
  matrix products  235 us (13%)
  blocking collectives  79.2 us (4%)
  other arithmetic  78.4 us (4%)
    reduce_scatter x4, waiting for transfers between devices, to_columns(): lax.psum_scatter(term_rows(jnp.int32(0), lax.axis_size('row') * row_count...  699 us
    all_gather x4, waiting for transfers between devices, to_rows(): gathered = lax.all_gather(moving, 'row', axis=0, tiled=True)  293 us
    reduce_scatter x4, waiting for transfers between devices, to_rows(): lax.psum_scatter(term_rows(jnp.int32(0), lax.axis_size('col') * row_count...  191 us
    all_gather x4, waiting for transfers between devices, to_columns(): gathered = lax.all_gather(moving, 'col', axis=0, tiled=True)  103 us
    psum x1, waiting for transfers between devices, body(): lax.psum(grad_stacked.astype(jnp.bfloat16), 'dp').astype(jnp.float32)  85.5 us
    dot_general x4, matrix products, product(): return jnp.dot(picked, weight, preferred_element_type=jnp.float32)  47.9 us
    psum x4, blocking collectives, norm_sums(): return lax.psum((first_sum, second_sum), 'row')  45.5 us
    dot_general x4, matrix products, product(): lax.dot_general(picked, weight, (((1,), (1,)), ((), ())), preferred_eleme...  45.2 us
  transfers between devices with their start and end apart: 17, of which 17 were waited for; matrix products, arithmetic and copies ran while one was open for 7% of the time, Pallas kernels for 0%

commit v1 on v0

--- a/solution.py
+++ b/solution.py
@@ -3,6 +3,8 @@
 import jax
 import jax.numpy as jnp
 from jax import lax
+from jax.experimental import pallas as pl
+from jax.experimental.pallas import tpu as pltpu
 from jax.sharding import PartitionSpec as P
 
 D = 1024
@@ -92,7 +94,7 @@
     return jnp.where(pattern & same_doc[None], raw_scores * (1.0 / math.sqrt(HD)), -1000000000.0)
 
 
-def attend_forward(queries, key_block, value_block, segments, pattern):
+def attend_plain(queries, key_block, value_block, segments, pattern):
 
     def one_seq(pieces):
         seq_queries, seq_keys, seq_values, labels = pieces
@@ -110,7 +112,7 @@
     return lax.map(one_seq, (queries, key_block, value_block, segments))
 
 
-def attend_backward(queries, key_block, value_block, segments, pattern, grad_heads, log_total):
+def attend_plain_backward(queries, key_block, value_block, segments, pattern, grad_heads, log_total):
 
     def one_seq(pieces):
         seq_queries, seq_keys, seq_values, labels, seq_grads, seq_log = pieces
@@ -182,7 +184,7 @@
     queries = proj_low[:, :head_width].reshape(seq_shape)
     key_block = proj_low[:, head_width : 2 * head_width].reshape(seq_shape)
     value_block = proj_low[:, 2 * head_width :].reshape(seq_shape)
-    heads_out, log_total = attend_forward(queries, key_block, value_block, segments, pattern)
+    heads_out, log_total = attend_plain(queries, key_block, value_block, segments, pattern)
     heads_low = heads_out.reshape(-1, head_width).astype(jnp.bfloat16)
     mixed_out, heads_all = to_rows(heads_low, w_output, False)
     residual = x_first + mixed_out
@@ -203,7 +205,7 @@
     grad_mixed = grad_residual.astype(jnp.bfloat16)
     grad_heads, grad_mixed_all = to_columns(grad_mixed, w_output, True)
     grad_heads = jnp.where(live_tokens[:, None], grad_heads, 0.0).astype(jnp.bfloat16)
-    grad_queries, grad_keys, grad_values = attend_backward(
+    grad_queries, grad_keys, grad_values = attend_plain_backward(
         queries, key_block, value_block, segments, pattern, grad_heads.reshape(seq_shape), log_total
     )
     grad_proj = jnp.concatenate(
@@ -257,45 +259,489 @@
     )
 
 
+SWAP = [(0, 1), (1, 0)]
+LOW = jnp.bfloat16
+FULL = jnp.float32
+TILE = 256
+BIG = 1e30
+
+
+def swap(array, axis):
+    return lax.ppermute(array, axis, SWAP)
+
+
+def dot_nn(left, right):
+    return lax.dot_general(left, right, (((1,), (0,)), ((), ())), preferred_element_type=FULL)
+
+
+def dot_nt(left, right):
+    return lax.dot_general(left, right, (((1,), (1,)), ((), ())), preferred_element_type=FULL)
+
+
+def dot_tn(left, right):
+    return lax.dot_general(left, right, (((0,), (0,)), ((), ())), preferred_element_type=FULL)
+
+
+def attention_extras(labels, random_blocks, global_blocks):
+    length = labels.shape[0]
+    blocks = length // BLK
+    block_ids = jnp.arange(blocks, dtype=jnp.int32)
+    nearby = jnp.abs(block_ids[:, None] - block_ids[None, :]) <= 1
+    chosen = jnp.any(random_blocks[:, :, :, None] == block_ids[None, None, None, :], axis=2)
+    marked = jnp.any(global_blocks[:, None] == block_ids[None, :], axis=0)
+    table = nearby[None] | chosen | marked[None, None, :] | marked[None, :, None]
+    heads = table.shape[0]
+    lane = jnp.arange(HD, dtype=jnp.int32)
+    place = jnp.arange(length, dtype=jnp.int32) // BLK
+    doc_lane = blocks + jnp.where(labels == 0, 4, labels - 1)
+    row_extra = ((lane[None, :] == place[:, None]) | (lane[None, :] == doc_lane[:, None])).astype(LOW)
+    table_keys = jnp.pad(jnp.swapaxes(table, 1, 2), ((0, 0), (0, 0), (0, HD - blocks)), constant_values=True)
+    table_keys = jnp.repeat(table_keys, BLK, axis=1)
+    is_doc = (lane >= blocks) & (lane <= blocks + 4)
+    doc_bad = is_doc[None, :] & (lane[None, :] != doc_lane[:, None])
+    doc_bad = doc_bad | (lane[None, :] == blocks + 4)
+    key_extra = jnp.where(table_keys & ~doc_bad[None], 0.0, -BIG)
+    key_extra = jnp.where((lane >= blocks + 5) & (lane <= blocks + 7), 1.0, key_extra).astype(LOW)
+    rows = jnp.stack((jnp.pad(row_extra, ((0, 0), (HD, 0))), jnp.pad(row_extra, ((0, 0), (0, HD)))))
+    even = jnp.pad(key_extra[0::2], ((0, 0), (0, 0), (HD, 0)))
+    odd = jnp.pad(key_extra[1::2], ((0, 0), (0, 0), (0, HD)))
+    keys = jnp.stack((even, odd), axis=1).reshape(heads, length, 2 * HD)
+    tiles = length // TILE
+    known = labels[None, :] == jnp.arange(1, 5, dtype=jnp.int32)[:, None]
+    present = jnp.any(known.reshape(4, tiles, TILE), axis=2)
+    wanted = jnp.any(present[:, :, None] & known[:, None, :], axis=0)
+    spots = jnp.arange(length, dtype=jnp.int32)
+    first = jnp.min(jnp.where(wanted, spots[None, :], length - 1), axis=1)
+    last = jnp.max(jnp.where(wanted, spots[None, :], 0), axis=1)
+    start = first // 128
+    count = jnp.maximum((last + 1 - start * 128 + 255) // 256, 1)
+    start = jnp.minimum(start, length // 128 - 2 * count)
+    return rows, keys, jnp.stack((start, count)).astype(jnp.int32)
+
+
+def attend_forward_kernel(where_ref, q_ref, k_ref, v_ref, rows_ref, keys_ref, out_ref, kept_ref, kk, vv):
+    length = q_ref.shape[0]
+    lane = lax.broadcasted_iota(jnp.int32, (length, 2 * HD), 1)
+    for e in range(2):
+        data = (lane < HD) if e == 0 else (lane >= HD)
+        kk[e] = jnp.where(data, k_ref[...], keys_ref[e])
+        vv[e] = jnp.where(data, v_ref[...], jnp.ones_like(v_ref[...]))
+    tile_lane = lax.broadcasted_iota(jnp.int32, (TILE, 2 * HD), 1)
+
+    def one_tile(t, carry):
+        rows = pl.ds(pl.multiple_of(t * TILE, TILE), TILE)
+        start = pl.multiple_of(where_ref[0, t] * 128, 128)
+        count = where_ref[1, t]
+        q_pair = q_ref[rows, :] * jnp.bfloat16(1.0 / math.sqrt(HD))
+        for n in range(1, length // TILE + 1):
+
+            @pl.when(count == n)
+            def _():
+                span = pl.ds(start, n * TILE)
+                outs = []
+                for e in range(2):
+                    data = (tile_lane < HD) if e == 0 else (tile_lane >= HD)
+                    base = HD if e == 0 else 0
+                    extra = rows_ref[e, rows, :]
+                    q_one = jnp.where(data, q_pair, extra)
+                    logits = dot_nt(q_one, kk[e, span, :])
+                    peak = jnp.max(logits, axis=1, keepdims=True)
+                    terms = jnp.exp(logits - peak)
+                    mixed = dot_nn(terms.astype(LOW), vv[e, span, :])
+                    total = pltpu.roll(mixed, HD, 1)
+                    outs.append(mixed / total)
+                    total_one = jnp.max(jnp.where(data, total, 0.0), axis=1, keepdims=True)
+                    padded = jnp.max(
+                        jnp.where(tile_lane == base + 20, extra.astype(FULL), 0.0), axis=1, keepdims=True
+                    )
+                    log_total = jnp.where(padded > 0.5, 0.0, -(peak + jnp.log(total_one)))
+                    high = log_total.astype(LOW).astype(FULL)
+                    middle = (log_total - high).astype(LOW).astype(FULL)
+                    low = log_total - high - middle
+                    packed = jnp.where(tile_lane == base + 21, high, q_one.astype(FULL))
+                    packed = jnp.where(tile_lane == base + 22, middle, packed)
+                    packed = jnp.where(tile_lane == base + 23, low, packed)
+                    kept_ref[e, rows, :] = packed.astype(LOW)
+                joined = jnp.where(tile_lane < HD, outs[0], outs[1])
+                out_ref[rows, :] = jnp.where(padded > 0.5, 0.0, joined).astype(LOW)
+
+        return carry
+
+    lax.fori_loop(0, length // TILE, one_tile, 0)
+
+
+def attend_forward(qkv, rows_extra, keys_extra, where_table):
+    length, width = qkv.shape
+    pairs = width // (3 * 2 * HD)
+    wide = 2 * HD
+    return pl.pallas_call(
+        attend_forward_kernel,
+        out_shape=(
+            jax.ShapeDtypeStruct((length, width // 3), LOW),
+            jax.ShapeDtypeStruct((2 * pairs, length, wide), LOW),
+        ),
+        grid_spec=pltpu.PrefetchScalarGridSpec(
+            num_scalar_prefetch=1,
+            grid=(pairs,),
+            in_specs=[
+                pl.BlockSpec((length, wide), lambda p, w: (0, p)),
+                pl.BlockSpec((length, wide), lambda p, w: (0, pairs + p)),
+                pl.BlockSpec((length, wide), lambda p, w: (0, 2 * pairs + p)),
+                pl.BlockSpec((2, length, wide), lambda p, w: (0, 0, 0)),
+                pl.BlockSpec((2, length, wide), lambda p, w: (p, 0, 0)),
+            ],
+            out_specs=(
+                pl.BlockSpec((length, wide), lambda p, w: (0, p)),
+                pl.BlockSpec((2, length, wide), lambda p, w: (p, 0, 0)),
+            ),
+            scratch_shapes=[pltpu.VMEM((2, length, wide), LOW), pltpu.VMEM((2, length, wide), LOW)],
+        ),
+        name="attend_forward",
+        cost_estimate=pl.CostEstimate(
+            flops=8 * pairs * length * length * HD, bytes_accessed=16 * length * width, transcendentals=0
+        ),
+    )(where_table, qkv, qkv, qkv, rows_extra, keys_extra)
+
+
+def attend_backward_kernel(
+    where_ref, kept_ref, k_ref, v_ref, keys_ref, heads_ref, grads_ref, dq_ref, dk_ref, dv_ref, kk, va, dk_sum, dv_sum
+):
+    length = k_ref.shape[0]
+    lane = lax.broadcasted_iota(jnp.int32, (length, 2 * HD), 1)
+    for e in range(2):
+        data = (lane < HD) if e == 0 else (lane >= HD)
+        base = HD if e == 0 else 0
+        kk[e] = jnp.where(data, k_ref[...], keys_ref[e])
+        ones = jnp.where((lane == base) | (lane == base + 1), 1.0, 0.0).astype(LOW)
+        va[e] = jnp.where(data, v_ref[...], ones)
+    dk_sum[...] = jnp.zeros_like(dk_sum)
+    dv_sum[...] = jnp.zeros_like(dv_sum)
+    tile_lane = lax.broadcasted_iota(jnp.int32, (TILE, 2 * HD), 1)
+
+    def one_tile(t, carry):
+        rows = pl.ds(pl.multiple_of(t * TILE, TILE), TILE)
+        start = pl.multiple_of(where_ref[0, t] * 128, 128)
+        count = where_ref[1, t]
+        grads = grads_ref[rows, :]
+        both = grads.astype(FULL) * heads_ref[rows, :].astype(FULL)
+        for n in range(1, length // TILE + 1):
+
+            @pl.when(count == n)
+            def _():
+                span = pl.ds(start, n * TILE)
+                outs = []
+                for e in range(2):
+                    data = (tile_lane < HD) if e == 0 else (tile_lane >= HD)
+                    base = HD if e == 0 else 0
+                    inner = -jnp.sum(jnp.where(data, both, 0.0), axis=1, keepdims=True)
+                    high = inner.astype(LOW).astype(FULL)
+                    only = jnp.where(data, grads, jnp.zeros_like(grads))
+                    packed = jnp.where(tile_lane == base, high, only.astype(FULL))
+                    packed = jnp.where(tile_lane == base + 1, inner - high, packed).astype(LOW)
+                    q_one = kept_ref[e, rows, :]
+                    q_only = jnp.where(data, q_one, jnp.zeros_like(q_one))
+                    probs = jnp.exp(dot_nt(kk[e, span, :], q_one))
+                    grad_raw = (probs * dot_nt(va[e, span, :], packed)).astype(LOW)
+                    dv_sum[span, :] += dot_nn(probs.astype(LOW), only)
+                    dk_sum[span, :] += dot_nn(grad_raw, q_only)
+                    outs.append(dot_tn(grad_raw, kk[e, span, :]))
+                joined = jnp.where(tile_lane < HD, outs[0], outs[1])
+                dq_ref[rows, :] = (joined * (1.0 / math.sqrt(HD))).astype(LOW)
+
+        return carry
+
+    lax.fori_loop(0, length // TILE, one_tile, 0)
+    dk_ref[...] = dk_sum[...].astype(LOW)
+    dv_ref[...] = dv_sum[...].astype(LOW)
+
+
+def attend_backward(kept, qkv, keys_extra, heads, grads, where_table):
+    length, width = qkv.shape
+    pairs = width // (3 * 2 * HD)
+    wide = 2 * HD
+    one = jax.ShapeDtypeStruct((length, width // 3), LOW)
+    lanes = pl.BlockSpec((length, wide), lambda p, w: (0, p))
+    stacked = pl.BlockSpec((2, length, wide), lambda p, w: (p, 0, 0))
+    return pl.pallas_call(
+        attend_backward_kernel,
+        out_shape=(one, one, one),
+        grid_spec=pltpu.PrefetchScalarGridSpec(
+            num_scalar_prefetch=1,
+            grid=(pairs,),
+            in_specs=[
+                stacked,
+                pl.BlockSpec((length, wide), lambda p, w: (0, pairs + p)),
+                pl.BlockSpec((length, wide), lambda p, w: (0, 2 * pairs + p)),
+                stacked,
+                lanes,
+                lanes,
+            ],
+            out_specs=(lanes, lanes, lanes),
+            scratch_shapes=[
+                pltpu.VMEM((2, length, wide), LOW),
+                pltpu.VMEM((2, length, wide), LOW),
+                pltpu.VMEM((length, wide), FULL),
+                pltpu.VMEM((length, wide), FULL),
+            ],
+        ),
+        name="attend_backward",
+        cost_estimate=pl.CostEstimate(
+            flops=20 * pairs * length * length * HD, bytes_accessed=20 * length * width, transcendentals=0
+        ),
+    )(where_table, kept, qkv, qkv, keys_extra, heads, grads)
+
+
+def swap_features(part):
+    got = swap(part, "core")
+    n = got.shape[1] // 4
+    return jnp.concatenate((got[:, n : 2 * n], got[:, :n], got[:, 3 * n :], got[:, 2 * n : 3 * n]), axis=1)
+
+
+def pick(pair, index):
+    return lax.dynamic_index_in_dim(pair, index, 0, keepdims=False)
+
+
+def ordered(own, other, index):
+    flip = index == 0
+    return jnp.stack((jnp.where(flip, own, other), jnp.where(flip, other, own)))
+
+
+def plane_gather(block, first_axis, second_axis):
+    near = {first_axis: swap(block, first_axis), second_axis: swap(block, second_axis)}
+    across = swap(near[first_axis], second_axis)
+    return block, near["col"], near["y"], across
+
+
+def plane_reduce(own, at_col, at_y, across, first_axis, second_axis):
+    near = {"col": at_col, "y": at_y}
+    arrived = swap(across, first_axis)
+    direct = swap(near[first_axis], first_axis)
+    onward = (near[second_axis].astype(FULL) + arrived.astype(FULL)).astype(LOW)
+    last = swap(onward, second_axis)
+    return (own.astype(FULL) + direct.astype(FULL) + last.astype(FULL)).astype(LOW)
+
+
+def fast_body(
+    inputs, gain_first, shift_first, w_query, w_key, w_value, w_output, gain_second, shift_second,
+    w_up, bias_up, w_down, bias_down, segments, random_blocks, global_blocks, cotangent,
+):
+    y_at, core_at, col_at = (lax.axis_index(name) for name in ("y", "core", "col"))
+    length = segments.shape[1]
+    narrow = inputs.shape[1]
+    inputs_pair = inputs.reshape(2, length, narrow)
+    cot_pair = cotangent.reshape(2, length, narrow)
+    x_own = pick(inputs_pair, y_at)
+    x_y = swap(pick(inputs_pair, 1 - y_at), "y")
+
+    def half(weight, axis, index):
+        size = weight.shape[axis] // 2
+        return lax.dynamic_slice_in_dim(weight, index * size, size, axis)
+
+    def chip_block(weights, axis, join):
+        mine = jnp.concatenate([half(w, axis, core_at) for w in weights], axis=axis)
+        theirs = swap(jnp.concatenate([half(w, axis, 1 - core_at) for w in weights], axis=axis), "core")
+        return jnp.concatenate((mine, theirs), axis=join)
+
+    qkv_block = chip_block((w_query, w_key, w_value), 1, 0)
+    qkv_own, qkv_x, qkv_y, qkv_xy = plane_gather(qkv_block, "y", "col")
+    x_core, x_ycore = swap(x_own, "core"), swap(x_y, "core")
+
+    vectors = jnp.stack((gain_first, shift_first, gain_second, shift_second, bias_down))
+    vectors = jnp.concatenate((vectors, swap(vectors, "core")), axis=1)
+    vectors = jnp.concatenate((vectors, swap(vectors, "y")), axis=1)
+    gain_one, shift_one, gain_two, shift_two, bias_low = (vectors[i] for i in range(5))
+    heads_half = half(random_blocks, 0, core_at)
+    hidden_bias = half(bias_up, 0, core_at)
+    small = jnp.concatenate((hidden_bias, heads_half.astype(FULL).reshape(-1)))
+    small = swap(small, "col")
+    hidden_bias_x = small[: hidden_bias.shape[0]]
+    heads_half_x = small[hidden_bias.shape[0] :].reshape(heads_half.shape).astype(jnp.int32)
+    moves = []
+    for y in range(2):
+        for core in range(2):
+            for col in range(2):
+                moves.append(((col * 2 + y) * 2 + core, (y * 2 + core) * 2 + col))
+    labels = lax.ppermute(segments, ("y", "core", "col"), moves)[0]
+    all_heads = jnp.concatenate((heads_half, heads_half_x), axis=0)
+    rows_extra, keys_extra, where_table = attention_extras(labels, all_heads, global_blocks)
+    near_heads = heads_half.shape[0]
+    live = (labels != 0)[:, None]
+
+    out_block = chip_block((w_output,), 0, 1)
+    up_block = chip_block((w_up,), 1, 0)
+    down_block = chip_block((w_down,), 0, 1)
+    out_own, out_x, out_y, out_xy = plane_gather(out_block, "col", "y")
+    up_own, up_x, up_y, up_xy = plane_gather(up_block, "col", "y")
+    down_own, down_x, down_y, down_xy = plane_gather(down_block, "y", "col")
+    cot_own = pick(cot_pair, y_at)
+    cot_y = swap(pick(cot_pair, 1 - y_at), "y")
+    cot = jnp.concatenate((cot_own, swap(cot_own, "core"), cot_y, swap(cot_y, "core")), axis=1)
+
+    x_full = jnp.concatenate((x_own, x_core, x_y, x_ycore), axis=1).astype(FULL)
+
+    def norm_stats(moving):
+        center = jnp.mean(moving, axis=1, keepdims=True)
+        spread = jnp.mean(moving * moving, axis=1, keepdims=True) - center * center
+        return center, lax.rsqrt(spread + EPS)
+
+    center_one, inverse_one = norm_stats(x_full)
+    normed_one = (x_full - center_one) * inverse_one
+    first = (normed_one * gain_one + shift_one).astype(LOW)
+
+    w_qkv = (jnp.concatenate((qkv_own, qkv_y), axis=0), jnp.concatenate((qkv_x, qkv_xy), axis=0))
+    qkv = [dot_nn(first, w).astype(LOW) for w in w_qkv]
+    keys_of = (keys_extra[:near_heads], keys_extra[near_heads:])
+    heads, kept = zip(*[attend_forward(qkv[i], rows_extra, keys_of[i], where_table) for i in range(2)])
+    w_out = (jnp.concatenate((out_own, out_y), axis=1), jnp.concatenate((out_x, out_xy), axis=1))
+    mixed_part = (dot_nn(heads[0], w_out[0]) + dot_nn(heads[1], w_out[1])).astype(LOW)
+    mixed = mixed_part.astype(FULL) + swap_features(mixed_part).astype(FULL)
+    residual = x_full + mixed
+    center_two, inverse_two = norm_stats(residual)
+    normed_two = (residual - center_two) * inverse_two
+    second = (normed_two * gain_two + shift_two).astype(LOW)
+
+    w_ups = (jnp.concatenate((up_own, up_y), axis=0), jnp.concatenate((up_x, up_xy), axis=0))
+    w_downs = (jnp.concatenate((down_own, down_y), axis=1), jnp.concatenate((down_x, down_xy), axis=1))
+    biases = (hidden_bias, hidden_bias_x)
+    low_part, second_part = 0.0, 0.0
+    up_grads, down_grads, bias_grads = [], [], []
+    for i in range(2):
+        upward = dot_nn(second, w_ups[i]) + biases[i]
+        activated, pull_back = jax.vjp(gelu_tanh, upward)
+        hidden = activated.astype(LOW)
+        grad_upward = pull_back(dot_nt(cot, w_downs[i]))[0].astype(LOW)
+        low_part = low_part + dot_nn(hidden, w_downs[i])
+        second_part = second_part + dot_nt(grad_upward, w_ups[i])
+        up_grads.append(dot_tn(second, grad_upward).astype(LOW))
+        down_grads.append(dot_tn(hidden, cot).astype(LOW))
+        bias_grads.append(jnp.sum(grad_upward, axis=0, dtype=FULL))
+
+    def own_columns(part):
+        low = part.astype(LOW)
+        n = narrow
+        mine = jnp.concatenate((low[:, :n], low[:, 2 * n : 3 * n]), axis=1)
+        theirs = swap(jnp.concatenate((low[:, n : 2 * n], low[:, 3 * n :]), axis=1), "core")
+        return mine.astype(FULL) + theirs.astype(FULL)
+
+    def mine_of(array):
+        return jnp.concatenate((array[..., :narrow], array[..., 2 * narrow : 3 * narrow]), axis=-1)
+
+    low_own = mine_of(residual) + own_columns(low_part) + mine_of(bias_low)
+
+    def to_shard(columns, dtype):
+        back = swap(columns[:, narrow:].astype(LOW), "y")
+        return ordered(columns[:, :narrow].astype(dtype), back.astype(dtype), y_at).reshape(2 * length, narrow)
+
+    layer_out = to_shard(low_own, LOW)
+
+    second_low = second_part.astype(LOW)
+    grad_second = second_low.astype(FULL) + swap_features(second_low).astype(FULL)
+    scaled = grad_second * gain_two
+    mean_one = jnp.mean(scaled, axis=1, keepdims=True)
+    mean_two = jnp.mean(scaled * normed_two, axis=1, keepdims=True)
+    grad_residual = cot.astype(FULL) + inverse_two * (scaled - mean_one - normed_two * mean_two)
+    grad_gain_two = jnp.sum(mine_of(grad_second * normed_two), axis=0)
+    grad_shift_two = jnp.sum(mine_of(grad_second), axis=0)
+    grad_mixed = grad_residual.astype(LOW)
+    grads = [jnp.where(live, dot_nt(grad_mixed, w), 0.0).astype(LOW) for w in w_out]
+    out_grads = [dot_tn(heads[i], grad_mixed).astype(LOW) for i in range(2)]
+    qkv_grads, first_part = [], 0.0
+    for i in range(2):
+        pieces = attend_backward(kept[i], qkv[i], keys_of[i], heads[i], grads[i], where_table)
+        joined = jnp.concatenate(pieces, axis=1)
+        qkv_grads.append(dot_tn(first, joined).astype(LOW))
+        first_part = first_part + dot_nt(joined, w_qkv[i])
+    scaled_part = first_part * gain_one
+    sums = jnp.stack((jnp.sum(scaled_part, axis=1), jnp.sum(scaled_part * normed_one, axis=1)))
+    sums = (sums + swap(sums, "core")) / (4 * narrow)
+    grad_first = own_columns(first_part)
+    normed_mine = mine_of(normed_one)
+    grad_x = inverse_one * (grad_first * mine_of(gain_one) - sums[0][:, None] - normed_mine * sums[1][:, None])
+    grad_inputs = to_shard(mine_of(grad_residual) + grad_x, FULL)
+    grad_gain_one = jnp.sum(grad_first * normed_mine, axis=0)
+    grad_shift_one = jnp.sum(grad_first, axis=0)
+
+    gains = jnp.stack((grad_gain_one, grad_shift_one, grad_gain_two, grad_shift_two)).reshape(4, 2, narrow)
+    down_bias = jnp.sum(cotangent, axis=0, dtype=FULL)
+    gains = jnp.stack([ordered(gains[i, 0], gains[i, 1], y_at) for i in range(4)])
+    bias_pair = ordered(down_bias, jnp.zeros_like(down_bias), y_at)
+    gains = jnp.concatenate((gains, bias_pair[None]), axis=0)
+    gains = jnp.stack((jnp.where(core_at == 0, gains, 0.0), jnp.where(core_at == 0, 0.0, gains)))
+    ups = ordered(bias_grads[0], bias_grads[1], col_at)
+    ups = jnp.stack((jnp.where(core_at == 0, ups, 0.0), jnp.where(core_at == 0, 0.0, ups)), axis=1)
+    flat = lax.psum(jnp.concatenate((gains.reshape(-1), ups.reshape(-1))), ("dp", "y", "core", "col"))
+    gains = flat[: gains.size].reshape(gains.shape)
+    gains = pick(pick(gains, core_at).swapaxes(0, 1), y_at)
+    grad_up_bias = pick(flat[gains.size * 4 :].reshape(2, -1), col_at)
+
+    h = narrow * 2
+
+    def finish(total, axis):
+        total = lax.psum(total, "dp")
+        size = total.shape[axis] // 2
+        keep = lax.slice_in_dim(total, 0, size, axis=axis)
+        got = swap(lax.slice_in_dim(total, size, 2 * size, axis=axis), "core")
+        return keep, got
+
+    def reduce_rows(pair, order):
+        return plane_reduce(pair[0][:h], pair[1][:h], pair[0][h:], pair[1][h:], *order)
+
+    def reduce_columns(pair, order):
+        return plane_reduce(pair[0][:, :h], pair[1][:, :h], pair[0][:, h:], pair[1][:, h:], *order)
+
+    def across_cores(keep, got, parts, axis):
+        out = []
+        size = keep.shape[axis] // parts
+        for i in range(parts):
+            a = lax.slice_in_dim(keep, i * size, (i + 1) * size, axis=axis)
+            b = lax.slice_in_dim(got, i * size, (i + 1) * size, axis=axis)
+            flip = core_at == 0
+            out.append(jnp.concatenate((jnp.where(flip, a, b), jnp.where(flip, b, a)), axis=axis).astype(FULL))
+        return out
+
+    (grad_down,) = across_cores(*finish(reduce_columns(down_grads, ("y", "col")), 1), 1, 0)
+    (grad_up,) = across_cores(*finish(reduce_rows(up_grads, ("col", "y")), 0), 1, 1)
+    (grad_out,) = across_cores(*finish(reduce_columns(out_grads, ("y", "col")), 1), 1, 0)
+    grad_qkv = across_cores(*finish(reduce_rows(qkv_grads, ("col", "y")), 0), 3, 1)
+    return (
+        layer_out, grad_inputs, gains[0], gains[1], *grad_qkv, grad_out, gains[2], gains[3],
+        grad_up, grad_up_bias, grad_down, gains[4],
+    )
+
+
+def whole_sequences(mesh):
+    return mesh.shape["row"] == 4 and mesh.shape["col"] == 2
+
+
+def placements(row):
+    tokens = P(("dp", "col"), row)
+    rows = P(row)
+    weight = P(row, "col")
+    turned = P("col", row)
+    placed = (
+        tokens, rows, rows, weight, weight, weight, turned, rows, rows, weight, P("col"), turned, rows,
+        P(("dp", *row), None), P("col", None, None), P(), tokens,
+    )
+    given = (
+        tokens, tokens, rows, rows, weight, weight, weight, turned, rows, rows, weight, P("col"), turned, rows,
+    )
+    return placed, given
+
+
 def solution(mesh):
-    placed = (
-        P(("dp", "col"), "row"),
-        P("row"),
-        P("row"),
-        P("row", "col"),
-        P("row", "col"),
-        P("row", "col"),
-        P("col", "row"),
-        P("row"),
-        P("row"),
-        P("row", "col"),
-        P("col"),
-        P("col", "row"),
-        P("row"),
-        P(("dp", "row"), None),
-        P("col", None, None),
-        P(),
-        P(("dp", "col"), "row"),
-    )
-    return jax.shard_map(
-        body,
-        mesh=mesh,
-        in_specs=placed,
-        out_specs=(
-            P(("dp", "col"), "row"),
-            P(("dp", "col"), "row"),
-            P("row"),
-            P("row"),
-            P("row", "col"),
-            P("row", "col"),
-            P("row", "col"),
-            P("col", "row"),
-            P("row"),
-            P("row"),
-            P("row", "col"),
-            P("col"),
-            P("col", "row"),
-            P("row"),
-        ),
-        check_vma=False,
-    )
+    sizes = mesh.shape
+    split = jax.sharding.Mesh(
+        mesh.devices.reshape(sizes["dp"], sizes["row"] // 2, 2, sizes["col"]), ("dp", "y", "core", "col")
+    )
+
+    def run(*arrays):
+        tokens, length = arrays[0].shape[0], arrays[13].shape[1]
+        if whole_sequences(mesh) and tokens == sizes["dp"] * sizes["col"] * 2 * length:
+            placed, given = placements(("y", "core"))
+            step = jax.shard_map(fast_body, mesh=split, in_specs=placed, out_specs=given, check_vma=False)
+        else:
+            placed, given = placements(("row",))
+            step = jax.shard_map(body, mesh=mesh, in_specs=placed, out_specs=given, check_vma=False)
+        return step(*arrays)
+
+    return run

time: 1800 us -> 571 us (0.32)
  waiting for transfers between devices: 1370 us -> 176 us
  matrix products: 235 us -> 88.5 us
  local copies, waits for them, and re-layouts: 10.8 us -> 69.5 us
  Pallas kernels: 0 us -> 51 us
  starting transfers between devices: 1.91 us -> 44.9 us
  blocking collectives: 79.2 us -> 45.6 us
    reduce_scatter x8 -> x0, waiting for transfers between devices: 890 us -> none  [the longest x4 699 us: to_columns(): lax.psum_scatter(term_rows(jnp.int32(0), lax.axis_size('row') * row_count...]
    all_gather x8 -> x0, waiting for transfers between devices: 396 us -> none  [the longest x4 293 us: to_rows(): gathered = lax.all_gather(moving, 'row', axis=0, tiled=True)]
    dot_general x17 -> x24, matrix products: 235 us -> 88.5 us  [the longest x8 35.4 us: dot_nt(): lax.dot_general(left, right, (((1,), (1,)), ((), ())), preferred_element_...]
    ppermute x0 -> x49, waiting for transfers between devices: none -> 118 us  [the longest x48 118 us: swap(): return lax.ppermute(array, axis, SWAP)]
    pallas_call x0 -> x4, Pallas kernels: none -> 51 us  [the longest x2 25.9 us: attend_backward(): pl.pallas_call(attend_backward_kernel, out_shape=(one, one, one), grid_sp...]
    ppermute x0 -> x49, starting transfers between devices: none -> 44.9 us  [the longest x48 43.6 us: swap(): return lax.ppermute(array, axis, SWAP)]
    psum x6 -> x1, blocking collectives: 79.2 us -> 45.6 us  [fast_body(): lax.psum(jnp.concatenate((gains.reshape(-1), ups.reshape(-1))), ('dp', 'y...]
    psum x1, waiting for transfers between devices: 85.5 us -> 57.6 us  [finish(): total = lax.psum(total, 'dp')]
  transfers between devices with their start and end apart: 17 -> 50, of which waited for: 17 -> 13; matrix products, arithmetic and copies ran while one was open for 7% -> 38% of each run, Pallas kernels for 0% -> 9%
where the time goes in v1:
time: 571 us; the launch traced here: 564 us
  waiting for transfers between devices  176 us (31%)
  matrix products  88.5 us (15%)
  other arithmetic  72.8 us (13%)
  local copies, waits for them, and re-layouts  69.5 us (12%)
  Pallas kernels  51 us (9%)
  blocking collectives  45.6 us (8%)
  starting transfers between devices  44.9 us (8%)
  between operations  15.7 us (3%)
    ppermute x48, waiting for transfers between devices, swap(): return lax.ppermute(array, axis, SWAP)  118 us
    psum x1, waiting for transfers between devices, finish(): total = lax.psum(total, 'dp')  57.6 us
    psum x1, blocking collectives, fast_body(): lax.psum(jnp.concatenate((gains.reshape(-1), ups.reshape(-1))), ('dp', 'y...  45.6 us
    ppermute x48, starting transfers between devices, swap(): return lax.ppermute(array, axis, SWAP)  43.6 us
    dot_general x8, matrix products, dot_nt(): lax.dot_general(left, right, (((1,), (1,)), ((), ())), preferred_element_...  35.4 us
    dot_general x8, matrix products, dot_nn(): lax.dot_general(left, right, (((1,), (0,)), ((), ())), preferred_element_...  31.6 us
    pallas_call x2, Pallas kernels, attend_backward(): pl.pallas_call(attend_backward_kernel, out_shape=(one, one, one), grid_sp...  25.9 us
    unnamed x202, local copies, waits for them, and re-layouts  25.2 us
  transfers between devices with their start and end apart: 50, of which 13 were waited for; matrix products, arithmetic and copies ran while one was open for 38% of the time, Pallas kernels for 9%

profile of v1, /device:TPU:0, one launch (start us, length us, event | category | flops | bytes accessed | tf_op | source)
XLA Modules:
  0.0 563.6 jit_solution(17547611328566772689)
XLA Ops:
  7.3 1.8 constant_dynamic-slice_fusion.15
  13.6 2.5 collective-permute-start.1
  23.5 2.1 constant_dynamic-slice_fusion.6
  25.6 2.2 constant_dynamic-slice_fusion.4
  47.1 3.0 collective-permute-done.13
  50.2 1.8 collective-permute-start.10
  52.2 1.9 pad_maximum_fusion.20
  58.3 7.0 %collective-permute-done.14 = bf16[256,512]{1,0:T(8,128)(2,1)S(1)} collective-permute-done((bf16[256,512]{1,0:T(8,128)(2,1)S(1)}, bf16[256,512]{1,0:T(8,128)(2,1)S(1)}, u32[]{:S(2)}, u32[]{:S(2)}) %collective-permute-start.14) | collective-permute-done | bytes 262176 | tf_op jit(solution)/shard_map/ppermute | solution.py:270
  67.4 1.7 collective-permute-start.19
  70.1 2.4 add_convert_fusion.4
  72.5 9.7 %collective-permute-done.7 = bf16[512,768]{1,0:T(8,128)(2,1)} collective-permute-done((bf16[512,768]{1,0:T(8,128)(2,1)}, bf16[512,768]{1,0:T(8,128)(2,1)}, u32[]{:S(2)}, u32[]{:S(2)}) %collective-permute-start.7) | collective-permute-done | bytes 786464 | tf_op jit(solution)/shard_map/ppermute | solution.py:270
  83.6 4.4 convolution_convert_fusion.7.q_ref.k_ref.v_ref
  87.9 12.2 %attend_forward.2 = (bf16[1024,256]{1,0:T(8,128)(2,1)}, bf16[4,1024,128]{2,1,0:T(8,128)(2,1)}) custom-call(s32[2,4]{1,0:T(2,128)} %pad_add_fusion.1.where_ref, bf16[1024,768]{1,0:T(8,128)(2,1)} %convolution_convert_fusion.7.q_ref.k_ref.v_ref, bf16[1024,768]{1,0:T(8,128)(2,1)} %convolution_convert_fusion.7.q_ref.k_ref.v_ref, ...), custom_call_target="tpu_custom_call" | custom-call | flops 1073741824 | bytes 12582912 | tf_op jit(solution)/shard_map/attend_forward/pallas_call | solution.py:377
  101.4 3.8 fusion.34
  105.2 18.3 %collective-permute-done.12 = bf16[512,768]{1,0:T(8,128)(2,1)} collective-permute-done((bf16[512,768]{1,0:T(8,128)(2,1)}, bf16[512,768]{1,0:T(8,128)(2,1)}, u32[]{:S(2)}, u32[]{:S(2)}) %collective-permute-start.12) | collective-permute-done | bytes 786464 | tf_op jit(solution)/shard_map/ppermute | solution.py:270
  124.7 3.1 convolution_convert_fusion.6.q_ref.k_ref.v_ref
  127.8 12.8 %attend_forward.3 = (bf16[1024,256]{1,0:T(8,128)(2,1)}, bf16[4,1024,128]{2,1,0:T(8,128)(2,1)}) custom-call(s32[2,4]{1,0:T(2,128)} %pad_add_fusion.1.where_ref, bf16[1024,768]{1,0:T(8,128)(2,1)} %convolution_convert_fusion.6.q_ref.k_ref.v_ref, bf16[1024,768]{1,0:T(8,128)(2,1)} %convolution_convert_fusion.6.q_ref.k_ref.v_ref, ...), custom_call_target="tpu_custom_call" | custom-call | flops 1073741824 | bytes 12582912 | tf_op jit(solution)/shard_map/attend_forward/pallas_call | solution.py:377
  140.6 3.3 add_convert_fusion.3
  144.0 2.0 copy.69
  151.6 2.0 copy.68
  159.6 14.6 %collective-permute-done.22 = bf16[1024,512]{1,0:T(8,128)(2,1)} collective-permute-done((bf16[1024,512]{1,0:T(8,128)(2,1)}, bf16[1024,512]{1,0:T(8,128)(2,1)}, u32[]{:S(2)}, u32[]{:S(2)}) %collective-permute-start.22) | collective-permute-done | bytes 1048608 | tf_op jit(solution)/shard_map/ppermute | solution.py:270
  175.9 7.7 %collective-permute-done.21 = bf16[512,1024]{1,0:T(8,128)(2,1)} collective-permute-done((bf16[512,1024]{1,0:T(8,128)(2,1)}, bf16[512,1024]{1,0:T(8,128)(2,1)}, u32[]{:S(2)}, u32[]{:S(2)}) %collective-permute-start.21) | collective-permute-done | bytes 1048608 | tf_op jit(solution)/shard_map/ppermute | solution.py:270
  184.9 10.8 %collective-permute-done.23 = bf16[1024,512]{1,0:T(8,128)(2,1)S(1)} collective-permute-done((bf16[1024,512]{1,0:T(8,128)(2,1)}, bf16[1024,512]{1,0:T(8,128)(2,1)S(1)}, u32[]{:S(2)}, u32[]{:S(2)}) %collective-permute-start.23) | collective-permute-done | bytes 1048608 | tf_op jit(solution)/shard_map/ppermute | solution.py:270
  195.9 1.8 fusion.70
  197.7 1.8 fusion.59
  200.2 2.4 fusion.76
  202.7 4.6 convolution_convert_fusion
  208.5 2.4 fusion.28
  211.0 4.6 convolution_convert_fusion.1
  218.0 7.5 %convert_reduce_fusion.1 = (f32[1024]{0:T(1024)S(1)}, bf16[1024,1024]{1,0:T(8,128)(2,1)}) fusion(f32[1024,1024]{1,0:T(8,128)S(1)} %fusion.76, f32[1024]{0:T(1024)S(1)} %slice.410, bf16[1024,1024]{1,0:T(8,128)(2,1)S(1)} %constant_dynamic-update-slice_fusion.6, bf16[1024,256]{0,1:T(8,128)(2,1)S(1)} %collective-permute-done.28, ...), kind=kOutput, calls=%fused_computation.24 | convolution fusion | flops 2179988480 | bytes 10493952 | tf_op jit(solution)/shard_map/dot_general | solution.py:278
  225.5 3.9 convolution_convert_fusion.2
  231.9 7.9 %convert_reduce_fusion.2 = (f32[1024]{0:T(1024)S(1)}, bf16[1024,1024]{1,0:T(8,128)(2,1)}) fusion(f32[1024,1024]{1,0:T(8,128)S(1)} %fusion.28, f32[1024]{0:T(1024)S(1)} %copy-done.72, bf16[1024,512]{1,0:T(8,128)(2,1)} %collective-permute-done.19, bf16[1024,256]{1,0:T(8,128)(2,1)S(1)} %copy-done.54, bf16[1024,256]{1,0:T(8,128)(2,1)S(1)} %copy-done.21, ...), kind=kOutput, calls=%fused_computation.25 | convolution fusion | flops 2186279936 | bytes 10493952 | tf_op jit(solution)/shard_map/dot_general | solution.py:278
  239.7 4.1 fusion.27
  243.8 2.4 add_convert_fusion
  246.4 7.2 %fusion.26 = f32[1024,1024]{0,1:T(8,128)} fusion(bf16[1024,512]{1,0:T(8,128)(2,1)} %collective-permute-done.19, bf16[1024,256]{1,0:T(8,128)(2,1)S(1)} %copy-done.54, bf16[1024,256]{1,0:T(8,128)(2,1)S(1)} %copy-done.21, f32[1024,1024]{1,0:T(8,128)} %copy-done.90, f32[1024]{0:T(1024)S(1)} %copy-done.72), kind=kOutput, calls=%fused_computation.102 | convolution fusion | flops 2164260864 | bytes 10489856 | tf_op jit(solution)/shard_map/dot_general | solution.py:274
  253.6 5.0 add_convert_fusion.1
  261.7 2.3 convolution_convert_fusion.3
  270.5 8.5 %collective-permute-done.25 = bf16[1024,256]{0,1:T(8,128)(2,1)S(1)} collective-permute-done((bf16[1024,256]{0,1:T(8,128)(2,1)S(1)}, bf16[1024,256]{0,1:T(8,128)(2,1)S(1)}, u32[]{:S(2)}, u32[]{:S(2)}) %collective-permute-start.25) | collective-permute-done | bytes 524320 | tf_op jit(solution)/shard_map/ppermute | solution.py:270
  281.1 2.3 copy.61
  283.3 1.8 fusion.68
  286.1 6.9 %multiply_reduce_fusion.4 = (f32[1024]{0:T(1024)S(1)}, f32[1024]{0:T(1024)S(1)}, f32[1024,1024]{0,1:T(8,128)}, f32[1024,1024]{0,1:T(8,128)}) fusion(f32[1024]{0:T(1024)S(1)} %bitcast.190, bf16[1024,256]{0,1:T(8,128)(2,1)S(1)} %get-tuple-element.77, bf16[1024,256]{0,1:T(8,128)(2,1)S(1)} %get-tuple-element.78, bf16[1024,256]{0,1:T(8,128)(2,1)S(1)} %get-tuple-element.79, ...), kind=kLoop, calls=%fused_computation.42 | loop fusion | flops 17823744 | bytes 16797696 | tf_op jit(solution)/shard_map/reduce_sum | solution.py:640
  293.1 7.7 %fusion.60 = (bf16[1024,1024]{0,1:T(8,128)(2,1)S(1)}, f32[1024,1024]{0,1:T(8,128)}) fusion(f32[1024]{0:T(1024)S(1)} %broadcast_multiply_fusion, f32[1024,1024]{0,1:T(8,128)S(1)} %copy-done.3, f32[1024]{0:T(1024)S(1)} %get-tuple-element.145, f32[1024]{0:T(1024)S(1)} %broadcast_multiply_fusion.1, f32[1024]{0:T(1024)S(1)} %bitcast.191, ...), kind=kLoop, calls=%fused_computation.279 | loop fusion | flops 28311552 | bytes 16797696 | tf_op jit(solution)/shard_map/convert_element_type | solution.py:645
  307.2 13.2 %attend_backward.3 = (bf16[1024,256]{1,0:T(8,128)(2,1)}, bf16[1024,256]{1,0:T(8,128)(2,1)}, bf16[1024,256]{1,0:T(8,128)(2,1)}) custom-call(s32[2,4]{1,0:T(2,128)} %pad_add_fusion.1.where_ref, bf16[4,1024,128]{2,1,0:T(8,128)(2,1)} %get-tuple-element.30.kept_ref, bf16[1024,768]{1,0:T(8,128)(2,1)} %convolution_convert_fusion.6.q_ref.k_ref.v_ref, ...), custom_call_target="tpu_custom_call" | custom-call | flops 2684354560 | bytes 15728640 | tf_op jit(solution)/shard_map/attend_backward/pallas_call | solution.py:465
  324.9 1.8 convolution_convert_fusion.4
  328.9 2.5 fusion.20.grads_ref
  331.4 12.8 %attend_backward.2 = (bf16[1024,256]{1,0:T(8,128)(2,1)}, bf16[1024,256]{1,0:T(8,128)(2,1)}, bf16[1024,256]{1,0:T(8,128)(2,1)}) custom-call(s32[2,4]{1,0:T(2,128)} %pad_add_fusion.1.where_ref, bf16[4,1024,128]{2,1,0:T(8,128)(2,1)} %get-tuple-element.26.kept_ref, bf16[1024,768]{1,0:T(8,128)(2,1)} %convolution_convert_fusion.7.q_ref.k_ref.v_ref, ...), custom_call_target="tpu_custom_call" | custom-call | flops 2684354560 | bytes 15728640 | tf_op jit(solution)/shard_map/attend_backward/pallas_call | solution.py:465
  344.2 1.9 constant_dynamic-update-slice_fusion.10
  348.5 1.9 fusion.62
  352.1 3.2 fusion.57
  355.3 6.2 %multiply_reduce_fusion.3 = (f32[1024]{0:T(1024)S(1)}, f32[1024]{0:T(1024)S(1)}, bf16[1024,1024]{0,1:T(8,128)(2,1)}, f32[1024,1024]{0,1:T(8,128)}) fusion(f32[1024]{0:T(1024)S(1)} %bitcast.202, f32[1024]{0:T(1024)S(1)} %get-tuple-element.150, f32[1024]{0:T(1024)S(1)} %copy-done.76, bf16[1024,256]{0,1:T(8,128)(2,1)S(1)} %copy-done.10, ...), kind=kOutput, calls=%fused_computation.41 | convolution fusion | flops 1627387904 | bytes 15749120 | tf_op jit(solution)/shard_map/dot_general | solution.py:278
  362.6 2.9 fusion.67
  371.5 4.8 collective-permute-start.34
  376.4 2.9 add_convert_fusion.5
  379.6 3.1 add_convert_fusion.7
  382.7 1.8 convolution_convert_fusion.5
  384.5 10.3 %collective-permute-done.34 = bf16[512,768]{1,0:T(8,128)(2,1)S(1)} collective-permute-done((bf16[512,768]{1,0:T(8,128)(2,1)S(1)}, bf16[512,768]{1,0:T(8,128)(2,1)S(1)}, u32[]{:S(2)}, u32[]{:S(2)}) %collective-permute-start.34) | collective-permute-done | bytes 786464 | tf_op jit(solution)/shard_map/ppermute | solution.py:270
  396.1 2.1 collective-permute-start.39
  398.3 16.4 %collective-permute-done.39 = bf16[256,512]{1,0:T(8,128)(2,1)S(1)} collective-permute-done((bf16[256,512]{1,0:T(8,128)(2,1)S(1)}, bf16[256,512]{1,0:T(8,128)(2,1)S(1)}, u32[]{:S(2)}, u32[]{:S(2)}) %collective-permute-start.39) | collective-permute-done | bytes 262176 | tf_op jit(solution)/shard_map/ppermute | solution.py:270
  417.4 3.6 fusion.19
  421.3 45.6 %psum.35 = f32[9216]{0:T(1024)S(1)} all-reduce(f32[9216]{0:T(1024)S(1)} %pad_maximum_fusion.27), channel_id=1, replica_groups=mesh['dp'=4,'y'=2,'core'=2,'col'=2] {'dp','y','core','col'}, use_global_device_ids=true, to_apply=%region_21.22 | all-reduce | flops 9216 | bytes 73728 | tf_op jit(solution)/shard_map/psum | solution.py:672
  467.0 2.3 collective-permute-start.32
  470.6 10.2 %collective-permute-done.32 = bf16[1024,256]{0,1:T(8,128)(2,1)S(1)} collective-permute-done((bf16[1024,256]{0,1:T(8,128)(2,1)S(1)}, bf16[1024,256]{0,1:T(8,128)(2,1)S(1)}, u32[]{:S(2)}, u32[]{:S(2)}) %collective-permute-start.32) | collective-permute-done | bytes 524320 | tf_op jit(solution)/shard_map/ppermute | solution.py:270
  481.9 57.6 %all-reduce.8.cloned.1.call-done = (bf16[512,768]{1,0:T(8,128)(2,1)}, bf16[256,512]{1,0:T(8,128)(2,1)}, bf16[512,1024]{1,0:T(8,128)(2,1)}, bf16[1024,512]{1,0:T(8,128)(2,1)}) async-done(((bf16[512,768]{1,0:T(8,128)(2,1)}, bf16[256,512]{1,0:T(8,128)(2,1)}, bf16[512,1024]{1,0:T(8,128)(2,1)}, bf16[1024,512]{1,0:T(8,128)(2,1)}), (bf16[512,768]{1,0:T(8,128)(2,1)}, bf16[256,512]{1,0:T(8,128)(2,1)}, ...) | async-done | bytes 3145744 | tf_op jit(solution)/shard_map/psum | solution.py:680
  544.2 1.8 copy.64
  (421 shorter events, 122.7 us)
Async XLA Ops:
  7.2 532.3 %all-reduce.8.cloned.1.call-start = ((), (), s32[]{:S(2)}) async-start(), calls=%async_computation | async-start | bytes 6291456 | tf_op jit(solution)/shard_map/psum | solution.py:680
  10.9 39.2 %collective-permute-start.6 = (bf16[256,768]{1,0:T(8,128)(2,1)}, bf16[256,768]{1,0:T(8,128)(2,1)}, u32[]{:S(2)}, u32[]{:S(2)}) collective-permute-start(bf16[256,768]{1,0:T(8,128)(2,1)} %pad_maximum_fusion.23), channel_id=1, source_target_pairs={{0,2},{2,0},{1,3},{3,1},{4,6},{6,4},{5,7},{7,5},{8,10},{10,8},{9,1... | collective-permute-start | bytes 1179656 | tf_op jit(solution)/shard_map/ppermute | solution.py:270
  13.6 38.3 %collective-permute-start.1 = (bf16[1024,256]{0,1:T(8,128)(2,1)}, bf16[1024,256]{0,1:T(8,128)(2,1)S(1)}, u32[]{:S(2)}, u32[]{:S(2)}) collective-permute-start(bf16[1024,256]{0,1:T(8,128)(2,1)} %bitcast.2), channel_id=1, source_target_pairs={{0,4},{4,0},{1,5},{5,1},{2,6},{6,2},{3,7},{7,3},{8,12},{12,8},{9,1... | collective-permute-start | bytes 1572872 | tf_op jit(solution)/shard_map/ppermute | solution.py:270
  16.8 20.5 %collective-permute-start.4 = (f32[5,256]{1,0:T(8,128)}, f32[5,256]{1,0:T(8,128)}, u32[]{:S(2)}, u32[]{:S(2)}) collective-permute-start(f32[5,256]{1,0:T(8,128)} %stack.135), channel_id=1, source_target_pairs={{0,2},{2,0},{1,3},{3,1},{4,6},{6,4},{5,7},{7,5},{8,10},{10,8},{9,1... | collective-permute-start | bytes 15368 | tf_op jit(solution)/shard_map/ppermute | solution.py:270
  17.1 10.7 %copy-start.60 = (s32[4,16,3]{2,1,0:T(8,128)}, s32[4,16,3]{2,1,0:T(8,128)S(1)}, u32[]{:S(2)}) copy-start(s32[4,16,3]{2,1,0:T(8,128)S(1)} %copy.67) | copy-start | bytes 2308
  17.9 15.1 %collective-permute-start.8 = (f32[1216]{0:T(1024)}, f32[1216]{0:T(1024)}, u32[]{:S(2)}, u32[]{:S(2)}) collective-permute-start(f32[1216]{0:T(1024)} %pad_maximum_fusion.30), channel_id=1, source_target_pairs={{0,1},{1,0},{2,3},{3,2},{4,5},{5,4},{6,7},{7,6},{8,9},{9,8},{10,11... | collective-permute-start | bytes 14600 | tf_op jit(solution)/shard_map/ppermute | solution.py:270
  19.4 8.7 %collective-permute-start.3 = (s32[1,1024]{1,0:T(1,128)}, s32[1,1024]{1,0:T(1,128)S(1)}, u32[]{:S(2)}, u32[]{:S(2)}) collective-permute-start(s32[1,1024]{1,0:T(1,128)} %param.30), channel_id=1, source_target_pairs={{0,0},{4,1},{1,2},{5,3},{2,4},{6,5},{3,6},{7,7},{8,8},{12,9},{9,10... | collective-permute-start | bytes 12296 | tf_op jit(solution)/shard_map/ppermute | solution.py:564
  25.6 28.9 %copy-start.22 = (bf16[256,1024]{1,0:T(8,128)(2,1)}, bf16[256,1024]{1,0:T(8,128)(2,1)S(1)}, u32[]{:S(2)}) copy-start(bf16[256,1024]{1,0:T(8,128)(2,1)S(1)} %get-tuple-element.108) | copy-start | bytes 1572868
  27.8 29.4 %copy-start.20 = (bf16[1024,256]{1,0:T(8,128)(2,1)}, bf16[1024,256]{1,0:T(8,128)(2,1)S(1)}, u32[]{:S(2)}) copy-start(bf16[1024,256]{1,0:T(8,128)(2,1)S(1)} %get-tuple-element.110) | copy-start | bytes 1572868
  28.1 10.8 %collective-permute-start.9 = (bf16[256,256]{1,0:T(8,128)(2,1)}, bf16[256,256]{1,0:T(8,128)(2,1)S(1)}, u32[]{:S(2)}, u32[]{:S(2)}) collective-permute-start(bf16[256,256]{1,0:T(8,128)(2,1)} %get-tuple-element.117), channel_id=1, source_target_pairs={{0,2},{2,0},{1,3},{3,1},{4,6},{6,4},{5,7},{7,5},{8,10},{10,8},{9,1... | collective-permute-start | bytes 393224 | tf_op jit(solution)/shard_map/ppermute | solution.py:270
  33.0 21.1 %collective-permute-start.16 = (bf16[256,1024]{1,0:T(8,128)(2,1)}, bf16[256,1024]{1,0:T(8,128)(2,1)S(1)}, u32[]{:S(2)}, u32[]{:S(2)}) collective-permute-start(bf16[256,1024]{1,0:T(8,128)(2,1)} %get-tuple-element.109), channel_id=1, source_target_pairs={{0,2},{2,0},{1,3},{3,1},{4,6},{6,4},{5,7},{7,5},{8,10},{10,8},{9,1... | collective-permute-start | bytes 1572872 | tf_op jit(solution)/shard_map/ppermute | solution.py:270
  37.7 17.9 %collective-permute-start.18 = (bf16[1024,256]{1,0:T(8,128)(2,1)S(1)}, bf16[1024,256]{1,0:T(8,128)(2,1)S(1)}, u32[]{:S(2)}, u32[]{:S(2)}) collective-permute-start(bf16[1024,256]{1,0:T(8,128)(2,1)S(1)} %copy-done.55), channel_id=1, source_target_pairs={{0,2},{2,0},{1,3},{3,1},{4,6},{6,4},{5,7},{7,5},{8,10},{10,8},{9,1... | collective-permute-start | bytes 1572872 | tf_op jit(solution)/shard_map/ppermute | solution.py:270
  38.9 3.8 collective-permute-start.5
  41.1 11.1 %copy-start.47 = (bf16[256,256]{1,0:T(8,128)(2,1)S(1)}, bf16[256,256]{1,0:T(8,128)(2,1)}, u32[]{:S(2)}) copy-start(bf16[256,256]{1,0:T(8,128)(2,1)} %get-tuple-element.120) | copy-start | bytes 393220
  42.7 7.4 %collective-permute-start.13 = (bf16[256,512]{1,0:T(8,128)(2,1)}, bf16[256,512]{1,0:T(8,128)(2,1)S(1)}, u32[]{:S(2)}, u32[]{:S(2)}) collective-permute-start(bf16[256,512]{1,0:T(8,128)(2,1)} %pad_maximum_fusion.24), channel_id=1, source_target_pairs={{0,1},{1,0},{2,3},{3,2},{4,5},{5,4},{6,7},{7,6},{8,9},{9,8},{10,11... | collective-permute-start | bytes 786440 | tf_op jit(solution)/shard_map/ppermute | solution.py:270
  47.1 23.0 %copy-start.73 = (f32[1,1024]{1,0:T(1,128)}, f32[1,1024]{1,0:T(1,128)S(1)}, u32[]{:S(2)}) copy-start(f32[1,1024]{1,0:T(1,128)S(1)} %get-tuple-element.128) | copy-start | bytes 12292
  50.1 16.5 %collective-permute-start = (bf16[1024,256]{0,1:T(8,128)(2,1)S(1)}, bf16[1024,256]{0,1:T(8,128)(2,1)S(1)}, u32[]{:S(2)}, u32[]{:S(2)}) collective-permute-start(bf16[1024,256]{0,1:T(8,128)(2,1)S(1)} %bitcast.163), channel_id=1, source_target_pairs={{0,2},{2,0},{1,3},{3,1},{4,6},{6,4},{5,7},{7,5},{8,10},{10,8},{9,1... | collective-permute-start | bytes 1572872 | tf_op jit(solution)/shard_map/ppermute | solution.py:270
  50.2 51.3 %collective-permute-start.10 = (bf16[256,512]{1,0:T(8,128)(2,1)}, bf16[256,512]{1,0:T(8,128)(2,1)}, u32[]{:S(2)}, u32[]{:S(2)}) collective-permute-start(bf16[256,512]{1,0:T(8,128)(2,1)} %pad_maximum_fusion.24), channel_id=1, source_target_pairs={{0,4},{4,0},{1,5},{5,1},{2,6},{6,2},{3,7},{7,3},{8,12},{12,8},{9,1... | collective-permute-start | bytes 786440 | tf_op jit(solution)/shard_map/ppermute | solution.py:270
  52.0 15.4 %collective-permute-start.2 = (bf16[1024,256]{0,1:T(8,128)(2,1)S(1)}, bf16[1024,256]{0,1:T(8,128)(2,1)S(1)}, u32[]{:S(2)}, u32[]{:S(2)}) collective-permute-start(bf16[1024,256]{0,1:T(8,128)(2,1)S(1)} %collective-permute-done.1), channel_id=1, source_target_pairs={{0,2},{2,0},{1,3},{3,1},{4,6},{6,4},{5,7},{7,5},{8,10},{10,8},{9,1... | collective-permute-start | bytes 1572872 | tf_op jit(solution)/shard_map/ppermute | solution.py:270
  54.1 11.1 %collective-permute-start.14 = (bf16[256,512]{1,0:T(8,128)(2,1)S(1)}, bf16[256,512]{1,0:T(8,128)(2,1)S(1)}, u32[]{:S(2)}, u32[]{:S(2)}) collective-permute-start(bf16[256,512]{1,0:T(8,128)(2,1)S(1)} %collective-permute-done.13), channel_id=1, source_target_pairs={{0,4},{4,0},{1,5},{5,1},{2,6},{6,2},{3,7},{7,3},{8,12},{12,8},{9,1... | collective-permute-start | bytes 786440 | tf_op jit(solution)/shard_map/ppermute | solution.py:270
  55.5 14.5 %copy-start.53 = (bf16[1024,256]{1,0:T(8,128)(2,1)}, bf16[1024,256]{1,0:T(8,128)(2,1)S(1)}, u32[]{:S(2)}) copy-start(bf16[1024,256]{1,0:T(8,128)(2,1)S(1)} %collective-permute-done.18) | copy-start | bytes 1572868
  55.5 26.6 %collective-permute-start.7 = (bf16[512,768]{1,0:T(8,128)(2,1)}, bf16[512,768]{1,0:T(8,128)(2,1)}, u32[]{:S(2)}, u32[]{:S(2)}) collective-permute-start(bf16[512,768]{1,0:T(8,128)(2,1)} %pad_maximum_fusion.20), channel_id=1, source_target_pairs={{0,4},{4,0},{1,5},{5,1},{2,6},{6,2},{3,7},{7,3},{8,12},{12,8},{9,1... | collective-permute-start | bytes 2359304 | tf_op jit(solution)/shard_map/ppermute | solution.py:270
  65.2 34.9 %collective-permute-start.11 = (bf16[512,768]{1,0:T(8,128)(2,1)}, bf16[512,768]{1,0:T(8,128)(2,1)}, u32[]{:S(2)}, u32[]{:S(2)}) collective-permute-start(bf16[512,768]{1,0:T(8,128)(2,1)} %pad_maximum_fusion.20), channel_id=1, source_target_pairs={{0,1},{1,0},{2,3},{3,2},{4,5},{5,4},{6,7},{7,6},{8,9},{9,8},{10,11... | collective-permute-start | bytes 2359304 | tf_op jit(solution)/shard_map/ppermute | solution.py:270
  66.7 83.9 %collective-permute-start.20 = (bf16[512,1024]{1,0:T(8,128)(2,1)}, bf16[512,1024]{1,0:T(8,128)(2,1)}, u32[]{:S(2)}, u32[]{:S(2)}) collective-permute-start(bf16[512,1024]{1,0:T(8,128)(2,1)} %pad_maximum_fusion.8), channel_id=1, source_target_pairs={{0,1},{1,0},{2,3},{3,2},{4,5},{5,4},{6,7},{7,6},{8,9},{9,8},{10,11... | collective-permute-start | bytes 3145736 | tf_op jit(solution)/shard_map/ppermute | solution.py:270
  67.4 86.3 %collective-permute-start.19 = (bf16[1024,512]{1,0:T(8,128)(2,1)}, bf16[1024,512]{1,0:T(8,128)(2,1)}, u32[]{:S(2)}, u32[]{:S(2)}) collective-permute-start(bf16[1024,512]{1,0:T(8,128)(2,1)} %pad_maximum_fusion.9), channel_id=1, source_target_pairs={{0,4},{4,0},{1,5},{5,1},{2,6},{6,2},{3,7},{7,3},{8,12},{12,8},{9,1... | collective-permute-start | bytes 3145736 | tf_op jit(solution)/shard_map/ppermute | solution.py:270
  72.5 52.2 %copy-start.14 = (bf16[1024,1024]{0,1:T(8,128)(2,1)}, bf16[1024,1024]{0,1:T(8,128)(2,1)S(1)}, u32[]{:S(2)}) copy-start(bf16[1024,1024]{0,1:T(8,128)(2,1)S(1)} %add_convert_fusion.4) | copy-start | bytes 6291460
  82.2 41.3 %collective-permute-start.12 = (bf16[512,768]{1,0:T(8,128)(2,1)}, bf16[512,768]{1,0:T(8,128)(2,1)}, u32[]{:S(2)}, u32[]{:S(2)}) collective-permute-start(bf16[512,768]{1,0:T(8,128)(2,1)} %collective-permute-done.7), channel_id=1, source_target_pairs={{0,1},{1,0},{2,3},{3,2},{4,5},{5,4},{6,7},{7,6},{8,9},{9,8},{10,11... | collective-permute-start | bytes 2359304 | tf_op jit(solution)/shard_map/ppermute | solution.py:270
  143.9 52.0 %collective-permute-start.15 = (bf16[1024,1024]{0,1:T(8,128)(2,1)S(1)}, bf16[1024,1024]{0,1:T(8,128)(2,1)}, u32[]{:S(2)}, u32[]{:S(2)}) collective-permute-start(bf16[1024,1024]{0,1:T(8,128)(2,1)S(1)} %add_convert_fusion.3), channel_id=1, source_target_pairs={{0,2},{2,0},{1,3},{3,1},{4,6},{6,4},{5,7},{7,5},{8,10},{10,8},{9,1... | collective-permute-start | bytes 6291464 | tf_op jit(solution)/shard_map/ppermute | solution.py:270
  146.0 29.5 %collective-permute-start.27 = (bf16[1024,256]{0,1:T(8,128)(2,1)}, bf16[1024,256]{0,1:T(8,128)(2,1)}, u32[]{:S(2)}, u32[]{:S(2)}) collective-permute-start(bf16[1024,256]{0,1:T(8,128)(2,1)} %bitcast.182), channel_id=1, source_target_pairs={{0,4},{4,0},{1,5},{5,1},{2,6},{6,2},{3,7},{7,3},{8,12},{12,8},{9,1... | collective-permute-start | bytes 1572872 | tf_op jit(solution)/shard_map/ppermute | solution.py:270
  147.8 26.3 %collective-permute-start.22 = (bf16[1024,512]{1,0:T(8,128)(2,1)}, bf16[1024,512]{1,0:T(8,128)(2,1)}, u32[]{:S(2)}, u32[]{:S(2)}) collective-permute-start(bf16[1024,512]{1,0:T(8,128)(2,1)} %pad_maximum_fusion.9), channel_id=1, source_target_pairs={{0,1},{1,0},{2,3},{3,2},{4,5},{5,4},{6,7},{7,6},{8,9},{9,8},{10,11... | collective-permute-start | bytes 3145736 | tf_op jit(solution)/shard_map/ppermute | solution.py:270
  150.6 33.0 %collective-permute-start.21 = (bf16[512,1024]{1,0:T(8,128)(2,1)}, bf16[512,1024]{1,0:T(8,128)(2,1)}, u32[]{:S(2)}, u32[]{:S(2)}) collective-permute-start(bf16[512,1024]{1,0:T(8,128)(2,1)} %collective-permute-done.20), channel_id=1, source_target_pairs={{0,4},{4,0},{1,5},{5,1},{2,6},{6,2},{3,7},{7,3},{8,12},{12,8},{9,1... | collective-permute-start | bytes 3145736 | tf_op jit(solution)/shard_map/ppermute | solution.py:270
  153.6 20.5 %copy-start.12 = (bf16[1,1024,256]{1,2,0:T(8,128)(2,1)S(1)}, bf16[1,1024,256]{1,2,0:T(8,128)(2,1)}, u32[]{:S(2)}) copy-start(bf16[1,1024,256]{1,2,0:T(8,128)(2,1)} %copy.68) | copy-start | bytes 1572868
  153.6 42.1 %collective-permute-start.23 = (bf16[1024,512]{1,0:T(8,128)(2,1)}, bf16[1024,512]{1,0:T(8,128)(2,1)S(1)}, u32[]{:S(2)}, u32[]{:S(2)}) collective-permute-start(bf16[1024,512]{1,0:T(8,128)(2,1)} %collective-permute-done.19), channel_id=1, source_target_pairs={{0,1},{1,0},{2,3},{3,2},{4,5},{5,4},{6,7},{7,6},{8,9},{9,8},{10,11... | collective-permute-start | bytes 3145736 | tf_op jit(solution)/shard_map/ppermute | solution.py:270
  174.1 28.5 %collective-permute-start.26 = (bf16[1024,256]{0,1:T(8,128)(2,1)S(1)}, bf16[1024,256]{0,1:T(8,128)(2,1)S(1)}, u32[]{:S(2)}, u32[]{:S(2)}) collective-permute-start(bf16[1024,256]{0,1:T(8,128)(2,1)S(1)} %bitcast.173), channel_id=1, source_target_pairs={{0,2},{2,0},{1,3},{3,1},{4,6},{6,4},{5,7},{7,5},{8,10},{10,8},{9,1... | collective-permute-start | bytes 1572872 | tf_op jit(solution)/shard_map/ppermute | solution.py:270
  175.5 32.3 %collective-permute-start.17 = (bf16[512,1024]{1,0:T(8,128)(2,1)}, bf16[512,1024]{1,0:T(8,128)(2,1)S(1)}, u32[]{:S(2)}, u32[]{:S(2)}) collective-permute-start(bf16[512,1024]{1,0:T(8,128)(2,1)} %pad_maximum_fusion.8), channel_id=1, source_target_pairs={{0,4},{4,0},{1,5},{5,1},{2,6},{6,2},{3,7},{7,3},{8,12},{12,8},{9,1... | collective-permute-start | bytes 3145736 | tf_op jit(solution)/shard_map/ppermute | solution.py:270
  183.6 19.1 %collective-permute-start.28 = (bf16[1024,256]{0,1:T(8,128)(2,1)}, bf16[1024,256]{0,1:T(8,128)(2,1)S(1)}, u32[]{:S(2)}, u32[]{:S(2)}) collective-permute-start(bf16[1024,256]{0,1:T(8,128)(2,1)} %collective-permute-done.27), channel_id=1, source_target_pairs={{0,2},{2,0},{1,3},{3,1},{4,6},{6,4},{5,7},{7,5},{8,10},{10,8},{9,1... | collective-permute-start | bytes 1572872 | tf_op jit(solution)/shard_map/ppermute | solution.py:270
  199.5 60.6 %copy-start.2 = (f32[1024,1024]{0,1:T(8,128)}, f32[1024,1024]{0,1:T(8,128)S(1)}, u32[]{:S(2)}) copy-start(f32[1024,1024]{0,1:T(8,128)S(1)} %get-tuple-element.52) | copy-start | bytes 12582916
  202.6 29.2 %copy-start.39 = (bf16[1024,256]{0,1:T(8,128)(2,1)}, bf16[1024,256]{0,1:T(8,128)(2,1)S(1)}, u32[]{:S(2)}) copy-start(bf16[1024,256]{0,1:T(8,128)(2,1)S(1)} %collective-permute-done.26) | copy-start | bytes 1572868
  202.7 29.2 %copy-start.41 = (bf16[1024,256]{0,1:T(8,128)(2,1)}, bf16[1024,256]{0,1:T(8,128)(2,1)S(1)}, u32[]{:S(2)}) copy-start(bf16[1024,256]{0,1:T(8,128)(2,1)S(1)} %collective-permute-done.28) | copy-start | bytes 1572868
  207.5 57.8 %collective-permute-start.46 = (bf16[1024,512]{1,0:T(8,128)(2,1)S(1)}, bf16[1024,512]{1,0:T(8,128)(2,1)S(1)}, u32[]{:S(2)}, u32[]{:S(2)}) collective-permute-start(bf16[1024,512]{1,0:T(8,128)(2,1)S(1)} %slice.479), channel_id=1, source_target_pairs={{0,4},{4,0},{1,5},{5,1},{2,6},{6,2},{3,7},{7,3},{8,12},{12,8},{9,1... | collective-permute-start | bytes 3145736 | tf_op jit(solution)/shard_map/ppermute | solution.py:270
  211.0 20.9 %copy-start.90 = (f32[1024,1024]{1,0:T(8,128)}, f32[1024,1024]{1,0:T(8,128)S(1)}, u32[]{:S(2)}) copy-start(f32[1024,1024]{1,0:T(8,128)S(1)} %fusion.28) | copy-start | bytes 12582916
  216.9 153.7 %collective-permute-start.45 = (bf16[1024,512]{1,0:T(8,128)(2,1)}, bf16[1024,512]{1,0:T(8,128)(2,1)}, u32[]{:S(2)}, u32[]{:S(2)}) collective-permute-start(bf16[1024,512]{1,0:T(8,128)(2,1)} %slice.477), channel_id=1, source_target_pairs={{0,4},{4,0},{1,5},{5,1},{2,6},{6,2},{3,7},{7,3},{8,12},{12,8},{9,1... | collective-permute-start | bytes 3145736 | tf_op jit(solution)/shard_map/ppermute | solution.py:270
  230.6 37.2 %collective-permute-start.42 = (bf16[512,1024]{1,0:T(8,128)(2,1)S(1)}, bf16[512,1024]{1,0:T(8,128)(2,1)S(1)}, u32[]{:S(2)}, u32[]{:S(2)}) collective-permute-start(bf16[512,1024]{1,0:T(8,128)(2,1)S(1)} %get-tuple-element.71), channel_id=1, source_target_pairs={{0,1},{1,0},{2,3},{3,2},{4,5},{5,4},{6,7},{7,6},{8,9},{9,8},{10,11... | collective-permute-start | bytes 3145736 | tf_op jit(solution)/shard_map/ppermute | solution.py:270
  246.3 37.0 %collective-permute-start.29 = (bf16[1024,1024]{0,1:T(8,128)(2,1)S(1)}, bf16[1024,1024]{0,1:T(8,128)(2,1)}, u32[]{:S(2)}, u32[]{:S(2)}) collective-permute-start(bf16[1024,1024]{0,1:T(8,128)(2,1)S(1)} %add_convert_fusion), channel_id=1, source_target_pairs={{0,2},{2,0},{1,3},{3,1},{4,6},{6,4},{5,7},{7,5},{8,10},{10,8},{9,1... | collective-permute-start | bytes 6291464 | tf_op jit(solution)/shard_map/ppermute | solution.py:270
  258.9 5.2 collective-permute-start.24
  264.0 115.3 %collective-permute-start.41 = (bf16[512,1024]{1,0:T(8,128)(2,1)}, bf16[512,1024]{1,0:T(8,128)(2,1)}, u32[]{:S(2)}, u32[]{:S(2)}) collective-permute-start(bf16[512,1024]{1,0:T(8,128)(2,1)} %get-tuple-element.70), channel_id=1, source_target_pairs={{0,1},{1,0},{2,3},{3,2},{4,5},{5,4},{6,7},{7,6},{8,9},{9,8},{10,11... | collective-permute-start | bytes 3145736 | tf_op jit(solution)/shard_map/ppermute | solution.py:270
  265.3 13.6 %collective-permute-start.25 = (bf16[1024,256]{0,1:T(8,128)(2,1)S(1)}, bf16[1024,256]{0,1:T(8,128)(2,1)S(1)}, u32[]{:S(2)}, u32[]{:S(2)}) collective-permute-start(bf16[1024,256]{0,1:T(8,128)(2,1)S(1)} %slice.417), channel_id=1, source_target_pairs={{0,4},{4,0},{1,5},{5,1},{2,6},{6,2},{3,7},{7,3},{8,12},{12,8},{9,1... | collective-permute-start | bytes 1572872 | tf_op jit(solution)/shard_map/ppermute | solution.py:270
  267.8 103.7 %collective-permute-start.47 = (bf16[1024,512]{1,0:T(8,128)(2,1)}, bf16[1024,512]{1,0:T(8,128)(2,1)}, u32[]{:S(2)}, u32[]{:S(2)}) collective-permute-start(bf16[1024,512]{1,0:T(8,128)(2,1)} %add_convert_fusion.6), channel_id=1, source_target_pairs={{0,1},{1,0},{2,3},{3,2},{4,5},{5,4},{6,7},{7,6},{8,9},{9,8},{10,11... | collective-permute-start | bytes 3145736 | tf_op jit(solution)/shard_map/ppermute | solution.py:270
  278.9 100.6 %collective-permute-start.43 = (bf16[512,1024]{1,0:T(8,128)(2,1)}, bf16[512,1024]{1,0:T(8,128)(2,1)}, u32[]{:S(2)}, u32[]{:S(2)}) collective-permute-start(bf16[512,1024]{1,0:T(8,128)(2,1)} %add_convert_fusion.8), channel_id=1, source_target_pairs={{0,4},{4,0},{1,5},{5,1},{2,6},{6,2},{3,7},{7,3},{8,12},{12,8},{9,1... | collective-permute-start | bytes 3145736 | tf_op jit(solution)/shard_map/ppermute | solution.py:270
  304.5 90.5 %collective-permute-start.38 = (bf16[256,512]{1,0:T(8,128)(2,1)}, bf16[256,512]{1,0:T(8,128)(2,1)}, u32[]{:S(2)}, u32[]{:S(2)}) collective-permute-start(bf16[256,512]{1,0:T(8,128)(2,1)} %slice.464), channel_id=1, source_target_pairs={{0,4},{4,0},{1,5},{5,1},{2,6},{6,2},{3,7},{7,3},{8,12},{12,8},{9,1... | collective-permute-start | bytes 786440 | tf_op jit(solution)/shard_map/ppermute | solution.py:270
  370.6 27.6 %collective-permute-start.37 = (bf16[256,512]{1,0:T(8,128)(2,1)S(1)}, bf16[256,512]{1,0:T(8,128)(2,1)S(1)}, u32[]{:S(2)}, u32[]{:S(2)}) collective-permute-start(bf16[256,512]{1,0:T(8,128)(2,1)S(1)} %slice.462), channel_id=1, source_target_pairs={{0,4},{4,0},{1,5},{5,1},{2,6},{6,2},{3,7},{7,3},{8,12},{12,8},{9,1... | collective-permute-start | bytes 786440 | tf_op jit(solution)/shard_map/ppermute | solution.py:270
  371.5 23.2 %collective-permute-start.34 = (bf16[512,768]{1,0:T(8,128)(2,1)S(1)}, bf16[512,768]{1,0:T(8,128)(2,1)S(1)}, u32[]{:S(2)}, u32[]{:S(2)}) collective-permute-start(bf16[512,768]{1,0:T(8,128)(2,1)S(1)} %copy-done.37), channel_id=1, source_target_pairs={{0,1},{1,0},{2,3},{3,2},{4,5},{5,4},{6,7},{7,6},{8,9},{9,8},{10,11... | collective-permute-start | bytes 2359304 | tf_op jit(solution)/shard_map/ppermute | solution.py:270
  379.3 36.2 %collective-permute-start.33 = (bf16[512,768]{1,0:T(8,128)(2,1)S(1)}, bf16[512,768]{1,0:T(8,128)(2,1)S(1)}, u32[]{:S(2)}, u32[]{:S(2)}) collective-permute-start(bf16[512,768]{1,0:T(8,128)(2,1)S(1)} %copy-done.36), channel_id=1, source_target_pairs={{0,1},{1,0},{2,3},{3,2},{4,5},{5,4},{6,7},{7,6},{8,9},{9,8},{10,11... | collective-permute-start | bytes 2359304 | tf_op jit(solution)/shard_map/ppermute | solution.py:270
  379.5 37.2 %collective-permute-start.30 = (bf16[1024,512]{0,1:T(8,128)(2,1)}, bf16[1024,512]{0,1:T(8,128)(2,1)}, u32[]{:S(2)}, u32[]{:S(2)}) collective-permute-start(bf16[1024,512]{0,1:T(8,128)(2,1)} %pad_maximum_fusion.13), channel_id=1, source_target_pairs={{0,2},{2,0},{1,3},{3,1},{4,6},{6,4},{5,7},{7,5},{8,10},{10,8},{9,1... | collective-permute-start | bytes 3145736 | tf_op jit(solution)/shard_map/ppermute | solution.py:270
  384.5 10.6 %copy-start.44 = (bf16[256,1024]{1,0:T(8,128)(2,1)S(1)}, bf16[256,1024]{1,0:T(8,128)(2,1)}, u32[]{:S(2)}) copy-start(bf16[256,1024]{1,0:T(8,128)(2,1)} %copy-done.43) | copy-start | bytes 1572868
  384.5 30.2 %copy-start.50 = (bf16[256,1024]{1,0:T(8,128)(2,1)S(1)}, bf16[256,1024]{1,0:T(8,128)(2,1)}, u32[]{:S(2)}) copy-start(bf16[256,1024]{1,0:T(8,128)(2,1)} %convolution_convert_fusion.9) | copy-start | bytes 1572868
  394.9 20.6 %collective-permute-start.35 = (bf16[512,768]{1,0:T(8,128)(2,1)S(1)}, bf16[512,768]{1,0:T(8,128)(2,1)S(1)}, u32[]{:S(2)}, u32[]{:S(2)}) collective-permute-start(bf16[512,768]{1,0:T(8,128)(2,1)S(1)} %add_convert_fusion.10), channel_id=1, source_target_pairs={{0,4},{4,0},{1,5},{5,1},{2,6},{6,2},{3,7},{7,3},{8,12},{12,8},{9,1... | collective-permute-start | bytes 2359304 | tf_op jit(solution)/shard_map/ppermute | solution.py:270
  396.1 18.6 %collective-permute-start.39 = (bf16[256,512]{1,0:T(8,128)(2,1)S(1)}, bf16[256,512]{1,0:T(8,128)(2,1)S(1)}, u32[]{:S(2)}, u32[]{:S(2)}) collective-permute-start(bf16[256,512]{1,0:T(8,128)(2,1)S(1)} %add_convert_fusion.12), channel_id=1, source_target_pairs={{0,1},{1,0},{2,3},{3,2},{4,5},{5,4},{6,7},{7,6},{8,9},{9,8},{10,11... | collective-permute-start | bytes 786440 | tf_op jit(solution)/shard_map/ppermute | solution.py:270
  398.2 18.5 %collective-permute-start.31 = (f32[2,1024]{1,0:T(2,128)S(1)}, f32[2,1024]{1,0:T(2,128)S(1)}, u32[]{:S(2)}, u32[]{:S(2)}) collective-permute-start(f32[2,1024]{1,0:T(2,128)S(1)} %pad_maximum_fusion.31), channel_id=1, source_target_pairs={{0,2},{2,0},{1,3},{3,1},{4,6},{6,4},{5,7},{7,5},{8,10},{10,8},{9,1... | collective-permute-start | bytes 24584 | tf_op jit(solution)/shard_map/ppermute | solution.py:270
  467.0 13.7 %collective-permute-start.32 = (bf16[1024,256]{0,1:T(8,128)(2,1)S(1)}, bf16[1024,256]{0,1:T(8,128)(2,1)S(1)}, u32[]{:S(2)}, u32[]{:S(2)}) collective-permute-start(bf16[1024,256]{0,1:T(8,128)(2,1)S(1)} %slice.537), channel_id=1, source_target_pairs={{0,4},{4,0},{1,5},{5,1},{2,6},{6,2},{3,7},{7,3},{8,12},{12,8},{9,1... | collective-permute-start | bytes 1572872 | tf_op jit(solution)/shard_map/ppermute | solution.py:270
  541.1 6.8 %collective-permute-start.40 = (bf16[256,256]{1,0:T(8,128)(2,1)}, bf16[256,256]{1,0:T(8,128)(2,1)}, u32[]{:S(2)}, u32[]{:S(2)}) collective-permute-start(bf16[256,256]{1,0:T(8,128)(2,1)} %slice.466), channel_id=1, source_target_pairs={{0,2},{2,0},{1,3},{3,1},{4,6},{6,4},{5,7},{7,5},{8,10},{10,8},{9,1... | collective-permute-start | bytes 393224 | tf_op jit(solution)/shard_map/ppermute | solution.py:270
  542.1 7.5 %collective-permute-start.36 = (bf16[256,768]{1,0:T(8,128)(2,1)S(1)}, bf16[256,768]{1,0:T(8,128)(2,1)}, u32[]{:S(2)}, u32[]{:S(2)}) collective-permute-start(bf16[256,768]{1,0:T(8,128)(2,1)S(1)} %slice.455), channel_id=1, source_target_pairs={{0,2},{2,0},{1,3},{3,1},{4,6},{6,4},{5,7},{7,5},{8,10},{10,8},{9,1... | collective-permute-start | bytes 1179656 | tf_op jit(solution)/shard_map/ppermute | solution.py:270
  547.1 6.2 %collective-permute-start.48 = (bf16[1024,256]{1,0:T(8,128)(2,1)S(1)}, bf16[1024,256]{1,0:T(8,128)(2,1)S(1)}, u32[]{:S(2)}, u32[]{:S(2)}) collective-permute-start(bf16[1024,256]{1,0:T(8,128)(2,1)S(1)} %slice.481), channel_id=1, source_target_pairs={{0,2},{2,0},{1,3},{3,1},{4,6},{6,4},{5,7},{7,5},{8,10},{10,8},{9,1... | collective-permute-start | bytes 1572872 | tf_op jit(solution)/shard_map/ppermute | solution.py:270
  547.3 7.6 %collective-permute-start.44 = (bf16[256,1024]{1,0:T(8,128)(2,1)S(1)}, bf16[256,1024]{1,0:T(8,128)(2,1)S(1)}, u32[]{:S(2)}, u32[]{:S(2)}) collective-permute-start(bf16[256,1024]{1,0:T(8,128)(2,1)S(1)} %slice.474), channel_id=1, source_target_pairs={{0,2},{2,0},{1,3},{3,1},{4,6},{6,4},{5,7},{7,5},{8,10},{10,8},{9,1... | collective-permute-start | bytes 1572872 | tf_op jit(solution)/shard_map/ppermute | solution.py:270
  (79 other events, 297.8 us)
Sparse Core Ops, SparseCore 0:
  416.9 122.5 all-reduce.7

commit v2 on v1

--- a/solution.py
+++ b/solution.py
@@ -404,10 +404,13 @@
 
 
 def attend_backward_kernel(
-    where_ref, kept_ref, k_ref, v_ref, keys_ref, heads_ref, grads_ref, dq_ref, dk_ref, dv_ref, kk, va, dk_sum, dv_sum
+    where_ref, kept_ref, k_ref, v_ref, keys_ref, heads_ref, grads_ref, out_ref, kk, va, dk_sum, dv_sum
 ):
     length = k_ref.shape[0]
-    lane = lax.broadcasted_iota(jnp.int32, (length, 2 * HD), 1)
+    wide = 2 * HD
+    third = out_ref.shape[1] // 3
+    pair = pl.program_id(0) * wide
+    lane = lax.broadcasted_iota(jnp.int32, (length, wide), 1)
     for e in range(2):
         data = (lane < HD) if e == 0 else (lane >= HD)
         base = HD if e == 0 else 0
@@ -416,7 +419,7 @@
         va[e] = jnp.where(data, v_ref[...], ones)
     dk_sum[...] = jnp.zeros_like(dk_sum)
     dv_sum[...] = jnp.zeros_like(dv_sum)
-    tile_lane = lax.broadcasted_iota(jnp.int32, (TILE, 2 * HD), 1)
+    tile_lane = lax.broadcasted_iota(jnp.int32, (TILE, wide), 1)
 
     def one_tile(t, carry):
         rows = pl.ds(pl.multiple_of(t * TILE, TILE), TILE)
@@ -446,25 +449,24 @@
                     dk_sum[span, :] += dot_nn(grad_raw, q_only)
                     outs.append(dot_tn(grad_raw, kk[e, span, :]))
                 joined = jnp.where(tile_lane < HD, outs[0], outs[1])
-                dq_ref[rows, :] = (joined * (1.0 / math.sqrt(HD))).astype(LOW)
+                lanes = pl.ds(pl.multiple_of(pair, wide), wide)
+                out_ref[rows, lanes] = (joined * (1.0 / math.sqrt(HD))).astype(LOW)
 
         return carry
 
     lax.fori_loop(0, length // TILE, one_tile, 0)
-    dk_ref[...] = dk_sum[...].astype(LOW)
-    dv_ref[...] = dv_sum[...].astype(LOW)
-
-
-def attend_backward(kept, qkv, keys_extra, heads, grads, where_table):
+    out_ref[:, pl.ds(pl.multiple_of(third + pair, wide), wide)] = dk_sum[...].astype(LOW)
+    out_ref[:, pl.ds(pl.multiple_of(2 * third + pair, wide), wide)] = dv_sum[...].astype(LOW)
+
+
+def attend_backward(kept, qkv, keys_extra, heads, grads, group, where_table):
     length, width = qkv.shape
     pairs = width // (3 * 2 * HD)
     wide = 2 * HD
-    one = jax.ShapeDtypeStruct((length, width // 3), LOW)
-    lanes = pl.BlockSpec((length, wide), lambda p, w: (0, p))
     stacked = pl.BlockSpec((2, length, wide), lambda p, w: (p, 0, 0))
     return pl.pallas_call(
         attend_backward_kernel,
-        out_shape=(one, one, one),
+        out_shape=jax.ShapeDtypeStruct((length, width), LOW),
         grid_spec=pltpu.PrefetchScalarGridSpec(
             num_scalar_prefetch=1,
             grid=(pairs,),
@@ -473,10 +475,10 @@
                 pl.BlockSpec((length, wide), lambda p, w: (0, pairs + p)),
                 pl.BlockSpec((length, wide), lambda p, w: (0, 2 * pairs + p)),
                 stacked,
-                lanes,
-                lanes,
+                pl.BlockSpec((length, wide), lambda p, w: (0, p)),
+                pl.BlockSpec((length, wide), lambda p, w: (0, group * pairs + p)),
             ],
-            out_specs=(lanes, lanes, lanes),
+            out_specs=pl.BlockSpec((length, width), lambda p, w: (0, 0)),
             scratch_shapes=[
                 pltpu.VMEM((2, length, wide), LOW),
                 pltpu.VMEM((2, length, wide), LOW),
@@ -491,10 +493,301 @@
     )(where_table, kept, qkv, qkv, keys_extra, heads, grads)
 
 
-def swap_features(part):
-    got = swap(part, "core")
-    n = got.shape[1] // 4
-    return jnp.concatenate((got[:, n : 2 * n], got[:, :n], got[:, 3 * n :], got[:, 2 * n : 3 * n]), axis=1)
+def row_tiles(count):
+    def spec(width):
+        return pl.BlockSpec((TILE, width), lambda t: (t, 0))
+
+    return spec
+
+
+def whole(shape):
+    return pl.BlockSpec(shape, lambda t: (0,) * len(shape))
+
+
+def cost(flops, moved):
+    return pl.CostEstimate(flops=int(flops), bytes_accessed=int(moved), transcendentals=0)
+
+
+def norm_parts(blocks):
+    width = sum(b.shape[1] for b in blocks)
+    total = sum(jnp.sum(b, axis=1, keepdims=True) for b in blocks)
+    squares = sum(jnp.sum(b * b, axis=1, keepdims=True) for b in blocks)
+    center = total / width
+    return center, lax.rsqrt(squares / width - center * center + EPS)
+
+
+def columns(ref, index, width):
+    return ref[:, index * width : (index + 1) * width]
+
+
+def first_norm_kernel(x0, x1, x2, x3, gain_ref, shift_ref, low_ref, high_ref):
+    blocks = [x[...].astype(FULL) for x in (x0, x1, x2, x3)]
+    n = blocks[0].shape[1]
+    center, inverse = norm_parts(blocks)
+    for i, block in enumerate(blocks):
+        value = (block - center) * inverse * columns(gain_ref, i, n) + columns(shift_ref, i, n)
+        (low_ref, high_ref)[i // 2][:, (i % 2) * n : (i % 2 + 1) * n] = value.astype(LOW)
+
+
+def first_norm(blocks, gain, shift):
+    length, n = blocks[0].shape
+    rows = row_tiles(length)
+    half = jax.ShapeDtypeStruct((length, 2 * n), LOW)
+    return pl.pallas_call(
+        first_norm_kernel,
+        out_shape=(half, half),
+        grid=(length // TILE,),
+        in_specs=[rows(n)] * 4 + [whole((1, 4 * n))] * 2,
+        out_specs=(rows(2 * n), rows(2 * n)),
+        name="first_norm",
+        cost_estimate=cost(20 * length * n, 16 * length * n),
+    )(*blocks, gain, shift)
+
+
+def second_norm_kernel(x0, x1, x2, x3, part_ref, got_ref, gain_ref, shift_ref, residual_ref, low_ref, high_ref):
+    n = x0.shape[1]
+    blocks = []
+    for i, x in enumerate((x0, x1, x2, x3)):
+        mixed = columns(part_ref, i, n).astype(FULL) + columns(got_ref, i ^ 1, n).astype(FULL)
+        blocks.append(x[...].astype(FULL) + mixed)
+    center, inverse = norm_parts(blocks)
+    for i, block in enumerate(blocks):
+        residual_ref[:, i * n : (i + 1) * n] = block
+        value = (block - center) * inverse * columns(gain_ref, i, n) + columns(shift_ref, i, n)
+        (low_ref, high_ref)[i // 2][:, (i % 2) * n : (i % 2 + 1) * n] = value.astype(LOW)
+
+
+def second_norm(blocks, part, got, gain, shift):
+    length, n = blocks[0].shape
+    rows = row_tiles(length)
+    half = jax.ShapeDtypeStruct((length, 2 * n), LOW)
+    return pl.pallas_call(
+        second_norm_kernel,
+        out_shape=(jax.ShapeDtypeStruct((length, 4 * n), FULL), half, half),
+        grid=(length // TILE,),
+        in_specs=[rows(n)] * 4 + [rows(4 * n)] * 2 + [whole((1, 4 * n))] * 2,
+        out_specs=(rows(4 * n), rows(2 * n), rows(2 * n)),
+        name="second_norm",
+        cost_estimate=cost(30 * length * n, 48 * length * n),
+    )(*blocks, part, got, gain, shift)
+
+
+def norm_gradient(blocks, part_ref, got_ref, gain_ref, sums_ref):
+    n = blocks[0].shape[1]
+    center, inverse = norm_parts(blocks)
+    normed = [(b - center) * inverse for b in blocks]
+    grads = [columns(part_ref, i, n).astype(FULL) + columns(got_ref, i ^ 1, n).astype(FULL) for i in range(4)]
+    scaled = [g * columns(gain_ref, i, n) for i, g in enumerate(grads)]
+    mean_one = sum(jnp.sum(s, axis=1, keepdims=True) for s in scaled) / (4 * n)
+    mean_two = sum(jnp.sum(s * z, axis=1, keepdims=True) for s, z in zip(scaled, normed)) / (4 * n)
+
+    @pl.when(pl.program_id(0) == 0)
+    def _():
+        sums_ref[...] = jnp.zeros_like(sums_ref)
+
+    for slot, i in enumerate((0, 2)):
+        place = slice(slot * n, (slot + 1) * n)
+        sums_ref[0:1, place] += jnp.sum(grads[i] * normed[i], axis=0, keepdims=True)
+        sums_ref[1:2, place] += jnp.sum(grads[i], axis=0, keepdims=True)
+    return [inverse * (s - mean_one - z * mean_two) for s, z in zip(scaled, normed)]
+
+
+def second_norm_back_kernel(
+    residual_ref, part_ref, got_ref, low_ref, high_ref, gain_ref, own_ref, other_ref, mixed_ref, sums_ref
+):
+    n = residual_ref.shape[1] // 4
+    blocks = [columns(residual_ref, i, n) for i in range(4)]
+    for i, grad in enumerate(norm_gradient(blocks, part_ref, got_ref, gain_ref, sums_ref)):
+        total = columns((low_ref, high_ref)[i // 2], i % 2, n).astype(FULL) + grad
+        mixed_ref[:, i * n : (i + 1) * n] = total.astype(LOW)
+        if i % 2 == 0:
+            (own_ref, other_ref)[i // 2][...] = total
+
+
+def second_norm_back(residual, part, got, low, high, gain):
+    length, width = residual.shape
+    n = width // 4
+    rows = row_tiles(length)
+    one = jax.ShapeDtypeStruct((length, n), FULL)
+    return pl.pallas_call(
+        second_norm_back_kernel,
+        out_shape=(one, one, jax.ShapeDtypeStruct((length, width), LOW), jax.ShapeDtypeStruct((8, 2 * n), FULL)),
+        grid=(length // TILE,),
+        in_specs=[rows(width)] * 3 + [rows(2 * n)] * 2 + [whole((1, width))],
+        out_specs=(rows(n), rows(n), rows(width), whole((8, 2 * n))),
+        name="second_norm_back",
+        cost_estimate=cost(60 * length * n, 64 * length * n),
+    )(residual, part, got, low, high, gain)
+
+
+def first_norm_back_kernel(
+    x0, x1, x2, x3, part_ref, got_ref, own_ref, other_ref, gain_ref, mine_ref, theirs_ref, sums_ref
+):
+    blocks = [x[...].astype(FULL) for x in (x0, x1, x2, x3)]
+    grads = norm_gradient(blocks, part_ref, got_ref, gain_ref, sums_ref)
+    mine_ref[...] = own_ref[...] + grads[0]
+    theirs_ref[...] = (other_ref[...] + grads[2]).astype(LOW)
+
+
+def first_norm_back(blocks, part, got, own, other, gain):
+    length, n = blocks[0].shape
+    rows = row_tiles(length)
+    return pl.pallas_call(
+        first_norm_back_kernel,
+        out_shape=(
+            jax.ShapeDtypeStruct((length, n), FULL),
+            jax.ShapeDtypeStruct((length, n), LOW),
+            jax.ShapeDtypeStruct((8, 2 * n), FULL),
+        ),
+        grid=(length // TILE,),
+        in_specs=[rows(n)] * 4 + [rows(4 * n)] * 2 + [rows(n)] * 2 + [whole((1, 4 * n))],
+        out_specs=(rows(n), rows(n), whole((8, 2 * n))),
+        name="first_norm_back",
+        cost_estimate=cost(60 * length * n, 40 * length * n),
+    )(*blocks, part, got, own, other, gain)
+
+
+def mix_kernel(h0, h1, w0, w1, out_ref):
+    out_ref[...] = (dot_nn(h0[...], w0[...]) + dot_nn(h1[...], w1[...])).astype(LOW)
+
+
+def mix_heads(heads, weights):
+    length, depth = heads[0].shape
+    width = weights[0].shape[1]
+    rows = row_tiles(length)
+    return pl.pallas_call(
+        mix_kernel,
+        out_shape=jax.ShapeDtypeStruct((length, width), LOW),
+        grid=(length // TILE,),
+        in_specs=[rows(depth)] * 2 + [whole((depth, width))] * 2,
+        out_specs=rows(width),
+        name="mix_heads",
+        cost_estimate=cost(4 * length * depth * width, 4 * length * (depth + width)),
+    )(*heads, *weights)
+
+
+ROOT = math.sqrt(2.0 / math.pi)
+
+
+def feed_forward_kernel(
+    at_ref, s_low, s_high, c_low, c_high, u_low, u_high, d_low, d_high, bias_ref,
+    part_ref, hidden0, hidden1, grad0, grad1, bias_sum, low_sum, high_sum,
+):
+    step = pl.program_id(0)
+    steps = pl.num_programs(0)
+    first = step < steps // 2
+
+    @pl.when(step == 0)
+    def _():
+        low_sum[...] = jnp.zeros_like(low_sum)
+        high_sum[...] = jnp.zeros_like(high_sum)
+
+    totals = 0.0
+    for t in range(s_low.shape[0] // TILE):
+        rows = slice(t * TILE, (t + 1) * TILE)
+        upward = dot_nn(s_low[rows, :], u_low[0]) + dot_nn(s_high[rows, :], u_high[0]) + bias_ref[0]
+        grad_hidden = dot_nt(c_low[rows, :], d_low[0]) + dot_nt(c_high[rows, :], d_high[0])
+        square = upward * upward
+        bent = jnp.tanh(upward * (ROOT + (ROOT * 0.044715) * square))
+        lifted = 0.5 + 0.5 * bent
+        slope = lifted + (0.5 * upward) * (1.0 - bent * bent) * (ROOT + (ROOT * 3 * 0.044715) * square)
+        hidden = (upward * lifted).astype(LOW)
+        grad = grad_hidden * slope
+        totals = totals + jnp.sum(grad, axis=0, keepdims=True)
+        grad = grad.astype(LOW)
+
+        @pl.when(first)
+        def _():
+            hidden0[rows, :] = hidden
+            grad0[rows, :] = grad
+
+        @pl.when(jnp.logical_not(first))
+        def _():
+            hidden1[rows, :] = hidden
+            grad1[rows, :] = grad
+
+        low_sum[rows, :] += dot_nt(grad, u_low[0])
+        high_sum[rows, :] += dot_nt(grad, u_high[0])
+    bias_sum[0] = jnp.broadcast_to(totals, bias_sum.shape[1:])
+
+    @pl.when(step == steps - 1)
+    def _():
+        n = low_sum.shape[1]
+        part_ref[:, :n] = low_sum[...].astype(LOW)
+        part_ref[:, n:] = high_sum[...].astype(LOW)
+
+
+def feed_forward(at, seconds, cots, ups, downs, biases):
+    length, h = seconds[0].shape
+    each = ups.shape[2]
+    tiles = each // TILE
+    keep = pl.BlockSpec((length, h), lambda i, at: (0, 0))
+
+    def up_spec(flip):
+        return pl.BlockSpec(
+            (1, h, TILE), lambda i, at: ((at[0] ^ flip) * 2 + (at[1] ^ (i // tiles)), 0, lax.rem(i, tiles))
+        )
+
+    def down_spec(flip):
+        return pl.BlockSpec(
+            (1, TILE, h), lambda i, at: ((at[0] ^ flip) * 2 + (at[1] ^ (i // tiles)), lax.rem(i, tiles), 0)
+        )
+
+    early = pl.BlockSpec((length, TILE), lambda i, at: (0, jnp.minimum(i, tiles - 1)))
+    late = pl.BlockSpec((length, TILE), lambda i, at: (0, jnp.maximum(i - tiles, 0)))
+    one = jax.ShapeDtypeStruct((length, each), LOW)
+    return pl.pallas_call(
+        feed_forward_kernel,
+        out_shape=(
+            jax.ShapeDtypeStruct((length, 2 * h), LOW), one, one, one, one,
+            jax.ShapeDtypeStruct((2 * tiles, 8, TILE), FULL),
+        ),
+        grid_spec=pltpu.PrefetchScalarGridSpec(
+            num_scalar_prefetch=1,
+            grid=(2 * tiles,),
+            in_specs=[keep] * 4
+            + [up_spec(0), up_spec(1), down_spec(0), down_spec(1)]
+            + [pl.BlockSpec((1, 1, TILE), lambda i, at: (i, 0, 0))],
+            out_specs=(
+                pl.BlockSpec((length, 2 * h), lambda i, at: (0, 0)), early, late, early, late,
+                pl.BlockSpec((1, 8, TILE), lambda i, at: (i, 0, 0)),
+            ),
+            scratch_shapes=[pltpu.VMEM((length, h), FULL), pltpu.VMEM((length, h), FULL)],
+        ),
+        name="feed_forward",
+        cost_estimate=cost(12 * length * 2 * h * each, 8 * length * h + 16 * h * each + 16 * length * each),
+    )(at, *seconds, *cots, ups, ups, downs, downs, biases.reshape(2 * tiles, 1, TILE))
+
+
+def layer_end_kernel(at_ref, h0, h1, w00, w01, w10, w11, own_ref, theirs_ref):
+    n = own_ref.shape[1] // 2
+    for j, (a, b) in enumerate(((w00, w01), (w10, w11))):
+        part = dot_nn(h0[...], a[0]) + dot_nn(h1[...], b[0])
+        own_ref[:, j * n : (j + 1) * n] = part[:, :n]
+        theirs_ref[:, j * n : (j + 1) * n] = part[:, n:].astype(LOW)
+
+
+def layer_end(at, hiddens, downs):
+    length, each = hiddens[0].shape
+    h = downs.shape[2]
+    rows = pl.BlockSpec((TILE, each), lambda t, at: (t, 0))
+    out = pl.BlockSpec((TILE, h), lambda t, at: (t, 0))
+
+    def weight(y, col):
+        return pl.BlockSpec((1, each, h), lambda t, at: ((at[0] ^ y) * 2 + (at[1] ^ col), 0, 0))
+
+    return pl.pallas_call(
+        layer_end_kernel,
+        out_shape=(jax.ShapeDtypeStruct((length, h), FULL), jax.ShapeDtypeStruct((length, h), LOW)),
+        grid_spec=pltpu.PrefetchScalarGridSpec(
+            num_scalar_prefetch=1,
+            grid=(length // TILE,),
+            in_specs=[rows, rows, weight(0, 0), weight(0, 1), weight(1, 0), weight(1, 1)],
+            out_specs=(out, out),
+        ),
+        name="layer_end",
+        cost_estimate=cost(8 * length * h * each, 8 * h * each + 12 * length * h),
+    )(at, *hiddens, downs, downs, downs, downs)
 
 
 def pick(pair, index):
@@ -506,56 +799,66 @@
     return jnp.stack((jnp.where(flip, own, other), jnp.where(flip, other, own)))
 
 
-def plane_gather(block, first_axis, second_axis):
-    near = {first_axis: swap(block, first_axis), second_axis: swap(block, second_axis)}
-    across = swap(near[first_axis], second_axis)
-    return block, near["col"], near["y"], across
-
-
-def plane_reduce(own, at_col, at_y, across, first_axis, second_axis):
-    near = {"col": at_col, "y": at_y}
-    arrived = swap(across, first_axis)
-    direct = swap(near[first_axis], first_axis)
-    onward = (near[second_axis].astype(FULL) + arrived.astype(FULL)).astype(LOW)
-    last = swap(onward, second_axis)
-    return (own.astype(FULL) + direct.astype(FULL) + last.astype(FULL)).astype(LOW)
+def swap_across(array):
+    return lax.ppermute(array, ("y", "col"), [(0, 3), (3, 0), (1, 2), (2, 1)])
+
+
+def plane_gather(block):
+    return block, swap(block, "y"), swap(block, "col"), swap_across(block)
+
+
+def plane_reduce(own, at_y, at_col, across):
+    got = (swap(at_y, "y"), swap(at_col, "col"), swap_across(across))
+    return (own.astype(FULL) + sum(g.astype(FULL) for g in got)).astype(LOW)
+
+
+def depth_sum(array, index):
+    near = array + lax.ppermute(array, "dp", [(0, 1), (3, 2)])
+    both = near + lax.ppermute(near, "dp", [(1, 2), (2, 1)])
+    back = lax.ppermute(both, "dp", [(1, 0), (2, 3)])
+    return jnp.where((index == 0) | (index == 3), back, both)
+
+
+def half(weight, axis, index):
+    size = weight.shape[axis] // 2
+    return lax.dynamic_slice_in_dim(weight, index * size, size, axis)
 
 
 def fast_body(
     inputs, gain_first, shift_first, w_query, w_key, w_value, w_output, gain_second, shift_second,
     w_up, bias_up, w_down, bias_down, segments, random_blocks, global_blocks, cotangent,
 ):
-    y_at, core_at, col_at = (lax.axis_index(name) for name in ("y", "core", "col"))
+    depth_at, y_at, core_at, col_at = (lax.axis_index(name) for name in ("dp", "y", "core", "col"))
     length = segments.shape[1]
-    narrow = inputs.shape[1]
-    inputs_pair = inputs.reshape(2, length, narrow)
-    cot_pair = cotangent.reshape(2, length, narrow)
-    x_own = pick(inputs_pair, y_at)
-    x_y = swap(pick(inputs_pair, 1 - y_at), "y")
-
-    def half(weight, axis, index):
-        size = weight.shape[axis] // 2
-        return lax.dynamic_slice_in_dim(weight, index * size, size, axis)
+    n = inputs.shape[1]
+    h = 2 * n
+    at = jnp.stack((y_at, col_at)).astype(jnp.int32)
 
     def chip_block(weights, axis, join):
         mine = jnp.concatenate([half(w, axis, core_at) for w in weights], axis=axis)
         theirs = swap(jnp.concatenate([half(w, axis, 1 - core_at) for w in weights], axis=axis), "core")
         return jnp.concatenate((mine, theirs), axis=join)
 
-    qkv_block = chip_block((w_query, w_key, w_value), 1, 0)
-    qkv_own, qkv_x, qkv_y, qkv_xy = plane_gather(qkv_block, "y", "col")
-    x_core, x_ycore = swap(x_own, "core"), swap(x_y, "core")
+    inputs_pair = inputs.reshape(2, length, n)
+    cot_pair = cotangent.reshape(2, length, n)
+    x_own = pick(inputs_pair, y_at)
+    x_y = swap(pick(inputs_pair, 1 - y_at), "y")
+    qkv_own, qkv_y, qkv_x, qkv_xy = plane_gather(chip_block((w_query, w_key, w_value), 1, 0))
+    xs = (x_own, swap(x_own, "core"), x_y, swap(x_y, "core"))
+    out_own, out_y, out_x, out_xy = plane_gather(chip_block((w_output,), 0, 1))
+    ups = lax.all_gather(chip_block((w_up,), 1, 0), ("y", "col"), axis=0, tiled=False)
+    downs = lax.all_gather(chip_block((w_down,), 0, 1), ("y", "col"), axis=0, tiled=False)
 
     vectors = jnp.stack((gain_first, shift_first, gain_second, shift_second, bias_down))
     vectors = jnp.concatenate((vectors, swap(vectors, "core")), axis=1)
     vectors = jnp.concatenate((vectors, swap(vectors, "y")), axis=1)
-    gain_one, shift_one, gain_two, shift_two, bias_low = (vectors[i] for i in range(5))
+    gain_one, shift_one, gain_two, shift_two, bias_low = (vectors[i : i + 1] for i in range(5))
     heads_half = half(random_blocks, 0, core_at)
     hidden_bias = half(bias_up, 0, core_at)
-    small = jnp.concatenate((hidden_bias, heads_half.astype(FULL).reshape(-1)))
-    small = swap(small, "col")
-    hidden_bias_x = small[: hidden_bias.shape[0]]
-    heads_half_x = small[hidden_bias.shape[0] :].reshape(heads_half.shape).astype(jnp.int32)
+    each = hidden_bias.shape[0]
+    small = swap(jnp.concatenate((hidden_bias, heads_half.astype(FULL).reshape(-1))), "col")
+    biases = jnp.concatenate((hidden_bias, small[:each]))
+    heads_half_x = small[each:].reshape(heads_half.shape).astype(jnp.int32)
     moves = []
     for y in range(2):
         for core in range(2):
@@ -565,152 +868,90 @@
     all_heads = jnp.concatenate((heads_half, heads_half_x), axis=0)
     rows_extra, keys_extra, where_table = attention_extras(labels, all_heads, global_blocks)
     near_heads = heads_half.shape[0]
+    keys_of = (keys_extra[:near_heads], keys_extra[near_heads:])
     live = (labels != 0)[:, None]
 
-    out_block = chip_block((w_output,), 0, 1)
-    up_block = chip_block((w_up,), 1, 0)
-    down_block = chip_block((w_down,), 0, 1)
-    out_own, out_x, out_y, out_xy = plane_gather(out_block, "col", "y")
-    up_own, up_x, up_y, up_xy = plane_gather(up_block, "col", "y")
-    down_own, down_x, down_y, down_xy = plane_gather(down_block, "y", "col")
     cot_own = pick(cot_pair, y_at)
     cot_y = swap(pick(cot_pair, 1 - y_at), "y")
-    cot = jnp.concatenate((cot_own, swap(cot_own, "core"), cot_y, swap(cot_y, "core")), axis=1)
-
-    x_full = jnp.concatenate((x_own, x_core, x_y, x_ycore), axis=1).astype(FULL)
-
-    def norm_stats(moving):
-        center = jnp.mean(moving, axis=1, keepdims=True)
-        spread = jnp.mean(moving * moving, axis=1, keepdims=True) - center * center
-        return center, lax.rsqrt(spread + EPS)
-
-    center_one, inverse_one = norm_stats(x_full)
-    normed_one = (x_full - center_one) * inverse_one
-    first = (normed_one * gain_one + shift_one).astype(LOW)
-
+    cots = tuple(jnp.concatenate((c, swap(c, "core")), axis=1) for c in (cot_own, cot_y))
+
+    firsts = first_norm(xs, gain_one, shift_one)
     w_qkv = (jnp.concatenate((qkv_own, qkv_y), axis=0), jnp.concatenate((qkv_x, qkv_xy), axis=0))
-    qkv = [dot_nn(first, w).astype(LOW) for w in w_qkv]
-    keys_of = (keys_extra[:near_heads], keys_extra[near_heads:])
-    heads, kept = zip(*[attend_forward(qkv[i], rows_extra, keys_of[i], where_table) for i in range(2)])
+    first = jnp.concatenate(firsts, axis=1)
     w_out = (jnp.concatenate((out_own, out_y), axis=1), jnp.concatenate((out_x, out_xy), axis=1))
-    mixed_part = (dot_nn(heads[0], w_out[0]) + dot_nn(heads[1], w_out[1])).astype(LOW)
-    mixed = mixed_part.astype(FULL) + swap_features(mixed_part).astype(FULL)
-    residual = x_full + mixed
-    center_two, inverse_two = norm_stats(residual)
-    normed_two = (residual - center_two) * inverse_two
-    second = (normed_two * gain_two + shift_two).astype(LOW)
-
-    w_ups = (jnp.concatenate((up_own, up_y), axis=0), jnp.concatenate((up_x, up_xy), axis=0))
-    w_downs = (jnp.concatenate((down_own, down_y), axis=1), jnp.concatenate((down_x, down_xy), axis=1))
-    biases = (hidden_bias, hidden_bias_x)
-    low_part, second_part = 0.0, 0.0
-    up_grads, down_grads, bias_grads = [], [], []
+    qkv, heads, kept = [], [], []
     for i in range(2):
-        upward = dot_nn(second, w_ups[i]) + biases[i]
-        activated, pull_back = jax.vjp(gelu_tanh, upward)
-        hidden = activated.astype(LOW)
-        grad_upward = pull_back(dot_nt(cot, w_downs[i]))[0].astype(LOW)
-        low_part = low_part + dot_nn(hidden, w_downs[i])
-        second_part = second_part + dot_nt(grad_upward, w_ups[i])
-        up_grads.append(dot_tn(second, grad_upward).astype(LOW))
-        down_grads.append(dot_tn(hidden, cot).astype(LOW))
-        bias_grads.append(jnp.sum(grad_upward, axis=0, dtype=FULL))
-
-    def own_columns(part):
-        low = part.astype(LOW)
-        n = narrow
-        mine = jnp.concatenate((low[:, :n], low[:, 2 * n : 3 * n]), axis=1)
-        theirs = swap(jnp.concatenate((low[:, n : 2 * n], low[:, 3 * n :]), axis=1), "core")
-        return mine.astype(FULL) + theirs.astype(FULL)
-
-    def mine_of(array):
-        return jnp.concatenate((array[..., :narrow], array[..., 2 * narrow : 3 * narrow]), axis=-1)
-
-    low_own = mine_of(residual) + own_columns(low_part) + mine_of(bias_low)
-
-    def to_shard(columns, dtype):
-        back = swap(columns[:, narrow:].astype(LOW), "y")
-        return ordered(columns[:, :narrow].astype(dtype), back.astype(dtype), y_at).reshape(2 * length, narrow)
-
-    layer_out = to_shard(low_own, LOW)
-
-    second_low = second_part.astype(LOW)
-    grad_second = second_low.astype(FULL) + swap_features(second_low).astype(FULL)
-    scaled = grad_second * gain_two
-    mean_one = jnp.mean(scaled, axis=1, keepdims=True)
-    mean_two = jnp.mean(scaled * normed_two, axis=1, keepdims=True)
-    grad_residual = cot.astype(FULL) + inverse_two * (scaled - mean_one - normed_two * mean_two)
-    grad_gain_two = jnp.sum(mine_of(grad_second * normed_two), axis=0)
-    grad_shift_two = jnp.sum(mine_of(grad_second), axis=0)
-    grad_mixed = grad_residual.astype(LOW)
-    grads = [jnp.where(live, dot_nt(grad_mixed, w), 0.0).astype(LOW) for w in w_out]
-    out_grads = [dot_tn(heads[i], grad_mixed).astype(LOW) for i in range(2)]
-    qkv_grads, first_part = [], 0.0
-    for i in range(2):
-        pieces = attend_backward(kept[i], qkv[i], keys_of[i], heads[i], grads[i], where_table)
-        joined = jnp.concatenate(pieces, axis=1)
-        qkv_grads.append(dot_tn(first, joined).astype(LOW))
-        first_part = first_part + dot_nt(joined, w_qkv[i])
-    scaled_part = first_part * gain_one
-    sums = jnp.stack((jnp.sum(scaled_part, axis=1), jnp.sum(scaled_part * normed_one, axis=1)))
-    sums = (sums + swap(sums, "core")) / (4 * narrow)
-    grad_first = own_columns(first_part)
-    normed_mine = mine_of(normed_one)
-    grad_x = inverse_one * (grad_first * mine_of(gain_one) - sums[0][:, None] - normed_mine * sums[1][:, None])
-    grad_inputs = to_shard(mine_of(grad_residual) + grad_x, FULL)
-    grad_gain_one = jnp.sum(grad_first * normed_mine, axis=0)
-    grad_shift_one = jnp.sum(grad_first, axis=0)
-
-    gains = jnp.stack((grad_gain_one, grad_shift_one, grad_gain_two, grad_shift_two)).reshape(4, 2, narrow)
-    down_bias = jnp.sum(cotangent, axis=0, dtype=FULL)
-    gains = jnp.stack([ordered(gains[i, 0], gains[i, 1], y_at) for i in range(4)])
-    bias_pair = ordered(down_bias, jnp.zeros_like(down_bias), y_at)
-    gains = jnp.concatenate((gains, bias_pair[None]), axis=0)
-    gains = jnp.stack((jnp.where(core_at == 0, gains, 0.0), jnp.where(core_at == 0, 0.0, gains)))
-    ups = ordered(bias_grads[0], bias_grads[1], col_at)
-    ups = jnp.stack((jnp.where(core_at == 0, ups, 0.0), jnp.where(core_at == 0, 0.0, ups)), axis=1)
-    flat = lax.psum(jnp.concatenate((gains.reshape(-1), ups.reshape(-1))), ("dp", "y", "core", "col"))
-    gains = flat[: gains.size].reshape(gains.shape)
-    gains = pick(pick(gains, core_at).swapaxes(0, 1), y_at)
-    grad_up_bias = pick(flat[gains.size * 4 :].reshape(2, -1), col_at)
-
-    h = narrow * 2
-
-    def finish(total, axis):
-        total = lax.psum(total, "dp")
-        size = total.shape[axis] // 2
-        keep = lax.slice_in_dim(total, 0, size, axis=axis)
-        got = swap(lax.slice_in_dim(total, size, 2 * size, axis=axis), "core")
-        return keep, got
-
-    def reduce_rows(pair, order):
-        return plane_reduce(pair[0][:h], pair[1][:h], pair[0][h:], pair[1][h:], *order)
-
-    def reduce_columns(pair, order):
-        return plane_reduce(pair[0][:, :h], pair[1][:, :h], pair[0][:, h:], pair[1][:, h:], *order)
-
-    def across_cores(keep, got, parts, axis):
+        qkv.append(dot_nn(first, w_qkv[i]).astype(LOW))
+        done, saved = attend_forward(qkv[i], rows_extra, keys_of[i], where_table)
+        heads.append(done)
+        kept.append(saved)
+    mixed_part = mix_heads(heads, w_out)
+    residual, *seconds = second_norm(xs, mixed_part, swap(mixed_part, "core"), gain_two, shift_two)
+
+    second_part, hidden0, hidden1, grad0, grad1, bias_sum = feed_forward(at, seconds, cots, ups, downs, biases)
+    hiddens, up_sides = (hidden0, hidden1), (grad0, grad1)
+    second_got = swap(second_part, "core")
+    down_grads = [[dot_tn(hid, c).astype(LOW) for c in cots] for hid in hiddens]
+    up_grads = [[dot_tn(s, g).astype(LOW) for s in seconds] for g in up_sides]
+    down_total = plane_reduce(down_grads[0][0], down_grads[0][1], down_grads[1][0], down_grads[1][1])
+    up_total = plane_reduce(up_grads[0][0], up_grads[0][1], up_grads[1][0], up_grads[1][1])
+
+    grad_own, grad_other, grad_mixed, sums_two = second_norm_back(residual, second_part, second_got, *cots, gain_two)
+    grads = jnp.where(live, dot_nt(grad_mixed, jnp.concatenate(w_out, axis=0)), 0.0).astype(LOW)
+    out_grads = [dot_tn(head, grad_mixed).astype(LOW) for head in heads]
+    out_total = plane_reduce(out_grads[0][:, :h], out_grads[0][:, h:], out_grads[1][:, :h], out_grads[1][:, h:])
+    qkv_sides, qkv_grads = [None, None], [None, None]
+    for i in (1, 0):
+        qkv_sides[i] = attend_backward(kept[i], qkv[i], keys_of[i], heads[i], grads, i, where_table)
+        qkv_grads[i] = [dot_tn(f, qkv_sides[i]).astype(LOW) for f in firsts]
+    qkv_total = plane_reduce(qkv_grads[0][0], qkv_grads[0][1], qkv_grads[1][0], qkv_grads[1][1])
+    first_part = dot_nt(jnp.concatenate(qkv_sides, axis=1), jnp.concatenate(w_qkv, axis=1)).astype(LOW)
+    mine, theirs, sums_one = first_norm_back(xs, first_part, swap(first_part, "core"), grad_own, grad_other, gain_one)
+    grad_inputs = ordered(mine, swap(theirs, "y").astype(FULL), y_at).reshape(2 * length, n)
+
+    ends_own, ends_other = layer_end(at, hiddens, downs)
+    kept_two = jnp.concatenate((residual[:, :n], residual[:, 2 * n : 3 * n]), axis=1)
+    bias_two = jnp.concatenate((bias_low[:, :n], bias_low[:, 2 * n : 3 * n]), axis=1)
+    ends = (kept_two + ends_own + swap(ends_other, "core").astype(FULL) + bias_two).astype(LOW)
+    layer_out = ordered(ends[:, :n], swap(ends[:, n:], "y"), y_at).reshape(2 * length, n)
+
+    gains = jnp.concatenate((sums_one[:2, :n], sums_two[:2, :n])).reshape(-1)
+    gains_y = jnp.concatenate((sums_one[:2, n:], sums_two[:2, n:])).reshape(-1)
+    up_bias = bias_sum[:, 0, :].reshape(-1)
+    got = swap(jnp.concatenate((gains_y, up_bias)), "y")
+    gains = gains + got[: 4 * n]
+    up_bias = up_bias + got[4 * n :]
+    near = jnp.concatenate((gains, jnp.sum(cotangent, axis=0, dtype=FULL), up_bias[:each]))
+    near = near + swap(jnp.concatenate((near[: 5 * n], up_bias[each:])), "col")
+    near = near + lax.ppermute(near, "dp", [(0, 1), (1, 0), (2, 3), (3, 2)])
+    near = near + lax.ppermute(near, "dp", [(0, 2), (2, 0), (1, 3), (3, 1)])
+    gains = near[: 5 * n].reshape(5, n)
+    up_bias = ordered(near[5 * n :], swap(near[5 * n :], "core"), core_at).reshape(-1)
+
+    def finish(total, axis, parts):
+        total = depth_sum(total, depth_at)
+        keep = lax.slice_in_dim(total, 0, n, axis=axis)
+        got = swap(lax.slice_in_dim(total, n, 2 * n, axis=axis), "core")
+        size = keep.shape[1 - axis] // parts
+        flip = core_at == 0
         out = []
-        size = keep.shape[axis] // parts
         for i in range(parts):
-            a = lax.slice_in_dim(keep, i * size, (i + 1) * size, axis=axis)
-            b = lax.slice_in_dim(got, i * size, (i + 1) * size, axis=axis)
-            flip = core_at == 0
-            out.append(jnp.concatenate((jnp.where(flip, a, b), jnp.where(flip, b, a)), axis=axis).astype(FULL))
+            a, b = (lax.slice_in_dim(z, i * size, (i + 1) * size, axis=1 - axis) for z in (keep, got))
+            out.append(jnp.concatenate((jnp.where(flip, a, b), jnp.where(flip, b, a)), axis=1 - axis).astype(FULL))
         return out
 
-    (grad_down,) = across_cores(*finish(reduce_columns(down_grads, ("y", "col")), 1), 1, 0)
-    (grad_up,) = across_cores(*finish(reduce_rows(up_grads, ("col", "y")), 0), 1, 1)
-    (grad_out,) = across_cores(*finish(reduce_columns(out_grads, ("y", "col")), 1), 1, 0)
-    grad_qkv = across_cores(*finish(reduce_rows(qkv_grads, ("col", "y")), 0), 3, 1)
+    (grad_down,) = finish(down_total, 1, 1)
+    (grad_up,) = finish(up_total, 0, 1)
+    (grad_out,) = finish(out_total, 1, 1)
+    grad_query, grad_key, grad_value = finish(qkv_total, 0, 3)
     return (
-        layer_out, grad_inputs, gains[0], gains[1], *grad_qkv, grad_out, gains[2], gains[3],
-        grad_up, grad_up_bias, grad_down, gains[4],
+        layer_out, grad_inputs, gains[0], gains[1], grad_query, grad_key, grad_value, grad_out, gains[2], gains[3],
+        grad_up, up_bias, grad_down, gains[4],
     )
 
 
 def whole_sequences(mesh):
-    return mesh.shape["row"] == 4 and mesh.shape["col"] == 2
+    return mesh.shape["row"] == 4 and mesh.shape["col"] == 2 and mesh.shape["dp"] == 4
 
 
 def placements(row):

time: 571 us -> 577 us (1.011)
  Pallas kernels: 51 us -> 130 us
  starting transfers between devices: 44.9 us -> 103 us
  blocking collectives: 45.6 us -> 0 us
  matrix products: 88.5 us -> 43.7 us
  local copies, waits for them, and re-layouts: 69.5 us -> 28.7 us
  other arithmetic: 72.8 us -> 47.7 us
  waiting for transfers between devices: 176 us -> 201 us
    ppermute x0 -> x20, waiting for transfers between devices: none -> 91.8 us  [the longest x6 62.7 us: swap_across(): return lax.ppermute(array, ('y', 'col'), [(0, 3), (3, 0), (1, 2), (2, 1)])]
    pallas_call x2 -> x9, Pallas kernels: 25.9 us -> 104 us  [the longest x1 32.1 us: feed_forward(): pl.pallas_call(feed_forward_kernel, out_shape=(jax.ShapeDtypeStruct((leng...]
    ppermute x0 -> x20, starting transfers between devices: none -> 74 us  [the longest x1 32.3 us: fast_body(): near = near + lax.ppermute(near, 'dp', [(0, 1), (1, 0), (2, 3), (3, 2)])]
    psum x1 -> x0, waiting for transfers between devices: 57.6 us -> none  [finish(): total = lax.psum(total, 'dp')]
    psum x1 -> x0, blocking collectives: 45.6 us -> none  [fast_body(): lax.psum(jnp.concatenate((gains.reshape(-1), ups.reshape(-1))), ('dp', 'y...]
    dot_general x8 -> x2, matrix products: 35.4 us -> 8.38 us  [dot_nt(): lax.dot_general(left, right, (((1,), (1,)), ((), ())), preferred_element_...]
    dot_general x8 -> x2, matrix products: 31.6 us -> 7.23 us  [dot_nn(): lax.dot_general(left, right, (((1,), (0,)), ((), ())), preferred_element_...]
    convert_element_type x19 -> x13, other arithmetic: 30 us -> 10.2 us  [the longest x6 6.42 us: finish(): jnp.concatenate((jnp.where(flip, a, b), jnp.where(flip, b, a)), axis=1 -...]
  transfers between devices with their start and end apart: 50 -> 61, of which waited for: 13 -> 23; matrix products, arithmetic and copies ran while one was open for 38% -> 18% of each run, Pallas kernels for 9% -> 15%
where the time goes in v2:
time: 577 us; the launch traced here: 570 us
  waiting for transfers between devices  201 us (35%)
  Pallas kernels  130 us (23%)
  starting transfers between devices  103 us (18%)
  other arithmetic  47.7 us (8%)
  matrix products  43.7 us (8%)
  local copies, waits for them, and re-layouts  28.7 us (5%)
  between operations  15.7 us (3%)
    ppermute x38, waiting for transfers between devices, swap(): return lax.ppermute(array, axis, SWAP)  110 us
    ppermute x6, waiting for transfers between devices, swap_across(): return lax.ppermute(array, ('y', 'col'), [(0, 3), (3, 0), (1, 2), (2, 1)])  62.7 us
    ppermute x1, starting transfers between devices, fast_body(): near = near + lax.ppermute(near, 'dp', [(0, 1), (1, 0), (2, 3), (3, 2)])  32.3 us
    pallas_call x1, Pallas kernels, feed_forward(): pl.pallas_call(feed_forward_kernel, out_shape=(jax.ShapeDtypeStruct((leng...  32.1 us
    pallas_call x2, Pallas kernels, attend_backward(): pl.pallas_call(attend_backward_kernel, out_shape=jax.ShapeDtypeStruct((le...  30.1 us
    dot_general x14, matrix products, dot_tn(): lax.dot_general(left, right, (((0,), (0,)), ((), ())), preferred_element_...  28.1 us
    ppermute x38, starting transfers between devices, swap(): return lax.ppermute(array, axis, SWAP)  27.5 us
    pallas_call x2, Pallas kernels, attend_forward(): pl.pallas_call(attend_forward_kernel, out_shape=(jax.ShapeDtypeStruct((le...  26.5 us
  transfers between devices with their start and end apart: 61, of which 23 were waited for; matrix products, arithmetic and copies ran while one was open for 18% of the time, Pallas kernels for 15%

profile of v2, /device:TPU:0, one launch (start us, length us, event | category | flops | bytes accessed | tf_op | source)
XLA Modules:
  0.0 570.2 jit_solution(570159165222779424)
XLA Ops:
  9.1 1.5 collective-permute-done.19
  13.1 2.6 collective-permute-start.1
  27.6 3.4 collective-permute-start.20
  36.8 3.1 collective-permute-start.8
  39.9 2.1 pad_maximum_fusion.4
  47.2 2.0 collective-permute-start.14
  49.1 1.9 pad_maximum_fusion.6
  51.8 1.6 pad_maximum_fusion.1
  53.4 7.7 %collective-permute-done.13 = bf16[256,512]{1,0:T(8,128)(2,1)S(1)} collective-permute-done((bf16[256,512]{1,0:T(8,128)(2,1)S(1)}, bf16[256,512]{1,0:T(8,128)(2,1)S(1)}, u32[]{:S(2)}, u32[]{:S(2)}) %collective-permute-start.13) | collective-permute-done | bytes 262176 | tf_op jit(solution)/shard_map/ppermute | solution.py:270
  62.3 1.5 pad_maximum_fusion.16
  63.8 8.6 %collective-permute-done.14 = bf16[256,512]{1,0:T(8,128)(2,1)S(1)} collective-permute-done((bf16[256,512]{1,0:T(8,128)(2,1)S(1)}, bf16[256,512]{1,0:T(8,128)(2,1)S(1)}, u32[]{:S(2)}, u32[]{:S(2)}) %collective-permute-start.14) | collective-permute-done | bytes 262176 | tf_op jit(solution)/shard_map/ppermute | solution.py:803
  72.5 26.9 %collective-permute-done.12 = bf16[256,512]{1,0:T(8,128)(2,1)S(1)} collective-permute-done((bf16[256,512]{1,0:T(8,128)(2,1)S(1)}, bf16[256,512]{1,0:T(8,128)(2,1)S(1)}, u32[]{:S(2)}, u32[]{:S(2)}) %collective-permute-start.12) | collective-permute-done | bytes 262176 | tf_op jit(solution)/shard_map/ppermute | solution.py:270
  100.3 1.5 collective-permute-start.9
  103.1 5.2 first_norm.1
  110.0 4.3 convolution_convert_fusion.1.q_ref.k_ref.v_ref
  114.2 13.3 %attend_forward.2 = (bf16[1024,256]{1,0:T(8,128)(2,1)}, bf16[4,1024,128]{2,1,0:T(8,128)(2,1)}) custom-call(s32[2,4]{1,0:T(2,128)} %pad_add_fusion.1.where_ref, bf16[1024,768]{1,0:T(8,128)(2,1)} %convolution_convert_fusion.1.q_ref.k_ref.v_ref, bf16[1024,768]{1,0:T(8,128)(2,1)} %convolution_convert_fusion.1.q_ref.k_ref.v_ref, ...), custom_call_target="tpu_custom_call" | custom-call | flops 1073741824 | bytes 12582912 | tf_op jit(solution)/shard_map/attend_forward/pallas_call | solution.py:377
  127.5 4.8 collective-permute-done.9
  133.5 26.0 %collective-permute-done.10 = bf16[512,768]{1,0:T(8,128)(2,1)} collective-permute-done((bf16[512,768]{1,0:T(8,128)(2,1)}, bf16[512,768]{1,0:T(8,128)(2,1)}, u32[]{:S(2)}, u32[]{:S(2)}) %collective-permute-start.10) | collective-permute-done | bytes 786464 | tf_op jit(solution)/shard_map/ppermute | solution.py:803
  160.6 3.0 convolution_convert_fusion.q_ref.k_ref.v_ref
  163.6 13.3 %attend_forward.3 = (bf16[1024,256]{1,0:T(8,128)(2,1)}, bf16[4,1024,128]{2,1,0:T(8,128)(2,1)}) custom-call(s32[2,4]{1,0:T(2,128)} %pad_add_fusion.1.where_ref, bf16[1024,768]{1,0:T(8,128)(2,1)} %convolution_convert_fusion.q_ref.k_ref.v_ref, bf16[1024,768]{1,0:T(8,128)(2,1)} %convolution_convert_fusion.q_ref.k_ref.v_ref, ...), custom_call_target="tpu_custom_call" | custom-call | flops 1073741824 | bytes 12582912 | tf_op jit(solution)/shard_map/attend_forward/pallas_call | solution.py:377
  176.9 5.1 mix_heads.1.part_ref
  185.4 12.3 %collective-permute-done.17 = bf16[1024,256]{1,0:T(8,128)(2,1)} collective-permute-done((bf16[1024,256]{1,0:T(8,128)(2,1)}, bf16[1024,256]{1,0:T(8,128)(2,1)}, u32[]{:S(2)}, u32[]{:S(2)}) %collective-permute-start.17) | collective-permute-done | bytes 524320 | tf_op jit(solution)/shard_map/ppermute | solution.py:270
  202.0 2.3 pad_maximum_fusion.2.c_low.low_ref
  205.8 6.2 %second_norm.1 = (f32[1024,1024]{1,0:T(8,128)}, bf16[1024,512]{1,0:T(8,128)(2,1)}, bf16[1024,512]{1,0:T(8,128)(2,1)}) custom-call(bf16[1024,256]{1,0:T(8,128)(2,1)} %copy-done.5, bf16[1024,256]{1,0:T(8,128)(2,1)} %copy-done.6, bf16[1024,256]{1,0:T(8,128)(2,1)} %copy-done.7, bf16[1024,256]{1,0:T(8,128)(2,1)} %copy-done.8, ...), custom_call_target="tpu_custom_call" | custom-call | flops 7864320 | bytes 12582912 | tf_op jit(solution)/shard_map/second_norm/pallas_call | solution.py:564
  212.0 2.7 fusion.62
  214.7 32.1 %feed_forward.1 = (bf16[1024,1024]{1,0:T(8,128)(2,1)}, bf16[1024,1024]{1,0:T(8,128)(2,1)}, bf16[1024,1024]{1,0:T(8,128)(2,1)}, bf16[1024,1024]{1,0:T(8,128)(2,1)...) custom-call(s32[2]{0:T(128)} %pad_add_fusion.2.at_ref, bf16[1024,512]{1,0:T(8,128)(2,1)} %get-tuple-element.43.s_low, ...), custom_call_target="tpu_custom_call" | custom-call | flops 12884901888 | bytes 29360128 | tf_op jit(solution)/shard_map/feed_forward/pallas_call | solution.py:739
  246.8 4.0 convolution_convert_fusion.6
  250.8 2.3 convolution_convert_fusion.7
  253.1 10.0 %layer_end.1 = (f32[1024,512]{1,0:T(8,128)}, bf16[1024,512]{1,0:T(8,128)(2,1)}) custom-call(s32[2]{0:T(128)} %pad_add_fusion.2.at_ref, bf16[1024,1024]{1,0:T(8,128)(2,1)} %get-tuple-element.45.h0, bf16[1024,1024]{1,0:T(8,128)(2,1)} %get-tuple-element.46.h1, bf16[4,1024,512]{2,1,0:T(8,128)(2,1)} %bitcast.125, bf16[4,1024,512]{2,1,0:T(8,128)(2,1)} %bitcast.126, ...), custom_call_target="tpu_custom_call" | custom-call | flops 4294967296 | bytes 10485760 | tf_op jit(solution)/shard_map/layer_end/pallas_call | solution.py:779
  263.7 2.4 collective-permute-start.46
  266.1 2.7 convolution_convert_fusion.8
  272.6 2.6 convolution_convert_fusion.3
  275.2 2.4 collective-permute-start.54
  277.6 13.3 %collective-permute-done.46 = bf16[512,1024]{1,0:T(8,128)(2,1)S(1)} collective-permute-done((bf16[512,1024]{1,0:T(8,128)(2,1)}, bf16[512,1024]{1,0:T(8,128)(2,1)S(1)}, u32[]{:S(2)}, u32[]{:S(2)}) %collective-permute-start.46) | collective-permute-done | bytes 1048608 | tf_op jit(solution)/shard_map/ppermute | solution.py:803
  292.1 20.6 %collective-permute-done.45 = bf16[512,1024]{1,0:T(8,128)(2,1)S(1)} collective-permute-done((bf16[512,1024]{1,0:T(8,128)(2,1)}, bf16[512,1024]{1,0:T(8,128)(2,1)S(1)}, u32[]{:S(2)}, u32[]{:S(2)}) %collective-permute-start.45) | collective-permute-done | bytes 1048608 | tf_op jit(solution)/shard_map/ppermute | solution.py:270
  316.1 2.7 convolution_convert_fusion.5
  321.1 14.8 %collective-permute-done.54 = bf16[1024,512]{1,0:T(8,128)(2,1)S(1)} collective-permute-done((bf16[1024,512]{1,0:T(8,128)(2,1)S(1)}, bf16[1024,512]{1,0:T(8,128)(2,1)S(1)}, u32[]{:S(2)}, u32[]{:S(2)}) %collective-permute-start.54) | collective-permute-done | bytes 1048608 | tf_op jit(solution)/shard_map/ppermute | solution.py:803
  335.9 4.0 collective-permute-start.47
  339.9 17.2 %collective-permute-done.53 = bf16[1024,512]{1,0:T(8,128)(2,1)S(1)} collective-permute-done((bf16[1024,512]{1,0:T(8,128)(2,1)S(1)}, bf16[1024,512]{1,0:T(8,128)(2,1)S(1)}, u32[]{:S(2)}, u32[]{:S(2)}) %collective-permute-start.53) | collective-permute-done | bytes 1048608 | tf_op jit(solution)/shard_map/ppermute | solution.py:270
  358.5 4.3 collective-permute-start.55
  362.8 6.3 %collective-permute-done.22 = bf16[1024,256]{1,0:T(8,128)(2,1)S(1)} collective-permute-done((bf16[1024,256]{1,0:T(8,128)(2,1)S(1)}, bf16[1024,256]{1,0:T(8,128)(2,1)S(1)}, u32[]{:S(2)}, u32[]{:S(2)}) %collective-permute-start.22) | collective-permute-done | bytes 524320 | tf_op jit(solution)/shard_map/ppermute | solution.py:270
  369.1 8.1 %second_norm_back.1 = (f32[1024,256]{1,0:T(8,128)}, f32[1024,256]{1,0:T(8,128)}, bf16[1024,1024]{1,0:T(8,128)(2,1)}, f32[8,512]{1,0:T(8,128)}) custom-call(f32[1024,1024]{1,0:T(8,128)} %get-tuple-element.42.residual_ref, bf16[1024,1024]{1,0:T(8,128)(2,1)} %get-tuple-element.50.part_ref, bf16[1024,1024]{1,0:T(8,128)(2,1)} %collective-permute-done.23.got_ref, ...), custom_call_target="tpu_custom_call" | custom-call | flops 15728640 | bytes 16777216 | tf_op jit(solution)/shard_map/second_norm_back/pallas_call | solution.py:612
  377.3 2.6 convolution_convert_fusion.14
  381.6 2.4 collective-permute-start.39
  385.8 2.3 select_convert_fusion.1.grads_ref
  388.1 14.9 %attend_backward.3 = bf16[1024,768]{1,0:T(8,128)(2,1)} custom-call(s32[2,4]{1,0:T(2,128)} %pad_add_fusion.1.where_ref, bf16[4,1024,128]{2,1,0:T(8,128)(2,1)} %get-tuple-element.52.kept_ref, bf16[1024,768]{1,0:T(8,128)(2,1)} %convolution_convert_fusion.q_ref.k_ref.v_ref, bf16[1024,768]{1,0:T(8,128)(2,1)} %convolution_convert_fusion.q_ref.k_ref.v_ref, ...), custom_call_target="tpu_custom_call" | custom-call | flops 2684354560 | bytes 15728640 | tf_op jit(solution)/shard_map/attend_backward/pallas_call | solution.py:467
  403.0 3.6 convolution_convert_fusion.10
  406.6 15.2 %attend_backward.2 = bf16[1024,768]{1,0:T(8,128)(2,1)} custom-call(s32[2,4]{1,0:T(2,128)} %pad_add_fusion.1.where_ref, bf16[4,1024,128]{2,1,0:T(8,128)(2,1)} %get-tuple-element.49.kept_ref, bf16[1024,768]{1,0:T(8,128)(2,1)} %convolution_convert_fusion.1.q_ref.k_ref.v_ref, bf16[1024,768]{1,0:T(8,128)(2,1)} %convolution_convert_fusion.1.q_ref.k_ref.v_ref, ...), custom_call_target="tpu_custom_call" | custom-call | flops 2684354560 | bytes 15728640 | tf_op jit(solution)/shard_map/attend_backward/pallas_call | solution.py:467
  423.2 3.6 collective-permute-start.40
  426.8 6.1 %fusion.18.part_ref = bf16[1024,1024]{1,0:T(8,128)(2,1)S(1)} fusion(bf16[1024,768]{1,0:T(8,128)(2,1)} %copy-done.36, bf16[512,768]{1,0:T(8,128)(2,1)} %collective-permute-done.7, bf16[256,768]{1,0:T(8,128)(2,1)} %collective-permute-done.6, bf16[256,256]{1,0:T(8,128)(2,1)S(1)} %get-tuple-element.104, bf16[256,256]{1,0:T(8,128)(2,1)S(1)} %get-tuple-element.128, ...), kind=kOutput, calls=%fused_computation.28 | convolution fusion | flops 3247439872 | bytes 8388608 | tf_op jit(solution)/shard_map/dot_general | solution.py:278
  439.9 1.6 add.253
  441.5 1.6 add.258
  443.8 5.2 collective-permute-done.42
  451.6 5.9 %collective-permute-done.31 = bf16[512,768]{1,0:T(8,128)(2,1)S(1)} collective-permute-done((bf16[512,768]{1,0:T(8,128)(2,1)S(1)}, bf16[512,768]{1,0:T(8,128)(2,1)S(1)}, u32[]{:S(2)}, u32[]{:S(2)}) %collective-permute-start.31) | collective-permute-done | bytes 786464 | tf_op jit(solution)/shard_map/ppermute | solution.py:270
  459.0 10.2 %collective-permute-start.33 = (bf16[512,768]{1,0:T(8,128)(2,1)S(1)}, bf16[512,768]{1,0:T(8,128)(2,1)}, u32[]{:S(2)}, u32[]{:S(2)}) collective-permute-start(bf16[512,768]{1,0:T(8,128)(2,1)S(1)} %add_convert_fusion.2), channel_id=1, source_target_pairs={{0,8},{24,16},{1,9},{25,17},{2,10},{26,18},{3,11},{27,19},{4,12},{... | collective-permute-start | bytes 2359304 | tf_op jit(solution)/shard_map/ppermute | solution.py:816
  474.0 6.8 %first_norm_back.1 = (f32[1024,256]{1,0:T(8,128)}, bf16[1024,256]{1,0:T(8,128)(2,1)}, f32[8,512]{1,0:T(8,128)}) custom-call(bf16[1024,256]{1,0:T(8,128)(2,1)} %copy-done.5, bf16[1024,256]{1,0:T(8,128)(2,1)} %copy-done.6, bf16[1024,256]{1,0:T(8,128)(2,1)} %copy-done.7, bf16[1024,256]{1,0:T(8,128)(2,1)} %copy-done.8, bf16[1024,1024]{1,0:T(8,128)(2,1)} %copy-done.21, ...), custom_call_target="tpu_custom_call" | custom-call | flops 15728640 | bytes 10485760 | tf_op jit(solution)/shard_map/first_norm_back/pallas_call | solution.py:635
  481.9 3.4 collective-permute-done.26
  489.1 32.3 %collective-permute-start.28 = (f32[2304]{0:T(1024)S(1)}, f32[2304]{0:T(1024)S(1)}, u32[]{:S(2)}, u32[]{:S(2)}) collective-permute-start(f32[2304]{0:T(1024)S(1)} %maximum_add_fusion.1), channel_id=1, source_target_pairs={{0,8},{8,0},{16,24},{24,16},{1,9},{9,1},{17,25},{25,17},{2,10},{10... | collective-permute-start | bytes 27656 | tf_op jit(solution)/shard_map/ppermute | solution.py:926
  523.1 2.0 collective-permute-start.29
  526.6 1.8 collective-permute-start.25
  528.4 6.6 %collective-permute-done.29 = f32[2304]{0:T(1024)S(1)} collective-permute-done((f32[2304]{0:T(1024)S(1)}, f32[2304]{0:T(1024)S(1)}, u32[]{:S(2)}, u32[]{:S(2)}) %collective-permute-start.29) | collective-permute-done | bytes 9248 | tf_op jit(solution)/shard_map/ppermute | solution.py:927
  538.4 1.6 maximum_convert_fusion
  540.1 1.5 maximum_convert_fusion.1
  541.6 17.0 %collective-permute-done.35 = bf16[512,768]{1,0:T(8,128)(2,1)S(1)} collective-permute-done((bf16[512,768]{1,0:T(8,128)(2,1)S(1)}, bf16[512,768]{1,0:T(8,128)(2,1)S(1)}, u32[]{:S(2)}, u32[]{:S(2)}) %collective-permute-start.35) | collective-permute-done | bytes 786464 | tf_op jit(solution)/shard_map/ppermute | solution.py:818
  (338 shorter events, 94.0 us)
Async XLA Ops:
  7.2 207.5 %all-gather.5.cloned.1.call-start = ((), (), s32[]{:S(2)}) async-start(), calls=%async_computation | async-start | bytes 5242880 | tf_op jit(solution)/shard_map/all_gather | solution.py:849
  8.5 2.1 collective-permute-start.19
  11.7 202.9 %all-gather.7.cloned.1.call-start = ((), (), s32[]{:S(2)}) async-start(), calls=%async_computation.1 | async-start | bytes 5242880 | tf_op jit(solution)/shard_map/all_gather | solution.py:850
  12.7 89.4 %collective-permute-start = (bf16[1024,256]{1,0:T(8,128)(2,1)S(1)}, bf16[1024,256]{1,0:T(8,128)(2,1)S(1)}, u32[]{:S(2)}, u32[]{:S(2)}) collective-permute-start(bf16[1024,256]{1,0:T(8,128)(2,1)S(1)} %get-tuple-element.91.x0), channel_id=1, source_target_pairs={{0,2},{2,0},{1,3},{3,1},{4,6},{6,4},{5,7},{7,5},{8,10},{10,8},{9,1... | collective-permute-start | bytes 1572872 | tf_op jit(solution)/shard_map/ppermute | solution.py:270
  13.1 38.8 %collective-permute-start.1 = (bf16[1024,256]{1,0:T(8,128)(2,1)}, bf16[1024,256]{1,0:T(8,128)(2,1)S(1)}, u32[]{:S(2)}, u32[]{:S(2)}) collective-permute-start(bf16[1024,256]{1,0:T(8,128)(2,1)} %get-tuple-element.90), channel_id=1, source_target_pairs={{0,4},{4,0},{1,5},{5,1},{2,6},{6,2},{3,7},{7,3},{8,12},{12,8},{9,1... | collective-permute-start | bytes 1572872 | tf_op jit(solution)/shard_map/ppermute | solution.py:270
  15.7 11.9 %collective-permute-start.3 = (s32[1,1024]{1,0:T(1,128)}, s32[1,1024]{1,0:T(1,128)S(1)}, u32[]{:S(2)}, u32[]{:S(2)}) collective-permute-start(s32[1,1024]{1,0:T(1,128)} %param.30), channel_id=1, source_target_pairs={{0,0},{4,1},{1,2},{5,3},{2,4},{6,5},{3,6},{7,7},{8,8},{12,9},{9,10... | collective-permute-start | bytes 12296 | tf_op jit(solution)/shard_map/ppermute | solution.py:867
  17.7 27.1 %collective-permute-start.4 = (f32[5,256]{1,0:T(8,128)}, f32[5,256]{1,0:T(8,128)}, u32[]{:S(2)}, u32[]{:S(2)}) collective-permute-start(f32[5,256]{1,0:T(8,128)} %stack.83), channel_id=1, source_target_pairs={{0,2},{2,0},{1,3},{3,1},{4,6},{6,4},{5,7},{7,5},{8,10},{10,8},{9,1... | collective-permute-start | bytes 15368 | tf_op jit(solution)/shard_map/ppermute | solution.py:270
  21.1 26.1 %collective-permute-start.6 = (bf16[256,768]{1,0:T(8,128)(2,1)}, bf16[256,768]{1,0:T(8,128)(2,1)}, u32[]{:S(2)}, u32[]{:S(2)}) collective-permute-start(bf16[256,768]{1,0:T(8,128)(2,1)} %pad_maximum_fusion.9), channel_id=1, source_target_pairs={{0,2},{2,0},{1,3},{3,1},{4,6},{6,4},{5,7},{7,5},{8,10},{10,8},{9,1... | collective-permute-start | bytes 1179656 | tf_op jit(solution)/shard_map/ppermute | solution.py:270
  27.6 9.2 %collective-permute-start.20 = (bf16[1024,256]{1,0:T(8,128)(2,1)}, bf16[1024,256]{1,0:T(8,128)(2,1)}, u32[]{:S(2)}, u32[]{:S(2)}) collective-permute-start(bf16[1024,256]{1,0:T(8,128)(2,1)} %get-tuple-element.85), channel_id=1, source_target_pairs={{0,2},{2,0},{1,3},{3,1},{4,6},{6,4},{5,7},{7,5},{8,10},{10,8},{9,1... | collective-permute-start | bytes 1572872 | tf_op jit(solution)/shard_map/ppermute | solution.py:270
  36.8 5.2 collective-permute-start.8
  42.1 4.2 collective-permute-start.11
  45.5 5.5 collective-permute-start.5
  46.3 53.1 %copy-start.34 = (bf16[256,256]{1,0:T(8,128)(2,1)}, bf16[256,256]{1,0:T(8,128)(2,1)S(1)}, u32[]{:S(2)}) copy-start(bf16[256,256]{1,0:T(8,128)(2,1)S(1)} %collective-permute-done.11) | copy-start | bytes 393220
  46.3 14.8 %collective-permute-start.13 = (bf16[256,512]{1,0:T(8,128)(2,1)S(1)}, bf16[256,512]{1,0:T(8,128)(2,1)S(1)}, u32[]{:S(2)}, u32[]{:S(2)}) collective-permute-start(bf16[256,512]{1,0:T(8,128)(2,1)S(1)} %pad_maximum_fusion.10), channel_id=1, source_target_pairs={{0,1},{1,0},{2,3},{3,2},{4,5},{5,4},{6,7},{7,6},{8,9},{9,8},{10,11... | collective-permute-start | bytes 786440 | tf_op jit(solution)/shard_map/ppermute | solution.py:270
  47.2 25.3 %collective-permute-start.14 = (bf16[256,512]{1,0:T(8,128)(2,1)S(1)}, bf16[256,512]{1,0:T(8,128)(2,1)S(1)}, u32[]{:S(2)}, u32[]{:S(2)}) collective-permute-start(bf16[256,512]{1,0:T(8,128)(2,1)S(1)} %pad_maximum_fusion.10), channel_id=1, source_target_pairs={{0,5},{5,0},{1,4},{4,1},{2,7},{7,2},{3,6},{6,3},{8,13},{13,8},{9,1... | collective-permute-start | bytes 786440 | tf_op jit(solution)/shard_map/ppermute | solution.py:803
  51.0 58.9 %collective-permute-start.7 = (bf16[512,768]{1,0:T(8,128)(2,1)}, bf16[512,768]{1,0:T(8,128)(2,1)}, u32[]{:S(2)}, u32[]{:S(2)}) collective-permute-start(bf16[512,768]{1,0:T(8,128)(2,1)} %pad_maximum_fusion.6), channel_id=1, source_target_pairs={{0,4},{4,0},{1,5},{5,1},{2,6},{6,2},{3,7},{7,3},{8,12},{12,8},{9,1... | collective-permute-start | bytes 2359304 | tf_op jit(solution)/shard_map/ppermute | solution.py:270
  51.8 50.3 %collective-permute-start.2 = (bf16[1024,256]{1,0:T(8,128)(2,1)S(1)}, bf16[1024,256]{1,0:T(8,128)(2,1)S(1)}, u32[]{:S(2)}, u32[]{:S(2)}) collective-permute-start(bf16[1024,256]{1,0:T(8,128)(2,1)S(1)} %collective-permute-done.1.x2), channel_id=1, source_target_pairs={{0,2},{2,0},{1,3},{3,1},{4,6},{6,4},{5,7},{7,5},{8,10},{10,8},{9,1... | collective-permute-start | bytes 1572872 | tf_op jit(solution)/shard_map/ppermute | solution.py:270
  61.1 38.2 %collective-permute-start.12 = (bf16[256,512]{1,0:T(8,128)(2,1)S(1)}, bf16[256,512]{1,0:T(8,128)(2,1)S(1)}, u32[]{:S(2)}, u32[]{:S(2)}) collective-permute-start(bf16[256,512]{1,0:T(8,128)(2,1)S(1)} %pad_maximum_fusion.10), channel_id=1, source_target_pairs={{0,4},{4,0},{1,5},{5,1},{2,6},{6,2},{3,7},{7,3},{8,12},{12,8},{9,1... | collective-permute-start | bytes 786440 | tf_op jit(solution)/shard_map/ppermute | solution.py:270
  72.5 37.3 %copy-start.24 = (bf16[256,1024]{1,0:T(8,128)(2,1)}, bf16[256,1024]{1,0:T(8,128)(2,1)S(1)}, u32[]{:S(2)}) copy-start(bf16[256,1024]{1,0:T(8,128)(2,1)S(1)} %constant_dynamic-update-slice_fusion.4.w1) | copy-start | bytes 1572868
  100.3 32.0 %collective-permute-start.9 = (bf16[512,768]{1,0:T(8,128)(2,1)}, bf16[512,768]{1,0:T(8,128)(2,1)}, u32[]{:S(2)}, u32[]{:S(2)}) collective-permute-start(bf16[512,768]{1,0:T(8,128)(2,1)} %pad_maximum_fusion.6), channel_id=1, source_target_pairs={{0,1},{1,0},{2,3},{3,2},{4,5},{5,4},{6,7},{7,6},{8,9},{9,8},{10,11... | collective-permute-start | bytes 2359304 | tf_op jit(solution)/shard_map/ppermute | solution.py:270
  101.8 57.7 %collective-permute-start.10 = (bf16[512,768]{1,0:T(8,128)(2,1)}, bf16[512,768]{1,0:T(8,128)(2,1)}, u32[]{:S(2)}, u32[]{:S(2)}) collective-permute-start(bf16[512,768]{1,0:T(8,128)(2,1)} %pad_maximum_fusion.6), channel_id=1, source_target_pairs={{0,5},{5,0},{1,4},{4,1},{2,7},{7,2},{3,6},{6,3},{8,13},{13,8},{9,1... | collective-permute-start | bytes 2359304 | tf_op jit(solution)/shard_map/ppermute | solution.py:803
  181.9 22.4 %collective-permute-start.15 = (bf16[1024,1024]{1,0:T(8,128)(2,1)}, bf16[1024,1024]{1,0:T(8,128)(2,1)S(1)}, u32[]{:S(2)}, u32[]{:S(2)}) collective-permute-start(bf16[1024,1024]{1,0:T(8,128)(2,1)} %mix_heads.1.part_ref), channel_id=1, source_target_pairs={{0,2},{2,0},{1,3},{3,1},{4,6},{6,4},{5,7},{7,5},{8,10},{10,8},{9,1... | collective-permute-start | bytes 6291464 | tf_op jit(solution)/shard_map/ppermute | solution.py:270
  183.1 14.6 %collective-permute-start.17 = (bf16[1024,256]{1,0:T(8,128)(2,1)}, bf16[1024,256]{1,0:T(8,128)(2,1)}, u32[]{:S(2)}, u32[]{:S(2)}) collective-permute-start(bf16[1024,256]{1,0:T(8,128)(2,1)} %get-tuple-element.88), channel_id=1, source_target_pairs={{0,4},{4,0},{1,5},{5,1},{2,6},{6,2},{3,7},{7,3},{8,12},{12,8},{9,1... | collective-permute-start | bytes 1572872 | tf_op jit(solution)/shard_map/ppermute | solution.py:270
  183.8 18.2 %collective-permute-start.16 = (bf16[1024,256]{1,0:T(8,128)(2,1)}, bf16[1024,256]{1,0:T(8,128)(2,1)}, u32[]{:S(2)}, u32[]{:S(2)}) collective-permute-start(bf16[1024,256]{1,0:T(8,128)(2,1)} %get-tuple-element.89), channel_id=1, source_target_pairs={{0,2},{2,0},{1,3},{3,1},{4,6},{6,4},{5,7},{7,5},{8,10},{10,8},{9,1... | collective-permute-start | bytes 1572872 | tf_op jit(solution)/shard_map/ppermute | solution.py:270
  197.7 6.6 %collective-permute-start.18 = (bf16[1024,256]{1,0:T(8,128)(2,1)}, bf16[1024,256]{1,0:T(8,128)(2,1)S(1)}, u32[]{:S(2)}, u32[]{:S(2)}) collective-permute-start(bf16[1024,256]{1,0:T(8,128)(2,1)} %collective-permute-done.17), channel_id=1, source_target_pairs={{0,2},{2,0},{1,3},{3,1},{4,6},{6,4},{5,7},{7,5},{8,10},{10,8},{9,1... | collective-permute-start | bytes 1572872 | tf_op jit(solution)/shard_map/ppermute | solution.py:270
  263.1 12.1 %collective-permute-start.21 = (bf16[1024,512]{1,0:T(8,128)(2,1)}, bf16[1024,512]{1,0:T(8,128)(2,1)S(1)}, u32[]{:S(2)}, u32[]{:S(2)}) collective-permute-start(bf16[1024,512]{1,0:T(8,128)(2,1)} %get-tuple-element.48), channel_id=1, source_target_pairs={{0,2},{2,0},{1,3},{3,1},{4,6},{6,4},{5,7},{7,5},{8,10},{10,8},{9,1... | collective-permute-start | bytes 3145736 | tf_op jit(solution)/shard_map/ppermute | solution.py:270
  263.7 105.5 %collective-permute-start.23 = (bf16[1024,1024]{1,0:T(8,128)(2,1)}, bf16[1024,1024]{1,0:T(8,128)(2,1)}, u32[]{:S(2)}, u32[]{:S(2)}) collective-permute-start(bf16[1024,1024]{1,0:T(8,128)(2,1)} %get-tuple-element.50.part_ref), channel_id=1, source_target_pairs={{0,2},{2,0},{1,3},{3,1},{4,6},{6,4},{5,7},{7,5},{8,10},{10,8},{9,1... | collective-permute-start | bytes 6291464 | tf_op jit(solution)/shard_map/ppermute | solution.py:270
  263.7 27.2 %collective-permute-start.46 = (bf16[512,1024]{1,0:T(8,128)(2,1)}, bf16[512,1024]{1,0:T(8,128)(2,1)S(1)}, u32[]{:S(2)}, u32[]{:S(2)}) collective-permute-start(bf16[512,1024]{1,0:T(8,128)(2,1)} %convolution_convert_fusion.6), channel_id=1, source_target_pairs={{0,5},{5,0},{1,4},{4,1},{2,7},{7,2},{3,6},{6,3},{8,13},{13,8},{9,1... | collective-permute-start | bytes 3145736 | tf_op jit(solution)/shard_map/ppermute | solution.py:803
  266.1 46.6 %collective-permute-start.45 = (bf16[512,1024]{1,0:T(8,128)(2,1)}, bf16[512,1024]{1,0:T(8,128)(2,1)S(1)}, u32[]{:S(2)}, u32[]{:S(2)}) collective-permute-start(bf16[512,1024]{1,0:T(8,128)(2,1)} %convolution_convert_fusion.7), channel_id=1, source_target_pairs={{0,1},{1,0},{2,3},{3,2},{4,5},{5,4},{6,7},{7,6},{8,9},{9,8},{10,11... | collective-permute-start | bytes 3145736 | tf_op jit(solution)/shard_map/ppermute | solution.py:270
  268.8 50.5 %collective-permute-start.44 = (bf16[512,1024]{1,0:T(8,128)(2,1)S(1)}, bf16[512,1024]{1,0:T(8,128)(2,1)S(1)}, u32[]{:S(2)}, u32[]{:S(2)}) collective-permute-start(bf16[512,1024]{1,0:T(8,128)(2,1)S(1)} %convolution_convert_fusion.8), channel_id=1, source_target_pairs={{0,4},{4,0},{1,5},{5,1},{2,6},{6,2},{3,7},{7,3},{8,12},{12,8},{9,1... | collective-permute-start | bytes 3145736 | tf_op jit(solution)/shard_map/ppermute | solution.py:270
  272.6 41.4 %copy-start.12 = (bf16[1024,512]{1,0:T(8,128)(2,1)S(1)}, bf16[1024,512]{1,0:T(8,128)(2,1)}, u32[]{:S(2)}) copy-start(bf16[1024,512]{1,0:T(8,128)(2,1)} %get-tuple-element.43.s_low) | copy-start | bytes 3145732
  275.2 60.7 %collective-permute-start.54 = (bf16[1024,512]{1,0:T(8,128)(2,1)S(1)}, bf16[1024,512]{1,0:T(8,128)(2,1)S(1)}, u32[]{:S(2)}, u32[]{:S(2)}) collective-permute-start(bf16[1024,512]{1,0:T(8,128)(2,1)S(1)} %convolution_convert_fusion.2), channel_id=1, source_target_pairs={{0,5},{5,0},{1,4},{4,1},{2,7},{7,2},{3,6},{6,3},{8,13},{13,8},{9,1... | collective-permute-start | bytes 3145736 | tf_op jit(solution)/shard_map/ppermute | solution.py:803
  290.9 66.2 %collective-permute-start.53 = (bf16[1024,512]{1,0:T(8,128)(2,1)S(1)}, bf16[1024,512]{1,0:T(8,128)(2,1)S(1)}, u32[]{:S(2)}, u32[]{:S(2)}) collective-permute-start(bf16[1024,512]{1,0:T(8,128)(2,1)S(1)} %convolution_convert_fusion.3), channel_id=1, source_target_pairs={{0,1},{1,0},{2,3},{3,2},{4,5},{5,4},{6,7},{7,6},{8,9},{9,8},{10,11... | collective-permute-start | bytes 3145736 | tf_op jit(solution)/shard_map/ppermute | solution.py:270
  312.7 45.2 %collective-permute-start.52 = (bf16[1024,512]{1,0:T(8,128)(2,1)S(1)}, bf16[1024,512]{1,0:T(8,128)(2,1)S(1)}, u32[]{:S(2)}, u32[]{:S(2)}) collective-permute-start(bf16[1024,512]{1,0:T(8,128)(2,1)S(1)} %convolution_convert_fusion.4), channel_id=1, source_target_pairs={{0,4},{4,0},{1,5},{5,1},{2,6},{6,2},{3,7},{7,3},{8,12},{12,8},{9,1... | collective-permute-start | bytes 3145736 | tf_op jit(solution)/shard_map/ppermute | solution.py:270
  319.4 49.7 %collective-permute-start.22 = (bf16[1024,256]{1,0:T(8,128)(2,1)S(1)}, bf16[1024,256]{1,0:T(8,128)(2,1)S(1)}, u32[]{:S(2)}, u32[]{:S(2)}) collective-permute-start(bf16[1024,256]{1,0:T(8,128)(2,1)S(1)} %slice.226), channel_id=1, source_target_pairs={{0,4},{4,0},{1,5},{5,1},{2,6},{6,2},{3,7},{7,3},{8,12},{12,8},{9,1... | collective-permute-start | bytes 1572872 | tf_op jit(solution)/shard_map/ppermute | solution.py:270
  335.9 101.6 %collective-permute-start.47 = (bf16[512,1024]{1,0:T(8,128)(2,1)S(1)}, bf16[512,1024]{1,0:T(8,128)(2,1)}, u32[]{:S(2)}, u32[]{:S(2)}) collective-permute-start(bf16[512,1024]{1,0:T(8,128)(2,1)S(1)} %add_convert_fusion.1), channel_id=1, source_target_pairs={{0,8},{24,16},{1,9},{25,17},{2,10},{26,18},{3,11},{27,19},{4,12},{... | collective-permute-start | bytes 3145736 | tf_op jit(solution)/shard_map/ppermute | solution.py:816
  358.5 79.1 %collective-permute-start.55 = (bf16[1024,512]{1,0:T(8,128)(2,1)S(1)}, bf16[1024,512]{1,0:T(8,128)(2,1)}, u32[]{:S(2)}, u32[]{:S(2)}) collective-permute-start(bf16[1024,512]{1,0:T(8,128)(2,1)S(1)} %add_convert_fusion), channel_id=1, source_target_pairs={{0,8},{24,16},{1,9},{25,17},{2,10},{26,18},{3,11},{27,19},{4,12},{... | collective-permute-start | bytes 3145736 | tf_op jit(solution)/shard_map/ppermute | solution.py:816
  381.6 40.2 %collective-permute-start.39 = (bf16[256,512]{1,0:T(8,128)(2,1)}, bf16[256,512]{1,0:T(8,128)(2,1)}, u32[]{:S(2)}, u32[]{:S(2)}) collective-permute-start(bf16[256,512]{1,0:T(8,128)(2,1)} %get-tuple-element.93), channel_id=1, source_target_pairs={{0,5},{5,0},{1,4},{4,1},{2,7},{7,2},{3,6},{6,3},{8,13},{13,8},{9,1... | collective-permute-start | bytes 786440 | tf_op jit(solution)/shard_map/ppermute | solution.py:803
  384.0 37.8 %collective-permute-start.38 = (bf16[256,512]{1,0:T(8,128)(2,1)}, bf16[256,512]{1,0:T(8,128)(2,1)}, u32[]{:S(2)}, u32[]{:S(2)}) collective-permute-start(bf16[256,512]{1,0:T(8,128)(2,1)} %get-tuple-element.92), channel_id=1, source_target_pairs={{0,1},{1,0},{2,3},{3,2},{4,5},{5,4},{6,7},{7,6},{8,9},{9,8},{10,11... | collective-permute-start | bytes 786440 | tf_op jit(solution)/shard_map/ppermute | solution.py:270
  384.7 37.1 %collective-permute-start.37 = (bf16[256,512]{1,0:T(8,128)(2,1)}, bf16[256,512]{1,0:T(8,128)(2,1)}, u32[]{:S(2)}, u32[]{:S(2)}) collective-permute-start(bf16[256,512]{1,0:T(8,128)(2,1)} %slice.241), channel_id=1, source_target_pairs={{0,4},{4,0},{1,5},{5,1},{2,6},{6,2},{3,7},{7,3},{8,12},{12,8},{9,1... | collective-permute-start | bytes 786440 | tf_op jit(solution)/shard_map/ppermute | solution.py:270
  421.8 21.3 %collective-permute-start.32 = (bf16[512,768]{1,0:T(8,128)(2,1)}, bf16[512,768]{1,0:T(8,128)(2,1)S(1)}, u32[]{:S(2)}, u32[]{:S(2)}) collective-permute-start(bf16[512,768]{1,0:T(8,128)(2,1)} %convolution_convert_fusion.10), channel_id=1, source_target_pairs={{0,5},{5,0},{1,4},{4,1},{2,7},{7,2},{3,6},{6,3},{8,13},{13,8},{9,1... | collective-permute-start | bytes 2359304 | tf_op jit(solution)/shard_map/ppermute | solution.py:803
  423.2 9.9 %collective-permute-start.40 = (bf16[256,512]{1,0:T(8,128)(2,1)S(1)}, bf16[256,512]{1,0:T(8,128)(2,1)S(1)}, u32[]{:S(2)}, u32[]{:S(2)}) collective-permute-start(bf16[256,512]{1,0:T(8,128)(2,1)S(1)} %add_convert_fusion.3), channel_id=1, source_target_pairs={{0,8},{24,16},{1,9},{25,17},{2,10},{26,18},{3,11},{27,19},{4,12},{... | collective-permute-start | bytes 786440 | tf_op jit(solution)/shard_map/ppermute | solution.py:816
  433.0 39.7 %collective-permute-start.24 = (bf16[1024,1024]{1,0:T(8,128)(2,1)S(1)}, bf16[1024,1024]{1,0:T(8,128)(2,1)S(1)}, u32[]{:S(2)}, u32[]{:S(2)}) collective-permute-start(bf16[1024,1024]{1,0:T(8,128)(2,1)S(1)} %fusion.18.part_ref), channel_id=1, source_target_pairs={{0,2},{2,0},{1,3},{3,1},{4,6},{6,4},{5,7},{7,5},{8,10},{10,8},{9,1... | collective-permute-start | bytes 6291464 | tf_op jit(solution)/shard_map/ppermute | solution.py:270
  433.1 1.9 collective-permute-start.41
  435.1 14.0 %collective-permute-start.42 = (bf16[256,512]{1,0:T(8,128)(2,1)S(1)}, bf16[256,512]{1,0:T(8,128)(2,1)S(1)}, u32[]{:S(2)}, u32[]{:S(2)}) collective-permute-start(bf16[256,512]{1,0:T(8,128)(2,1)S(1)} %add.249), channel_id=1, source_target_pairs={{8,0},{16,24},{9,1},{17,25},{10,2},{18,26},{11,3},{19,27},{12,4},{... | collective-permute-start | bytes 786440 | tf_op jit(solution)/shard_map/ppermute | solution.py:818
  437.5 20.0 %collective-permute-start.31 = (bf16[512,768]{1,0:T(8,128)(2,1)S(1)}, bf16[512,768]{1,0:T(8,128)(2,1)S(1)}, u32[]{:S(2)}, u32[]{:S(2)}) collective-permute-start(bf16[512,768]{1,0:T(8,128)(2,1)S(1)} %convolution_convert_fusion.11), channel_id=1, source_target_pairs={{0,1},{1,0},{2,3},{3,2},{4,5},{5,4},{6,7},{7,6},{8,9},{9,8},{10,11... | collective-permute-start | bytes 2359304 | tf_op jit(solution)/shard_map/ppermute | solution.py:270
  437.6 21.0 %collective-permute-start.30 = (bf16[512,768]{1,0:T(8,128)(2,1)S(1)}, bf16[512,768]{1,0:T(8,128)(2,1)S(1)}, u32[]{:S(2)}, u32[]{:S(2)}) collective-permute-start(bf16[512,768]{1,0:T(8,128)(2,1)S(1)} %convolution_convert_fusion.12), channel_id=1, source_target_pairs={{0,4},{4,0},{1,5},{5,1},{2,6},{6,2},{3,7},{7,3},{8,12},{12,8},{9,1... | collective-permute-start | bytes 2359304 | tf_op jit(solution)/shard_map/ppermute | solution.py:270
  443.1 26.2 %collective-permute-start.48 = (bf16[512,1024]{1,0:T(8,128)(2,1)S(1)}, bf16[512,1024]{1,0:T(8,128)(2,1)S(1)}, u32[]{:S(2)}, u32[]{:S(2)}) collective-permute-start(bf16[512,1024]{1,0:T(8,128)(2,1)S(1)} %add.253), channel_id=1, source_target_pairs={{8,16},{16,8},{9,17},{17,9},{10,18},{18,10},{11,19},{19,11},{12,20... | collective-permute-start | bytes 3145736 | tf_op jit(solution)/shard_map/ppermute | solution.py:817
  449.1 21.9 %collective-permute-start.56 = (bf16[1024,512]{1,0:T(8,128)(2,1)S(1)}, bf16[1024,512]{1,0:T(8,128)(2,1)S(1)}, u32[]{:S(2)}, u32[]{:S(2)}) collective-permute-start(bf16[1024,512]{1,0:T(8,128)(2,1)S(1)} %add.258), channel_id=1, source_target_pairs={{8,16},{16,8},{9,17},{17,9},{10,18},{18,10},{11,19},{19,11},{12,20... | collective-permute-start | bytes 3145736 | tf_op jit(solution)/shard_map/ppermute | solution.py:817
  457.5 15.1 %collective-permute-start.43 = (bf16[256,256]{1,0:T(8,128)(2,1)S(1)}, bf16[256,256]{1,0:T(8,128)(2,1)S(1)}, u32[]{:S(2)}, u32[]{:S(2)}) collective-permute-start(bf16[256,256]{1,0:T(8,128)(2,1)S(1)} %slice.245), channel_id=1, source_target_pairs={{0,2},{2,0},{1,3},{3,1},{4,6},{6,4},{5,7},{7,5},{8,10},{10,8},{9,1... | collective-permute-start | bytes 393224 | tf_op jit(solution)/shard_map/ppermute | solution.py:270
  459.0 27.5 %collective-permute-start.33 = (bf16[512,768]{1,0:T(8,128)(2,1)S(1)}, bf16[512,768]{1,0:T(8,128)(2,1)}, u32[]{:S(2)}, u32[]{:S(2)}) collective-permute-start(bf16[512,768]{1,0:T(8,128)(2,1)S(1)} %add_convert_fusion.2), channel_id=1, source_target_pairs={{0,8},{24,16},{1,9},{25,17},{2,10},{26,18},{3,11},{27,19},{4,12},{... | collective-permute-start | bytes 2359304 | tf_op jit(solution)/shard_map/ppermute | solution.py:816
  469.7 51.7 %collective-permute-start.49 = (bf16[512,1024]{1,0:T(8,128)(2,1)S(1)}, bf16[512,1024]{1,0:T(8,128)(2,1)}, u32[]{:S(2)}, u32[]{:S(2)}) collective-permute-start(bf16[512,1024]{1,0:T(8,128)(2,1)S(1)} %add.254), channel_id=1, source_target_pairs={{8,0},{16,24},{9,1},{17,25},{10,2},{18,26},{11,3},{19,27},{12,4},{... | collective-permute-start | bytes 3145736 | tf_op jit(solution)/shard_map/ppermute | solution.py:818
  471.3 53.8 %collective-permute-start.57 = (bf16[1024,512]{1,0:T(8,128)(2,1)S(1)}, bf16[1024,512]{1,0:T(8,128)(2,1)}, u32[]{:S(2)}, u32[]{:S(2)}) collective-permute-start(bf16[1024,512]{1,0:T(8,128)(2,1)S(1)} %add.259), channel_id=1, source_target_pairs={{8,0},{16,24},{9,1},{17,25},{10,2},{18,26},{11,3},{19,27},{12,4},{... | collective-permute-start | bytes 3145736 | tf_op jit(solution)/shard_map/ppermute | solution.py:818
  481.5 3.8 collective-permute-start.26
  485.3 3.8 collective-permute-start.27
  487.9 48.9 %collective-permute-start.34 = (bf16[512,768]{1,0:T(8,128)(2,1)S(1)}, bf16[512,768]{1,0:T(8,128)(2,1)S(1)}, u32[]{:S(2)}, u32[]{:S(2)}) collective-permute-start(bf16[512,768]{1,0:T(8,128)(2,1)S(1)} %add.243), channel_id=1, source_target_pairs={{8,16},{16,8},{9,17},{17,9},{10,18},{18,10},{11,19},{19,11},{12,20... | collective-permute-start | bytes 2359304 | tf_op jit(solution)/shard_map/ppermute | solution.py:817
  489.1 34.0 %collective-permute-start.28 = (f32[2304]{0:T(1024)S(1)}, f32[2304]{0:T(1024)S(1)}, u32[]{:S(2)}, u32[]{:S(2)}) collective-permute-start(f32[2304]{0:T(1024)S(1)} %maximum_add_fusion.1), channel_id=1, source_target_pairs={{0,8},{8,0},{16,24},{24,16},{1,9},{9,1},{17,25},{25,17},{2,10},{10... | collective-permute-start | bytes 27656 | tf_op jit(solution)/shard_map/ppermute | solution.py:926
  522.8 15.6 %collective-permute-start.50 = (bf16[256,1024]{1,0:T(8,128)(2,1)S(1)}, bf16[256,1024]{1,0:T(8,128)(2,1)S(1)}, u32[]{:S(2)}, u32[]{:S(2)}) collective-permute-start(bf16[256,1024]{1,0:T(8,128)(2,1)S(1)} %slice.249), channel_id=1, source_target_pairs={{0,2},{2,0},{1,3},{3,1},{4,6},{6,4},{5,7},{7,5},{8,10},{10,8},{9,1... | collective-permute-start | bytes 1572872 | tf_op jit(solution)/shard_map/ppermute | solution.py:270
  523.1 11.9 %collective-permute-start.29 = (f32[2304]{0:T(1024)S(1)}, f32[2304]{0:T(1024)S(1)}, u32[]{:S(2)}, u32[]{:S(2)}) collective-permute-start(f32[2304]{0:T(1024)S(1)} %add.238), channel_id=1, source_target_pairs={{0,16},{16,0},{8,24},{24,8},{1,17},{17,1},{9,25},{25,9},{2,18},{18... | collective-permute-start | bytes 27656 | tf_op jit(solution)/shard_map/ppermute | solution.py:927
  526.5 13.5 %collective-permute-start.58 = (bf16[1024,256]{1,0:T(8,128)(2,1)S(1)}, bf16[1024,256]{1,0:T(8,128)(2,1)S(1)}, u32[]{:S(2)}, u32[]{:S(2)}) collective-permute-start(bf16[1024,256]{1,0:T(8,128)(2,1)S(1)} %slice.252), channel_id=1, source_target_pairs={{0,2},{2,0},{1,3},{3,1},{4,6},{6,4},{5,7},{7,5},{8,10},{10,8},{9,1... | collective-permute-start | bytes 1572872 | tf_op jit(solution)/shard_map/ppermute | solution.py:270
  526.6 32.2 %collective-permute-start.25 = (bf16[1024,256]{1,0:T(8,128)(2,1)S(1)}, bf16[1024,256]{1,0:T(8,128)(2,1)S(1)}, u32[]{:S(2)}, u32[]{:S(2)}) collective-permute-start(bf16[1024,256]{1,0:T(8,128)(2,1)S(1)} %copy-done.57), channel_id=1, source_target_pairs={{0,4},{4,0},{1,5},{5,1},{2,6},{6,2},{3,7},{7,3},{8,12},{12,8},{9,1... | collective-permute-start | bytes 1572872 | tf_op jit(solution)/shard_map/ppermute | solution.py:270
  535.0 1.2 collective-permute-start.51
  537.0 21.5 %collective-permute-start.35 = (bf16[512,768]{1,0:T(8,128)(2,1)S(1)}, bf16[512,768]{1,0:T(8,128)(2,1)S(1)}, u32[]{:S(2)}, u32[]{:S(2)}) collective-permute-start(bf16[512,768]{1,0:T(8,128)(2,1)S(1)} %add.244), channel_id=1, source_target_pairs={{8,0},{16,24},{9,1},{17,25},{10,2},{18,26},{11,3},{19,27},{12,4},{... | collective-permute-start | bytes 2359304 | tf_op jit(solution)/shard_map/ppermute | solution.py:818
  558.7 1.8 collective-permute-start.36
  (57 other events, 370.3 us)
Sparse Core Ops, SparseCore 0:
  11.9 83.2 all-gather.4
  97.0 73.3 all-gather.6

commit v3 on v2

--- a/solution.py
+++ b/solution.py
@@ -544,7 +544,7 @@
     )(*blocks, gain, shift)
 
 
-def second_norm_kernel(x0, x1, x2, x3, part_ref, got_ref, gain_ref, shift_ref, residual_ref, low_ref, high_ref):
+def second_norm_kernel(x0, x1, x2, x3, part_ref, got_ref, gain_ref, shift_ref, residual_ref, second_ref):
     n = x0.shape[1]
     blocks = []
     for i, x in enumerate((x0, x1, x2, x3)):
@@ -554,19 +554,18 @@
     for i, block in enumerate(blocks):
         residual_ref[:, i * n : (i + 1) * n] = block
         value = (block - center) * inverse * columns(gain_ref, i, n) + columns(shift_ref, i, n)
-        (low_ref, high_ref)[i // 2][:, (i % 2) * n : (i % 2 + 1) * n] = value.astype(LOW)
+        second_ref[i // 2, :, (i % 2) * n : (i % 2 + 1) * n] = value.astype(LOW)
 
 
 def second_norm(blocks, part, got, gain, shift):
     length, n = blocks[0].shape
     rows = row_tiles(length)
-    half = jax.ShapeDtypeStruct((length, 2 * n), LOW)
     return pl.pallas_call(
         second_norm_kernel,
-        out_shape=(jax.ShapeDtypeStruct((length, 4 * n), FULL), half, half),
+        out_shape=(jax.ShapeDtypeStruct((length, 4 * n), FULL), jax.ShapeDtypeStruct((2, length, 2 * n), LOW)),
         grid=(length // TILE,),
         in_specs=[rows(n)] * 4 + [rows(4 * n)] * 2 + [whole((1, 4 * n))] * 2,
-        out_specs=(rows(4 * n), rows(2 * n), rows(2 * n)),
+        out_specs=(rows(4 * n), pl.BlockSpec((2, TILE, 2 * n), lambda t: (0, t, 0))),
         name="second_norm",
         cost_estimate=cost(30 * length * n, 48 * length * n),
     )(*blocks, part, got, gain, shift)
@@ -593,18 +592,18 @@
 
 
 def second_norm_back_kernel(
-    residual_ref, part_ref, got_ref, low_ref, high_ref, gain_ref, own_ref, other_ref, mixed_ref, sums_ref
+    residual_ref, part_ref, got_ref, cots_ref, gain_ref, own_ref, other_ref, mixed_ref, sums_ref
 ):
     n = residual_ref.shape[1] // 4
     blocks = [columns(residual_ref, i, n) for i in range(4)]
     for i, grad in enumerate(norm_gradient(blocks, part_ref, got_ref, gain_ref, sums_ref)):
-        total = columns((low_ref, high_ref)[i // 2], i % 2, n).astype(FULL) + grad
+        total = cots_ref[i // 2, :, (i % 2) * n : (i % 2 + 1) * n].astype(FULL) + grad
         mixed_ref[:, i * n : (i + 1) * n] = total.astype(LOW)
         if i % 2 == 0:
             (own_ref, other_ref)[i // 2][...] = total
 
 
-def second_norm_back(residual, part, got, low, high, gain):
+def second_norm_back(residual, part, got, cots, gain):
     length, width = residual.shape
     n = width // 4
     rows = row_tiles(length)
@@ -613,11 +612,11 @@
         second_norm_back_kernel,
         out_shape=(one, one, jax.ShapeDtypeStruct((length, width), LOW), jax.ShapeDtypeStruct((8, 2 * n), FULL)),
         grid=(length // TILE,),
-        in_specs=[rows(width)] * 3 + [rows(2 * n)] * 2 + [whole((1, width))],
+        in_specs=[rows(width)] * 3 + [pl.BlockSpec((2, TILE, 2 * n), lambda t: (0, t, 0)), whole((1, width))],
         out_specs=(rows(n), rows(n), rows(width), whole((8, 2 * n))),
         name="second_norm_back",
         cost_estimate=cost(60 * length * n, 64 * length * n),
-    )(residual, part, got, low, high, gain)
+    )(residual, part, got, cots, gain)
 
 
 def first_norm_back_kernel(
@@ -670,12 +669,9 @@
 
 
 def feed_forward_kernel(
-    at_ref, s_low, s_high, c_low, c_high, u_low, u_high, d_low, d_high, bias_ref,
-    part_ref, hidden0, hidden1, grad0, grad1, bias_sum, low_sum, high_sum,
+    at_ref, s_ref, c_ref, u_low, u_high, d_low, d_high, bias_ref, part_ref, hidden_ref, grad_ref, bias_sum, low_sum, high_sum
 ):
     step = pl.program_id(0)
-    steps = pl.num_programs(0)
-    first = step < steps // 2
 
     @pl.when(step == 0)
     def _():
@@ -683,98 +679,151 @@
         high_sum[...] = jnp.zeros_like(high_sum)
 
     totals = 0.0
-    for t in range(s_low.shape[0] // TILE):
+    for t in range(s_ref.shape[1] // TILE):
         rows = slice(t * TILE, (t + 1) * TILE)
-        upward = dot_nn(s_low[rows, :], u_low[0]) + dot_nn(s_high[rows, :], u_high[0]) + bias_ref[0]
-        grad_hidden = dot_nt(c_low[rows, :], d_low[0]) + dot_nt(c_high[rows, :], d_high[0])
+        upward = dot_nn(s_ref[0, rows, :], u_low[0]) + dot_nn(s_ref[1, rows, :], u_high[0]) + bias_ref[0]
+        grad_hidden = dot_nt(c_ref[0, rows, :], d_low[0]) + dot_nt(c_ref[1, rows, :], d_high[0])
         square = upward * upward
         bent = jnp.tanh(upward * (ROOT + (ROOT * 0.044715) * square))
         lifted = 0.5 + 0.5 * bent
         slope = lifted + (0.5 * upward) * (1.0 - bent * bent) * (ROOT + (ROOT * 3 * 0.044715) * square)
-        hidden = (upward * lifted).astype(LOW)
+        hidden_ref[0, rows, :] = (upward * lifted).astype(LOW)
         grad = grad_hidden * slope
         totals = totals + jnp.sum(grad, axis=0, keepdims=True)
         grad = grad.astype(LOW)
-
-        @pl.when(first)
-        def _():
-            hidden0[rows, :] = hidden
-            grad0[rows, :] = grad
-
-        @pl.when(jnp.logical_not(first))
-        def _():
-            hidden1[rows, :] = hidden
-            grad1[rows, :] = grad
-
+        grad_ref[0, rows, :] = grad
         low_sum[rows, :] += dot_nt(grad, u_low[0])
         high_sum[rows, :] += dot_nt(grad, u_high[0])
     bias_sum[0] = jnp.broadcast_to(totals, bias_sum.shape[1:])
 
-    @pl.when(step == steps - 1)
+    @pl.when(step == pl.num_programs(0) - 1)
     def _():
         n = low_sum.shape[1]
         part_ref[:, :n] = low_sum[...].astype(LOW)
         part_ref[:, n:] = high_sum[...].astype(LOW)
 
 
-def feed_forward(at, seconds, cots, ups, downs, biases):
-    length, h = seconds[0].shape
-    each = ups.shape[2]
+def feed_forward(at, seconds, cots, weights, biases):
+    _, length, h = seconds.shape
+    each = weights.shape[1] // 2
     tiles = each // TILE
-    keep = pl.BlockSpec((length, h), lambda i, at: (0, 0))
+    per = h // TILE
+    keep = pl.BlockSpec((2, length, h), lambda i, at: (0, 0, 0))
 
     def up_spec(flip):
         return pl.BlockSpec(
-            (1, h, TILE), lambda i, at: ((at[0] ^ flip) * 2 + (at[1] ^ (i // tiles)), 0, lax.rem(i, tiles))
+            (1, h, TILE),
+            lambda i, at: (
+                (at[0] ^ flip) * 2 + (at[1] ^ (i // tiles)), lax.rem(i, tiles) // per, lax.rem(lax.rem(i, tiles), per)
+            ),
         )
 
     def down_spec(flip):
         return pl.BlockSpec(
-            (1, TILE, h), lambda i, at: ((at[0] ^ flip) * 2 + (at[1] ^ (i // tiles)), lax.rem(i, tiles), 0)
+            (1, TILE, h), lambda i, at: ((at[0] ^ flip) * 2 + (at[1] ^ (i // tiles)), tiles + lax.rem(i, tiles), 0)
         )
 
-    early = pl.BlockSpec((length, TILE), lambda i, at: (0, jnp.minimum(i, tiles - 1)))
-    late = pl.BlockSpec((length, TILE), lambda i, at: (0, jnp.maximum(i - tiles, 0)))
-    one = jax.ShapeDtypeStruct((length, each), LOW)
+    side = pl.BlockSpec((1, length, TILE), lambda i, at: (i // tiles, 0, lax.rem(i, tiles)))
+    one = jax.ShapeDtypeStruct((2, length, each), LOW)
     return pl.pallas_call(
         feed_forward_kernel,
         out_shape=(
-            jax.ShapeDtypeStruct((length, 2 * h), LOW), one, one, one, one,
-            jax.ShapeDtypeStruct((2 * tiles, 8, TILE), FULL),
+            jax.ShapeDtypeStruct((length, 2 * h), LOW), one, one, jax.ShapeDtypeStruct((2 * tiles, 8, TILE), FULL),
         ),
         grid_spec=pltpu.PrefetchScalarGridSpec(
             num_scalar_prefetch=1,
             grid=(2 * tiles,),
-            in_specs=[keep] * 4
+            in_specs=[keep] * 2
             + [up_spec(0), up_spec(1), down_spec(0), down_spec(1)]
             + [pl.BlockSpec((1, 1, TILE), lambda i, at: (i, 0, 0))],
             out_specs=(
-                pl.BlockSpec((length, 2 * h), lambda i, at: (0, 0)), early, late, early, late,
+                pl.BlockSpec((length, 2 * h), lambda i, at: (0, 0)), side, side,
                 pl.BlockSpec((1, 8, TILE), lambda i, at: (i, 0, 0)),
             ),
             scratch_shapes=[pltpu.VMEM((length, h), FULL), pltpu.VMEM((length, h), FULL)],
         ),
         name="feed_forward",
         cost_estimate=cost(12 * length * 2 * h * each, 8 * length * h + 16 * h * each + 16 * length * each),
-    )(at, *seconds, *cots, ups, ups, downs, downs, biases.reshape(2 * tiles, 1, TILE))
+    )(at, seconds, cots, weights, weights, weights, weights, biases.reshape(2 * tiles, 1, TILE))
+
+
+def up_grads_kernel(at_ref, s_ref, grad_ref, out_ref, turned):
+    h = out_ref.shape[2]
+
+    @pl.when(pl.program_id(1) == 0)
+    def _():
+        turned[...] = s_ref[0].T
+
+    for i in range(out_ref.shape[1] // h):
+        part = dot_nn(turned[...], grad_ref[0, :, i * h : (i + 1) * h])
+        out_ref[0, i * h : (i + 1) * h, :] = part.astype(LOW)
+
+
+def up_grads(at, seconds, grads):
+    _, length, h = seconds.shape
+    each = grads.shape[2]
+    return pl.pallas_call(
+        up_grads_kernel,
+        out_shape=jax.ShapeDtypeStruct((4, each, h), LOW),
+        grid_spec=pltpu.PrefetchScalarGridSpec(
+            num_scalar_prefetch=1,
+            grid=(2, 2),
+            in_specs=[
+                pl.BlockSpec((1, length, h), lambda y, c, at: (y, 0, 0)),
+                pl.BlockSpec((1, length, each), lambda y, c, at: (c, 0, 0)),
+            ],
+            out_specs=pl.BlockSpec((1, each, h), lambda y, c, at: ((at[0] ^ y) * 2 + (at[1] ^ c), 0, 0)),
+            scratch_shapes=[pltpu.VMEM((h, length), LOW)],
+        ),
+        name="up_grads",
+        cost_estimate=cost(8 * length * h * each, 4 * length * each + 8 * h * each),
+    )(at, seconds, grads)
+
+
+def down_grads_kernel(at_ref, hidden_ref, c_ref, out_ref):
+    turned = hidden_ref[0].T
+    for y in range(2):
+        out_ref[at_ref[0] ^ y, 0] = dot_nn(turned, c_ref[y]).astype(LOW)
+
+
+def down_grads(at, hiddens, cots):
+    _, length, h = cots.shape
+    each = hiddens.shape[2]
+    return pl.pallas_call(
+        down_grads_kernel,
+        out_shape=jax.ShapeDtypeStruct((2, 2, each, h), LOW),
+        grid_spec=pltpu.PrefetchScalarGridSpec(
+            num_scalar_prefetch=1,
+            grid=(2, each // h),
+            in_specs=[
+                pl.BlockSpec((1, length, h), lambda c, b, at: (c, 0, b)),
+                pl.BlockSpec((2, length, h), lambda c, b, at: (0, 0, 0)),
+            ],
+            out_specs=pl.BlockSpec((2, 1, h, h), lambda c, b, at: (0, at[1] ^ c, b, 0)),
+        ),
+        name="down_grads",
+        cost_estimate=cost(8 * length * h * each, 4 * length * each + 8 * h * each),
+    )(at, hiddens, cots)
 
 
 def layer_end_kernel(at_ref, h0, h1, w00, w01, w10, w11, own_ref, theirs_ref):
     n = own_ref.shape[1] // 2
     for j, (a, b) in enumerate(((w00, w01), (w10, w11))):
-        part = dot_nn(h0[...], a[0]) + dot_nn(h1[...], b[0])
+        part = dot_nn(h0[0], a[0]) + dot_nn(h1[0], b[0])
         own_ref[:, j * n : (j + 1) * n] = part[:, :n]
         theirs_ref[:, j * n : (j + 1) * n] = part[:, n:].astype(LOW)
 
 
-def layer_end(at, hiddens, downs):
-    length, each = hiddens[0].shape
-    h = downs.shape[2]
-    rows = pl.BlockSpec((TILE, each), lambda t, at: (t, 0))
+def layer_end(at, hiddens, weights):
+    _, length, each = hiddens.shape
+    h = weights.shape[2]
     out = pl.BlockSpec((TILE, h), lambda t, at: (t, 0))
 
+    def rows(c):
+        return pl.BlockSpec((1, TILE, each), lambda t, at: (c, t, 0))
+
     def weight(y, col):
-        return pl.BlockSpec((1, each, h), lambda t, at: ((at[0] ^ y) * 2 + (at[1] ^ col), 0, 0))
+        return pl.BlockSpec((1, each, h), lambda t, at: ((at[0] ^ y) * 2 + (at[1] ^ col), 1, 0))
 
     return pl.pallas_call(
         layer_end_kernel,
@@ -782,12 +831,16 @@
         grid_spec=pltpu.PrefetchScalarGridSpec(
             num_scalar_prefetch=1,
             grid=(length // TILE,),
-            in_specs=[rows, rows, weight(0, 0), weight(0, 1), weight(1, 0), weight(1, 1)],
+            in_specs=[rows(0), rows(1), weight(0, 0), weight(0, 1), weight(1, 0), weight(1, 1)],
             out_specs=(out, out),
         ),
         name="layer_end",
         cost_estimate=cost(8 * length * h * each, 8 * h * each + 12 * length * h),
-    )(at, *hiddens, downs, downs, downs, downs)
+    )(at, hiddens, hiddens, weights, weights, weights, weights)
+
+
+def after(values, *late):
+    return lax.optimization_barrier((values, late))[0]
 
 
 def pick(pair, index):
@@ -807,16 +860,33 @@
     return block, swap(block, "y"), swap(block, "col"), swap_across(block)
 
 
-def plane_reduce(own, at_y, at_col, across):
-    got = (swap(at_y, "y"), swap(at_col, "col"), swap_across(across))
+def plane_exchange(at_y, at_col, across):
+    return swap(at_y, "y"), swap(at_col, "col"), swap_across(across)
+
+
+def plane_sum(own, got):
     return (own.astype(FULL) + sum(g.astype(FULL) for g in got)).astype(LOW)
 
 
-def depth_sum(array, index):
-    near = array + lax.ppermute(array, "dp", [(0, 1), (3, 2)])
-    both = near + lax.ppermute(near, "dp", [(1, 2), (2, 1)])
-    back = lax.ppermute(both, "dp", [(1, 0), (2, 3)])
-    return jnp.where((index == 0) | (index == 3), back, both)
+def add_low(left, right):
+    return (left.astype(FULL) + right.astype(FULL)).astype(LOW)
+
+
+PAIRS = [(0, 1), (1, 0), (2, 3), (3, 2)]
+FAR = [(0, 2), (2, 0), (1, 3), (3, 1)]
+
+
+def depth_pair(array, odd):
+    halves = array.reshape(2, array.shape[0] // 2, array.shape[1])
+    return add_low(pick(halves, odd), lax.ppermute(pick(halves, 1 - odd), "dp", PAIRS))
+
+
+def depth_far(part):
+    return add_low(part, lax.ppermute(part, "dp", FAR))
+
+
+def depth_join(part, odd):
+    return ordered(part, lax.ppermute(part, "dp", PAIRS), odd).reshape(-1, part.shape[1])
 
 
 def half(weight, axis, index):
@@ -840,14 +910,19 @@
         return jnp.concatenate((mine, theirs), axis=join)
 
     inputs_pair = inputs.reshape(2, length, n)
-    cot_pair = cotangent.reshape(2, length, n)
     x_own = pick(inputs_pair, y_at)
     x_y = swap(pick(inputs_pair, 1 - y_at), "y")
-    qkv_own, qkv_y, qkv_x, qkv_xy = plane_gather(chip_block((w_query, w_key, w_value), 1, 0))
+    qkv_block = chip_block((w_query, w_key, w_value), 1, 0)
+    qkv_own, qkv_y, qkv_x, qkv_xy = plane_gather(qkv_block)
     xs = (x_own, swap(x_own, "core"), x_y, swap(x_y, "core"))
+    w_up, w_down = after((w_up, w_down), qkv_block)
+    up_block, down_block = chip_block((w_up,), 1, 0), chip_block((w_down,), 0, 1)
+    ups = up_block.shape[1] // h
+    ffn_block = jnp.concatenate([up_block[:, i * h : (i + 1) * h] for i in range(ups)] + [down_block])
+    ffn_block, w_output, cotangent_late = after((ffn_block, w_output, cotangent), qkv_y, qkv_x)
+    ffn = lax.all_gather(ffn_block, ("y", "col"), axis=0, tiled=False)
     out_own, out_y, out_x, out_xy = plane_gather(chip_block((w_output,), 0, 1))
-    ups = lax.all_gather(chip_block((w_up,), 1, 0), ("y", "col"), axis=0, tiled=False)
-    downs = lax.all_gather(chip_block((w_down,), 0, 1), ("y", "col"), axis=0, tiled=False)
+    cot_pair = cotangent_late.reshape(2, length, n)
 
     vectors = jnp.stack((gain_first, shift_first, gain_second, shift_second, bias_down))
     vectors = jnp.concatenate((vectors, swap(vectors, "core")), axis=1)
@@ -873,11 +948,13 @@
 
     cot_own = pick(cot_pair, y_at)
     cot_y = swap(pick(cot_pair, 1 - y_at), "y")
-    cots = tuple(jnp.concatenate((c, swap(c, "core")), axis=1) for c in (cot_own, cot_y))
+    cot_swapped = swap(cot_y, "core")
+    cots = jnp.stack([jnp.concatenate(c, axis=1) for c in ((cot_own, swap(cot_own, "core")), (cot_y, cot_swapped))])
 
     firsts = first_norm(xs, gain_one, shift_one)
     w_qkv = (jnp.concatenate((qkv_own, qkv_y), axis=0), jnp.concatenate((qkv_x, qkv_xy), axis=0))
     first = jnp.concatenate(firsts, axis=1)
+    out_own = after(out_own, cot_y, cot_swapped)
     w_out = (jnp.concatenate((out_own, out_y), axis=1), jnp.concatenate((out_x, out_xy), axis=1))
     qkv, heads, kept = [], [], []
     for i in range(2):
@@ -886,30 +963,36 @@
         heads.append(done)
         kept.append(saved)
     mixed_part = mix_heads(heads, w_out)
-    residual, *seconds = second_norm(xs, mixed_part, swap(mixed_part, "core"), gain_two, shift_two)
-
-    second_part, hidden0, hidden1, grad0, grad1, bias_sum = feed_forward(at, seconds, cots, ups, downs, biases)
-    hiddens, up_sides = (hidden0, hidden1), (grad0, grad1)
-    second_got = swap(second_part, "core")
-    down_grads = [[dot_tn(hid, c).astype(LOW) for c in cots] for hid in hiddens]
-    up_grads = [[dot_tn(s, g).astype(LOW) for s in seconds] for g in up_sides]
-    down_total = plane_reduce(down_grads[0][0], down_grads[0][1], down_grads[1][0], down_grads[1][1])
-    up_total = plane_reduce(up_grads[0][0], up_grads[0][1], up_grads[1][0], up_grads[1][1])
-
-    grad_own, grad_other, grad_mixed, sums_two = second_norm_back(residual, second_part, second_got, *cots, gain_two)
+    residual, seconds = second_norm(xs, mixed_part, swap(mixed_part, "core"), gain_two, shift_two)
+
+    second_part, hiddens, up_sides, bias_sum = feed_forward(at, seconds, cots, ffn, biases)
+    down_parts = down_grads(at, hiddens, cots).reshape(4, -1, h)
+    down_scattered = lax.psum_scatter(down_parts, ("y", "col"), scatter_dimension=0, tiled=True)[0]
+    up_parts = up_grads(at, seconds, after(up_sides, down_parts))
+    up_scattered = lax.psum_scatter(up_parts, ("y", "col"), scatter_dimension=0, tiled=True)[0]
+    second_got = after(swap(second_part, "core"), up_parts)
+
+    grad_own, grad_other, grad_mixed, sums_two = second_norm_back(residual, second_part, second_got, cots, gain_two)
     grads = jnp.where(live, dot_nt(grad_mixed, jnp.concatenate(w_out, axis=0)), 0.0).astype(LOW)
-    out_grads = [dot_tn(head, grad_mixed).astype(LOW) for head in heads]
-    out_total = plane_reduce(out_grads[0][:, :h], out_grads[0][:, h:], out_grads[1][:, :h], out_grads[1][:, h:])
+    out_grads = [[dot_tn(grad_mixed[:, j * h : (j + 1) * h], head).astype(LOW) for j in range(2)] for head in heads]
     qkv_sides, qkv_grads = [None, None], [None, None]
     for i in (1, 0):
         qkv_sides[i] = attend_backward(kept[i], qkv[i], keys_of[i], heads[i], grads, i, where_table)
         qkv_grads[i] = [dot_tn(f, qkv_sides[i]).astype(LOW) for f in firsts]
-    qkv_total = plane_reduce(qkv_grads[0][0], qkv_grads[0][1], qkv_grads[1][0], qkv_grads[1][1])
+    odd = lax.rem(depth_at, 2)
+    out_got = plane_exchange(out_grads[0][1], out_grads[1][0], out_grads[1][1])
+    qkv_got = plane_exchange(qkv_grads[0][1], qkv_grads[1][0], qkv_grads[1][1])
+    qkv_sides = after(qkv_sides, qkv_grads)
     first_part = dot_nt(jnp.concatenate(qkv_sides, axis=1), jnp.concatenate(w_qkv, axis=1)).astype(LOW)
+    first_part = after(first_part, out_got)
     mine, theirs, sums_one = first_norm_back(xs, first_part, swap(first_part, "core"), grad_own, grad_other, gain_one)
     grad_inputs = ordered(mine, swap(theirs, "y").astype(FULL), y_at).reshape(2 * length, n)
-
-    ends_own, ends_other = layer_end(at, hiddens, downs)
+    down_part = depth_pair(after(down_scattered, qkv_grads[0]), odd)
+
+    ends_own, ends_other = layer_end(at, after(hiddens, sums_one, down_part), ffn)
+    residual, up_scattered, down_part = lax.optimization_barrier((residual, up_scattered, down_part, ends_own))[:3]
+    up_total = lax.psum(up_scattered, "dp")
+    down_part = depth_far(down_part)
     kept_two = jnp.concatenate((residual[:, :n], residual[:, 2 * n : 3 * n]), axis=1)
     bias_two = jnp.concatenate((bias_low[:, :n], bias_low[:, 2 * n : 3 * n]), axis=1)
     ends = (kept_two + ends_own + swap(ends_other, "core").astype(FULL) + bias_two).astype(LOW)
@@ -929,7 +1012,6 @@
     up_bias = ordered(near[5 * n :], swap(near[5 * n :], "core"), core_at).reshape(-1)
 
     def finish(total, axis, parts):
-        total = depth_sum(total, depth_at)
         keep = lax.slice_in_dim(total, 0, n, axis=axis)
         got = swap(lax.slice_in_dim(total, n, 2 * n, axis=axis), "core")
         size = keep.shape[1 - axis] // parts
@@ -940,12 +1022,17 @@
             out.append(jnp.concatenate((jnp.where(flip, a, b), jnp.where(flip, b, a)), axis=1 - axis).astype(FULL))
         return out
 
+    four = jnp.concatenate(
+        (plane_sum(after(qkv_grads[0][0], up_scattered), qkv_got), plane_sum(out_grads[0][0], out_got)), axis=1
+    )
+    four = depth_pair(four, odd)
+    down_total = depth_join(after(down_part, four), odd)
+    four = depth_join(depth_far(four), odd)
+    grad_query, grad_key, grad_value, grad_out = finish(four, 0, 4)
     (grad_down,) = finish(down_total, 1, 1)
-    (grad_up,) = finish(up_total, 0, 1)
-    (grad_out,) = finish(out_total, 1, 1)
-    grad_query, grad_key, grad_value = finish(qkv_total, 0, 3)
+    (grad_up,) = finish(jnp.concatenate([up_total[i * h : (i + 1) * h] for i in range(ups)], axis=1), 0, 1)
     return (
-        layer_out, grad_inputs, gains[0], gains[1], grad_query, grad_key, grad_value, grad_out, gains[2], gains[3],
+        layer_out, grad_inputs, gains[0], gains[1], grad_query, grad_key, grad_value, grad_out.T, gains[2], gains[3],
         grad_up, up_bias, grad_down, gains[4],
     )
 

time: 577 us -> 484 us (0.84)
  starting transfers between devices: 103 us -> 51.3 us
  waiting for transfers between devices: 201 us -> 168 us
  matrix products: 43.7 us -> 30.5 us
  other arithmetic: 47.7 us -> 34.6 us
  Pallas kernels: 130 us -> 142 us
    ppermute x6 -> x4, waiting for transfers between devices: 62.7 us -> 6.84 us  [swap_across(): return lax.ppermute(array, ('y', 'col'), [(0, 3), (3, 0), (1, 2), (2, 1)])]
    ppermute x38 -> x33, waiting for transfers between devices: 110 us -> 57.9 us  [swap(): return lax.ppermute(array, axis, SWAP)]
    ppermute x12 -> x6, waiting for transfers between devices: 22.3 us -> 56.2 us  [the longest x2 32.8 us: depth_far(): return add_low(part, lax.ppermute(part, 'dp', FAR))]
    ppermute x1, starting transfers between devices: 32.3 us -> 3.74 us  [fast_body(): near = near + lax.ppermute(near, 'dp', [(0, 1), (1, 0), (2, 3), (3, 2)])]
    psum x0 -> x1, waiting for transfers between devices: none -> 24.9 us  [fast_body(): up_total = lax.psum(up_scattered, 'dp')]
    ppermute x12 -> x6, starting transfers between devices: 30.2 us -> 8.08 us  [the longest x2 5.58 us: depth_far(): return add_low(part, lax.ppermute(part, 'dp', FAR))]
    pallas_call x0 -> x2, Pallas kernels: none -> 20.3 us  [the longest x1 11.2 us: up_grads(): pl.pallas_call(up_grads_kernel, out_shape=jax.ShapeDtypeStruct((4, each,...]
    unnamed x2 -> x6, waiting for transfers between devices: 0.03 us -> 20.2 us
  transfers between devices with their start and end apart: 61 -> 50, of which waited for: 23 -> 21; matrix products, arithmetic and copies ran while one was open for 18% -> 17% of each run, Pallas kernels for 15% -> 22%
where the time goes in v3:
time: 484 us; the launch traced here: 476 us
  waiting for transfers between devices  168 us (35%)
  Pallas kernels  142 us (29%)
  starting transfers between devices  51.3 us (11%)
  other arithmetic  34.6 us (7%)
  local copies, waits for them, and re-layouts  33.8 us (7%)
  matrix products  30.5 us (6%)
  between operations  15.1 us (3%)
    ppermute x33, waiting for transfers between devices, swap(): return lax.ppermute(array, axis, SWAP)  57.9 us
    ppermute x2, waiting for transfers between devices, depth_far(): return add_low(part, lax.ppermute(part, 'dp', FAR))  32.8 us
    ppermute x33, starting transfers between devices, swap(): return lax.ppermute(array, axis, SWAP)  27.9 us
    pallas_call x2, Pallas kernels, attend_backward(): pl.pallas_call(attend_backward_kernel, out_shape=jax.ShapeDtypeStruct((le...  27.6 us
    pallas_call x1, Pallas kernels, feed_forward(): pl.pallas_call(feed_forward_kernel, out_shape=(jax.ShapeDtypeStruct((leng...  27.1 us
    pallas_call x2, Pallas kernels, attend_forward(): pl.pallas_call(attend_forward_kernel, out_shape=(jax.ShapeDtypeStruct((le...  25.5 us
    psum x1, waiting for transfers between devices, fast_body(): up_total = lax.psum(up_scattered, 'dp')  24.9 us
    unnamed x6, waiting for transfers between devices  20.2 us
  transfers between devices with their start and end apart: 50, of which 21 were waited for; matrix products, arithmetic and copies ran while one was open for 17% of the time, Pallas kernels for 22%

profile of v3, /device:TPU:0, one launch (start us, length us, event | category | flops | bytes accessed | tf_op | source)
XLA Modules:
  0.0 475.7 jit_solution(17855174933654547955)
XLA Ops:
  14.1 2.9 collective-permute-start.7
  16.9 1.5 collective-permute-start.9
  20.0 14.8 %collective-permute-done.7 = bf16[512,768]{1,0:T(8,128)(2,1)} collective-permute-done((bf16[512,768]{1,0:T(8,128)(2,1)S(1)}, bf16[512,768]{1,0:T(8,128)(2,1)}, u32[]{:S(2)}, u32[]{:S(2)}) %collective-permute-start.7) | collective-permute-done | bytes 786464 | tf_op jit(solution)/shard_map/ppermute | solution.py:270
  38.3 1.8 collective-permute-start.8
  50.1 3.5 collective-permute-start.2
  54.7 2.4 collective-permute-start.5
  57.1 1.5 pad_maximum_fusion.3
  59.3 1.5 pad_maximum_fusion.17
  60.9 5.0 %collective-permute-start.10 = (bf16[512,768]{1,0:T(8,128)(2,1)S(1)}, bf16[512,768]{1,0:T(8,128)(2,1)}, u32[]{:S(2)}, u32[]{:S(2)}) collective-permute-start(bf16[512,768]{1,0:T(8,128)(2,1)S(1)} %pad_maximum_fusion.7), channel_id=1, source_target_pairs={{0,5},{5,0},{1,4},{4,1},{2,7},{7,2},{3,6},{6,3},{8,13},{13,8},{9,1... | collective-permute-start | bytes 2359304 | tf_op jit(solution)/shard_map/ppermute | solution.py:856
  66.9 5.0 %first_norm.1 = (bf16[1024,512]{1,0:T(8,128)(2,1)}, bf16[1024,512]{1,0:T(8,128)(2,1)}) custom-call(bf16[1024,256]{1,0:T(8,128)(2,1)} %copy-done.2, bf16[1024,256]{1,0:T(8,128)(2,1)} %copy-done.4, bf16[1024,256]{1,0:T(8,128)(2,1)} %copy-done.3, bf16[1024,256]{1,0:T(8,128)(2,1)} %copy-done.5, f32[1,1024]{1,0:T(1,128)} %get-tuple-element.201.gain_ref, ...), custom_call_target="tpu_custom_call" | custom-call | flops 5242880 | bytes 4194304 | tf_op jit(solution)/shard_map/first_norm/pallas_call | solution.py:536
  71.9 1.5 constant_dynamic-update-slice_fusion.1
  74.6 2.0 collective-permute-start.14
  76.7 4.1 convolution_convert_fusion.1.q_ref.k_ref.v_ref
  82.0 6.8 %collective-permute-done.10 = bf16[512,768]{1,0:T(8,128)(2,1)} collective-permute-done((bf16[512,768]{1,0:T(8,128)(2,1)S(1)}, bf16[512,768]{1,0:T(8,128)(2,1)}, u32[]{:S(2)}, u32[]{:S(2)}) %collective-permute-start.10) | collective-permute-done | bytes 786464 | tf_op jit(solution)/shard_map/ppermute | solution.py:856
  90.7 11.2 %collective-permute-done.14 = bf16[1024,256]{1,0:T(8,128)(2,1)S(1)} collective-permute-done((bf16[1024,256]{1,0:T(8,128)(2,1)S(1)}, bf16[1024,256]{1,0:T(8,128)(2,1)S(1)}, u32[]{:S(2)}, u32[]{:S(2)}) %collective-permute-start.14) | collective-permute-done | bytes 524320 | tf_op jit(solution)/shard_map/ppermute | solution.py:270
  102.0 2.9 convolution_convert_fusion.q_ref.k_ref.v_ref
  104.9 1.6 collective-permute-start.18
  106.6 12.7 %attend_forward.3 = (bf16[1024,256]{1,0:T(8,128)(2,1)}, bf16[4,1024,128]{2,1,0:T(8,128)(2,1)}) custom-call(s32[2,4]{1,0:T(2,128)} %pad_add_fusion.1.where_ref, bf16[1024,768]{1,0:T(8,128)(2,1)} %convolution_convert_fusion.q_ref.k_ref.v_ref, bf16[1024,768]{1,0:T(8,128)(2,1)} %convolution_convert_fusion.q_ref.k_ref.v_ref, ...), custom_call_target="tpu_custom_call" | custom-call | flops 1073741824 | bytes 12582912 | tf_op jit(solution)/shard_map/attend_forward/pallas_call | solution.py:377
  119.3 12.9 %attend_forward.2 = (bf16[1024,256]{1,0:T(8,128)(2,1)}, bf16[4,1024,128]{2,1,0:T(8,128)(2,1)}) custom-call(s32[2,4]{1,0:T(2,128)} %pad_add_fusion.1.where_ref, bf16[1024,768]{1,0:T(8,128)(2,1)} %convolution_convert_fusion.1.q_ref.k_ref.v_ref, bf16[1024,768]{1,0:T(8,128)(2,1)} %convolution_convert_fusion.1.q_ref.k_ref.v_ref, ...), custom_call_target="tpu_custom_call" | custom-call | flops 1073741824 | bytes 12582912 | tf_op jit(solution)/shard_map/attend_forward/pallas_call | solution.py:377
  134.1 12.6 %collective-permute-done.16 = bf16[256,512]{1,0:T(8,128)(2,1)S(1)} collective-permute-done((bf16[256,512]{1,0:T(8,128)(2,1)S(1)}, bf16[256,512]{1,0:T(8,128)(2,1)S(1)}, u32[]{:S(2)}, u32[]{:S(2)}) %collective-permute-start.16) | collective-permute-done | bytes 262176 | tf_op jit(solution)/shard_map/ppermute | solution.py:270
  147.6 4.8 %mix_heads.1.part_ref = bf16[1024,1024]{1,0:T(8,128)(2,1)} custom-call(bf16[1024,256]{1,0:T(8,128)(2,1)} %get-tuple-element.55.h0.heads_ref, bf16[1024,256]{1,0:T(8,128)(2,1)} %get-tuple-element.56.h1.heads_ref, bf16[256,1024]{1,0:T(8,128)(2,1)} %copy-done.14, bf16[256,1024]{1,0:T(8,128)(2,1)} %copy-done.12), custom_call_target="tpu_custom_call" | custom-call | flops 1073741824 | bytes 5242880 | tf_op jit(solution)/shard_map/mix_heads/pallas_call | solution.py:657
  154.1 3.5 collective-permute-done.20
  161.8 6.3 %second_norm.1 = (f32[1024,1024]{1,0:T(8,128)}, bf16[2,1024,512]{2,1,0:T(8,128)(2,1)}) custom-call(bf16[1024,256]{1,0:T(8,128)(2,1)} %copy-done.2, bf16[1024,256]{1,0:T(8,128)(2,1)} %copy-done.4, bf16[1024,256]{1,0:T(8,128)(2,1)} %copy-done.3, bf16[1024,256]{1,0:T(8,128)(2,1)} %copy-done.5, bf16[1024,1024]{1,0:T(8,128)(2,1)} %mix_heads.1.part_ref, ...), custom_call_target="tpu_custom_call" | custom-call | flops 7864320 | bytes 12582912 | tf_op jit(solution)/shard_map/second_norm/pallas_call | solution.py:563
  168.1 27.1 %feed_forward.1 = (bf16[1024,1024]{1,0:T(8,128)(2,1)}, bf16[2,1024,1024]{2,1,0:T(8,128)(2,1)}, bf16[2,1024,1024]{2,1,0:T(8,128)(2,1)}, f32[8,8,256]{2,1,0:T(8,128)}) custom-call(s32[2]{0:T(128)} %pad_add_fusion.2.at_ref, bf16[2,1024,512]{2,1,0:T(8,128)(2,1)} %get-tuple-element.63.s_ref, bf16[2,1024,512]{2,1,0:T(8,128)(2,1)} %pad_maximum_fusion.1.c_ref.cots_ref, ...), custom_call_target="tpu_custom_call" | custom-call | flops 12884901888 | bytes 29360128 | tf_op jit(solution)/shard_map/feed_forward/pallas_call | solution.py:728
  195.2 9.2 %down_grads.1 = bf16[2,2,1024,512]{3,2,1,0:T(8,128)(2,1)} custom-call(s32[2]{0:T(128)} %pad_add_fusion.2.at_ref, bf16[2,1024,1024]{2,1,0:T(8,128)(2,1)} %get-tuple-element.80.hidden_ref.h0.h1, bf16[2,1024,512]{2,1,0:T(8,128)(2,1)} %pad_maximum_fusion.1.c_ref.cots_ref), custom_call_target="tpu_custom_call" | custom-call | flops 4294967296 | bytes 8388608 | tf_op jit(solution)/shard_map/down_grads/pallas_call | solution.py:792
  204.5 1.5 copy-done.7
  206.1 11.2 %up_grads.1 = bf16[4,1024,512]{2,1,0:T(8,128)(2,1)} custom-call(s32[2]{0:T(128)} %pad_add_fusion.2.at_ref, bf16[2,1024,512]{2,1,0:T(8,128)(2,1)} %get-tuple-element.63.s_ref, bf16[2,1024,1024]{2,1,0:T(8,128)(2,1)} %get-tuple-element.67.grad_ref), custom_call_target="tpu_custom_call" | custom-call | flops 4294967296 | bytes 8388608 | tf_op jit(solution)/shard_map/up_grads/pallas_call | solution.py:765
  217.4 8.7 %second_norm_back.1 = (f32[1024,256]{1,0:T(8,128)}, f32[1024,256]{1,0:T(8,128)}, bf16[1024,1024]{1,0:T(8,128)(2,1)}, f32[8,512]{1,0:T(8,128)}) custom-call(f32[1024,1024]{1,0:T(8,128)} %get-tuple-element.82.residual_ref, bf16[1024,1024]{1,0:T(8,128)(2,1)} %get-tuple-element.69.part_ref, bf16[1024,1024]{1,0:T(8,128)(2,1)} %collective-permute-done.21.got_ref, ...), custom_call_target="tpu_custom_call" | custom-call | flops 15728640 | bytes 16777216 | tf_op jit(solution)/shard_map/second_norm_back/pallas_call | solution.py:611
  226.1 2.7 convolution_convert_fusion.7
  232.4 2.3 collective-permute-start.23
  234.7 2.3 select_convert_fusion.1.grads_ref
  237.0 13.6 %attend_backward.2 = bf16[1024,768]{1,0:T(8,128)(2,1)} custom-call(s32[2,4]{1,0:T(2,128)} %pad_add_fusion.1.where_ref, bf16[4,1024,128]{2,1,0:T(8,128)(2,1)} %get-tuple-element.68.kept_ref, bf16[1024,768]{1,0:T(8,128)(2,1)} %convolution_convert_fusion.1.q_ref.k_ref.v_ref, bf16[1024,768]{1,0:T(8,128)(2,1)} %convolution_convert_fusion.1.q_ref.k_ref.v_ref, ...), custom_call_target="tpu_custom_call" | custom-call | flops 2684354560 | bytes 15728640 | tf_op jit(solution)/shard_map/attend_backward/pallas_call | solution.py:467
  250.6 13.9 %attend_backward.3 = bf16[1024,768]{1,0:T(8,128)(2,1)} custom-call(s32[2,4]{1,0:T(2,128)} %pad_add_fusion.1.where_ref, bf16[4,1024,128]{2,1,0:T(8,128)(2,1)} %get-tuple-element.73.kept_ref, bf16[1024,768]{1,0:T(8,128)(2,1)} %convolution_convert_fusion.q_ref.k_ref.v_ref, bf16[1024,768]{1,0:T(8,128)(2,1)} %convolution_convert_fusion.q_ref.k_ref.v_ref, ...), custom_call_target="tpu_custom_call" | custom-call | flops 2684354560 | bytes 15728640 | tf_op jit(solution)/shard_map/attend_backward/pallas_call | solution.py:467
  264.6 3.5 convolution_convert_fusion.4
  268.1 1.9 convolution_convert_fusion.5
  270.0 1.9 convolution_convert_fusion.2
  271.9 1.9 convolution_convert_fusion.3
  273.9 4.8 %fusion.20.part_ref = bf16[1024,1024]{1,0:T(8,128)(2,1)S(1)} fusion(bf16[1024,768]{1,0:T(8,128)(2,1)S(1)} %copy-done.34, bf16[512,768]{1,0:T(8,128)(2,1)} %collective-permute-done.7, bf16[256,768]{1,0:T(8,128)(2,1)S(1)} %copy-done.37, bf16[256,256]{1,0:T(8,128)(2,1)S(1)} %get-tuple-element.196, bf16[256,256]{1,0:T(8,128)(2,1)S(1)} %get-tuple-element.222, ...), kind=kOutput, calls=%fused_computation.30 | convolution fusion | flops 3247439872 | bytes 8388608 | tf_op jit(solution)/shard_map/dot_general | solution.py:278
  280.7 2.2 collective-permute-done.26.got_ref
  284.3 7.2 %first_norm_back.1 = (f32[1024,256]{1,0:T(8,128)}, bf16[1024,256]{1,0:T(8,128)(2,1)}, f32[8,512]{1,0:T(8,128)}) custom-call(bf16[1024,256]{1,0:T(8,128)(2,1)} %copy-done.2, bf16[1024,256]{1,0:T(8,128)(2,1)} %copy-done.4, bf16[1024,256]{1,0:T(8,128)(2,1)} %copy-done.3, bf16[1024,256]{1,0:T(8,128)(2,1)} %copy-done.5, bf16[1024,1024]{1,0:T(8,128)(2,1)} %copy-done.10, ...), custom_call_target="tpu_custom_call" | custom-call | flops 15728640 | bytes 10485760 | tf_op jit(solution)/shard_map/first_norm_back/pallas_call | solution.py:634
  292.3 4.0 collective-permute-done.30
  297.2 3.0 collective-permute-done.31
  300.1 3.7 collective-permute-start.32
  306.2 2.0 collective-permute-start.35
  308.6 2.6 collective-permute-start.33
  311.2 1.9 fusion.49
  313.1 2.3 collective-permute-done.33
  315.4 1.6 collective-permute-start.29
  317.7 9.6 %layer_end.1 = (f32[1024,512]{1,0:T(8,128)}, bf16[1024,512]{1,0:T(8,128)(2,1)}) custom-call(s32[2]{0:T(128)} %pad_add_fusion.2.at_ref, bf16[2,1024,1024]{2,1,0:T(8,128)(2,1)} %get-tuple-element.80.hidden_ref.h0.h1, bf16[2,1024,1024]{2,1,0:T(8,128)(2,1)} %get-tuple-element.80.hidden_ref.h0.h1, bf16[4,2048,512]{2,1,0:T(8,128)(2,1)} %bitcast.138, ...), custom_call_target="tpu_custom_call" | custom-call | flops 4294967296 | bytes 10485760 | tf_op jit(solution)/shard_map/layer_end/pallas_call | solution.py:828
  327.3 20.2 %reduce-scatter.7.cloned.1.call-done = bf16[1,1024,512]{2,1,0:T(8,128)(2,1)} async-done(((bf16[4,1024,512]{2,1,0:T(8,128)(2,1)}), bf16[1,1024,512]{2,1,0:T(8,128)(2,1)}) %reduce-scatter.7.cloned.1.call-update) | async-done | bytes 1048592
  347.5 2.4 collective-permute-start.43
  349.9 2.3 collective-permute-done.35
  352.7 1.5 add_convert_fusion
  355.4 1.8 collective-permute-start.37
  358.0 15.6 %collective-permute-done.43 = bf16[512,512]{1,0:T(8,128)(2,1)} collective-permute-done((bf16[512,512]{1,0:T(8,128)(2,1)S(1)}, bf16[512,512]{1,0:T(8,128)(2,1)}, u32[]{:S(2)}, u32[]{:S(2)}) %collective-permute-start.43) | collective-permute-done | bytes 524320 | tf_op jit(solution)/shard_map/ppermute | solution.py:885
  374.9 4.0 collective-permute-done.37
  382.9 3.2 collective-permute-start.38
  386.1 1.7 fusion.75
  387.8 19.4 %collective-permute-done.44 = bf16[512,512]{1,0:T(8,128)(2,1)S(1)} collective-permute-done((bf16[512,512]{1,0:T(8,128)(2,1)S(1)}, bf16[512,512]{1,0:T(8,128)(2,1)S(1)}, u32[]{:S(2)}, u32[]{:S(2)}) %collective-permute-start.44) | collective-permute-done | bytes 524320 | tf_op jit(solution)/shard_map/ppermute | solution.py:889
  408.2 17.1 %collective-permute-done.38 = bf16[256,1024]{0,1:T(8,128)(2,1)S(1)} collective-permute-done((bf16[256,1024]{0,1:T(8,128)(2,1)S(1)}, bf16[256,1024]{0,1:T(8,128)(2,1)S(1)}, u32[]{:S(2)}, u32[]{:S(2)}) %collective-permute-start.38) | collective-permute-done | bytes 524320 | tf_op jit(solution)/shard_map/ppermute | solution.py:885
  427.1 1.8 fusion.19
  429.7 1.6 collective-permute-start.28
  431.4 24.9 %all-reduce.9.cloned.1.call-done = bf16[1024,512]{1,0:T(8,128)(2,1)} async-done(((bf16[1024,512]{1,0:T(8,128)(2,1)}), bf16[1024,512]{1,0:T(8,128)(2,1)}) %all-reduce.9.cloned.1.call-update) | async-done | bytes 1048592 | tf_op jit(solution)/shard_map/psum | solution.py:994
  463.4 1.6 maximum_convert_fusion
  (300 shorter events, 72.0 us)
Async XLA Ops:
  7.2 30.9 %copy-start = (s32[8,16,3]{1,0,2:T(8,128)S(1)}, s32[8,16,3]{1,0,2:T(8,128)}, u32[]{:S(2)}) copy-start(s32[8,16,3]{1,0,2:T(8,128)} %param.31) | copy-start | bytes 4612
  7.2 160.9 %all-gather.3.cloned.1.call-start = ((), (), s32[]{:S(2)}) async-start(), calls=%async_computation.3 | async-start | bytes 10485760 | tf_op jit(solution)/shard_map/all_gather | solution.py:923
  9.5 1.9 collective-permute-start.6
  13.3 5.1 %collective-permute-start.11 = (bf16[256,1024]{1,0:T(8,128)(2,1)S(1)}, bf16[256,1024]{1,0:T(8,128)(2,1)S(1)}, u32[]{:S(2)}, u32[]{:S(2)}) collective-permute-start(bf16[256,1024]{1,0:T(8,128)(2,1)S(1)} %get-tuple-element.185), channel_id=1, source_target_pairs={{0,2},{2,0},{1,3},{3,1},{4,6},{6,4},{5,7},{7,5},{8,10},{10,8},{9,1... | collective-permute-start | bytes 1572872 | tf_op jit(solution)/shard_map/ppermute | solution.py:270
  13.9 4.6 collective-permute-start.12
  14.1 20.8 %collective-permute-start.7 = (bf16[512,768]{1,0:T(8,128)(2,1)S(1)}, bf16[512,768]{1,0:T(8,128)(2,1)}, u32[]{:S(2)}, u32[]{:S(2)}) collective-permute-start(bf16[512,768]{1,0:T(8,128)(2,1)S(1)} %pad_maximum_fusion.7), channel_id=1, source_target_pairs={{0,4},{4,0},{1,5},{5,1},{2,6},{6,2},{3,7},{7,3},{8,12},{12,8},{9,1... | collective-permute-start | bytes 2359304 | tf_op jit(solution)/shard_map/ppermute | solution.py:270
  16.9 19.4 %collective-permute-start.9 = (bf16[512,768]{1,0:T(8,128)(2,1)S(1)}, bf16[512,768]{1,0:T(8,128)(2,1)}, u32[]{:S(2)}, u32[]{:S(2)}) collective-permute-start(bf16[512,768]{1,0:T(8,128)(2,1)S(1)} %pad_maximum_fusion.7), channel_id=1, source_target_pairs={{0,1},{1,0},{2,3},{3,2},{4,5},{5,4},{6,7},{7,6},{8,9},{9,8},{10,11... | collective-permute-start | bytes 2359304 | tf_op jit(solution)/shard_map/ppermute | solution.py:270
  20.0 16.9 %copy-start.42 = (f32[256]{0:T(256)S(1)}, f32[256]{0:T(256)}, u32[]{:S(2)}) copy-start(f32[256]{0:T(256)} %param.29) | copy-start | bytes 3076
  20.0 16.9 %copy-start.45 = (f32[256]{0:T(256)S(1)}, f32[256]{0:T(256)}, u32[]{:S(2)}) copy-start(f32[256]{0:T(256)} %param.18) | copy-start | bytes 3076
  20.0 16.9 %copy-start.46 = (f32[256]{0:T(256)S(1)}, f32[256]{0:T(256)}, u32[]{:S(2)}) copy-start(f32[256]{0:T(256)} %param.19) | copy-start | bytes 3076
  20.0 16.9 %copy-start.47 = (f32[256]{0:T(256)S(1)}, f32[256]{0:T(256)}, u32[]{:S(2)}) copy-start(f32[256]{0:T(256)} %param.24) | copy-start | bytes 3076
  20.0 16.9 %copy-start.48 = (f32[256]{0:T(256)S(1)}, f32[256]{0:T(256)}, u32[]{:S(2)}) copy-start(f32[256]{0:T(256)} %param.25) | copy-start | bytes 3076
  20.0 18.0 %copy-start.44 = (f32[2048]{0:T(1024)S(1)}, f32[2048]{0:T(1024)}, u32[]{:S(2)}) copy-start(f32[2048]{0:T(1024)} %param.27) | copy-start | bytes 24580
  20.0 20.1 %copy-start.50 = (s32[1,1024]{1,0:T(1,128)S(1)}, s32[1,1024]{1,0:T(1,128)}, u32[]{:S(2)}) copy-start(s32[1,1024]{1,0:T(1,128)} %param.30) | copy-start | bytes 12292
  20.0 21.8 %copy-start.51 = (s32[2]{0:T(128)S(1)}, s32[2]{0:T(128)}, u32[]{:S(2)}) copy-start(s32[2]{0:T(128)} %param.32) | copy-start | bytes 28
  36.4 267.5 %reduce-scatter.9.cloned.1.call-start = ((), (), s32[]{:S(2)}) async-start(), calls=%async_computation.5 | async-start | bytes 5242880
  36.5 13.6 %collective-permute-start.1 = (bf16[1024,256]{1,0:T(8,128)(2,1)S(1)}, bf16[1024,256]{1,0:T(8,128)(2,1)S(1)}, u32[]{:S(2)}, u32[]{:S(2)}) collective-permute-start(bf16[1024,256]{1,0:T(8,128)(2,1)S(1)} %get-tuple-element.186), channel_id=1, source_target_pairs={{0,4},{4,0},{1,5},{5,1},{2,6},{6,2},{3,7},{7,3},{8,12},{12,8},{9,1... | collective-permute-start | bytes 1572872 | tf_op jit(solution)/shard_map/ppermute | solution.py:270
  36.9 29.0 %collective-permute-start = (bf16[1024,256]{1,0:T(8,128)(2,1)S(1)}, bf16[1024,256]{1,0:T(8,128)(2,1)S(1)}, u32[]{:S(2)}, u32[]{:S(2)}) collective-permute-start(bf16[1024,256]{1,0:T(8,128)(2,1)S(1)} %get-tuple-element.187.x0), channel_id=1, source_target_pairs={{0,2},{2,0},{1,3},{3,1},{4,6},{6,4},{5,7},{7,5},{8,10},{10,8},{9,1... | collective-permute-start | bytes 1572872 | tf_op jit(solution)/shard_map/ppermute | solution.py:270
  37.6 16.5 %collective-permute-start.4 = (f32[5,256]{1,0:T(8,128)}, f32[5,256]{1,0:T(8,128)}, u32[]{:S(2)}, u32[]{:S(2)}) collective-permute-start(f32[5,256]{1,0:T(8,128)} %stack.104), channel_id=1, source_target_pairs={{0,2},{2,0},{1,3},{3,1},{4,6},{6,4},{5,7},{7,5},{8,10},{10,8},{9,1... | collective-permute-start | bytes 15368 | tf_op jit(solution)/shard_map/ppermute | solution.py:270
  38.3 7.9 %collective-permute-start.8 = (f32[1216]{0:T(1024)S(1)}, f32[1216]{0:T(1024)S(1)}, u32[]{:S(2)}, u32[]{:S(2)}) collective-permute-start(f32[1216]{0:T(1024)S(1)} %pad_maximum_fusion.15), channel_id=1, source_target_pairs={{0,1},{1,0},{2,3},{3,2},{4,5},{5,4},{6,7},{7,6},{8,9},{9,8},{10,11... | collective-permute-start | bytes 14600 | tf_op jit(solution)/shard_map/ppermute | solution.py:270
  40.1 2.4 collective-permute-start.3
  50.1 15.8 %collective-permute-start.2 = (bf16[1024,256]{1,0:T(8,128)(2,1)S(1)}, bf16[1024,256]{1,0:T(8,128)(2,1)S(1)}, u32[]{:S(2)}, u32[]{:S(2)}) collective-permute-start(bf16[1024,256]{1,0:T(8,128)(2,1)S(1)} %collective-permute-done.1.x2), channel_id=1, source_target_pairs={{0,2},{2,0},{1,3},{3,1},{4,6},{6,4},{5,7},{7,5},{8,10},{10,8},{9,1... | collective-permute-start | bytes 1572872 | tf_op jit(solution)/shard_map/ppermute | solution.py:270
  54.7 4.6 collective-permute-start.5
  60.9 28.0 %collective-permute-start.10 = (bf16[512,768]{1,0:T(8,128)(2,1)S(1)}, bf16[512,768]{1,0:T(8,128)(2,1)}, u32[]{:S(2)}, u32[]{:S(2)}) collective-permute-start(bf16[512,768]{1,0:T(8,128)(2,1)S(1)} %pad_maximum_fusion.7), channel_id=1, source_target_pairs={{0,5},{5,0},{1,4},{4,1},{2,7},{7,2},{3,6},{6,3},{8,13},{13,8},{9,1... | collective-permute-start | bytes 2359304 | tf_op jit(solution)/shard_map/ppermute | solution.py:856
  74.6 27.4 %collective-permute-start.14 = (bf16[1024,256]{1,0:T(8,128)(2,1)S(1)}, bf16[1024,256]{1,0:T(8,128)(2,1)S(1)}, u32[]{:S(2)}, u32[]{:S(2)}) collective-permute-start(bf16[1024,256]{1,0:T(8,128)(2,1)S(1)} %get-tuple-element.181), channel_id=1, source_target_pairs={{0,4},{4,0},{1,5},{5,1},{2,6},{6,2},{3,7},{7,3},{8,12},{12,8},{9,1... | collective-permute-start | bytes 1572872 | tf_op jit(solution)/shard_map/ppermute | solution.py:270
  76.6 13.4 %collective-permute-start.13 = (bf16[256,256]{1,0:T(8,128)(2,1)S(1)}, bf16[256,256]{1,0:T(8,128)(2,1)S(1)}, u32[]{:S(2)}, u32[]{:S(2)}) collective-permute-start(bf16[256,256]{1,0:T(8,128)(2,1)S(1)} %get-tuple-element.189), channel_id=1, source_target_pairs={{0,2},{2,0},{1,3},{3,1},{4,6},{6,4},{5,7},{7,5},{8,10},{10,8},{9,1... | collective-permute-start | bytes 393224 | tf_op jit(solution)/shard_map/ppermute | solution.py:270
  90.1 42.9 %collective-permute-start.17 = (bf16[256,512]{1,0:T(8,128)(2,1)S(1)}, bf16[256,512]{1,0:T(8,128)(2,1)S(1)}, u32[]{:S(2)}, u32[]{:S(2)}) collective-permute-start(bf16[256,512]{1,0:T(8,128)(2,1)S(1)} %pad_maximum_fusion.11), channel_id=1, source_target_pairs={{0,1},{1,0},{2,3},{3,2},{4,5},{5,4},{6,7},{7,6},{8,9},{9,8},{10,11... | collective-permute-start | bytes 786440 | tf_op jit(solution)/shard_map/ppermute | solution.py:270
  101.9 32.1 %collective-permute-start.15 = (bf16[1024,256]{1,0:T(8,128)(2,1)S(1)}, bf16[1024,256]{1,0:T(8,128)(2,1)S(1)}, u32[]{:S(2)}, u32[]{:S(2)}) collective-permute-start(bf16[1024,256]{1,0:T(8,128)(2,1)S(1)} %collective-permute-done.14), channel_id=1, source_target_pairs={{0,2},{2,0},{1,3},{3,1},{4,6},{6,4},{5,7},{7,5},{8,10},{10,8},{9,1... | collective-permute-start | bytes 1572872 | tf_op jit(solution)/shard_map/ppermute | solution.py:270
  104.9 28.1 %collective-permute-start.18 = (bf16[256,512]{1,0:T(8,128)(2,1)S(1)}, bf16[256,512]{1,0:T(8,128)(2,1)}, u32[]{:S(2)}, u32[]{:S(2)}) collective-permute-start(bf16[256,512]{1,0:T(8,128)(2,1)S(1)} %pad_maximum_fusion.11), channel_id=1, source_target_pairs={{0,5},{5,0},{1,4},{4,1},{2,7},{7,2},{3,6},{6,3},{8,13},{13,8},{9,1... | collective-permute-start | bytes 786440 | tf_op jit(solution)/shard_map/ppermute | solution.py:856
  132.1 14.6 %collective-permute-start.16 = (bf16[256,512]{1,0:T(8,128)(2,1)S(1)}, bf16[256,512]{1,0:T(8,128)(2,1)S(1)}, u32[]{:S(2)}, u32[]{:S(2)}) collective-permute-start(bf16[256,512]{1,0:T(8,128)(2,1)S(1)} %pad_maximum_fusion.11), channel_id=1, source_target_pairs={{0,4},{4,0},{1,5},{5,1},{2,6},{6,2},{3,7},{7,3},{8,12},{12,8},{9,1... | collective-permute-start | bytes 786440 | tf_op jit(solution)/shard_map/ppermute | solution.py:270
  152.4 8.1 %collective-permute-start.19 = (bf16[1024,1024]{1,0:T(8,128)(2,1)}, bf16[1024,1024]{1,0:T(8,128)(2,1)S(1)}, u32[]{:S(2)}, u32[]{:S(2)}) collective-permute-start(bf16[1024,1024]{1,0:T(8,128)(2,1)} %mix_heads.1.part_ref), channel_id=1, source_target_pairs={{0,2},{2,0},{1,3},{3,1},{4,6},{6,4},{5,7},{7,5},{8,10},{10,8},{9,1... | collective-permute-start | bytes 6291464 | tf_op jit(solution)/shard_map/ppermute | solution.py:270
  152.4 5.2 %collective-permute-start.20 = (bf16[1024,256]{1,0:T(8,128)(2,1)}, bf16[1024,256]{1,0:T(8,128)(2,1)}, u32[]{:S(2)}, u32[]{:S(2)}) collective-permute-start(bf16[1024,256]{1,0:T(8,128)(2,1)} %get-tuple-element.180), channel_id=1, source_target_pairs={{0,2},{2,0},{1,3},{3,1},{4,6},{6,4},{5,7},{7,5},{8,10},{10,8},{9,1... | collective-permute-start | bytes 1572872 | tf_op jit(solution)/shard_map/ppermute | solution.py:270
  204.4 143.0 %reduce-scatter.7.cloned.1.call-start = ((), (), s32[]{:S(2)}) async-start(), calls=%async_computation.4 | async-start | bytes 5242880
  206.0 11.4 %collective-permute-start.21 = (bf16[1024,1024]{1,0:T(8,128)(2,1)S(1)}, bf16[1024,1024]{1,0:T(8,128)(2,1)}, u32[]{:S(2)}, u32[]{:S(2)}) collective-permute-start(bf16[1024,1024]{1,0:T(8,128)(2,1)S(1)} %copy-done.7), channel_id=1, source_target_pairs={{0,2},{2,0},{1,3},{3,1},{4,6},{6,4},{5,7},{7,5},{8,10},{10,8},{9,1... | collective-permute-start | bytes 6291464 | tf_op jit(solution)/shard_map/ppermute | solution.py:270
  217.3 239.0 %all-reduce.9.cloned.1.call-start = ((), (), s32[]{:S(2)}) async-start(), calls=%async_computation.2 | async-start | bytes 2097152 | tf_op jit(solution)/shard_map/psum | solution.py:994
  230.0 48.7 %collective-permute-start.25 = (bf16[512,256]{1,0:T(8,128)(2,1)}, bf16[512,256]{1,0:T(8,128)(2,1)}, u32[]{:S(2)}, u32[]{:S(2)}) collective-permute-start(bf16[512,256]{1,0:T(8,128)(2,1)} %convolution_convert_fusion.7), channel_id=1, source_target_pairs={{0,5},{5,0},{1,4},{4,1},{2,7},{7,2},{3,6},{6,3},{8,13},{13,8},{9,1... | collective-permute-start | bytes 786440 | tf_op jit(solution)/shard_map/ppermute | solution.py:856
  230.4 48.3 %collective-permute-start.24 = (bf16[512,256]{1,0:T(8,128)(2,1)}, bf16[512,256]{1,0:T(8,128)(2,1)}, u32[]{:S(2)}, u32[]{:S(2)}) collective-permute-start(bf16[512,256]{1,0:T(8,128)(2,1)} %convolution_convert_fusion.8), channel_id=1, source_target_pairs={{0,1},{1,0},{2,3},{3,2},{4,5},{5,4},{6,7},{7,6},{8,9},{9,8},{10,11... | collective-permute-start | bytes 786440 | tf_op jit(solution)/shard_map/ppermute | solution.py:270
  232.4 46.3 %collective-permute-start.23 = (bf16[512,256]{1,0:T(8,128)(2,1)}, bf16[512,256]{1,0:T(8,128)(2,1)}, u32[]{:S(2)}, u32[]{:S(2)}) collective-permute-start(bf16[512,256]{1,0:T(8,128)(2,1)} %convolution_convert_fusion.9), channel_id=1, source_target_pairs={{0,4},{4,0},{1,5},{5,1},{2,6},{6,2},{3,7},{7,3},{8,12},{12,8},{9,1... | collective-permute-start | bytes 786440 | tf_op jit(solution)/shard_map/ppermute | solution.py:270
  278.7 4.2 collective-permute-start.26
  284.3 20.8 %copy-start.43 = (f32[256]{0:T(256)S(1)}, f32[256]{0:T(256)}, u32[]{:S(2)}) copy-start(f32[256]{0:T(256)} %param.29) | copy-start | bytes 3076
  284.3 26.9 %copy-start.31 = (bf16[1024,256]{1,0:T(8,128)(2,1)S(1)}, bf16[1024,256]{1,0:T(8,128)(2,1)}, u32[]{:S(2)}) copy-start(bf16[1024,256]{1,0:T(8,128)(2,1)} %get-tuple-element.55.h0.heads_ref) | copy-start | bytes 1572868
  292.2 4.1 collective-permute-start.30
  296.4 3.8 collective-permute-start.31
  300.1 8.5 %collective-permute-start.32 = (f32[2304]{0:T(1024)S(1)}, f32[2304]{0:T(1024)S(1)}, u32[]{:S(2)}, u32[]{:S(2)}) collective-permute-start(f32[2304]{0:T(1024)S(1)} %maximum_add_fusion.1), channel_id=1, source_target_pairs={{0,8},{8,0},{16,24},{24,16},{1,9},{9,1},{17,25},{25,17},{2,10},{10... | collective-permute-start | bytes 27656 | tf_op jit(solution)/shard_map/ppermute | solution.py:1009
  305.0 12.6 %collective-permute-start.22 = (bf16[512,512]{1,0:T(8,128)(2,1)S(1)}, bf16[512,512]{1,0:T(8,128)(2,1)S(1)}, u32[]{:S(2)}, u32[]{:S(2)}) collective-permute-start(bf16[512,512]{1,0:T(8,128)(2,1)S(1)} %dynamic-slice_bitcast_fusion), channel_id=1, source_target_pairs={{0,8},{8,0},{16,24},{24,16},{1,9},{9,1},{17,25},{25,17},{2,10},{10... | collective-permute-start | bytes 1572872 | tf_op jit(solution)/shard_map/ppermute | solution.py:881
  305.1 42.4 %collective-permute-start.36 = (bf16[512,768]{1,0:T(8,128)(2,1)}, bf16[512,768]{1,0:T(8,128)(2,1)S(1)}, u32[]{:S(2)}, u32[]{:S(2)}) collective-permute-start(bf16[512,768]{1,0:T(8,128)(2,1)} %convolution_convert_fusion.2), channel_id=1, source_target_pairs={{0,5},{5,0},{1,4},{4,1},{2,7},{7,2},{3,6},{6,3},{8,13},{13,8},{9,1... | collective-permute-start | bytes 2359304 | tf_op jit(solution)/shard_map/ppermute | solution.py:856
  306.2 45.9 %collective-permute-start.35 = (bf16[512,768]{1,0:T(8,128)(2,1)}, bf16[512,768]{1,0:T(8,128)(2,1)S(1)}, u32[]{:S(2)}, u32[]{:S(2)}) collective-permute-start(bf16[512,768]{1,0:T(8,128)(2,1)} %convolution_convert_fusion.3), channel_id=1, source_target_pairs={{0,1},{1,0},{2,3},{3,2},{4,5},{5,4},{6,7},{7,6},{8,9},{9,8},{10,11... | collective-permute-start | bytes 2359304 | tf_op jit(solution)/shard_map/ppermute | solution.py:270
  308.2 44.4 %collective-permute-start.34 = (bf16[512,768]{1,0:T(8,128)(2,1)}, bf16[512,768]{1,0:T(8,128)(2,1)}, u32[]{:S(2)}, u32[]{:S(2)}) collective-permute-start(bf16[512,768]{1,0:T(8,128)(2,1)} %convolution_convert_fusion.4), channel_id=1, source_target_pairs={{0,4},{4,0},{1,5},{5,1},{2,6},{6,2},{3,7},{7,3},{8,12},{12,8},{9,1... | collective-permute-start | bytes 2359304 | tf_op jit(solution)/shard_map/ppermute | solution.py:270
  308.6 6.7 %collective-permute-start.33 = (f32[2304]{0:T(1024)S(1)}, f32[2304]{0:T(1024)S(1)}, u32[]{:S(2)}, u32[]{:S(2)}) collective-permute-start(f32[2304]{0:T(1024)S(1)} %add.228), channel_id=1, source_target_pairs={{0,16},{16,0},{8,24},{24,8},{1,17},{17,1},{9,25},{25,9},{2,18},{18... | collective-permute-start | bytes 27656 | tf_op jit(solution)/shard_map/ppermute | solution.py:1010
  315.4 64.7 %collective-permute-start.29 = (bf16[1024,256]{1,0:T(8,128)(2,1)}, bf16[1024,256]{1,0:T(8,128)(2,1)}, u32[]{:S(2)}, u32[]{:S(2)}) collective-permute-start(bf16[1024,256]{1,0:T(8,128)(2,1)} %get-tuple-element.85), channel_id=1, source_target_pairs={{0,4},{4,0},{1,5},{5,1},{2,6},{6,2},{3,7},{7,3},{8,12},{12,8},{9,1... | collective-permute-start | bytes 1572872 | tf_op jit(solution)/shard_map/ppermute | solution.py:270
  317.5 39.6 %collective-permute-start.42 = (f32[1024]{0:T(1024)S(1)}, f32[1024]{0:T(1024)S(1)}, u32[]{:S(2)}, u32[]{:S(2)}) collective-permute-start(f32[1024]{0:T(1024)S(1)} %slice.255), channel_id=1, source_target_pairs={{0,2},{2,0},{1,3},{3,1},{4,6},{6,4},{5,7},{7,5},{8,10},{10,8},{9,1... | collective-permute-start | bytes 12296 | tf_op jit(solution)/shard_map/ppermute | solution.py:270
  317.7 35.0 %copy-start.25 = (bf16[512,768]{1,0:T(8,128)(2,1)S(1)}, bf16[512,768]{1,0:T(8,128)(2,1)}, u32[]{:S(2)}) copy-start(bf16[512,768]{1,0:T(8,128)(2,1)} %convolution_convert_fusion.5) | copy-start | bytes 2359300
  347.5 26.2 %collective-permute-start.43 = (bf16[512,512]{1,0:T(8,128)(2,1)S(1)}, bf16[512,512]{1,0:T(8,128)(2,1)}, u32[]{:S(2)}, u32[]{:S(2)}) collective-permute-start(bf16[512,512]{1,0:T(8,128)(2,1)S(1)} %fusion.43), channel_id=1, source_target_pairs={{0,16},{16,0},{8,24},{24,8},{1,17},{17,1},{9,25},{25,9},{2,18},{18... | collective-permute-start | bytes 1572872 | tf_op jit(solution)/shard_map/ppermute | solution.py:885
  355.4 23.4 %collective-permute-start.37 = (bf16[256,1024]{0,1:T(8,128)(2,1)}, bf16[256,1024]{0,1:T(8,128)(2,1)}, u32[]{:S(2)}, u32[]{:S(2)}) collective-permute-start(bf16[256,1024]{0,1:T(8,128)(2,1)} %bitcast.46), channel_id=1, source_target_pairs={{0,8},{8,0},{16,24},{24,16},{1,9},{9,1},{17,25},{25,17},{2,10},{10... | collective-permute-start | bytes 1572872 | tf_op jit(solution)/shard_map/ppermute | solution.py:881
  357.8 22.3 %copy-start.23 = (f32[1024,256]{1,0:T(8,128)S(1)}, f32[1024,256]{1,0:T(8,128)}, u32[]{:S(2)}) copy-start(f32[1024,256]{1,0:T(8,128)} %get-tuple-element.84) | copy-start | bytes 3145732
  380.0 27.2 %collective-permute-start.44 = (bf16[512,512]{1,0:T(8,128)(2,1)S(1)}, bf16[512,512]{1,0:T(8,128)(2,1)S(1)}, u32[]{:S(2)}, u32[]{:S(2)}) collective-permute-start(bf16[512,512]{1,0:T(8,128)(2,1)S(1)} %add_convert_fusion.1), channel_id=1, source_target_pairs={{0,8},{8,0},{16,24},{24,16},{1,9},{9,1},{17,25},{25,17},{2,10},{10... | collective-permute-start | bytes 1572872 | tf_op jit(solution)/shard_map/ppermute | solution.py:889
  381.3 44.8 %collective-permute-start.27 = (bf16[1024,512]{1,0:T(8,128)(2,1)}, bf16[1024,512]{1,0:T(8,128)(2,1)S(1)}, u32[]{:S(2)}, u32[]{:S(2)}) collective-permute-start(bf16[1024,512]{1,0:T(8,128)(2,1)} %get-tuple-element.83), channel_id=1, source_target_pairs={{0,2},{2,0},{1,3},{3,1},{4,6},{6,4},{5,7},{7,5},{8,10},{10,8},{9,1... | collective-permute-start | bytes 3145736 | tf_op jit(solution)/shard_map/ppermute | solution.py:270
  382.9 42.5 %collective-permute-start.38 = (bf16[256,1024]{0,1:T(8,128)(2,1)S(1)}, bf16[256,1024]{0,1:T(8,128)(2,1)S(1)}, u32[]{:S(2)}, u32[]{:S(2)}) collective-permute-start(bf16[256,1024]{0,1:T(8,128)(2,1)S(1)} %fusion.42), channel_id=1, source_target_pairs={{0,16},{16,0},{8,24},{24,8},{1,17},{17,1},{9,25},{25,9},{2,18},{18... | collective-permute-start | bytes 1572872 | tf_op jit(solution)/shard_map/ppermute | solution.py:885
  407.3 19.8 %copy-start.8 = (f32[1024,512]{1,0:T(8,128)S(1)}, f32[1024,512]{1,0:T(8,128)}, u32[]{:S(2)}) copy-start(f32[1024,512]{1,0:T(8,128)} %get-tuple-element.81) | copy-start | bytes 6291460
  408.2 52.3 %collective-permute-start.45 = (bf16[1024,256]{1,0:T(8,128)(2,1)}, bf16[1024,256]{1,0:T(8,128)(2,1)}, u32[]{:S(2)}, u32[]{:S(2)}) collective-permute-start(bf16[1024,256]{1,0:T(8,128)(2,1)} %slice.257), channel_id=1, source_target_pairs={{0,2},{2,0},{1,3},{3,1},{4,6},{6,4},{5,7},{7,5},{8,10},{10,8},{9,1... | collective-permute-start | bytes 1572872 | tf_op jit(solution)/shard_map/ppermute | solution.py:270
  425.5 32.2 %collective-permute-start.39 = (bf16[256,1024]{0,1:T(8,128)(2,1)S(1)}, bf16[256,1024]{0,1:T(8,128)(2,1)S(1)}, u32[]{:S(2)}, u32[]{:S(2)}) collective-permute-start(bf16[256,1024]{0,1:T(8,128)(2,1)S(1)} %add_convert_fusion.2), channel_id=1, source_target_pairs={{0,8},{8,0},{16,24},{24,16},{1,9},{9,1},{17,25},{25,17},{2,10},{10... | collective-permute-start | bytes 1572872 | tf_op jit(solution)/shard_map/ppermute | solution.py:889
  429.7 28.6 %collective-permute-start.28 = (bf16[1024,256]{1,0:T(8,128)(2,1)}, bf16[1024,256]{1,0:T(8,128)(2,1)}, u32[]{:S(2)}, u32[]{:S(2)}) collective-permute-start(bf16[1024,256]{1,0:T(8,128)(2,1)} %slice.234), channel_id=1, source_target_pairs={{0,4},{4,0},{1,5},{5,1},{2,6},{6,2},{3,7},{7,3},{8,12},{12,8},{9,1... | collective-permute-start | bytes 1572872 | tf_op jit(solution)/shard_map/ppermute | solution.py:270
  457.6 5.5 %collective-permute-start.41 = (bf16[256,1024]{1,0:T(8,128)(2,1)S(1)}, bf16[256,1024]{1,0:T(8,128)(2,1)S(1)}, u32[]{:S(2)}, u32[]{:S(2)}) collective-permute-start(bf16[256,1024]{1,0:T(8,128)(2,1)S(1)} %pad_maximum_fusion.8), channel_id=1, source_target_pairs={{0,2},{2,0},{1,3},{3,1},{4,6},{6,4},{5,7},{7,5},{8,10},{10,8},{9,1... | collective-permute-start | bytes 1572872 | tf_op jit(solution)/shard_map/ppermute | solution.py:270
  457.8 7.1 %collective-permute-start.40 = (bf16[256,1024]{0,1:T(8,128)(2,1)S(1)}, bf16[256,1024]{0,1:T(8,128)(2,1)S(1)}, u32[]{:S(2)}, u32[]{:S(2)}) collective-permute-start(bf16[256,1024]{0,1:T(8,128)(2,1)S(1)} %get-tuple-element.177), channel_id=1, source_target_pairs={{0,2},{2,0},{1,3},{3,1},{4,6},{6,4},{5,7},{7,5},{8,10},{10,8},{9,1... | collective-permute-start | bytes 1572872 | tf_op jit(solution)/shard_map/ppermute | solution.py:270
  (41 other events, 216.5 us)
Sparse Core Ops, SparseCore 0:
  36.5 120.2 all-gather.2
  204.5 60.4 reduce-scatter.8
  268.0 79.3 reduce-scatter.6
  383.0 73.2 all-reduce.8

commit v4 on v3

--- a/solution.py
+++ b/solution.py
@@ -951,10 +951,11 @@
     cot_swapped = swap(cot_y, "core")
     cots = jnp.stack([jnp.concatenate(c, axis=1) for c in ((cot_own, swap(cot_own, "core")), (cot_y, cot_swapped))])
 
-    firsts = first_norm(xs, gain_one, shift_one)
+    firsts = first_norm(after(xs, qkv_xy), gain_one, shift_one)
+    qkv_x = after(qkv_x, out_y, out_x, out_xy, cot_y)
     w_qkv = (jnp.concatenate((qkv_own, qkv_y), axis=0), jnp.concatenate((qkv_x, qkv_xy), axis=0))
     first = jnp.concatenate(firsts, axis=1)
-    out_own = after(out_own, cot_y, cot_swapped)
+    out_own = after(out_own, cots)
     w_out = (jnp.concatenate((out_own, out_y), axis=1), jnp.concatenate((out_x, out_xy), axis=1))
     qkv, heads, kept = [], [], []
     for i in range(2):
@@ -981,22 +982,26 @@
         qkv_grads[i] = [dot_tn(f, qkv_sides[i]).astype(LOW) for f in firsts]
     odd = lax.rem(depth_at, 2)
     out_got = plane_exchange(out_grads[0][1], out_grads[1][0], out_grads[1][1])
-    qkv_got = plane_exchange(qkv_grads[0][1], qkv_grads[1][0], qkv_grads[1][1])
     qkv_sides = after(qkv_sides, qkv_grads)
     first_part = dot_nt(jnp.concatenate(qkv_sides, axis=1), jnp.concatenate(w_qkv, axis=1)).astype(LOW)
-    first_part = after(first_part, out_got)
+    down_part = depth_pair(after(down_scattered, qkv_sides[0]), odd)
+    down_part = depth_far(down_part)
+    first_part = after(first_part, out_got, down_part)
     mine, theirs, sums_one = first_norm_back(xs, first_part, swap(first_part, "core"), grad_own, grad_other, gain_one)
-    grad_inputs = ordered(mine, swap(theirs, "y").astype(FULL), y_at).reshape(2 * length, n)
-    down_part = depth_pair(after(down_scattered, qkv_grads[0]), odd)
-
-    ends_own, ends_other = layer_end(at, after(hiddens, sums_one, down_part), ffn)
-    residual, up_scattered, down_part = lax.optimization_barrier((residual, up_scattered, down_part, ends_own))[:3]
-    up_total = lax.psum(up_scattered, "dp")
-    down_part = depth_far(down_part)
+    theirs = swap(theirs, "y")
+    grad_inputs = ordered(mine, theirs.astype(FULL), y_at).reshape(2 * length, n)
+
+    up_scattered = after(up_scattered, sums_one)
+    up_part = depth_pair(up_scattered, odd)
+    qkv_got = plane_exchange(*after((qkv_grads[0][1], qkv_grads[1][0], qkv_grads[1][1]), up_scattered))
+    ends_own, ends_other = layer_end(at, after(hiddens, up_scattered), ffn)
+    up_far = depth_far(after(up_part, ends_own))
+    down_total = depth_join(after(down_part, ends_own), odd)
     kept_two = jnp.concatenate((residual[:, :n], residual[:, 2 * n : 3 * n]), axis=1)
     bias_two = jnp.concatenate((bias_low[:, :n], bias_low[:, 2 * n : 3 * n]), axis=1)
     ends = (kept_two + ends_own + swap(ends_other, "core").astype(FULL) + bias_two).astype(LOW)
-    layer_out = ordered(ends[:, :n], swap(ends[:, n:], "y"), y_at).reshape(2 * length, n)
+    ends_got = swap(ends[:, n:], "y")
+    layer_out = ordered(ends[:, :n], ends_got, y_at).reshape(2 * length, n)
 
     gains = jnp.concatenate((sums_one[:2, :n], sums_two[:2, :n])).reshape(-1)
     gains_y = jnp.concatenate((sums_one[:2, n:], sums_two[:2, n:])).reshape(-1)
@@ -1023,11 +1028,12 @@
         return out
 
     four = jnp.concatenate(
-        (plane_sum(after(qkv_grads[0][0], up_scattered), qkv_got), plane_sum(out_grads[0][0], out_got)), axis=1
-    )
-    four = depth_pair(four, odd)
-    down_total = depth_join(after(down_part, four), odd)
-    four = depth_join(depth_far(four), odd)
+        (plane_sum(after(qkv_grads[0][0], up_part), qkv_got), plane_sum(out_grads[0][0], out_got)), axis=1
+    )
+    four = depth_pair(after(four, up_far, near), odd)
+    up_total = depth_join(up_far, odd)
+    four = depth_far(after(four, theirs, ends))
+    four = depth_join(after(four, ends_got), odd)
     grad_query, grad_key, grad_value, grad_out = finish(four, 0, 4)
     (grad_down,) = finish(down_total, 1, 1)
     (grad_up,) = finish(jnp.concatenate([up_total[i * h : (i + 1) * h] for i in range(ups)], axis=1), 0, 1)

time: 484 us -> 479 us (0.990)
  starting transfers between devices: 51.3 us -> 60.8 us
  waiting for transfers between devices: 168 us -> 159 us
    psum x1 -> x0, waiting for transfers between devices: 24.9 us -> none  [fast_body(): up_total = lax.psum(up_scattered, 'dp')]
    ppermute x2 -> x3, waiting for transfers between devices: 3.98 us -> 26.2 us  [depth_pair(): lax.ppermute(pick(halves, 1 - odd), 'dp', PAIRS)]
    unnamed x6 -> x5, waiting for transfers between devices: 20.2 us -> 0.05 us
    ppermute x33, waiting for transfers between devices: 57.9 us -> 38.3 us  [swap(): return lax.ppermute(array, axis, SWAP)]
    ppermute x4, waiting for transfers between devices: 6.84 us -> 26.1 us  [swap_across(): return lax.ppermute(array, ('y', 'col'), [(0, 3), (3, 0), (1, 2), (2, 1)])]
    ppermute x2 -> x3, waiting for transfers between devices: 32.8 us -> 44.7 us  [depth_far(): return add_low(part, lax.ppermute(part, 'dp', FAR))]
    ppermute x4, starting transfers between devices: 8.25 us -> 17.1 us  [swap_across(): return lax.ppermute(array, ('y', 'col'), [(0, 3), (3, 0), (1, 2), (2, 1)])]
    ppermute x2 -> x3, waiting for transfers between devices: 19.4 us -> 21.4 us  [depth_join(): lax.ppermute(part, 'dp', PAIRS)]
  transfers between devices with their start and end apart: 50 -> 52, of which waited for: 21 -> 22; matrix products, arithmetic and copies ran while one was open for 17% -> 17% of each run, Pallas kernels for 22% -> 22%
where the time goes in v4:
time: 479 us; the launch traced here: 472 us
  waiting for transfers between devices  159 us (33%)
  Pallas kernels  141 us (29%)
  starting transfers between devices  60.8 us (13%)
  matrix products  32.9 us (7%)
  local copies, waits for them, and re-layouts  31.4 us (7%)
  other arithmetic  31 us (6%)
  between operations  15.3 us (3%)
    ppermute x3, waiting for transfers between devices, depth_far(): return add_low(part, lax.ppermute(part, 'dp', FAR))  44.7 us
    ppermute x33, waiting for transfers between devices, swap(): return lax.ppermute(array, axis, SWAP)  38.3 us
    ppermute x33, starting transfers between devices, swap(): return lax.ppermute(array, axis, SWAP)  30.4 us
    pallas_call x2, Pallas kernels, attend_backward(): pl.pallas_call(attend_backward_kernel, out_shape=jax.ShapeDtypeStruct((le...  27.7 us
    pallas_call x1, Pallas kernels, feed_forward(): pl.pallas_call(feed_forward_kernel, out_shape=(jax.ShapeDtypeStruct((leng...  27.1 us
    ppermute x3, waiting for transfers between devices, depth_pair(): lax.ppermute(pick(halves, 1 - odd), 'dp', PAIRS)  26.2 us
    ppermute x4, waiting for transfers between devices, swap_across(): return lax.ppermute(array, ('y', 'col'), [(0, 3), (3, 0), (1, 2), (2, 1)])  26.1 us
    pallas_call x2, Pallas kernels, attend_forward(): pl.pallas_call(attend_forward_kernel, out_shape=(jax.ShapeDtypeStruct((le...  25.8 us
  transfers between devices with their start and end apart: 52, of which 22 were waited for; matrix products, arithmetic and copies ran while one was open for 17% of the time, Pallas kernels for 22%

profile of v4, /device:TPU:0, one launch (start us, length us, event | category | flops | bytes accessed | tf_op | source)
XLA Modules:
  0.0 472.0 jit_solution(16624011845376209487)
XLA Ops:
  13.3 2.9 collective-permute-start.8
  16.2 1.5 collective-permute-start.10
  17.7 1.5 fusion.16
  19.3 15.0 %collective-permute-done.8 = bf16[512,768]{1,0:T(8,128)(2,1)} collective-permute-done((bf16[512,768]{1,0:T(8,128)(2,1)}, bf16[512,768]{1,0:T(8,128)(2,1)}, u32[]{:S(2)}, u32[]{:S(2)}) %collective-permute-start.8) | collective-permute-done | bytes 786464 | tf_op jit(solution)/shard_map/ppermute | solution.py:270
  38.0 3.1 collective-permute-start.6
  47.9 12.3 %collective-permute-start.5 = (bf16[512,768]{1,0:T(8,128)(2,1)}, bf16[512,768]{1,0:T(8,128)(2,1)S(1)}, u32[]{:S(2)}, u32[]{:S(2)}) collective-permute-start(bf16[512,768]{1,0:T(8,128)(2,1)} %pad_maximum_fusion.7), channel_id=1, source_target_pairs={{0,5},{5,0},{1,4},{4,1},{2,7},{7,2},{3,6},{6,3},{8,13},{13,8},{9,1... | collective-permute-start | bytes 2359304 | tf_op jit(solution)/shard_map/ppermute | solution.py:856
  61.7 2.5 collective-permute-start.7
  64.1 1.6 pad_maximum_fusion.3
  67.6 20.5 %collective-permute-done.5 = bf16[512,768]{1,0:T(8,128)(2,1)S(1)} collective-permute-done((bf16[512,768]{1,0:T(8,128)(2,1)}, bf16[512,768]{1,0:T(8,128)(2,1)S(1)}, u32[]{:S(2)}, u32[]{:S(2)}) %collective-permute-start.5) | collective-permute-done | bytes 786464 | tf_op jit(solution)/shard_map/ppermute | solution.py:856
  89.7 5.0 %first_norm.1 = (bf16[1024,512]{1,0:T(8,128)(2,1)}, bf16[1024,512]{1,0:T(8,128)(2,1)}) custom-call(bf16[1024,256]{1,0:T(8,128)(2,1)} %copy-done.2, bf16[1024,256]{1,0:T(8,128)(2,1)} %copy-done.3, bf16[1024,256]{1,0:T(8,128)(2,1)} %copy-done.4, bf16[1024,256]{1,0:T(8,128)(2,1)} %copy-done.5, f32[1,1024]{1,0:T(1,128)} %get-tuple-element.221.gain_ref, ...), custom_call_target="tpu_custom_call" | custom-call | flops 5242880 | bytes 4194304 | tf_op jit(solution)/shard_map/first_norm/pallas_call | solution.py:536
  94.7 1.5 constant_dynamic-update-slice_fusion.1
  98.6 2.7 collective-permute-start.16
  101.4 4.1 convolution_convert_fusion.1.q_ref.k_ref.v_ref
  105.8 12.8 %attend_forward.2 = (bf16[1024,256]{1,0:T(8,128)(2,1)}, bf16[4,1024,128]{2,1,0:T(8,128)(2,1)}) custom-call(s32[2,4]{1,0:T(2,128)} %pad_add_fusion.1.where_ref, bf16[1024,768]{1,0:T(8,128)(2,1)} %convolution_convert_fusion.1.q_ref.k_ref.v_ref, bf16[1024,768]{1,0:T(8,128)(2,1)} %convolution_convert_fusion.1.q_ref.k_ref.v_ref, ...), custom_call_target="tpu_custom_call" | custom-call | flops 1073741824 | bytes 12582912 | tf_op jit(solution)/shard_map/attend_forward/pallas_call | solution.py:377
  119.7 5.6 %collective-permute-done.16 = bf16[256,512]{1,0:T(8,128)(2,1)} collective-permute-done((bf16[256,512]{1,0:T(8,128)(2,1)S(1)}, bf16[256,512]{1,0:T(8,128)(2,1)}, u32[]{:S(2)}, u32[]{:S(2)}) %collective-permute-start.16) | collective-permute-done | bytes 262176 | tf_op jit(solution)/shard_map/ppermute | solution.py:856
  126.6 2.9 convolution_convert_fusion.q_ref.k_ref.v_ref
  129.5 13.0 %attend_forward.3 = (bf16[1024,256]{1,0:T(8,128)(2,1)}, bf16[4,1024,128]{2,1,0:T(8,128)(2,1)}) custom-call(s32[2,4]{1,0:T(2,128)} %pad_add_fusion.1.where_ref, bf16[1024,768]{1,0:T(8,128)(2,1)} %convolution_convert_fusion.q_ref.k_ref.v_ref, bf16[1024,768]{1,0:T(8,128)(2,1)} %convolution_convert_fusion.q_ref.k_ref.v_ref, ...), custom_call_target="tpu_custom_call" | custom-call | flops 1073741824 | bytes 12582912 | tf_op jit(solution)/shard_map/attend_forward/pallas_call | solution.py:377
  145.0 1.5 pad_maximum_fusion.1.c_ref.cots_ref
  147.3 4.8 %mix_heads.1.part_ref = bf16[1024,1024]{1,0:T(8,128)(2,1)} custom-call(bf16[1024,256]{1,0:T(8,128)(2,1)} %get-tuple-element.69.h0.heads_ref, bf16[1024,256]{1,0:T(8,128)(2,1)} %get-tuple-element.75.h1.heads_ref, bf16[256,1024]{1,0:T(8,128)(2,1)} %copy-done.11, bf16[256,1024]{1,0:T(8,128)(2,1)} %copy-done.9), custom_call_target="tpu_custom_call" | custom-call | flops 1073741824 | bytes 5242880 | tf_op jit(solution)/shard_map/mix_heads/pallas_call | solution.py:657
  153.8 2.8 collective-permute-done.20.got_ref
  157.9 6.3 %second_norm.1 = (f32[1024,1024]{1,0:T(8,128)}, bf16[2,1024,512]{2,1,0:T(8,128)(2,1)}) custom-call(bf16[1024,256]{1,0:T(8,128)(2,1)} %copy-done.2, bf16[1024,256]{1,0:T(8,128)(2,1)} %copy-done.3, bf16[1024,256]{1,0:T(8,128)(2,1)} %copy-done.4, bf16[1024,256]{1,0:T(8,128)(2,1)} %copy-done.5, bf16[1024,1024]{1,0:T(8,128)(2,1)} %mix_heads.1.part_ref, ...), custom_call_target="tpu_custom_call" | custom-call | flops 7864320 | bytes 12582912 | tf_op jit(solution)/shard_map/second_norm/pallas_call | solution.py:563
  164.2 27.1 %feed_forward.1 = (bf16[1024,1024]{1,0:T(8,128)(2,1)}, bf16[2,1024,1024]{2,1,0:T(8,128)(2,1)}, bf16[2,1024,1024]{2,1,0:T(8,128)(2,1)}, f32[8,8,256]{2,1,0:T(8,128)}) custom-call(s32[2]{0:T(128)} %pad_add_fusion.2.at_ref, bf16[2,1024,512]{2,1,0:T(8,128)(2,1)} %get-tuple-element.78.s_ref, bf16[2,1024,512]{2,1,0:T(8,128)(2,1)} %pad_maximum_fusion.1.c_ref.cots_ref, ...), custom_call_target="tpu_custom_call" | custom-call | flops 12884901888 | bytes 29360128 | tf_op jit(solution)/shard_map/feed_forward/pallas_call | solution.py:728
  191.4 9.2 %down_grads.1 = bf16[2,2,1024,512]{3,2,1,0:T(8,128)(2,1)} custom-call(s32[2]{0:T(128)} %pad_add_fusion.2.at_ref, bf16[2,1024,1024]{2,1,0:T(8,128)(2,1)} %get-tuple-element.96.hidden_ref.h0.h1, bf16[2,1024,512]{2,1,0:T(8,128)(2,1)} %pad_maximum_fusion.1.c_ref.cots_ref), custom_call_target="tpu_custom_call" | custom-call | flops 4294967296 | bytes 8388608 | tf_op jit(solution)/shard_map/down_grads/pallas_call | solution.py:792
  200.6 1.5 copy-done.7
  202.5 10.5 %up_grads.1 = bf16[4,1024,512]{2,1,0:T(8,128)(2,1)} custom-call(s32[2]{0:T(128)} %pad_add_fusion.2.at_ref, bf16[2,1024,512]{2,1,0:T(8,128)(2,1)} %get-tuple-element.78.s_ref, bf16[2,1024,1024]{2,1,0:T(8,128)(2,1)} %get-tuple-element.82.grad_ref), custom_call_target="tpu_custom_call" | custom-call | flops 4294967296 | bytes 8388608 | tf_op jit(solution)/shard_map/up_grads/pallas_call | solution.py:765
  213.1 8.2 %second_norm_back.1 = (f32[1024,256]{1,0:T(8,128)}, f32[1024,256]{1,0:T(8,128)}, bf16[1024,1024]{1,0:T(8,128)(2,1)}, f32[8,512]{1,0:T(8,128)}) custom-call(f32[1024,1024]{1,0:T(8,128)} %get-tuple-element.77.residual_ref, bf16[1024,1024]{1,0:T(8,128)(2,1)} %get-tuple-element.84.part_ref, bf16[1024,1024]{1,0:T(8,128)(2,1)} %collective-permute-done.21.got_ref, ...), custom_call_target="tpu_custom_call" | custom-call | flops 15728640 | bytes 16777216 | tf_op jit(solution)/shard_map/second_norm_back/pallas_call | solution.py:611
  221.2 3.9 select_convert_fusion.1.grads_ref
  225.1 13.7 %attend_backward.2 = bf16[1024,768]{1,0:T(8,128)(2,1)} custom-call(s32[2,4]{1,0:T(2,128)} %pad_add_fusion.1.where_ref, bf16[4,1024,128]{2,1,0:T(8,128)(2,1)} %get-tuple-element.83.kept_ref, bf16[1024,768]{1,0:T(8,128)(2,1)} %convolution_convert_fusion.1.q_ref.k_ref.v_ref, bf16[1024,768]{1,0:T(8,128)(2,1)} %convolution_convert_fusion.1.q_ref.k_ref.v_ref, ...), custom_call_target="tpu_custom_call" | custom-call | flops 2684354560 | bytes 15728640 | tf_op jit(solution)/shard_map/attend_backward/pallas_call | solution.py:467
  238.8 13.9 %attend_backward.3 = bf16[1024,768]{1,0:T(8,128)(2,1)} custom-call(s32[2,4]{1,0:T(2,128)} %pad_add_fusion.1.where_ref, bf16[4,1024,128]{2,1,0:T(8,128)(2,1)} %get-tuple-element.87.kept_ref, bf16[1024,768]{1,0:T(8,128)(2,1)} %convolution_convert_fusion.q_ref.k_ref.v_ref, bf16[1024,768]{1,0:T(8,128)(2,1)} %convolution_convert_fusion.q_ref.k_ref.v_ref, ...), custom_call_target="tpu_custom_call" | custom-call | flops 2684354560 | bytes 15728640 | tf_op jit(solution)/shard_map/attend_backward/pallas_call | solution.py:467
  252.8 2.6 convolution_convert_fusion.5
  255.4 1.9 convolution_convert_fusion.4
  257.3 1.9 convolution_convert_fusion.3
  259.3 1.9 convolution_convert_fusion.2
  264.6 1.6 collective-permute-start.25
  266.1 1.8 convolution_convert_fusion.8
  268.0 4.5 collective-permute-start.23
  272.5 1.5 convolution_convert_fusion.7
  274.1 4.2 collective-permute-done.25
  278.5 2.5 collective-permute-start.26
  281.0 6.5 %fusion.20.part_ref = bf16[1024,1024]{1,0:T(8,128)(2,1)} fusion(bf16[1024,768]{1,0:T(8,128)(2,1)S(1)} %copy-done.37, bf16[512,768]{1,0:T(8,128)(2,1)} %collective-permute-done.8, bf16[256,768]{1,0:T(8,128)(2,1)S(1)} %copy-done.40, bf16[256,256]{1,0:T(8,128)(2,1)S(1)} %get-tuple-element.216, bf16[256,256]{1,0:T(8,128)(2,1)S(1)} %copy-done.27, ...), kind=kOutput, calls=%fused_computation.30 | convolution fusion | flops 3247439872 | bytes 8388608 | tf_op jit(solution)/shard_map/dot_general | solution.py:278
  287.5 16.1 %collective-permute-done.26 = bf16[512,512]{1,0:T(8,128)(2,1)S(1)} collective-permute-done((bf16[512,512]{1,0:T(8,128)(2,1)S(1)}, bf16[512,512]{1,0:T(8,128)(2,1)S(1)}, u32[]{:S(2)}, u32[]{:S(2)}) %collective-permute-start.26) | collective-permute-done | bytes 524320 | tf_op jit(solution)/shard_map/ppermute | solution.py:885
  304.9 2.7 fusion.76
  309.2 6.9 %first_norm_back.1 = (f32[1024,256]{1,0:T(8,128)}, bf16[1024,256]{1,0:T(8,128)(2,1)}, f32[8,512]{1,0:T(8,128)}) custom-call(bf16[1024,256]{1,0:T(8,128)(2,1)} %copy-done.2, bf16[1024,256]{1,0:T(8,128)(2,1)} %copy-done.3, bf16[1024,256]{1,0:T(8,128)(2,1)} %copy-done.4, bf16[1024,256]{1,0:T(8,128)(2,1)} %copy-done.5, bf16[1024,1024]{1,0:T(8,128)(2,1)} %fusion.20.part_ref, ...), custom_call_target="tpu_custom_call" | custom-call | flops 15728640 | bytes 10485760 | tf_op jit(solution)/shard_map/first_norm_back/pallas_call | solution.py:634
  318.2 2.4 collective-permute-done.31
  320.6 4.9 %collective-permute-start.32 = (f32[2304]{0:T(1024)S(1)}, f32[2304]{0:T(1024)S(1)}, u32[]{:S(2)}, u32[]{:S(2)}) collective-permute-start(f32[2304]{0:T(1024)S(1)} %fusion.65), channel_id=1, source_target_pairs={{0,1},{1,0},{2,3},{3,2},{4,5},{5,4},{6,7},{7,6},{8,9},{9,8},{10,11... | collective-permute-start | bytes 27656 | tf_op jit(solution)/shard_map/ppermute | solution.py:270
  325.5 2.6 fusion.50
  328.2 9.7 %layer_end.1 = (f32[1024,512]{1,0:T(8,128)}, bf16[1024,512]{1,0:T(8,128)(2,1)}) custom-call(s32[2]{0:T(128)} %pad_add_fusion.2.at_ref, bf16[2,1024,1024]{2,1,0:T(8,128)(2,1)} %get-tuple-element.96.hidden_ref.h0.h1, bf16[2,1024,1024]{2,1,0:T(8,128)(2,1)} %get-tuple-element.96.hidden_ref.h0.h1, bf16[4,2048,512]{2,1,0:T(8,128)(2,1)} %bitcast.144, ...), custom_call_target="tpu_custom_call" | custom-call | flops 4294967296 | bytes 10485760 | tf_op jit(solution)/shard_map/layer_end/pallas_call | solution.py:828
  338.6 2.0 collective-permute-start.38
  340.6 1.8 collective-permute-start.34
  342.7 2.6 collective-permute-done.34
  346.6 1.9 collective-permute-start.47
  349.1 8.3 %collective-permute-done.35 = bf16[512,512]{1,0:T(8,128)(2,1)S(1)} collective-permute-done((bf16[512,512]{1,0:T(8,128)(2,1)S(1)}, bf16[512,512]{1,0:T(8,128)(2,1)S(1)}, u32[]{:S(2)}, u32[]{:S(2)}) %collective-permute-start.35) | collective-permute-done | bytes 524320 | tf_op jit(solution)/shard_map/ppermute | solution.py:881
  358.5 8.9 %collective-permute-done.47 = bf16[512,512]{1,0:T(8,128)(2,1)S(1)} collective-permute-done((bf16[512,512]{1,0:T(8,128)(2,1)S(1)}, bf16[512,512]{1,0:T(8,128)(2,1)S(1)}, u32[]{:S(2)}, u32[]{:S(2)}) %collective-permute-start.47) | collective-permute-done | bytes 524320 | tf_op jit(solution)/shard_map/ppermute | solution.py:889
  368.5 1.5 collective-permute-done.30
  370.0 1.8 collective-permute-start.39
  374.3 2.0 collective-permute-done.37
  376.3 10.0 %collective-permute-done.36 = bf16[512,768]{1,0:T(8,128)(2,1)S(1)} collective-permute-done((bf16[512,768]{1,0:T(8,128)(2,1)S(1)}, bf16[512,768]{1,0:T(8,128)(2,1)S(1)}, u32[]{:S(2)}, u32[]{:S(2)}) %collective-permute-start.36) | collective-permute-done | bytes 786464 | tf_op jit(solution)/shard_map/ppermute | solution.py:270
  386.8 8.1 %collective-permute-done.39 = bf16[512,512]{1,0:T(8,128)(2,1)S(1)} collective-permute-done((bf16[512,512]{1,0:T(8,128)(2,1)S(1)}, bf16[512,512]{1,0:T(8,128)(2,1)S(1)}, u32[]{:S(2)}, u32[]{:S(2)}) %collective-permute-start.39) | collective-permute-done | bytes 524320 | tf_op jit(solution)/shard_map/ppermute | solution.py:885
  397.8 2.0 collective-permute-start.40
  399.8 2.8 fusion.19
  406.2 13.7 %collective-permute-done.40 = bf16[256,1024]{0,1:T(8,128)(2,1)} collective-permute-done((bf16[256,1024]{0,1:T(8,128)(2,1)}, bf16[256,1024]{0,1:T(8,128)(2,1)}, u32[]{:S(2)}, u32[]{:S(2)}) %collective-permute-start.40) | collective-permute-done | bytes 524320 | tf_op jit(solution)/shard_map/ppermute | solution.py:881
  424.6 20.4 %collective-permute-done.41 = bf16[256,1024]{0,1:T(8,128)(2,1)S(1)} collective-permute-done((bf16[256,1024]{0,1:T(8,128)(2,1)S(1)}, bf16[256,1024]{0,1:T(8,128)(2,1)S(1)}, u32[]{:S(2)}, u32[]{:S(2)}) %collective-permute-start.41) | collective-permute-done | bytes 524320 | tf_op jit(solution)/shard_map/ppermute | solution.py:885
  446.6 12.5 %collective-permute-done.42 = bf16[256,1024]{0,1:T(8,128)(2,1)S(1)} collective-permute-done((bf16[256,1024]{0,1:T(8,128)(2,1)S(1)}, bf16[256,1024]{0,1:T(8,128)(2,1)S(1)}, u32[]{:S(2)}, u32[]{:S(2)}) %collective-permute-start.42) | collective-permute-done | bytes 524320 | tf_op jit(solution)/shard_map/ppermute | solution.py:889
  459.5 1.6 maximum_convert_fusion
  (328 shorter events, 66.7 us)
Async XLA Ops:
  7.2 33.8 %copy-start = (s32[8,16,3]{1,0,2:T(8,128)S(1)}, s32[8,16,3]{1,0,2:T(8,128)}, u32[]{:S(2)}) copy-start(s32[8,16,3]{1,0,2:T(8,128)} %param.31) | copy-start | bytes 4612
  7.2 157.0 %all-gather.3.cloned.1.call-start = ((), (), s32[]{:S(2)}) async-start(), calls=%async_computation.2 | async-start | bytes 10485760 | tf_op jit(solution)/shard_map/all_gather | solution.py:923
  9.5 91.8 %copy-start.26 = (bf16[256,256]{1,0:T(8,128)(2,1)}, bf16[256,256]{1,0:T(8,128)(2,1)S(1)}, u32[]{:S(2)}) copy-start(bf16[256,256]{1,0:T(8,128)(2,1)S(1)} %get-tuple-element.242) | copy-start | bytes 393220
  9.6 1.9 collective-permute-start.4
  12.6 5.1 %collective-permute-start.11 = (bf16[256,1024]{1,0:T(8,128)(2,1)S(1)}, bf16[256,1024]{1,0:T(8,128)(2,1)S(1)}, u32[]{:S(2)}, u32[]{:S(2)}) collective-permute-start(bf16[256,1024]{1,0:T(8,128)(2,1)S(1)} %get-tuple-element.205), channel_id=1, source_target_pairs={{0,2},{2,0},{1,3},{3,1},{4,6},{6,4},{5,7},{7,5},{8,10},{10,8},{9,1... | collective-permute-start | bytes 1572872 | tf_op jit(solution)/shard_map/ppermute | solution.py:270
  13.1 4.6 collective-permute-start.12
  13.3 21.0 %collective-permute-start.8 = (bf16[512,768]{1,0:T(8,128)(2,1)}, bf16[512,768]{1,0:T(8,128)(2,1)}, u32[]{:S(2)}, u32[]{:S(2)}) collective-permute-start(bf16[512,768]{1,0:T(8,128)(2,1)} %pad_maximum_fusion.7), channel_id=1, source_target_pairs={{0,4},{4,0},{1,5},{5,1},{2,6},{6,2},{3,7},{7,3},{8,12},{12,8},{9,1... | collective-permute-start | bytes 2359304 | tf_op jit(solution)/shard_map/ppermute | solution.py:270
  16.2 19.5 %collective-permute-start.10 = (bf16[512,768]{1,0:T(8,128)(2,1)}, bf16[512,768]{1,0:T(8,128)(2,1)S(1)}, u32[]{:S(2)}, u32[]{:S(2)}) collective-permute-start(bf16[512,768]{1,0:T(8,128)(2,1)} %pad_maximum_fusion.7), channel_id=1, source_target_pairs={{0,1},{1,0},{2,3},{3,2},{4,5},{5,4},{6,7},{7,6},{8,9},{9,8},{10,11... | collective-permute-start | bytes 2359304 | tf_op jit(solution)/shard_map/ppermute | solution.py:270
  19.3 22.0 %copy-start.52 = (f32[2048]{0:T(1024)S(1)}, f32[2048]{0:T(1024)}, u32[]{:S(2)}) copy-start(f32[2048]{0:T(1024)} %param.27) | copy-start | bytes 24580
  19.3 23.4 %copy-start.61 = (s32[2]{0:T(128)S(1)}, s32[2]{0:T(128)}, u32[]{:S(2)}) copy-start(s32[2]{0:T(128)} %param.32) | copy-start | bytes 28
  35.7 227.6 %reduce-scatter.9.cloned.1.call-start = ((), (), s32[]{:S(2)}) async-start(), calls=%async_computation.4 | async-start | bytes 5242880
  36.7 30.9 %collective-permute-start = (bf16[1024,256]{1,0:T(8,128)(2,1)S(1)}, bf16[1024,256]{1,0:T(8,128)(2,1)S(1)}, u32[]{:S(2)}, u32[]{:S(2)}) collective-permute-start(bf16[1024,256]{1,0:T(8,128)(2,1)S(1)} %get-tuple-element.63.x0), channel_id=1, source_target_pairs={{0,2},{2,0},{1,3},{3,1},{4,6},{6,4},{5,7},{7,5},{8,10},{10,8},{9,1... | collective-permute-start | bytes 1572872 | tf_op jit(solution)/shard_map/ppermute | solution.py:270
  36.8 23.8 %collective-permute-start.1 = (bf16[1024,256]{1,0:T(8,128)(2,1)S(1)}, bf16[1024,256]{1,0:T(8,128)(2,1)S(1)}, u32[]{:S(2)}, u32[]{:S(2)}) collective-permute-start(bf16[1024,256]{1,0:T(8,128)(2,1)S(1)} %get-tuple-element.206), channel_id=1, source_target_pairs={{0,4},{4,0},{1,5},{5,1},{2,6},{6,2},{3,7},{7,3},{8,12},{12,8},{9,1... | collective-permute-start | bytes 1572872 | tf_op jit(solution)/shard_map/ppermute | solution.py:270
  37.2 5.5 %collective-permute-start.3 = (s32[1,1024]{1,0:T(1,128)S(1)}, s32[1,1024]{1,0:T(1,128)S(1)}, u32[]{:S(2)}, u32[]{:S(2)}) collective-permute-start(s32[1,1024]{1,0:T(1,128)S(1)} %copy-done.60), channel_id=1, source_target_pairs={{0,0},{4,1},{1,2},{5,3},{2,4},{6,5},{3,6},{7,7},{8,8},{12,9},{9,10... | collective-permute-start | bytes 12296 | tf_op jit(solution)/shard_map/ppermute | solution.py:942
  37.9 23.1 %copy-start.44 = (f32[5,256]{1,0:T(8,128)}, f32[5,256]{1,0:T(8,128)S(1)}, u32[]{:S(2)}) copy-start(f32[5,256]{1,0:T(8,128)S(1)} %stack.107) | copy-start | bytes 15364
  38.0 23.1 %collective-permute-start.6 = (f32[5,256]{1,0:T(8,128)S(1)}, f32[5,256]{1,0:T(8,128)S(1)}, u32[]{:S(2)}, u32[]{:S(2)}) collective-permute-start(f32[5,256]{1,0:T(8,128)S(1)} %stack.107), channel_id=1, source_target_pairs={{0,2},{2,0},{1,3},{3,1},{4,6},{6,4},{5,7},{7,5},{8,10},{10,8},{9,1... | collective-permute-start | bytes 15368 | tf_op jit(solution)/shard_map/ppermute | solution.py:270
  41.3 5.1 %collective-permute-start.9 = (f32[1216]{0:T(1024)S(1)}, f32[1216]{0:T(1024)S(1)}, u32[]{:S(2)}, u32[]{:S(2)}) collective-permute-start(f32[1216]{0:T(1024)S(1)} %pad_maximum_fusion.15), channel_id=1, source_target_pairs={{0,1},{1,0},{2,3},{3,2},{4,5},{5,4},{6,7},{7,6},{8,9},{9,8},{10,11... | collective-permute-start | bytes 14600 | tf_op jit(solution)/shard_map/ppermute | solution.py:270
  47.9 40.2 %collective-permute-start.5 = (bf16[512,768]{1,0:T(8,128)(2,1)}, bf16[512,768]{1,0:T(8,128)(2,1)S(1)}, u32[]{:S(2)}, u32[]{:S(2)}) collective-permute-start(bf16[512,768]{1,0:T(8,128)(2,1)} %pad_maximum_fusion.7), channel_id=1, source_target_pairs={{0,5},{5,0},{1,4},{4,1},{2,7},{7,2},{3,6},{6,3},{8,13},{13,8},{9,1... | collective-permute-start | bytes 2359304 | tf_op jit(solution)/shard_map/ppermute | solution.py:856
  60.6 7.0 %collective-permute-start.2 = (bf16[1024,256]{1,0:T(8,128)(2,1)S(1)}, bf16[1024,256]{1,0:T(8,128)(2,1)S(1)}, u32[]{:S(2)}, u32[]{:S(2)}) collective-permute-start(bf16[1024,256]{1,0:T(8,128)(2,1)S(1)} %collective-permute-done.1.x2), channel_id=1, source_target_pairs={{0,2},{2,0},{1,3},{3,1},{4,6},{6,4},{5,7},{7,5},{8,10},{10,8},{9,1... | collective-permute-start | bytes 1572872 | tf_op jit(solution)/shard_map/ppermute | solution.py:270
  61.6 26.5 %copy-start.41 = (bf16[512,256]{1,0:T(8,128)(2,1)S(1)}, bf16[512,256]{1,0:T(8,128)(2,1)}, u32[]{:S(2)}) copy-start(bf16[512,256]{1,0:T(8,128)(2,1)} %param.23) | copy-start | bytes 786436
  61.7 26.6 %copy-start.6 = (bf16[2048,256]{1,0:T(8,128)(2,1)S(1)}, bf16[2048,256]{1,0:T(8,128)(2,1)}, u32[]{:S(2)}) copy-start(bf16[2048,256]{1,0:T(8,128)(2,1)} %param.33) | copy-start | bytes 3145732
  61.7 5.3 %collective-permute-start.7 = (f32[5,512]{1,0:T(8,128)S(1)}, f32[5,512]{1,0:T(8,128)S(1)}, u32[]{:S(2)}, u32[]{:S(2)}) collective-permute-start(f32[5,512]{1,0:T(8,128)S(1)} %pad_maximum_fusion.12), channel_id=1, source_target_pairs={{0,4},{4,0},{1,5},{5,1},{2,6},{6,2},{3,7},{7,3},{8,12},{12,8},{9,1... | collective-permute-start | bytes 30728 | tf_op jit(solution)/shard_map/ppermute | solution.py:270
  67.0 27.7 %copy-start.48 = (f32[5,512]{1,0:T(8,128)}, f32[5,512]{1,0:T(8,128)S(1)}, u32[]{:S(2)}) copy-start(f32[5,512]{1,0:T(8,128)S(1)} %collective-permute-done.7) | copy-start | bytes 30724
  67.6 22.1 %copy-start.3 = (bf16[1024,256]{1,0:T(8,128)(2,1)}, bf16[1024,256]{1,0:T(8,128)(2,1)S(1)}, u32[]{:S(2)}) copy-start(bf16[1024,256]{1,0:T(8,128)(2,1)S(1)} %collective-permute-done.x1) | copy-start | bytes 1572868
  67.6 22.1 %copy-start.5 = (bf16[1024,256]{1,0:T(8,128)(2,1)}, bf16[1024,256]{1,0:T(8,128)(2,1)S(1)}, u32[]{:S(2)}) copy-start(bf16[1024,256]{1,0:T(8,128)(2,1)S(1)} %collective-permute-done.2.x3) | copy-start | bytes 1572868
  88.1 8.2 %collective-permute-start.13 = (bf16[256,256]{1,0:T(8,128)(2,1)S(1)}, bf16[256,256]{1,0:T(8,128)(2,1)S(1)}, u32[]{:S(2)}, u32[]{:S(2)}) collective-permute-start(bf16[256,256]{1,0:T(8,128)(2,1)S(1)} %get-tuple-element.209), channel_id=1, source_target_pairs={{0,2},{2,0},{1,3},{3,1},{4,6},{6,4},{5,7},{7,5},{8,10},{10,8},{9,1... | collective-permute-start | bytes 393224 | tf_op jit(solution)/shard_map/ppermute | solution.py:270
  89.2 37.2 %collective-permute-start.17 = (bf16[1024,256]{1,0:T(8,128)(2,1)}, bf16[1024,256]{1,0:T(8,128)(2,1)}, u32[]{:S(2)}, u32[]{:S(2)}) collective-permute-start(bf16[1024,256]{1,0:T(8,128)(2,1)} %get-tuple-element.201), channel_id=1, source_target_pairs={{0,4},{4,0},{1,5},{5,1},{2,6},{6,2},{3,7},{7,3},{8,12},{12,8},{9,1... | collective-permute-start | bytes 1572872 | tf_op jit(solution)/shard_map/ppermute | solution.py:270
  89.6 53.0 %collective-permute-start.18 = (bf16[1024,256]{1,0:T(8,128)(2,1)S(1)}, bf16[1024,256]{1,0:T(8,128)(2,1)}, u32[]{:S(2)}, u32[]{:S(2)}) collective-permute-start(bf16[1024,256]{1,0:T(8,128)(2,1)S(1)} %get-tuple-element.200), channel_id=1, source_target_pairs={{0,2},{2,0},{1,3},{3,1},{4,6},{6,4},{5,7},{7,5},{8,10},{10,8},{9,1... | collective-permute-start | bytes 1572872 | tf_op jit(solution)/shard_map/ppermute | solution.py:270
  98.2 20.4 %collective-permute-start.15 = (bf16[256,512]{1,0:T(8,128)(2,1)S(1)}, bf16[256,512]{1,0:T(8,128)(2,1)}, u32[]{:S(2)}, u32[]{:S(2)}) collective-permute-start(bf16[256,512]{1,0:T(8,128)(2,1)S(1)} %pad_maximum_fusion.11), channel_id=1, source_target_pairs={{0,1},{1,0},{2,3},{3,2},{4,5},{5,4},{6,7},{7,6},{8,9},{9,8},{10,11... | collective-permute-start | bytes 786440 | tf_op jit(solution)/shard_map/ppermute | solution.py:270
  98.6 26.7 %collective-permute-start.16 = (bf16[256,512]{1,0:T(8,128)(2,1)S(1)}, bf16[256,512]{1,0:T(8,128)(2,1)}, u32[]{:S(2)}, u32[]{:S(2)}) collective-permute-start(bf16[256,512]{1,0:T(8,128)(2,1)S(1)} %pad_maximum_fusion.11), channel_id=1, source_target_pairs={{0,5},{5,0},{1,4},{4,1},{2,7},{7,2},{3,6},{6,3},{8,13},{13,8},{9,1... | collective-permute-start | bytes 786440 | tf_op jit(solution)/shard_map/ppermute | solution.py:856
  105.4 20.9 %collective-permute-start.14 = (bf16[256,512]{1,0:T(8,128)(2,1)S(1)}, bf16[256,512]{1,0:T(8,128)(2,1)S(1)}, u32[]{:S(2)}, u32[]{:S(2)}) collective-permute-start(bf16[256,512]{1,0:T(8,128)(2,1)S(1)} %pad_maximum_fusion.11), channel_id=1, source_target_pairs={{0,4},{4,0},{1,5},{5,1},{2,6},{6,2},{3,7},{7,3},{8,12},{12,8},{9,1... | collective-permute-start | bytes 786440 | tf_op jit(solution)/shard_map/ppermute | solution.py:270
  126.3 17.4 %collective-permute-start.19 = (bf16[1024,256]{1,0:T(8,128)(2,1)}, bf16[1024,256]{1,0:T(8,128)(2,1)}, u32[]{:S(2)}, u32[]{:S(2)}) collective-permute-start(bf16[1024,256]{1,0:T(8,128)(2,1)} %collective-permute-done.17), channel_id=1, source_target_pairs={{0,2},{2,0},{1,3},{3,1},{4,6},{6,4},{5,7},{7,5},{8,10},{10,8},{9,1... | collective-permute-start | bytes 1572872 | tf_op jit(solution)/shard_map/ppermute | solution.py:270
  152.1 4.5 collective-permute-start.20
  200.6 127.5 %reduce-scatter.7.cloned.1.call-start = ((), (), s32[]{:S(2)}) async-start(), calls=%async_computation.3 | async-start | bytes 5242880
  202.1 10.9 %collective-permute-start.21 = (bf16[1024,1024]{1,0:T(8,128)(2,1)S(1)}, bf16[1024,1024]{1,0:T(8,128)(2,1)}, u32[]{:S(2)}, u32[]{:S(2)}) collective-permute-start(bf16[1024,1024]{1,0:T(8,128)(2,1)S(1)} %copy-done.7), channel_id=1, source_target_pairs={{0,2},{2,0},{1,3},{3,1},{4,6},{6,4},{5,7},{7,5},{8,10},{10,8},{9,1... | collective-permute-start | bytes 6291464 | tf_op jit(solution)/shard_map/ppermute | solution.py:270
  262.4 41.3 %collective-permute-start.22 = (bf16[512,256]{1,0:T(8,128)(2,1)}, bf16[512,256]{1,0:T(8,128)(2,1)}, u32[]{:S(2)}, u32[]{:S(2)}) collective-permute-start(bf16[512,256]{1,0:T(8,128)(2,1)} %convolution_convert_fusion.9), channel_id=1, source_target_pairs={{0,4},{4,0},{1,5},{5,1},{2,6},{6,2},{3,7},{7,3},{8,12},{12,8},{9,1... | collective-permute-start | bytes 786440 | tf_op jit(solution)/shard_map/ppermute | solution.py:270
  264.6 13.7 %collective-permute-start.25 = (bf16[512,512]{1,0:T(8,128)(2,1)S(1)}, bf16[512,512]{1,0:T(8,128)(2,1)S(1)}, u32[]{:S(2)}, u32[]{:S(2)}) collective-permute-start(bf16[512,512]{1,0:T(8,128)(2,1)S(1)} %dynamic-slice_bitcast_fusion.1), channel_id=1, source_target_pairs={{0,8},{8,0},{16,24},{24,16},{1,9},{9,1},{17,25},{25,17},{2,10},{10... | collective-permute-start | bytes 1572872 | tf_op jit(solution)/shard_map/ppermute | solution.py:881
  268.0 35.7 %collective-permute-start.23 = (bf16[512,256]{1,0:T(8,128)(2,1)S(1)}, bf16[512,256]{1,0:T(8,128)(2,1)}, u32[]{:S(2)}, u32[]{:S(2)}) collective-permute-start(bf16[512,256]{1,0:T(8,128)(2,1)S(1)} %convolution_convert_fusion.8), channel_id=1, source_target_pairs={{0,1},{1,0},{2,3},{3,2},{4,5},{5,4},{6,7},{7,6},{8,9},{9,8},{10,11... | collective-permute-start | bytes 786440 | tf_op jit(solution)/shard_map/ppermute | solution.py:270
  274.0 29.7 %collective-permute-start.24 = (bf16[512,256]{1,0:T(8,128)(2,1)S(1)}, bf16[512,256]{1,0:T(8,128)(2,1)}, u32[]{:S(2)}, u32[]{:S(2)}) collective-permute-start(bf16[512,256]{1,0:T(8,128)(2,1)S(1)} %convolution_convert_fusion.7), channel_id=1, source_target_pairs={{0,5},{5,0},{1,4},{4,1},{2,7},{7,2},{3,6},{6,3},{8,13},{13,8},{9,1... | collective-permute-start | bytes 786440 | tf_op jit(solution)/shard_map/ppermute | solution.py:856
  278.5 25.1 %collective-permute-start.26 = (bf16[512,512]{1,0:T(8,128)(2,1)S(1)}, bf16[512,512]{1,0:T(8,128)(2,1)S(1)}, u32[]{:S(2)}, u32[]{:S(2)}) collective-permute-start(bf16[512,512]{1,0:T(8,128)(2,1)S(1)} %fusion.44), channel_id=1, source_target_pairs={{0,16},{16,0},{8,24},{24,8},{1,17},{17,1},{9,25},{25,9},{2,18},{18... | collective-permute-start | bytes 1572872 | tf_op jit(solution)/shard_map/ppermute | solution.py:885
  303.8 5.4 %collective-permute-start.27 = (bf16[1024,1024]{1,0:T(8,128)(2,1)}, bf16[1024,1024]{1,0:T(8,128)(2,1)}, u32[]{:S(2)}, u32[]{:S(2)}) collective-permute-start(bf16[1024,1024]{1,0:T(8,128)(2,1)} %fusion.20.part_ref), channel_id=1, source_target_pairs={{0,2},{2,0},{1,3},{3,1},{4,6},{6,4},{5,7},{7,5},{8,10},{10,8},{9,1... | collective-permute-start | bytes 6291464 | tf_op jit(solution)/shard_map/ppermute | solution.py:270
  316.8 3.8 collective-permute-start.31
  320.6 7.5 %collective-permute-start.32 = (f32[2304]{0:T(1024)S(1)}, f32[2304]{0:T(1024)S(1)}, u32[]{:S(2)}, u32[]{:S(2)}) collective-permute-start(f32[2304]{0:T(1024)S(1)} %fusion.65), channel_id=1, source_target_pairs={{0,1},{1,0},{2,3},{3,2},{4,5},{5,4},{6,7},{7,6},{8,9},{9,8},{10,11... | collective-permute-start | bytes 27656 | tf_op jit(solution)/shard_map/ppermute | solution.py:270
  328.1 12.5 %collective-permute-start.33 = (f32[2304]{0:T(1024)S(1)}, f32[2304]{0:T(1024)S(1)}, u32[]{:S(2)}, u32[]{:S(2)}) collective-permute-start(f32[2304]{0:T(1024)S(1)} %maximum_add_fusion.1), channel_id=1, source_target_pairs={{0,8},{8,0},{16,24},{24,16},{1,9},{9,1},{17,25},{25,17},{2,10},{10... | collective-permute-start | bytes 27656 | tf_op jit(solution)/shard_map/ppermute | solution.py:1014
  338.0 29.4 %copy-start.59 = (bf16[512,768]{1,0:T(8,128)(2,1)S(1)}, bf16[512,768]{1,0:T(8,128)(2,1)}, u32[]{:S(2)}) copy-start(bf16[512,768]{1,0:T(8,128)(2,1)} %convolution_convert_fusion.4) | copy-start | bytes 2359300
  338.0 61.8 %collective-permute-start.28 = (bf16[1024,512]{1,0:T(8,128)(2,1)}, bf16[1024,512]{1,0:T(8,128)(2,1)}, u32[]{:S(2)}, u32[]{:S(2)}) collective-permute-start(bf16[1024,512]{1,0:T(8,128)(2,1)} %get-tuple-element.98), channel_id=1, source_target_pairs={{0,2},{2,0},{1,3},{3,1},{4,6},{6,4},{5,7},{7,5},{8,10},{10,8},{9,1... | collective-permute-start | bytes 3145736 | tf_op jit(solution)/shard_map/ppermute | solution.py:270
  338.0 31.9 %collective-permute-start.30 = (bf16[1024,256]{1,0:T(8,128)(2,1)}, bf16[1024,256]{1,0:T(8,128)(2,1)S(1)}, u32[]{:S(2)}, u32[]{:S(2)}) collective-permute-start(bf16[1024,256]{1,0:T(8,128)(2,1)} %get-tuple-element.100), channel_id=1, source_target_pairs={{0,4},{4,0},{1,5},{5,1},{2,6},{6,2},{3,7},{7,3},{8,12},{12,8},{9,1... | collective-permute-start | bytes 1572872 | tf_op jit(solution)/shard_map/ppermute | solution.py:270
  338.6 35.7 %collective-permute-start.38 = (bf16[512,768]{1,0:T(8,128)(2,1)}, bf16[512,768]{1,0:T(8,128)(2,1)S(1)}, u32[]{:S(2)}, u32[]{:S(2)}) collective-permute-start(bf16[512,768]{1,0:T(8,128)(2,1)} %convolution_convert_fusion.2), channel_id=1, source_target_pairs={{0,5},{5,0},{1,4},{4,1},{2,7},{7,2},{3,6},{6,3},{8,13},{13,8},{9,1... | collective-permute-start | bytes 2359304 | tf_op jit(solution)/shard_map/ppermute | solution.py:856
  340.6 4.7 collective-permute-start.34
  342.5 29.3 %copy-start.21 = (f32[1024,256]{1,0:T(8,128)S(1)}, f32[1024,256]{1,0:T(8,128)}, u32[]{:S(2)}) copy-start(f32[1024,256]{1,0:T(8,128)} %get-tuple-element.99) | copy-start | bytes 3145732
  342.5 14.9 %collective-permute-start.35 = (bf16[512,512]{1,0:T(8,128)(2,1)S(1)}, bf16[512,512]{1,0:T(8,128)(2,1)S(1)}, u32[]{:S(2)}, u32[]{:S(2)}) collective-permute-start(bf16[512,512]{1,0:T(8,128)(2,1)S(1)} %dynamic-slice_bitcast_fusion), channel_id=1, source_target_pairs={{0,8},{8,0},{16,24},{24,16},{1,9},{9,1},{17,25},{25,17},{2,10},{10... | collective-permute-start | bytes 1572872 | tf_op jit(solution)/shard_map/ppermute | solution.py:881
  345.4 1.2 collective-permute-start.46
  346.6 20.8 %collective-permute-start.47 = (bf16[512,512]{1,0:T(8,128)(2,1)S(1)}, bf16[512,512]{1,0:T(8,128)(2,1)S(1)}, u32[]{:S(2)}, u32[]{:S(2)}) collective-permute-start(bf16[512,512]{1,0:T(8,128)(2,1)S(1)} %add_convert_fusion.3), channel_id=1, source_target_pairs={{0,8},{8,0},{16,24},{24,16},{1,9},{9,1},{17,25},{25,17},{2,10},{10... | collective-permute-start | bytes 1572872 | tf_op jit(solution)/shard_map/ppermute | solution.py:889
  357.4 18.9 %collective-permute-start.37 = (bf16[512,768]{1,0:T(8,128)(2,1)}, bf16[512,768]{1,0:T(8,128)(2,1)S(1)}, u32[]{:S(2)}, u32[]{:S(2)}) collective-permute-start(bf16[512,768]{1,0:T(8,128)(2,1)} %convolution_convert_fusion.3), channel_id=1, source_target_pairs={{0,1},{1,0},{2,3},{3,2},{4,5},{5,4},{6,7},{7,6},{8,9},{9,8},{10,11... | collective-permute-start | bytes 2359304 | tf_op jit(solution)/shard_map/ppermute | solution.py:270
  367.4 18.9 %collective-permute-start.36 = (bf16[512,768]{1,0:T(8,128)(2,1)S(1)}, bf16[512,768]{1,0:T(8,128)(2,1)S(1)}, u32[]{:S(2)}, u32[]{:S(2)}) collective-permute-start(bf16[512,768]{1,0:T(8,128)(2,1)S(1)} %copy-done.59), channel_id=1, source_target_pairs={{0,4},{4,0},{1,5},{5,1},{2,6},{6,2},{3,7},{7,3},{8,12},{12,8},{9,1... | collective-permute-start | bytes 2359304 | tf_op jit(solution)/shard_map/ppermute | solution.py:270
  370.0 25.0 %collective-permute-start.39 = (bf16[512,512]{1,0:T(8,128)(2,1)S(1)}, bf16[512,512]{1,0:T(8,128)(2,1)S(1)}, u32[]{:S(2)}, u32[]{:S(2)}) collective-permute-start(bf16[512,512]{1,0:T(8,128)(2,1)S(1)} %fusion.43), channel_id=1, source_target_pairs={{0,16},{16,0},{8,24},{24,8},{1,17},{17,1},{9,25},{25,9},{2,18},{18... | collective-permute-start | bytes 1572872 | tf_op jit(solution)/shard_map/ppermute | solution.py:885
  374.3 30.8 %collective-permute-start.48 = (bf16[1024,256]{1,0:T(8,128)(2,1)}, bf16[1024,256]{1,0:T(8,128)(2,1)}, u32[]{:S(2)}, u32[]{:S(2)}) collective-permute-start(bf16[1024,256]{1,0:T(8,128)(2,1)} %slice.251), channel_id=1, source_target_pairs={{0,2},{2,0},{1,3},{3,1},{4,6},{6,4},{5,7},{7,5},{8,10},{10,8},{9,1... | collective-permute-start | bytes 1572872 | tf_op jit(solution)/shard_map/ppermute | solution.py:270
  395.9 27.4 %collective-permute-start.44 = (bf16[512,512]{1,0:T(8,128)(2,1)}, bf16[512,512]{1,0:T(8,128)(2,1)}, u32[]{:S(2)}, u32[]{:S(2)}) collective-permute-start(bf16[512,512]{1,0:T(8,128)(2,1)} %add_convert_fusion.2), channel_id=1, source_target_pairs={{0,8},{8,0},{16,24},{24,16},{1,9},{9,1},{17,25},{25,17},{2,10},{10... | collective-permute-start | bytes 1572872 | tf_op jit(solution)/shard_map/ppermute | solution.py:889
  397.8 22.2 %collective-permute-start.40 = (bf16[256,1024]{0,1:T(8,128)(2,1)}, bf16[256,1024]{0,1:T(8,128)(2,1)}, u32[]{:S(2)}, u32[]{:S(2)}) collective-permute-start(bf16[256,1024]{0,1:T(8,128)(2,1)} %bitcast.49), channel_id=1, source_target_pairs={{0,8},{8,0},{16,24},{24,16},{1,9},{9,1},{17,25},{25,17},{2,10},{10... | collective-permute-start | bytes 1572872 | tf_op jit(solution)/shard_map/ppermute | solution.py:881
  403.4 41.8 %collective-permute-start.29 = (bf16[1024,256]{1,0:T(8,128)(2,1)}, bf16[1024,256]{1,0:T(8,128)(2,1)S(1)}, u32[]{:S(2)}, u32[]{:S(2)}) collective-permute-start(bf16[1024,256]{1,0:T(8,128)(2,1)} %slice.230), channel_id=1, source_target_pairs={{0,4},{4,0},{1,5},{5,1},{2,6},{6,2},{3,7},{7,3},{8,12},{12,8},{9,1... | collective-permute-start | bytes 1572872 | tf_op jit(solution)/shard_map/ppermute | solution.py:270
  421.2 23.9 %collective-permute-start.41 = (bf16[256,1024]{0,1:T(8,128)(2,1)S(1)}, bf16[256,1024]{0,1:T(8,128)(2,1)S(1)}, u32[]{:S(2)}, u32[]{:S(2)}) collective-permute-start(bf16[256,1024]{0,1:T(8,128)(2,1)S(1)} %fusion.42), channel_id=1, source_target_pairs={{0,16},{16,0},{8,24},{24,8},{1,17},{17,1},{9,25},{25,9},{2,18},{18... | collective-permute-start | bytes 1572872 | tf_op jit(solution)/shard_map/ppermute | solution.py:885
  445.2 13.9 %collective-permute-start.42 = (bf16[256,1024]{0,1:T(8,128)(2,1)S(1)}, bf16[256,1024]{0,1:T(8,128)(2,1)S(1)}, u32[]{:S(2)}, u32[]{:S(2)}) collective-permute-start(bf16[256,1024]{0,1:T(8,128)(2,1)S(1)} %add_convert_fusion.1), channel_id=1, source_target_pairs={{0,8},{8,0},{16,24},{24,16},{1,9},{9,1},{17,25},{25,17},{2,10},{10... | collective-permute-start | bytes 1572872 | tf_op jit(solution)/shard_map/ppermute | solution.py:889
  445.4 13.9 %collective-permute-start.45 = (bf16[256,1024]{1,0:T(8,128)(2,1)S(1)}, bf16[256,1024]{1,0:T(8,128)(2,1)S(1)}, u32[]{:S(2)}, u32[]{:S(2)}) collective-permute-start(bf16[256,1024]{1,0:T(8,128)(2,1)S(1)} %pad_maximum_fusion.8), channel_id=1, source_target_pairs={{0,2},{2,0},{1,3},{3,1},{4,6},{6,4},{5,7},{7,5},{8,10},{10,8},{9,1... | collective-permute-start | bytes 1572872 | tf_op jit(solution)/shard_map/ppermute | solution.py:270
  459.2 2.0 collective-permute-start.43
  (54 other events, 446.0 us)
Sparse Core Ops, SparseCore 0:
  35.9 124.1 all-gather.2
  200.7 51.3 reduce-scatter.8
  255.0 63.8 reduce-scatter.6

commit v5 on v4

--- a/solution.py
+++ b/solution.py
@@ -991,18 +991,6 @@
     theirs = swap(theirs, "y")
     grad_inputs = ordered(mine, theirs.astype(FULL), y_at).reshape(2 * length, n)
 
-    up_scattered = after(up_scattered, sums_one)
-    up_part = depth_pair(up_scattered, odd)
-    qkv_got = plane_exchange(*after((qkv_grads[0][1], qkv_grads[1][0], qkv_grads[1][1]), up_scattered))
-    ends_own, ends_other = layer_end(at, after(hiddens, up_scattered), ffn)
-    up_far = depth_far(after(up_part, ends_own))
-    down_total = depth_join(after(down_part, ends_own), odd)
-    kept_two = jnp.concatenate((residual[:, :n], residual[:, 2 * n : 3 * n]), axis=1)
-    bias_two = jnp.concatenate((bias_low[:, :n], bias_low[:, 2 * n : 3 * n]), axis=1)
-    ends = (kept_two + ends_own + swap(ends_other, "core").astype(FULL) + bias_two).astype(LOW)
-    ends_got = swap(ends[:, n:], "y")
-    layer_out = ordered(ends[:, :n], ends_got, y_at).reshape(2 * length, n)
-
     gains = jnp.concatenate((sums_one[:2, :n], sums_two[:2, :n])).reshape(-1)
     gains_y = jnp.concatenate((sums_one[:2, n:], sums_two[:2, n:])).reshape(-1)
     up_bias = bias_sum[:, 0, :].reshape(-1)
@@ -1011,6 +999,19 @@
     up_bias = up_bias + got[4 * n :]
     near = jnp.concatenate((gains, jnp.sum(cotangent, axis=0, dtype=FULL), up_bias[:each]))
     near = near + swap(jnp.concatenate((near[: 5 * n], up_bias[each:])), "col")
+    up_scattered = after(up_scattered, near)
+    up_part = depth_pair(up_scattered, odd)
+    qkv_got = plane_exchange(*after((qkv_grads[0][1], qkv_grads[1][0], qkv_grads[1][1]), up_scattered))
+    up_far = depth_far(up_part)
+    ends_own, ends_other = layer_end(at, after(hiddens, up_part), ffn)
+    down_total = depth_join(after(down_part, up_far), odd)
+    kept_two = jnp.concatenate((residual[:, :n], residual[:, 2 * n : 3 * n]), axis=1)
+    bias_two = jnp.concatenate((bias_low[:, :n], bias_low[:, 2 * n : 3 * n]), axis=1)
+    ends = (kept_two + ends_own + swap(ends_other, "core").astype(FULL) + bias_two).astype(LOW)
+    ends_got = swap(ends[:, n:], "y")
+    layer_out = ordered(ends[:, :n], ends_got, y_at).reshape(2 * length, n)
+
+    near = after(near, up_part)
     near = near + lax.ppermute(near, "dp", [(0, 1), (1, 0), (2, 3), (3, 2)])
     near = near + lax.ppermute(near, "dp", [(0, 2), (2, 0), (1, 3), (3, 1)])
     gains = near[: 5 * n].reshape(5, n)
@@ -1030,7 +1031,7 @@
     four = jnp.concatenate(
         (plane_sum(after(qkv_grads[0][0], up_part), qkv_got), plane_sum(out_grads[0][0], out_got)), axis=1
     )
-    four = depth_pair(after(four, up_far, near), odd)
+    four = depth_pair(after(four, up_far, near, ends_own), odd)
     up_total = depth_join(up_far, odd)
     four = depth_far(after(four, theirs, ends))
     four = depth_join(after(four, ends_got), odd)

time: 479 us -> 474 us (0.990)
    ppermute x3, waiting for transfers between devices: 44.7 us -> 20.3 us  [depth_far(): return add_low(part, lax.ppermute(part, 'dp', FAR))]
    ppermute x3, waiting for transfers between devices: 21.4 us -> 41.4 us  [depth_join(): lax.ppermute(part, 'dp', PAIRS)]
    ppermute x3, waiting for transfers between devices: 26.2 us -> 13.2 us  [depth_pair(): lax.ppermute(pick(halves, 1 - odd), 'dp', PAIRS)]
    ppermute x33, waiting for transfers between devices: 38.3 us -> 48 us  [swap(): return lax.ppermute(array, axis, SWAP)]
    ppermute x1, waiting for transfers between devices: 2.62 us -> 9.97 us  [fast_body(): near = near + lax.ppermute(near, 'dp', [(0, 2), (2, 0), (1, 3), (3, 1)])]
    unnamed x143 -> x147, local copies, waits for them, and re-layouts: 13.8 us -> 16.6 us
  transfers between devices with their start and end apart: 52 -> 52, of which waited for: 22 -> 18; matrix products, arithmetic and copies ran while one was open for 17% -> 18% of each run, Pallas kernels for 22% -> 22%
where the time goes in v5:
time: 474 us; the launch traced here: 468 us
  waiting for transfers between devices  157 us (33%)
  Pallas kernels  139 us (29%)
  starting transfers between devices  58.4 us (12%)
  local copies, waits for them, and re-layouts  35.6 us (8%)
  other arithmetic  32.1 us (7%)
  matrix products  31.1 us (7%)
  between operations  15.3 us (3%)
    ppermute x33, waiting for transfers between devices, swap(): return lax.ppermute(array, axis, SWAP)  48 us
    ppermute x3, waiting for transfers between devices, depth_join(): lax.ppermute(part, 'dp', PAIRS)  41.4 us
    ppermute x33, starting transfers between devices, swap(): return lax.ppermute(array, axis, SWAP)  29.8 us
    pallas_call x1, Pallas kernels, feed_forward(): pl.pallas_call(feed_forward_kernel, out_shape=(jax.ShapeDtypeStruct((leng...  27.1 us
    pallas_call x2, Pallas kernels, attend_backward(): pl.pallas_call(attend_backward_kernel, out_shape=jax.ShapeDtypeStruct((le...  26.6 us
    pallas_call x2, Pallas kernels, attend_forward(): pl.pallas_call(attend_forward_kernel, out_shape=(jax.ShapeDtypeStruct((le...  25 us
    ppermute x4, waiting for transfers between devices, swap_across(): return lax.ppermute(array, ('y', 'col'), [(0, 3), (3, 0), (1, 2), (2, 1)])  23.7 us
    ppermute x4, starting transfers between devices, swap_across(): return lax.ppermute(array, ('y', 'col'), [(0, 3), (3, 0), (1, 2), (2, 1)])  20.9 us
  transfers between devices with their start and end apart: 52, of which 18 were waited for; matrix products, arithmetic and copies ran while one was open for 18% of the time, Pallas kernels for 22%

profile of v5, /device:TPU:0, one launch (start us, length us, event | category | flops | bytes accessed | tf_op | source)
XLA Modules:
  0.0 468.3 jit_solution(3738376872769396843)
XLA Ops:
  13.2 2.9 collective-permute-start.8
  16.1 1.5 collective-permute-start.10
  17.7 1.5 fusion.16
  19.2 15.0 %collective-permute-done.8 = bf16[512,768]{1,0:T(8,128)(2,1)} collective-permute-done((bf16[512,768]{1,0:T(8,128)(2,1)}, bf16[512,768]{1,0:T(8,128)(2,1)}, u32[]{:S(2)}, u32[]{:S(2)}) %collective-permute-start.8) | collective-permute-done | bytes 786464 | tf_op jit(solution)/shard_map/ppermute | solution.py:270
  38.5 3.1 collective-permute-start.6
  49.0 13.3 %collective-permute-start.5 = (bf16[512,768]{1,0:T(8,128)(2,1)}, bf16[512,768]{1,0:T(8,128)(2,1)S(1)}, u32[]{:S(2)}, u32[]{:S(2)}) collective-permute-start(bf16[512,768]{1,0:T(8,128)(2,1)} %pad_maximum_fusion.7), channel_id=1, source_target_pairs={{0,5},{5,0},{1,4},{4,1},{2,7},{7,2},{3,6},{6,3},{8,13},{13,8},{9,1... | collective-permute-start | bytes 2359304 | tf_op jit(solution)/shard_map/ppermute | solution.py:856
  63.9 2.5 collective-permute-start.7
  66.4 1.6 pad_maximum_fusion.3
  69.8 18.2 %collective-permute-done.5 = bf16[512,768]{1,0:T(8,128)(2,1)S(1)} collective-permute-done((bf16[512,768]{1,0:T(8,128)(2,1)}, bf16[512,768]{1,0:T(8,128)(2,1)S(1)}, u32[]{:S(2)}, u32[]{:S(2)}) %collective-permute-start.5) | collective-permute-done | bytes 786464 | tf_op jit(solution)/shard_map/ppermute | solution.py:856
  89.7 5.0 %first_norm.1 = (bf16[1024,512]{1,0:T(8,128)(2,1)}, bf16[1024,512]{1,0:T(8,128)(2,1)}) custom-call(bf16[1024,256]{1,0:T(8,128)(2,1)} %copy-done.2, bf16[1024,256]{1,0:T(8,128)(2,1)} %copy-done.3, bf16[1024,256]{1,0:T(8,128)(2,1)} %copy-done.4, bf16[1024,256]{1,0:T(8,128)(2,1)} %copy-done.5, f32[1,1024]{1,0:T(1,128)} %get-tuple-element.221.gain_ref, ...), custom_call_target="tpu_custom_call" | custom-call | flops 5242880 | bytes 4194304 | tf_op jit(solution)/shard_map/first_norm/pallas_call | solution.py:536
  94.7 1.5 constant_dynamic-update-slice_fusion.1
  98.6 2.6 collective-permute-start.16
  101.2 4.1 convolution_convert_fusion.1.q_ref.k_ref.v_ref
  105.9 12.4 %attend_forward.2 = (bf16[1024,256]{1,0:T(8,128)(2,1)}, bf16[4,1024,128]{2,1,0:T(8,128)(2,1)}) custom-call(s32[2,4]{1,0:T(2,128)} %pad_add_fusion.1.where_ref, bf16[1024,768]{1,0:T(8,128)(2,1)} %convolution_convert_fusion.1.q_ref.k_ref.v_ref, bf16[1024,768]{1,0:T(8,128)(2,1)} %convolution_convert_fusion.1.q_ref.k_ref.v_ref, ...), custom_call_target="tpu_custom_call" | custom-call | flops 1073741824 | bytes 12582912 | tf_op jit(solution)/shard_map/attend_forward/pallas_call | solution.py:377
  119.5 5.5 %collective-permute-done.16 = bf16[256,512]{1,0:T(8,128)(2,1)} collective-permute-done((bf16[256,512]{1,0:T(8,128)(2,1)S(1)}, bf16[256,512]{1,0:T(8,128)(2,1)}, u32[]{:S(2)}, u32[]{:S(2)}) %collective-permute-start.16) | collective-permute-done | bytes 262176 | tf_op jit(solution)/shard_map/ppermute | solution.py:856
  126.3 3.0 convolution_convert_fusion.q_ref.k_ref.v_ref
  129.2 12.6 %attend_forward.3 = (bf16[1024,256]{1,0:T(8,128)(2,1)}, bf16[4,1024,128]{2,1,0:T(8,128)(2,1)}) custom-call(s32[2,4]{1,0:T(2,128)} %pad_add_fusion.1.where_ref, bf16[1024,768]{1,0:T(8,128)(2,1)} %convolution_convert_fusion.q_ref.k_ref.v_ref, bf16[1024,768]{1,0:T(8,128)(2,1)} %convolution_convert_fusion.q_ref.k_ref.v_ref, ...), custom_call_target="tpu_custom_call" | custom-call | flops 1073741824 | bytes 12582912 | tf_op jit(solution)/shard_map/attend_forward/pallas_call | solution.py:377
  144.3 1.5 pad_maximum_fusion.1.c_ref.cots_ref
  147.6 4.8 %mix_heads.1.part_ref = bf16[1024,1024]{1,0:T(8,128)(2,1)} custom-call(bf16[1024,256]{1,0:T(8,128)(2,1)} %get-tuple-element.69.h0.heads_ref, bf16[1024,256]{1,0:T(8,128)(2,1)} %get-tuple-element.75.h1.heads_ref, bf16[256,1024]{1,0:T(8,128)(2,1)} %copy-done.14, bf16[256,1024]{1,0:T(8,128)(2,1)} %copy-done.12), custom_call_target="tpu_custom_call" | custom-call | flops 1073741824 | bytes 5242880 | tf_op jit(solution)/shard_map/mix_heads/pallas_call | solution.py:657
  154.1 2.8 collective-permute-done.20.got_ref
  158.2 6.3 %second_norm.1 = (f32[1024,1024]{1,0:T(8,128)}, bf16[2,1024,512]{2,1,0:T(8,128)(2,1)}) custom-call(bf16[1024,256]{1,0:T(8,128)(2,1)} %copy-done.2, bf16[1024,256]{1,0:T(8,128)(2,1)} %copy-done.3, bf16[1024,256]{1,0:T(8,128)(2,1)} %copy-done.4, bf16[1024,256]{1,0:T(8,128)(2,1)} %copy-done.5, bf16[1024,1024]{1,0:T(8,128)(2,1)} %mix_heads.1.part_ref, ...), custom_call_target="tpu_custom_call" | custom-call | flops 7864320 | bytes 12582912 | tf_op jit(solution)/shard_map/second_norm/pallas_call | solution.py:563
  164.5 27.1 %feed_forward.1 = (bf16[1024,1024]{1,0:T(8,128)(2,1)}, bf16[2,1024,1024]{2,1,0:T(8,128)(2,1)}, bf16[2,1024,1024]{2,1,0:T(8,128)(2,1)}, f32[8,8,256]{2,1,0:T(8,128)}) custom-call(s32[2]{0:T(128)} %pad_add_fusion.2.at_ref, bf16[2,1024,512]{2,1,0:T(8,128)(2,1)} %get-tuple-element.78.s_ref, bf16[2,1024,512]{2,1,0:T(8,128)(2,1)} %pad_maximum_fusion.1.c_ref.cots_ref, ...), custom_call_target="tpu_custom_call" | custom-call | flops 12884901888 | bytes 29360128 | tf_op jit(solution)/shard_map/feed_forward/pallas_call | solution.py:728
  191.6 9.2 %down_grads.1 = bf16[2,2,1024,512]{3,2,1,0:T(8,128)(2,1)} custom-call(s32[2]{0:T(128)} %pad_add_fusion.2.at_ref, bf16[2,1024,1024]{2,1,0:T(8,128)(2,1)} %get-tuple-element.98.hidden_ref.h0.h1, bf16[2,1024,512]{2,1,0:T(8,128)(2,1)} %pad_maximum_fusion.1.c_ref.cots_ref), custom_call_target="tpu_custom_call" | custom-call | flops 4294967296 | bytes 8388608 | tf_op jit(solution)/shard_map/down_grads/pallas_call | solution.py:792
  200.9 1.5 copy-done.7
  202.8 10.5 %up_grads.1 = bf16[4,1024,512]{2,1,0:T(8,128)(2,1)} custom-call(s32[2]{0:T(128)} %pad_add_fusion.2.at_ref, bf16[2,1024,512]{2,1,0:T(8,128)(2,1)} %get-tuple-element.78.s_ref, bf16[2,1024,1024]{2,1,0:T(8,128)(2,1)} %get-tuple-element.82.grad_ref), custom_call_target="tpu_custom_call" | custom-call | flops 4294967296 | bytes 8388608 | tf_op jit(solution)/shard_map/up_grads/pallas_call | solution.py:765
  213.3 8.1 %second_norm_back.1 = (f32[1024,256]{1,0:T(8,128)}, f32[1024,256]{1,0:T(8,128)}, bf16[1024,1024]{1,0:T(8,128)(2,1)}, f32[8,512]{1,0:T(8,128)}) custom-call(f32[1024,1024]{1,0:T(8,128)} %get-tuple-element.77.residual_ref, bf16[1024,1024]{1,0:T(8,128)(2,1)} %get-tuple-element.84.part_ref, bf16[1024,1024]{1,0:T(8,128)(2,1)} %collective-permute-done.21.got_ref, ...), custom_call_target="tpu_custom_call" | custom-call | flops 15728640 | bytes 16777216 | tf_op jit(solution)/shard_map/second_norm_back/pallas_call | solution.py:611
  221.4 4.0 select_convert_fusion.1.grads_ref
  225.4 13.1 %attend_backward.2 = bf16[1024,768]{1,0:T(8,128)(2,1)} custom-call(s32[2,4]{1,0:T(2,128)} %pad_add_fusion.1.where_ref, bf16[4,1024,128]{2,1,0:T(8,128)(2,1)} %get-tuple-element.83.kept_ref, bf16[1024,768]{1,0:T(8,128)(2,1)} %convolution_convert_fusion.1.q_ref.k_ref.v_ref, bf16[1024,768]{1,0:T(8,128)(2,1)} %convolution_convert_fusion.1.q_ref.k_ref.v_ref, ...), custom_call_target="tpu_custom_call" | custom-call | flops 2684354560 | bytes 15728640 | tf_op jit(solution)/shard_map/attend_backward/pallas_call | solution.py:467
  238.6 13.4 %attend_backward.3 = bf16[1024,768]{1,0:T(8,128)(2,1)} custom-call(s32[2,4]{1,0:T(2,128)} %pad_add_fusion.1.where_ref, bf16[4,1024,128]{2,1,0:T(8,128)(2,1)} %get-tuple-element.87.kept_ref, bf16[1024,768]{1,0:T(8,128)(2,1)} %convolution_convert_fusion.q_ref.k_ref.v_ref, bf16[1024,768]{1,0:T(8,128)(2,1)} %convolution_convert_fusion.q_ref.k_ref.v_ref, ...), custom_call_target="tpu_custom_call" | custom-call | flops 2684354560 | bytes 15728640 | tf_op jit(solution)/shard_map/attend_backward/pallas_call | solution.py:467
  252.0 3.6 convolution_convert_fusion.5
  255.6 1.9 convolution_convert_fusion.4
  257.5 1.9 convolution_convert_fusion.3
  259.5 1.9 convolution_convert_fusion.2
  262.6 4.9 %collective-permute-start.22 = (bf16[512,256]{1,0:T(8,128)(2,1)}, bf16[512,256]{1,0:T(8,128)(2,1)}, u32[]{:S(2)}, u32[]{:S(2)}) collective-permute-start(bf16[512,256]{1,0:T(8,128)(2,1)} %convolution_convert_fusion.9), channel_id=1, source_target_pairs={{0,4},{4,0},{1,5},{5,1},{2,6},{6,2},{3,7},{7,3},{8,12},{12,8},{9,1... | collective-permute-start | bytes 786440 | tf_op jit(solution)/shard_map/ppermute | solution.py:270
  269.7 1.9 convolution_convert_fusion.8
  272.1 3.5 collective-permute-start.24
  275.7 6.9 %collective-permute-done.25 = bf16[512,512]{1,0:T(8,128)(2,1)S(1)} collective-permute-done((bf16[512,512]{1,0:T(8,128)(2,1)S(1)}, bf16[512,512]{1,0:T(8,128)(2,1)S(1)}, u32[]{:S(2)}, u32[]{:S(2)}) %collective-permute-start.25) | collective-permute-done | bytes 524320 | tf_op jit(solution)/shard_map/ppermute | solution.py:881
  282.8 4.7 fusion.20.part_ref
  287.5 20.3 %collective-permute-done.26 = bf16[512,512]{1,0:T(8,128)(2,1)S(1)} collective-permute-done((bf16[512,512]{1,0:T(8,128)(2,1)S(1)}, bf16[512,512]{1,0:T(8,128)(2,1)S(1)}, u32[]{:S(2)}, u32[]{:S(2)}) %collective-permute-start.26) | collective-permute-done | bytes 524320 | tf_op jit(solution)/shard_map/ppermute | solution.py:885
  312.8 1.7 collective-permute-done.27.got_ref
  314.5 6.8 %first_norm_back.1 = (f32[1024,256]{1,0:T(8,128)}, bf16[1024,256]{1,0:T(8,128)(2,1)}, f32[8,512]{1,0:T(8,128)}) custom-call(bf16[1024,256]{1,0:T(8,128)(2,1)} %copy-done.2, bf16[1024,256]{1,0:T(8,128)(2,1)} %copy-done.3, bf16[1024,256]{1,0:T(8,128)(2,1)} %copy-done.4, bf16[1024,256]{1,0:T(8,128)(2,1)} %copy-done.5, bf16[1024,1024]{1,0:T(8,128)(2,1)} %copy-done.11, ...), custom_call_target="tpu_custom_call" | custom-call | flops 15728640 | bytes 10485760 | tf_op jit(solution)/shard_map/first_norm_back/pallas_call | solution.py:634
  322.1 2.5 collective-permute-start.28
  324.6 1.7 collective-permute-done.28
  326.4 1.7 fusion.76
  328.2 2.1 collective-permute-start.33
  331.6 2.5 fusion.50
  335.5 1.9 collective-permute-start.37
  337.6 22.5 %collective-permute-done.33 = bf16[1024,256]{1,0:T(8,128)(2,1)S(1)} collective-permute-done((bf16[1024,256]{1,0:T(8,128)(2,1)}, bf16[1024,256]{1,0:T(8,128)(2,1)S(1)}, u32[]{:S(2)}, u32[]{:S(2)}) %collective-permute-start.33) | collective-permute-done | bytes 524320 | tf_op jit(solution)/shard_map/ppermute | solution.py:270
  360.5 1.5 pad_maximum_fusion.2
  362.0 3.3 collective-permute-start.39
  365.6 9.6 %layer_end.1 = (f32[1024,512]{1,0:T(8,128)}, bf16[1024,512]{1,0:T(8,128)(2,1)}) custom-call(s32[2]{0:T(128)} %pad_add_fusion.2.at_ref, bf16[2,1024,1024]{2,1,0:T(8,128)(2,1)} %get-tuple-element.98.hidden_ref.h0.h1, bf16[2,1024,1024]{2,1,0:T(8,128)(2,1)} %get-tuple-element.98.hidden_ref.h0.h1, bf16[4,2048,512]{2,1,0:T(8,128)(2,1)} %bitcast.144, ...), custom_call_target="tpu_custom_call" | custom-call | flops 4294967296 | bytes 10485760 | tf_op jit(solution)/shard_map/layer_end/pallas_call | solution.py:828
  375.2 10.0 %collective-permute-done.35 = f32[2304]{0:T(1024)S(1)} collective-permute-done((f32[2304]{0:T(1024)S(1)}, f32[2304]{0:T(1024)S(1)}, u32[]{:S(2)}, u32[]{:S(2)}) %collective-permute-start.35) | collective-permute-done | bytes 9248 | tf_op jit(solution)/shard_map/ppermute | solution.py:1016
  386.4 2.0 add_convert_fusion
  390.8 2.0 copy.63
  393.5 2.0 collective-permute-start.44
  395.5 2.0 copy.69
  397.6 2.5 fusion.19
  400.1 1.5 collective-permute-start.32
  401.6 6.4 %collective-permute-done.40 = bf16[256,1024]{0,1:T(8,128)(2,1)} collective-permute-done((bf16[256,1024]{0,1:T(8,128)(2,1)}, bf16[256,1024]{0,1:T(8,128)(2,1)}, u32[]{:S(2)}, u32[]{:S(2)}) %collective-permute-start.40) | collective-permute-done | bytes 524320 | tf_op jit(solution)/shard_map/ppermute | solution.py:881
  409.3 21.1 %collective-permute-done.44 = bf16[512,512]{1,0:T(8,128)(2,1)} collective-permute-done((bf16[512,512]{1,0:T(8,128)(2,1)S(1)}, bf16[512,512]{1,0:T(8,128)(2,1)}, u32[]{:S(2)}, u32[]{:S(2)}) %collective-permute-start.44) | collective-permute-done | bytes 524320 | tf_op jit(solution)/shard_map/ppermute | solution.py:889
  431.7 8.9 %collective-permute-done.47 = bf16[512,512]{1,0:T(8,128)(2,1)S(1)} collective-permute-done((bf16[512,512]{1,0:T(8,128)(2,1)S(1)}, bf16[512,512]{1,0:T(8,128)(2,1)S(1)}, u32[]{:S(2)}, u32[]{:S(2)}) %collective-permute-start.47) | collective-permute-done | bytes 524320 | tf_op jit(solution)/shard_map/ppermute | solution.py:889
  442.6 1.6 maximum_convert_fusion
  444.2 11.3 %collective-permute-done.42 = bf16[256,1024]{0,1:T(8,128)(2,1)S(1)} collective-permute-done((bf16[256,1024]{0,1:T(8,128)(2,1)S(1)}, bf16[256,1024]{0,1:T(8,128)(2,1)S(1)}, u32[]{:S(2)}, u32[]{:S(2)}) %collective-permute-start.42) | collective-permute-done | bytes 524320 | tf_op jit(solution)/shard_map/ppermute | solution.py:889
  455.7 1.5 maximum_convert_fusion.1
  (332 shorter events, 62.3 us)
Async XLA Ops:
  7.2 34.4 %copy-start = (s32[8,16,3]{1,0,2:T(8,128)S(1)}, s32[8,16,3]{1,0,2:T(8,128)}, u32[]{:S(2)}) copy-start(s32[8,16,3]{1,0,2:T(8,128)} %param.31) | copy-start | bytes 4612
  7.2 157.3 %all-gather.3.cloned.1.call-start = ((), (), s32[]{:S(2)}) async-start(), calls=%async_computation.2 | async-start | bytes 10485760 | tf_op jit(solution)/shard_map/all_gather | solution.py:923
  9.5 1.9 collective-permute-start.4
  12.5 5.1 %collective-permute-start.11 = (bf16[256,1024]{1,0:T(8,128)(2,1)S(1)}, bf16[256,1024]{1,0:T(8,128)(2,1)S(1)}, u32[]{:S(2)}, u32[]{:S(2)}) collective-permute-start(bf16[256,1024]{1,0:T(8,128)(2,1)S(1)} %get-tuple-element.205), channel_id=1, source_target_pairs={{0,2},{2,0},{1,3},{3,1},{4,6},{6,4},{5,7},{7,5},{8,10},{10,8},{9,1... | collective-permute-start | bytes 1572872 | tf_op jit(solution)/shard_map/ppermute | solution.py:270
  13.0 4.6 collective-permute-start.12
  13.2 21.0 %collective-permute-start.8 = (bf16[512,768]{1,0:T(8,128)(2,1)}, bf16[512,768]{1,0:T(8,128)(2,1)}, u32[]{:S(2)}, u32[]{:S(2)}) collective-permute-start(bf16[512,768]{1,0:T(8,128)(2,1)} %pad_maximum_fusion.7), channel_id=1, source_target_pairs={{0,4},{4,0},{1,5},{5,1},{2,6},{6,2},{3,7},{7,3},{8,12},{12,8},{9,1... | collective-permute-start | bytes 2359304 | tf_op jit(solution)/shard_map/ppermute | solution.py:270
  16.1 19.5 %collective-permute-start.10 = (bf16[512,768]{1,0:T(8,128)(2,1)}, bf16[512,768]{1,0:T(8,128)(2,1)S(1)}, u32[]{:S(2)}, u32[]{:S(2)}) collective-permute-start(bf16[512,768]{1,0:T(8,128)(2,1)} %pad_maximum_fusion.7), channel_id=1, source_target_pairs={{0,1},{1,0},{2,3},{3,2},{4,5},{5,4},{6,7},{7,6},{8,9},{9,8},{10,11... | collective-permute-start | bytes 2359304 | tf_op jit(solution)/shard_map/ppermute | solution.py:270
  19.2 22.6 %copy-start.51 = (f32[2048]{0:T(1024)S(1)}, f32[2048]{0:T(1024)}, u32[]{:S(2)}) copy-start(f32[2048]{0:T(1024)} %param.27) | copy-start | bytes 24580
  19.2 24.1 %copy-start.62 = (s32[2]{0:T(128)S(1)}, s32[2]{0:T(128)}, u32[]{:S(2)}) copy-start(s32[2]{0:T(128)} %param.32) | copy-start | bytes 28
  35.7 231.9 %reduce-scatter.9.cloned.1.call-start = ((), (), s32[]{:S(2)}) async-start(), calls=%async_computation.4 | async-start | bytes 5242880
  37.4 32.4 %collective-permute-start = (bf16[1024,256]{1,0:T(8,128)(2,1)S(1)}, bf16[1024,256]{1,0:T(8,128)(2,1)S(1)}, u32[]{:S(2)}, u32[]{:S(2)}) collective-permute-start(bf16[1024,256]{1,0:T(8,128)(2,1)S(1)} %get-tuple-element.63.x0), channel_id=1, source_target_pairs={{0,2},{2,0},{1,3},{3,1},{4,6},{6,4},{5,7},{7,5},{8,10},{10,8},{9,1... | collective-permute-start | bytes 1572872 | tf_op jit(solution)/shard_map/ppermute | solution.py:270
  37.4 25.4 %collective-permute-start.1 = (bf16[1024,256]{1,0:T(8,128)(2,1)}, bf16[1024,256]{1,0:T(8,128)(2,1)S(1)}, u32[]{:S(2)}, u32[]{:S(2)}) collective-permute-start(bf16[1024,256]{1,0:T(8,128)(2,1)} %get-tuple-element.206), channel_id=1, source_target_pairs={{0,4},{4,0},{1,5},{5,1},{2,6},{6,2},{3,7},{7,3},{8,12},{12,8},{9,1... | collective-permute-start | bytes 1572872 | tf_op jit(solution)/shard_map/ppermute | solution.py:270
  37.8 5.6 %collective-permute-start.3 = (s32[1,1024]{1,0:T(1,128)S(1)}, s32[1,1024]{1,0:T(1,128)S(1)}, u32[]{:S(2)}, u32[]{:S(2)}) collective-permute-start(s32[1,1024]{1,0:T(1,128)S(1)} %copy-done.61), channel_id=1, source_target_pairs={{0,0},{4,1},{1,2},{5,3},{2,4},{6,5},{3,6},{7,7},{8,8},{12,9},{9,10... | collective-permute-start | bytes 12296 | tf_op jit(solution)/shard_map/ppermute | solution.py:942
  38.5 24.7 %copy-start.43 = (f32[5,256]{1,0:T(8,128)}, f32[5,256]{1,0:T(8,128)S(1)}, u32[]{:S(2)}) copy-start(f32[5,256]{1,0:T(8,128)S(1)} %stack.107) | copy-start | bytes 15364
  38.5 24.7 %collective-permute-start.6 = (f32[5,256]{1,0:T(8,128)S(1)}, f32[5,256]{1,0:T(8,128)S(1)}, u32[]{:S(2)}, u32[]{:S(2)}) collective-permute-start(f32[5,256]{1,0:T(8,128)S(1)} %stack.107), channel_id=1, source_target_pairs={{0,2},{2,0},{1,3},{3,1},{4,6},{6,4},{5,7},{7,5},{8,10},{10,8},{9,1... | collective-permute-start | bytes 15368 | tf_op jit(solution)/shard_map/ppermute | solution.py:270
  41.9 5.2 %collective-permute-start.9 = (f32[1216]{0:T(1024)S(1)}, f32[1216]{0:T(1024)S(1)}, u32[]{:S(2)}, u32[]{:S(2)}) collective-permute-start(f32[1216]{0:T(1024)S(1)} %pad_maximum_fusion.15), channel_id=1, source_target_pairs={{0,1},{1,0},{2,3},{3,2},{4,5},{5,4},{6,7},{7,6},{8,9},{9,8},{10,11... | collective-permute-start | bytes 14600 | tf_op jit(solution)/shard_map/ppermute | solution.py:270
  49.0 39.0 %collective-permute-start.5 = (bf16[512,768]{1,0:T(8,128)(2,1)}, bf16[512,768]{1,0:T(8,128)(2,1)S(1)}, u32[]{:S(2)}, u32[]{:S(2)}) collective-permute-start(bf16[512,768]{1,0:T(8,128)(2,1)} %pad_maximum_fusion.7), channel_id=1, source_target_pairs={{0,5},{5,0},{1,4},{4,1},{2,7},{7,2},{3,6},{6,3},{8,13},{13,8},{9,1... | collective-permute-start | bytes 2359304 | tf_op jit(solution)/shard_map/ppermute | solution.py:856
  62.8 7.0 %collective-permute-start.2 = (bf16[1024,256]{1,0:T(8,128)(2,1)S(1)}, bf16[1024,256]{1,0:T(8,128)(2,1)S(1)}, u32[]{:S(2)}, u32[]{:S(2)}) collective-permute-start(bf16[1024,256]{1,0:T(8,128)(2,1)S(1)} %collective-permute-done.1.x2), channel_id=1, source_target_pairs={{0,2},{2,0},{1,3},{3,1},{4,6},{6,4},{5,7},{7,5},{8,10},{10,8},{9,1... | collective-permute-start | bytes 1572872 | tf_op jit(solution)/shard_map/ppermute | solution.py:270
  63.9 24.2 %copy-start.40 = (bf16[512,256]{1,0:T(8,128)(2,1)S(1)}, bf16[512,256]{1,0:T(8,128)(2,1)}, u32[]{:S(2)}) copy-start(bf16[512,256]{1,0:T(8,128)(2,1)} %param.23) | copy-start | bytes 786436
  63.9 24.3 %copy-start.6 = (bf16[2048,256]{1,0:T(8,128)(2,1)S(1)}, bf16[2048,256]{1,0:T(8,128)(2,1)}, u32[]{:S(2)}) copy-start(bf16[2048,256]{1,0:T(8,128)(2,1)} %param.33) | copy-start | bytes 3145732
  63.9 5.3 %collective-permute-start.7 = (f32[5,512]{1,0:T(8,128)S(1)}, f32[5,512]{1,0:T(8,128)S(1)}, u32[]{:S(2)}, u32[]{:S(2)}) collective-permute-start(f32[5,512]{1,0:T(8,128)S(1)} %pad_maximum_fusion.12), channel_id=1, source_target_pairs={{0,4},{4,0},{1,5},{5,1},{2,6},{6,2},{3,7},{7,3},{8,12},{12,8},{9,1... | collective-permute-start | bytes 30728 | tf_op jit(solution)/shard_map/ppermute | solution.py:270
  69.2 20.4 %copy-start.47 = (f32[5,512]{1,0:T(8,128)}, f32[5,512]{1,0:T(8,128)S(1)}, u32[]{:S(2)}) copy-start(f32[5,512]{1,0:T(8,128)S(1)} %collective-permute-done.7) | copy-start | bytes 30724
  88.1 8.3 %collective-permute-start.13 = (bf16[256,256]{1,0:T(8,128)(2,1)S(1)}, bf16[256,256]{1,0:T(8,128)(2,1)S(1)}, u32[]{:S(2)}, u32[]{:S(2)}) collective-permute-start(bf16[256,256]{1,0:T(8,128)(2,1)S(1)} %get-tuple-element.209), channel_id=1, source_target_pairs={{0,2},{2,0},{1,3},{3,1},{4,6},{6,4},{5,7},{7,5},{8,10},{10,8},{9,1... | collective-permute-start | bytes 393224 | tf_op jit(solution)/shard_map/ppermute | solution.py:270
  89.1 36.9 %collective-permute-start.17 = (bf16[1024,256]{1,0:T(8,128)(2,1)}, bf16[1024,256]{1,0:T(8,128)(2,1)}, u32[]{:S(2)}, u32[]{:S(2)}) collective-permute-start(bf16[1024,256]{1,0:T(8,128)(2,1)} %get-tuple-element.201), channel_id=1, source_target_pairs={{0,4},{4,0},{1,5},{5,1},{2,6},{6,2},{3,7},{7,3},{8,12},{12,8},{9,1... | collective-permute-start | bytes 1572872 | tf_op jit(solution)/shard_map/ppermute | solution.py:270
  89.6 52.3 %collective-permute-start.18 = (bf16[1024,256]{1,0:T(8,128)(2,1)S(1)}, bf16[1024,256]{1,0:T(8,128)(2,1)}, u32[]{:S(2)}, u32[]{:S(2)}) collective-permute-start(bf16[1024,256]{1,0:T(8,128)(2,1)S(1)} %get-tuple-element.200), channel_id=1, source_target_pairs={{0,2},{2,0},{1,3},{3,1},{4,6},{6,4},{5,7},{7,5},{8,10},{10,8},{9,1... | collective-permute-start | bytes 1572872 | tf_op jit(solution)/shard_map/ppermute | solution.py:270
  98.1 20.3 %collective-permute-start.15 = (bf16[256,512]{1,0:T(8,128)(2,1)S(1)}, bf16[256,512]{1,0:T(8,128)(2,1)}, u32[]{:S(2)}, u32[]{:S(2)}) collective-permute-start(bf16[256,512]{1,0:T(8,128)(2,1)S(1)} %pad_maximum_fusion.11), channel_id=1, source_target_pairs={{0,1},{1,0},{2,3},{3,2},{4,5},{5,4},{6,7},{7,6},{8,9},{9,8},{10,11... | collective-permute-start | bytes 786440 | tf_op jit(solution)/shard_map/ppermute | solution.py:270
  98.6 26.4 %collective-permute-start.16 = (bf16[256,512]{1,0:T(8,128)(2,1)S(1)}, bf16[256,512]{1,0:T(8,128)(2,1)}, u32[]{:S(2)}, u32[]{:S(2)}) collective-permute-start(bf16[256,512]{1,0:T(8,128)(2,1)S(1)} %pad_maximum_fusion.11), channel_id=1, source_target_pairs={{0,5},{5,0},{1,4},{4,1},{2,7},{7,2},{3,6},{6,3},{8,13},{13,8},{9,1... | collective-permute-start | bytes 786440 | tf_op jit(solution)/shard_map/ppermute | solution.py:856
  105.3 20.7 %collective-permute-start.14 = (bf16[256,512]{1,0:T(8,128)(2,1)S(1)}, bf16[256,512]{1,0:T(8,128)(2,1)}, u32[]{:S(2)}, u32[]{:S(2)}) collective-permute-start(bf16[256,512]{1,0:T(8,128)(2,1)S(1)} %pad_maximum_fusion.11), channel_id=1, source_target_pairs={{0,4},{4,0},{1,5},{5,1},{2,6},{6,2},{3,7},{7,3},{8,12},{12,8},{9,1... | collective-permute-start | bytes 786440 | tf_op jit(solution)/shard_map/ppermute | solution.py:270
  126.0 17.0 %collective-permute-start.19 = (bf16[1024,256]{1,0:T(8,128)(2,1)}, bf16[1024,256]{1,0:T(8,128)(2,1)}, u32[]{:S(2)}, u32[]{:S(2)}) collective-permute-start(bf16[1024,256]{1,0:T(8,128)(2,1)} %collective-permute-done.17), channel_id=1, source_target_pairs={{0,2},{2,0},{1,3},{3,1},{4,6},{6,4},{5,7},{7,5},{8,10},{10,8},{9,1... | collective-permute-start | bytes 1572872 | tf_op jit(solution)/shard_map/ppermute | solution.py:270
  152.4 4.5 collective-permute-start.20
  200.8 129.5 %reduce-scatter.7.cloned.1.call-start = ((), (), s32[]{:S(2)}) async-start(), calls=%async_computation.3 | async-start | bytes 5242880
  202.4 10.9 %collective-permute-start.21 = (bf16[1024,1024]{1,0:T(8,128)(2,1)S(1)}, bf16[1024,1024]{1,0:T(8,128)(2,1)}, u32[]{:S(2)}, u32[]{:S(2)}) collective-permute-start(bf16[1024,1024]{1,0:T(8,128)(2,1)S(1)} %copy-done.7), channel_id=1, source_target_pairs={{0,2},{2,0},{1,3},{3,1},{4,6},{6,4},{5,7},{7,5},{8,10},{10,8},{9,1... | collective-permute-start | bytes 6291464 | tf_op jit(solution)/shard_map/ppermute | solution.py:270
  262.6 46.2 %collective-permute-start.22 = (bf16[512,256]{1,0:T(8,128)(2,1)}, bf16[512,256]{1,0:T(8,128)(2,1)}, u32[]{:S(2)}, u32[]{:S(2)}) collective-permute-start(bf16[512,256]{1,0:T(8,128)(2,1)} %convolution_convert_fusion.9), channel_id=1, source_target_pairs={{0,4},{4,0},{1,5},{5,1},{2,6},{6,2},{3,7},{7,3},{8,12},{12,8},{9,1... | collective-permute-start | bytes 786440 | tf_op jit(solution)/shard_map/ppermute | solution.py:270
  268.8 13.8 %collective-permute-start.25 = (bf16[512,512]{1,0:T(8,128)(2,1)S(1)}, bf16[512,512]{1,0:T(8,128)(2,1)S(1)}, u32[]{:S(2)}, u32[]{:S(2)}) collective-permute-start(bf16[512,512]{1,0:T(8,128)(2,1)S(1)} %dynamic-slice_bitcast_fusion.1), channel_id=1, source_target_pairs={{0,8},{8,0},{16,24},{24,16},{1,9},{9,1},{17,25},{25,17},{2,10},{10... | collective-permute-start | bytes 1572872 | tf_op jit(solution)/shard_map/ppermute | solution.py:881
  271.6 37.2 %collective-permute-start.23 = (bf16[512,256]{1,0:T(8,128)(2,1)S(1)}, bf16[512,256]{1,0:T(8,128)(2,1)S(1)}, u32[]{:S(2)}, u32[]{:S(2)}) collective-permute-start(bf16[512,256]{1,0:T(8,128)(2,1)S(1)} %convolution_convert_fusion.8), channel_id=1, source_target_pairs={{0,1},{1,0},{2,3},{3,2},{4,5},{5,4},{6,7},{7,6},{8,9},{9,8},{10,11... | collective-permute-start | bytes 786440 | tf_op jit(solution)/shard_map/ppermute | solution.py:270
  272.1 37.4 %collective-permute-start.24 = (bf16[512,256]{1,0:T(8,128)(2,1)S(1)}, bf16[512,256]{1,0:T(8,128)(2,1)S(1)}, u32[]{:S(2)}, u32[]{:S(2)}) collective-permute-start(bf16[512,256]{1,0:T(8,128)(2,1)S(1)} %convolution_convert_fusion.7), channel_id=1, source_target_pairs={{0,5},{5,0},{1,4},{4,1},{2,7},{7,2},{3,6},{6,3},{8,13},{13,8},{9,1... | collective-permute-start | bytes 786440 | tf_op jit(solution)/shard_map/ppermute | solution.py:856
  282.7 25.1 %collective-permute-start.26 = (bf16[512,512]{1,0:T(8,128)(2,1)S(1)}, bf16[512,512]{1,0:T(8,128)(2,1)S(1)}, u32[]{:S(2)}, u32[]{:S(2)}) collective-permute-start(bf16[512,512]{1,0:T(8,128)(2,1)S(1)} %fusion.44), channel_id=1, source_target_pairs={{0,16},{16,0},{8,24},{24,8},{1,17},{17,1},{9,25},{25,9},{2,18},{18... | collective-permute-start | bytes 1572872 | tf_op jit(solution)/shard_map/ppermute | solution.py:885
  287.5 27.1 %copy-start.11 = (bf16[1024,1024]{1,0:T(8,128)(2,1)}, bf16[1024,1024]{1,0:T(8,128)(2,1)S(1)}, u32[]{:S(2)}) copy-start(bf16[1024,1024]{1,0:T(8,128)(2,1)S(1)} %fusion.20.part_ref) | copy-start | bytes 6291460
  287.5 23.8 %copy-start.50 = (f32[256]{0:T(256)S(1)}, f32[256]{0:T(256)}, u32[]{:S(2)}) copy-start(f32[256]{0:T(256)} %param.29) | copy-start | bytes 3076
  310.2 4.3 collective-permute-start.27
  322.1 4.2 collective-permute-start.28
  326.4 3.9 collective-permute-start.29
  328.2 31.9 %collective-permute-start.33 = (bf16[1024,256]{1,0:T(8,128)(2,1)}, bf16[1024,256]{1,0:T(8,128)(2,1)S(1)}, u32[]{:S(2)}, u32[]{:S(2)}) collective-permute-start(bf16[1024,256]{1,0:T(8,128)(2,1)} %get-tuple-element.102), channel_id=1, source_target_pairs={{0,4},{4,0},{1,5},{5,1},{2,6},{6,2},{3,7},{7,3},{8,12},{12,8},{9,1... | collective-permute-start | bytes 1572872 | tf_op jit(solution)/shard_map/ppermute | solution.py:270
  330.3 29.8 %copy-start.24 = (f32[1024,256]{1,0:T(8,128)S(1)}, f32[1024,256]{1,0:T(8,128)}, u32[]{:S(2)}) copy-start(f32[1024,256]{1,0:T(8,128)} %get-tuple-element.101) | copy-start | bytes 3145732
  331.5 28.8 %collective-permute-start.30 = (bf16[512,512]{1,0:T(8,128)(2,1)S(1)}, bf16[512,512]{1,0:T(8,128)(2,1)S(1)}, u32[]{:S(2)}, u32[]{:S(2)}) collective-permute-start(bf16[512,512]{1,0:T(8,128)(2,1)S(1)} %dynamic-slice_bitcast_fusion), channel_id=1, source_target_pairs={{0,8},{8,0},{16,24},{24,16},{1,9},{9,1},{17,25},{25,17},{2,10},{10... | collective-permute-start | bytes 1572872 | tf_op jit(solution)/shard_map/ppermute | solution.py:881
  334.1 26.2 %copy-start.19 = (bf16[1,1024,512]{2,1,0:T(8,128)(2,1)S(1)}, bf16[1,1024,512]{2,1,0:T(8,128)(2,1)}, u32[]{:S(2)}) copy-start(bf16[1,1024,512]{2,1,0:T(8,128)(2,1)} %reduce-scatter.7.cloned.1.call-done) | copy-start | bytes 3145732
  334.1 51.7 %collective-permute-start.38 = (bf16[512,768]{1,0:T(8,128)(2,1)}, bf16[512,768]{1,0:T(8,128)(2,1)}, u32[]{:S(2)}, u32[]{:S(2)}) collective-permute-start(bf16[512,768]{1,0:T(8,128)(2,1)} %convolution_convert_fusion.2), channel_id=1, source_target_pairs={{0,5},{5,0},{1,4},{4,1},{2,7},{7,2},{3,6},{6,3},{8,13},{13,8},{9,1... | collective-permute-start | bytes 2359304 | tf_op jit(solution)/shard_map/ppermute | solution.py:856
  335.5 50.8 %collective-permute-start.37 = (bf16[512,768]{1,0:T(8,128)(2,1)}, bf16[512,768]{1,0:T(8,128)(2,1)}, u32[]{:S(2)}, u32[]{:S(2)}) collective-permute-start(bf16[512,768]{1,0:T(8,128)(2,1)} %convolution_convert_fusion.3), channel_id=1, source_target_pairs={{0,1},{1,0},{2,3},{3,2},{4,5},{5,4},{6,7},{7,6},{8,9},{9,8},{10,11... | collective-permute-start | bytes 2359304 | tf_op jit(solution)/shard_map/ppermute | solution.py:270
  337.4 49.0 %collective-permute-start.36 = (bf16[512,768]{1,0:T(8,128)(2,1)}, bf16[512,768]{1,0:T(8,128)(2,1)}, u32[]{:S(2)}, u32[]{:S(2)}) collective-permute-start(bf16[512,768]{1,0:T(8,128)(2,1)} %convolution_convert_fusion.4), channel_id=1, source_target_pairs={{0,4},{4,0},{1,5},{5,1},{2,6},{6,2},{3,7},{7,3},{8,12},{12,8},{9,1... | collective-permute-start | bytes 2359304 | tf_op jit(solution)/shard_map/ppermute | solution.py:270
  360.4 4.8 %collective-permute-start.34 = (f32[2304]{0:T(1024)S(1)}, f32[2304]{0:T(1024)S(1)}, u32[]{:S(2)}, u32[]{:S(2)}) collective-permute-start(f32[2304]{0:T(1024)S(1)} %maximum_add_fusion.1), channel_id=1, source_target_pairs={{0,8},{8,0},{16,24},{24,16},{1,9},{9,1},{17,25},{25,17},{2,10},{10... | collective-permute-start | bytes 27656 | tf_op jit(solution)/shard_map/ppermute | solution.py:1015
  362.0 26.6 %collective-permute-start.39 = (bf16[512,512]{1,0:T(8,128)(2,1)S(1)}, bf16[512,512]{1,0:T(8,128)(2,1)}, u32[]{:S(2)}, u32[]{:S(2)}) collective-permute-start(bf16[512,512]{1,0:T(8,128)(2,1)S(1)} %fusion.43), channel_id=1, source_target_pairs={{0,16},{16,0},{8,24},{24,8},{1,17},{17,1},{9,25},{25,9},{2,18},{18... | collective-permute-start | bytes 1572872 | tf_op jit(solution)/shard_map/ppermute | solution.py:885
  365.3 21.1 %copy-start.29 = (bf16[512,768]{1,0:T(8,128)(2,1)S(1)}, bf16[512,768]{1,0:T(8,128)(2,1)}, u32[]{:S(2)}) copy-start(bf16[512,768]{1,0:T(8,128)(2,1)} %convolution_convert_fusion.5) | copy-start | bytes 2359300
  365.3 19.9 %collective-permute-start.35 = (f32[2304]{0:T(1024)S(1)}, f32[2304]{0:T(1024)S(1)}, u32[]{:S(2)}, u32[]{:S(2)}) collective-permute-start(f32[2304]{0:T(1024)S(1)} %add.236), channel_id=1, source_target_pairs={{0,16},{16,0},{8,24},{24,8},{1,17},{17,1},{9,25},{25,9},{2,18},{18... | collective-permute-start | bytes 27656 | tf_op jit(solution)/shard_map/ppermute | solution.py:1016
  385.2 12.4 %collective-permute-start.31 = (bf16[1024,512]{1,0:T(8,128)(2,1)}, bf16[1024,512]{1,0:T(8,128)(2,1)}, u32[]{:S(2)}, u32[]{:S(2)}) collective-permute-start(bf16[1024,512]{1,0:T(8,128)(2,1)} %get-tuple-element.100), channel_id=1, source_target_pairs={{0,2},{2,0},{1,3},{3,1},{4,6},{6,4},{5,7},{7,5},{8,10},{10,8},{9,1... | collective-permute-start | bytes 3145736 | tf_op jit(solution)/shard_map/ppermute | solution.py:270
  385.8 7.1 %collective-permute-start.46 = (f32[1024]{0:T(1024)S(1)}, f32[1024]{0:T(1024)S(1)}, u32[]{:S(2)}, u32[]{:S(2)}) collective-permute-start(f32[1024]{0:T(1024)S(1)} %slice.249), channel_id=1, source_target_pairs={{0,2},{2,0},{1,3},{3,1},{4,6},{6,4},{5,7},{7,5},{8,10},{10,8},{9,1... | collective-permute-start | bytes 12296 | tf_op jit(solution)/shard_map/ppermute | solution.py:270
  392.9 15.1 %collective-permute-start.40 = (bf16[256,1024]{0,1:T(8,128)(2,1)}, bf16[256,1024]{0,1:T(8,128)(2,1)}, u32[]{:S(2)}, u32[]{:S(2)}) collective-permute-start(bf16[256,1024]{0,1:T(8,128)(2,1)} %bitcast.164), channel_id=1, source_target_pairs={{0,8},{8,0},{16,24},{24,16},{1,9},{9,1},{17,25},{25,17},{2,10},{10... | collective-permute-start | bytes 1572872 | tf_op jit(solution)/shard_map/ppermute | solution.py:881
  393.5 36.9 %collective-permute-start.44 = (bf16[512,512]{1,0:T(8,128)(2,1)S(1)}, bf16[512,512]{1,0:T(8,128)(2,1)}, u32[]{:S(2)}, u32[]{:S(2)}) collective-permute-start(bf16[512,512]{1,0:T(8,128)(2,1)S(1)} %add_convert_fusion.2), channel_id=1, source_target_pairs={{0,8},{8,0},{16,24},{24,16},{1,9},{9,1},{17,25},{25,17},{2,10},{10... | collective-permute-start | bytes 1572872 | tf_op jit(solution)/shard_map/ppermute | solution.py:889
  397.6 43.1 %collective-permute-start.47 = (bf16[512,512]{1,0:T(8,128)(2,1)S(1)}, bf16[512,512]{1,0:T(8,128)(2,1)S(1)}, u32[]{:S(2)}, u32[]{:S(2)}) collective-permute-start(bf16[512,512]{1,0:T(8,128)(2,1)S(1)} %copy-done.8), channel_id=1, source_target_pairs={{0,8},{8,0},{16,24},{24,16},{1,9},{9,1},{17,25},{25,17},{2,10},{10... | collective-permute-start | bytes 1572872 | tf_op jit(solution)/shard_map/ppermute | solution.py:889
  400.1 41.0 %collective-permute-start.32 = (bf16[1024,256]{1,0:T(8,128)(2,1)S(1)}, bf16[1024,256]{1,0:T(8,128)(2,1)S(1)}, u32[]{:S(2)}, u32[]{:S(2)}) collective-permute-start(bf16[1024,256]{1,0:T(8,128)(2,1)S(1)} %slice.234), channel_id=1, source_target_pairs={{0,4},{4,0},{1,5},{5,1},{2,6},{6,2},{3,7},{7,3},{8,12},{12,8},{9,1... | collective-permute-start | bytes 1572872 | tf_op jit(solution)/shard_map/ppermute | solution.py:270
  409.2 31.8 %collective-permute-start.41 = (bf16[256,1024]{0,1:T(8,128)(2,1)S(1)}, bf16[256,1024]{0,1:T(8,128)(2,1)S(1)}, u32[]{:S(2)}, u32[]{:S(2)}) collective-permute-start(bf16[256,1024]{0,1:T(8,128)(2,1)S(1)} %fusion.42), channel_id=1, source_target_pairs={{0,16},{16,0},{8,24},{24,8},{1,17},{17,1},{9,25},{25,9},{2,18},{18... | collective-permute-start | bytes 1572872 | tf_op jit(solution)/shard_map/ppermute | solution.py:885
  431.6 10.7 %collective-permute-start.45 = (bf16[256,1024]{1,0:T(8,128)(2,1)S(1)}, bf16[256,1024]{1,0:T(8,128)(2,1)S(1)}, u32[]{:S(2)}, u32[]{:S(2)}) collective-permute-start(bf16[256,1024]{1,0:T(8,128)(2,1)S(1)} %pad_maximum_fusion.8), channel_id=1, source_target_pairs={{0,2},{2,0},{1,3},{3,1},{4,6},{6,4},{5,7},{7,5},{8,10},{10,8},{9,1... | collective-permute-start | bytes 1572872 | tf_op jit(solution)/shard_map/ppermute | solution.py:270
  440.9 14.8 %collective-permute-start.48 = (bf16[1024,256]{1,0:T(8,128)(2,1)S(1)}, bf16[1024,256]{1,0:T(8,128)(2,1)S(1)}, u32[]{:S(2)}, u32[]{:S(2)}) collective-permute-start(bf16[1024,256]{1,0:T(8,128)(2,1)S(1)} %slice.251), channel_id=1, source_target_pairs={{0,2},{2,0},{1,3},{3,1},{4,6},{6,4},{5,7},{7,5},{8,10},{10,8},{9,1... | collective-permute-start | bytes 1572872 | tf_op jit(solution)/shard_map/ppermute | solution.py:270
  441.1 14.4 %collective-permute-start.42 = (bf16[256,1024]{0,1:T(8,128)(2,1)S(1)}, bf16[256,1024]{0,1:T(8,128)(2,1)S(1)}, u32[]{:S(2)}, u32[]{:S(2)}) collective-permute-start(bf16[256,1024]{0,1:T(8,128)(2,1)S(1)} %add_convert_fusion.1), channel_id=1, source_target_pairs={{0,8},{8,0},{16,24},{24,16},{1,9},{9,1},{17,25},{25,17},{2,10},{10... | collective-permute-start | bytes 1572872 | tf_op jit(solution)/shard_map/ppermute | solution.py:889
  455.6 2.0 collective-permute-start.43
  (56 other events, 443.1 us)
Sparse Core Ops, SparseCore 0:
  35.8 124.1 all-gather.2
  200.9 51.9 reduce-scatter.8
  255.9 63.8 reduce-scatter.6

commit v6 on v5

--- a/solution.py
+++ b/solution.py
@@ -988,8 +988,6 @@
     down_part = depth_far(down_part)
     first_part = after(first_part, out_got, down_part)
     mine, theirs, sums_one = first_norm_back(xs, first_part, swap(first_part, "core"), grad_own, grad_other, gain_one)
-    theirs = swap(theirs, "y")
-    grad_inputs = ordered(mine, theirs.astype(FULL), y_at).reshape(2 * length, n)
 
     gains = jnp.concatenate((sums_one[:2, :n], sums_two[:2, :n])).reshape(-1)
     gains_y = jnp.concatenate((sums_one[:2, n:], sums_two[:2, n:])).reshape(-1)
@@ -1003,6 +1001,8 @@
     up_part = depth_pair(up_scattered, odd)
     qkv_got = plane_exchange(*after((qkv_grads[0][1], qkv_grads[1][0], qkv_grads[1][1]), up_scattered))
     up_far = depth_far(up_part)
+    theirs = swap(after(theirs, up_far), "y")
+    grad_inputs = ordered(mine, theirs.astype(FULL), y_at).reshape(2 * length, n)
     ends_own, ends_other = layer_end(at, after(hiddens, up_part), ffn)
     down_total = depth_join(after(down_part, up_far), odd)
     kept_two = jnp.concatenate((residual[:, :n], residual[:, 2 * n : 3 * n]), axis=1)

time: 474 us -> 461 us (0.973)
  waiting for transfers between devices: 157 us -> 145 us
  starting transfers between devices: 58.4 us -> 53.2 us
    ppermute x33, waiting for transfers between devices: 48 us -> 32.7 us  [swap(): return lax.ppermute(array, axis, SWAP)]
    ppermute x33, starting transfers between devices: 29.8 us -> 23 us  [swap(): return lax.ppermute(array, axis, SWAP)]
    ppermute x3, waiting for transfers between devices: 13.2 us -> 18.6 us  [depth_pair(): lax.ppermute(pick(halves, 1 - odd), 'dp', PAIRS)]
    unnamed x147 -> x153, local copies, waits for them, and re-layouts: 16.6 us -> 17.5 us
  transfers between devices with their start and end apart: 52 -> 52, of which waited for: 18 -> 21; matrix products, arithmetic and copies ran while one was open for 18% -> 18% of each run, Pallas kernels for 22% -> 23%
where the time goes in v6:
time: 461 us; the launch traced here: 455 us
  waiting for transfers between devices  145 us (31%)
  Pallas kernels  141 us (31%)
  starting transfers between devices  53.2 us (12%)
  local copies, waits for them, and re-layouts  36.5 us (8%)
  other arithmetic  33.2 us (7%)
  matrix products  30.6 us (7%)
  between operations  15.3 us (3%)
    ppermute x3, waiting for transfers between devices, depth_join(): lax.ppermute(part, 'dp', PAIRS)  38.6 us
    ppermute x33, waiting for transfers between devices, swap(): return lax.ppermute(array, axis, SWAP)  32.7 us
    pallas_call x2, Pallas kernels, attend_backward(): pl.pallas_call(attend_backward_kernel, out_shape=jax.ShapeDtypeStruct((le...  27.6 us
    pallas_call x1, Pallas kernels, feed_forward(): pl.pallas_call(feed_forward_kernel, out_shape=(jax.ShapeDtypeStruct((leng...  27.1 us
    pallas_call x2, Pallas kernels, attend_forward(): pl.pallas_call(attend_forward_kernel, out_shape=(jax.ShapeDtypeStruct((le...  25.9 us
    ppermute x4, waiting for transfers between devices, swap_across(): return lax.ppermute(array, ('y', 'col'), [(0, 3), (3, 0), (1, 2), (2, 1)])  23.3 us
    ppermute x33, starting transfers between devices, swap(): return lax.ppermute(array, axis, SWAP)  23 us
    ppermute x3, waiting for transfers between devices, depth_far(): return add_low(part, lax.ppermute(part, 'dp', FAR))  20.6 us
  transfers between devices with their start and end apart: 52, of which 21 were waited for; matrix products, arithmetic and copies ran while one was open for 18% of the time, Pallas kernels for 23%

profile of v6, /device:TPU:0, one launch (start us, length us, event | category | flops | bytes accessed | tf_op | source)
XLA Modules:
  0.0 454.7 jit_solution(3733918586332328386)
XLA Ops:
  13.3 2.9 collective-permute-start.8
  16.1 1.5 collective-permute-start.10
  17.7 1.5 fusion.16
  19.3 15.0 %collective-permute-done.8 = bf16[512,768]{1,0:T(8,128)(2,1)} collective-permute-done((bf16[512,768]{1,0:T(8,128)(2,1)}, bf16[512,768]{1,0:T(8,128)(2,1)}, u32[]{:S(2)}, u32[]{:S(2)}) %collective-permute-start.8) | collective-permute-done | bytes 786464 | tf_op jit(solution)/shard_map/ppermute | solution.py:270
  38.5 3.1 collective-permute-start.6
  41.9 1.4 collective-permute-start.9
  49.1 13.3 %collective-permute-start.5 = (bf16[512,768]{1,0:T(8,128)(2,1)}, bf16[512,768]{1,0:T(8,128)(2,1)S(1)}, u32[]{:S(2)}, u32[]{:S(2)}) collective-permute-start(bf16[512,768]{1,0:T(8,128)(2,1)} %pad_maximum_fusion.7), channel_id=1, source_target_pairs={{0,5},{5,0},{1,4},{4,1},{2,7},{7,2},{3,6},{6,3},{8,13},{13,8},{9,1... | collective-permute-start | bytes 2359304 | tf_op jit(solution)/shard_map/ppermute | solution.py:856
  63.9 2.5 collective-permute-start.7
  66.4 1.6 pad_maximum_fusion.3
  69.8 18.2 %collective-permute-done.5 = bf16[512,768]{1,0:T(8,128)(2,1)S(1)} collective-permute-done((bf16[512,768]{1,0:T(8,128)(2,1)}, bf16[512,768]{1,0:T(8,128)(2,1)S(1)}, u32[]{:S(2)}, u32[]{:S(2)}) %collective-permute-start.5) | collective-permute-done | bytes 786464 | tf_op jit(solution)/shard_map/ppermute | solution.py:856
  89.7 5.0 %first_norm.1 = (bf16[1024,512]{1,0:T(8,128)(2,1)}, bf16[1024,512]{1,0:T(8,128)(2,1)}) custom-call(bf16[1024,256]{1,0:T(8,128)(2,1)} %copy-done.2, bf16[1024,256]{1,0:T(8,128)(2,1)} %copy-done.3, bf16[1024,256]{1,0:T(8,128)(2,1)} %copy-done.4, bf16[1024,256]{1,0:T(8,128)(2,1)} %copy-done.5, f32[1,1024]{1,0:T(1,128)} %get-tuple-element.223.gain_ref, ...), custom_call_target="tpu_custom_call" | custom-call | flops 5242880 | bytes 4194304 | tf_op jit(solution)/shard_map/first_norm/pallas_call | solution.py:536
  94.7 1.5 constant_dynamic-update-slice_fusion.1
  98.6 2.6 collective-permute-start.16
  101.2 4.1 convolution_convert_fusion.1.q_ref.k_ref.v_ref
  106.0 12.8 %attend_forward.2 = (bf16[1024,256]{1,0:T(8,128)(2,1)}, bf16[4,1024,128]{2,1,0:T(8,128)(2,1)}) custom-call(s32[2,4]{1,0:T(2,128)} %pad_add_fusion.1.where_ref, bf16[1024,768]{1,0:T(8,128)(2,1)} %convolution_convert_fusion.1.q_ref.k_ref.v_ref, bf16[1024,768]{1,0:T(8,128)(2,1)} %convolution_convert_fusion.1.q_ref.k_ref.v_ref, ...), custom_call_target="tpu_custom_call" | custom-call | flops 1073741824 | bytes 12582912 | tf_op jit(solution)/shard_map/attend_forward/pallas_call | solution.py:377
  120.0 5.1 %collective-permute-done.16 = bf16[256,512]{1,0:T(8,128)(2,1)} collective-permute-done((bf16[256,512]{1,0:T(8,128)(2,1)S(1)}, bf16[256,512]{1,0:T(8,128)(2,1)}, u32[]{:S(2)}, u32[]{:S(2)}) %collective-permute-start.16) | collective-permute-done | bytes 262176 | tf_op jit(solution)/shard_map/ppermute | solution.py:856
  126.3 2.9 convolution_convert_fusion.q_ref.k_ref.v_ref
  129.2 13.0 %attend_forward.3 = (bf16[1024,256]{1,0:T(8,128)(2,1)}, bf16[4,1024,128]{2,1,0:T(8,128)(2,1)}) custom-call(s32[2,4]{1,0:T(2,128)} %pad_add_fusion.1.where_ref, bf16[1024,768]{1,0:T(8,128)(2,1)} %convolution_convert_fusion.q_ref.k_ref.v_ref, bf16[1024,768]{1,0:T(8,128)(2,1)} %convolution_convert_fusion.q_ref.k_ref.v_ref, ...), custom_call_target="tpu_custom_call" | custom-call | flops 1073741824 | bytes 12582912 | tf_op jit(solution)/shard_map/attend_forward/pallas_call | solution.py:377
  144.7 1.5 pad_maximum_fusion.1.c_ref.cots_ref
  148.0 4.8 %mix_heads.1.part_ref = bf16[1024,1024]{1,0:T(8,128)(2,1)} custom-call(bf16[1024,256]{1,0:T(8,128)(2,1)} %get-tuple-element.70.h0.heads_ref, bf16[1024,256]{1,0:T(8,128)(2,1)} %get-tuple-element.76.h1.heads_ref, bf16[256,1024]{1,0:T(8,128)(2,1)} %copy-done.15, bf16[256,1024]{1,0:T(8,128)(2,1)} %copy-done.13), custom_call_target="tpu_custom_call" | custom-call | flops 1073741824 | bytes 5242880 | tf_op jit(solution)/shard_map/mix_heads/pallas_call | solution.py:657
  154.5 2.8 collective-permute-done.20.got_ref
  158.6 6.3 %second_norm.1 = (f32[1024,1024]{1,0:T(8,128)}, bf16[2,1024,512]{2,1,0:T(8,128)(2,1)}) custom-call(bf16[1024,256]{1,0:T(8,128)(2,1)} %copy-done.2, bf16[1024,256]{1,0:T(8,128)(2,1)} %copy-done.3, bf16[1024,256]{1,0:T(8,128)(2,1)} %copy-done.4, bf16[1024,256]{1,0:T(8,128)(2,1)} %copy-done.5, bf16[1024,1024]{1,0:T(8,128)(2,1)} %mix_heads.1.part_ref, ...), custom_call_target="tpu_custom_call" | custom-call | flops 7864320 | bytes 12582912 | tf_op jit(solution)/shard_map/second_norm/pallas_call | solution.py:563
  164.9 27.1 %feed_forward.1 = (bf16[1024,1024]{1,0:T(8,128)(2,1)}, bf16[2,1024,1024]{2,1,0:T(8,128)(2,1)}, bf16[2,1024,1024]{2,1,0:T(8,128)(2,1)}, f32[8,8,256]{2,1,0:T(8,128)}) custom-call(s32[2]{0:T(128)} %pad_add_fusion.2.at_ref, bf16[2,1024,512]{2,1,0:T(8,128)(2,1)} %get-tuple-element.79.s_ref, bf16[2,1024,512]{2,1,0:T(8,128)(2,1)} %pad_maximum_fusion.1.c_ref.cots_ref, ...), custom_call_target="tpu_custom_call" | custom-call | flops 12884901888 | bytes 29360128 | tf_op jit(solution)/shard_map/feed_forward/pallas_call | solution.py:728
  192.0 9.2 %down_grads.1 = bf16[2,2,1024,512]{3,2,1,0:T(8,128)(2,1)} custom-call(s32[2]{0:T(128)} %pad_add_fusion.2.at_ref, bf16[2,1024,1024]{2,1,0:T(8,128)(2,1)} %get-tuple-element.99.hidden_ref.h0.h1, bf16[2,1024,512]{2,1,0:T(8,128)(2,1)} %pad_maximum_fusion.1.c_ref.cots_ref), custom_call_target="tpu_custom_call" | custom-call | flops 4294967296 | bytes 8388608 | tf_op jit(solution)/shard_map/down_grads/pallas_call | solution.py:792
  201.3 1.5 copy-done.7
  203.2 10.5 %up_grads.1 = bf16[4,1024,512]{2,1,0:T(8,128)(2,1)} custom-call(s32[2]{0:T(128)} %pad_add_fusion.2.at_ref, bf16[2,1024,512]{2,1,0:T(8,128)(2,1)} %get-tuple-element.79.s_ref, bf16[2,1024,1024]{2,1,0:T(8,128)(2,1)} %get-tuple-element.83.grad_ref), custom_call_target="tpu_custom_call" | custom-call | flops 4294967296 | bytes 8388608 | tf_op jit(solution)/shard_map/up_grads/pallas_call | solution.py:765
  213.7 8.0 %second_norm_back.1 = (f32[1024,256]{1,0:T(8,128)}, f32[1024,256]{1,0:T(8,128)}, bf16[1024,1024]{1,0:T(8,128)(2,1)}, f32[8,512]{1,0:T(8,128)}) custom-call(f32[1024,1024]{1,0:T(8,128)} %get-tuple-element.78.residual_ref, bf16[1024,1024]{1,0:T(8,128)(2,1)} %get-tuple-element.85.part_ref, bf16[1024,1024]{1,0:T(8,128)(2,1)} %collective-permute-done.21.got_ref, ...), custom_call_target="tpu_custom_call" | custom-call | flops 15728640 | bytes 16777216 | tf_op jit(solution)/shard_map/second_norm_back/pallas_call | solution.py:611
  221.7 4.0 select_convert_fusion.1.grads_ref
  225.7 13.7 %attend_backward.2 = bf16[1024,768]{1,0:T(8,128)(2,1)} custom-call(s32[2,4]{1,0:T(2,128)} %pad_add_fusion.1.where_ref, bf16[4,1024,128]{2,1,0:T(8,128)(2,1)} %get-tuple-element.84.kept_ref, bf16[1024,768]{1,0:T(8,128)(2,1)} %convolution_convert_fusion.1.q_ref.k_ref.v_ref, bf16[1024,768]{1,0:T(8,128)(2,1)} %convolution_convert_fusion.1.q_ref.k_ref.v_ref, ...), custom_call_target="tpu_custom_call" | custom-call | flops 2684354560 | bytes 15728640 | tf_op jit(solution)/shard_map/attend_backward/pallas_call | solution.py:467
  239.4 13.9 %attend_backward.3 = bf16[1024,768]{1,0:T(8,128)(2,1)} custom-call(s32[2,4]{1,0:T(2,128)} %pad_add_fusion.1.where_ref, bf16[4,1024,128]{2,1,0:T(8,128)(2,1)} %get-tuple-element.88.kept_ref, bf16[1024,768]{1,0:T(8,128)(2,1)} %convolution_convert_fusion.q_ref.k_ref.v_ref, bf16[1024,768]{1,0:T(8,128)(2,1)} %convolution_convert_fusion.q_ref.k_ref.v_ref, ...), custom_call_target="tpu_custom_call" | custom-call | flops 2684354560 | bytes 15728640 | tf_op jit(solution)/shard_map/attend_backward/pallas_call | solution.py:467
  253.4 3.5 convolution_convert_fusion.5
  256.9 1.9 convolution_convert_fusion.4
  258.8 1.9 convolution_convert_fusion.3
  260.7 1.9 convolution_convert_fusion.2
  266.3 4.2 collective-permute-start.25
  270.5 1.9 convolution_convert_fusion.8
  273.0 1.5 collective-permute-start.24
  274.5 8.0 %collective-permute-done.25 = bf16[512,512]{1,0:T(8,128)(2,1)S(1)} collective-permute-done((bf16[512,512]{1,0:T(8,128)(2,1)S(1)}, bf16[512,512]{1,0:T(8,128)(2,1)S(1)}, u32[]{:S(2)}, u32[]{:S(2)}) %collective-permute-start.25) | collective-permute-done | bytes 524320 | tf_op jit(solution)/shard_map/ppermute | solution.py:881
  282.7 4.7 %fusion.20.part_ref = bf16[1024,1024]{1,0:T(8,128)(2,1)S(1)} fusion(bf16[1024,768]{1,0:T(8,128)(2,1)S(1)} %copy-done.37, bf16[512,768]{1,0:T(8,128)(2,1)} %collective-permute-done.8, bf16[256,768]{1,0:T(8,128)(2,1)S(1)} %copy-done.40, bf16[256,256]{1,0:T(8,128)(2,1)S(1)} %get-tuple-element.218, bf16[256,256]{1,0:T(8,128)(2,1)S(1)} %get-tuple-element.244, ...), kind=kOutput, calls=%fused_computation.30 | convolution fusion | flops 3247439872 | bytes 8388608 | tf_op jit(solution)/shard_map/dot_general | solution.py:278
  287.4 20.6 %collective-permute-done.26 = bf16[512,512]{1,0:T(8,128)(2,1)S(1)} collective-permute-done((bf16[512,512]{1,0:T(8,128)(2,1)S(1)}, bf16[512,512]{1,0:T(8,128)(2,1)S(1)}, u32[]{:S(2)}, u32[]{:S(2)}) %collective-permute-start.26) | collective-permute-done | bytes 524320 | tf_op jit(solution)/shard_map/ppermute | solution.py:885
  311.0 2.3 collective-permute-done.27.got_ref
  314.7 6.8 %first_norm_back.1 = (f32[1024,256]{1,0:T(8,128)}, bf16[1024,256]{1,0:T(8,128)(2,1)}, f32[8,512]{1,0:T(8,128)}) custom-call(bf16[1024,256]{1,0:T(8,128)(2,1)} %copy-done.2, bf16[1024,256]{1,0:T(8,128)(2,1)} %copy-done.3, bf16[1024,256]{1,0:T(8,128)(2,1)} %copy-done.4, bf16[1024,256]{1,0:T(8,128)(2,1)} %copy-done.5, bf16[1024,1024]{1,0:T(8,128)(2,1)} %copy-done.11, ...), custom_call_target="tpu_custom_call" | custom-call | flops 15728640 | bytes 10485760 | tf_op jit(solution)/shard_map/first_norm_back/pallas_call | solution.py:634
  322.9 3.1 collective-permute-done.28
  326.1 3.7 collective-permute-done.29
  331.7 1.8 fusion.76
  335.7 1.5 collective-permute-start.37
  337.1 5.6 %collective-permute-done.30 = bf16[512,512]{1,0:T(8,128)(2,1)S(1)} collective-permute-done((bf16[512,512]{1,0:T(8,128)(2,1)S(1)}, bf16[512,512]{1,0:T(8,128)(2,1)S(1)}, u32[]{:S(2)}, u32[]{:S(2)}) %collective-permute-start.30) | collective-permute-done | bytes 524320 | tf_op jit(solution)/shard_map/ppermute | solution.py:881
  343.2 2.2 fusion.50
  345.3 1.5 collective-permute-start.33
  348.3 9.6 %layer_end.1 = (f32[1024,512]{1,0:T(8,128)}, bf16[1024,512]{1,0:T(8,128)(2,1)}) custom-call(s32[2]{0:T(128)} %pad_add_fusion.2.at_ref, bf16[2,1024,1024]{2,1,0:T(8,128)(2,1)} %get-tuple-element.99.hidden_ref.h0.h1, bf16[2,1024,1024]{2,1,0:T(8,128)(2,1)} %get-tuple-element.99.hidden_ref.h0.h1, bf16[4,2048,512]{2,1,0:T(8,128)(2,1)} %bitcast.144, ...), custom_call_target="tpu_custom_call" | custom-call | flops 4294967296 | bytes 10485760 | tf_op jit(solution)/shard_map/layer_end/pallas_call | solution.py:828
  357.9 10.9 %collective-permute-done.36 = f32[2304]{0:T(1024)S(1)} collective-permute-done((f32[2304]{0:T(1024)S(1)}, f32[2304]{0:T(1024)S(1)}, u32[]{:S(2)}, u32[]{:S(2)}) %collective-permute-start.36) | collective-permute-done | bytes 9248 | tf_op jit(solution)/shard_map/ppermute | solution.py:1016
  370.0 2.0 add_convert_fusion
  374.5 2.0 copy.63
  379.5 2.0 copy.69
  382.5 2.5 fusion.19
  385.0 1.5 collective-permute-start.32
  386.5 5.1 %collective-permute-done.40 = bf16[256,1024]{0,1:T(8,128)(2,1)} collective-permute-done((bf16[256,1024]{0,1:T(8,128)(2,1)}, bf16[256,1024]{0,1:T(8,128)(2,1)}, u32[]{:S(2)}, u32[]{:S(2)}) %collective-permute-start.40) | collective-permute-done | bytes 524320 | tf_op jit(solution)/shard_map/ppermute | solution.py:881
  392.8 1.5 collective-permute-done.34
  394.8 19.3 %collective-permute-done.44 = bf16[512,512]{1,0:T(8,128)(2,1)} collective-permute-done((bf16[512,512]{1,0:T(8,128)(2,1)S(1)}, bf16[512,512]{1,0:T(8,128)(2,1)}, u32[]{:S(2)}, u32[]{:S(2)}) %collective-permute-start.44) | collective-permute-done | bytes 524320 | tf_op jit(solution)/shard_map/ppermute | solution.py:889
  415.3 8.9 %collective-permute-done.47 = bf16[512,512]{1,0:T(8,128)(2,1)S(1)} collective-permute-done((bf16[512,512]{1,0:T(8,128)(2,1)S(1)}, bf16[512,512]{1,0:T(8,128)(2,1)S(1)}, u32[]{:S(2)}, u32[]{:S(2)}) %collective-permute-start.47) | collective-permute-done | bytes 524320 | tf_op jit(solution)/shard_map/ppermute | solution.py:889
  426.8 1.5 pad_maximum_fusion.2
  429.9 1.6 maximum_convert_fusion
  431.5 10.4 %collective-permute-done.42 = bf16[256,1024]{0,1:T(8,128)(2,1)S(1)} collective-permute-done((bf16[256,1024]{0,1:T(8,128)(2,1)S(1)}, bf16[256,1024]{0,1:T(8,128)(2,1)S(1)}, u32[]{:S(2)}, u32[]{:S(2)}) %collective-permute-start.42) | collective-permute-done | bytes 524320 | tf_op jit(solution)/shard_map/ppermute | solution.py:889
  442.1 1.5 maximum_convert_fusion.1
  (338 shorter events, 69.4 us)
Async XLA Ops:
  7.2 34.4 %copy-start = (s32[8,16,3]{1,0,2:T(8,128)S(1)}, s32[8,16,3]{1,0,2:T(8,128)}, u32[]{:S(2)}) copy-start(s32[8,16,3]{1,0,2:T(8,128)} %param.31) | copy-start | bytes 4612
  7.2 157.7 %all-gather.3.cloned.1.call-start = ((), (), s32[]{:S(2)}) async-start(), calls=%async_computation.2 | async-start | bytes 10485760 | tf_op jit(solution)/shard_map/all_gather | solution.py:923
  9.5 1.9 collective-permute-start.4
  12.5 5.1 %collective-permute-start.11 = (bf16[256,1024]{1,0:T(8,128)(2,1)S(1)}, bf16[256,1024]{1,0:T(8,128)(2,1)S(1)}, u32[]{:S(2)}, u32[]{:S(2)}) collective-permute-start(bf16[256,1024]{1,0:T(8,128)(2,1)S(1)} %get-tuple-element.207), channel_id=1, source_target_pairs={{0,2},{2,0},{1,3},{3,1},{4,6},{6,4},{5,7},{7,5},{8,10},{10,8},{9,1... | collective-permute-start | bytes 1572872 | tf_op jit(solution)/shard_map/ppermute | solution.py:270
  13.1 4.6 %collective-permute-start.12 = (bf16[1024,256]{1,0:T(8,128)(2,1)S(1)}, bf16[1024,256]{1,0:T(8,128)(2,1)S(1)}, u32[]{:S(2)}, u32[]{:S(2)}) collective-permute-start(bf16[1024,256]{1,0:T(8,128)(2,1)S(1)} %get-tuple-element.205), channel_id=1, source_target_pairs={{0,2},{2,0},{1,3},{3,1},{4,6},{6,4},{5,7},{7,5},{8,10},{10,8},{9,1... | collective-permute-start | bytes 1572872 | tf_op jit(solution)/shard_map/ppermute | solution.py:270
  13.3 21.0 %collective-permute-start.8 = (bf16[512,768]{1,0:T(8,128)(2,1)}, bf16[512,768]{1,0:T(8,128)(2,1)}, u32[]{:S(2)}, u32[]{:S(2)}) collective-permute-start(bf16[512,768]{1,0:T(8,128)(2,1)} %pad_maximum_fusion.7), channel_id=1, source_target_pairs={{0,4},{4,0},{1,5},{5,1},{2,6},{6,2},{3,7},{7,3},{8,12},{12,8},{9,1... | collective-permute-start | bytes 2359304 | tf_op jit(solution)/shard_map/ppermute | solution.py:270
  16.1 19.5 %collective-permute-start.10 = (bf16[512,768]{1,0:T(8,128)(2,1)}, bf16[512,768]{1,0:T(8,128)(2,1)S(1)}, u32[]{:S(2)}, u32[]{:S(2)}) collective-permute-start(bf16[512,768]{1,0:T(8,128)(2,1)} %pad_maximum_fusion.7), channel_id=1, source_target_pairs={{0,1},{1,0},{2,3},{3,2},{4,5},{5,4},{6,7},{7,6},{8,9},{9,8},{10,11... | collective-permute-start | bytes 2359304 | tf_op jit(solution)/shard_map/ppermute | solution.py:270
  19.2 22.6 %copy-start.52 = (f32[2048]{0:T(1024)S(1)}, f32[2048]{0:T(1024)}, u32[]{:S(2)}) copy-start(f32[2048]{0:T(1024)} %param.27) | copy-start | bytes 24580
  19.2 24.1 %copy-start.65 = (s32[2]{0:T(128)S(1)}, s32[2]{0:T(128)}, u32[]{:S(2)}) copy-start(s32[2]{0:T(128)} %param.32) | copy-start | bytes 28
  35.7 229.4 %reduce-scatter.9.cloned.1.call-start = ((), (), s32[]{:S(2)}) async-start(), calls=%async_computation.4 | async-start | bytes 5242880
  37.4 32.4 %collective-permute-start = (bf16[1024,256]{1,0:T(8,128)(2,1)S(1)}, bf16[1024,256]{1,0:T(8,128)(2,1)S(1)}, u32[]{:S(2)}, u32[]{:S(2)}) collective-permute-start(bf16[1024,256]{1,0:T(8,128)(2,1)S(1)} %get-tuple-element.64.x0), channel_id=1, source_target_pairs={{0,2},{2,0},{1,3},{3,1},{4,6},{6,4},{5,7},{7,5},{8,10},{10,8},{9,1... | collective-permute-start | bytes 1572872 | tf_op jit(solution)/shard_map/ppermute | solution.py:270
  37.4 25.4 %collective-permute-start.1 = (bf16[1024,256]{1,0:T(8,128)(2,1)}, bf16[1024,256]{1,0:T(8,128)(2,1)S(1)}, u32[]{:S(2)}, u32[]{:S(2)}) collective-permute-start(bf16[1024,256]{1,0:T(8,128)(2,1)} %get-tuple-element.208), channel_id=1, source_target_pairs={{0,4},{4,0},{1,5},{5,1},{2,6},{6,2},{3,7},{7,3},{8,12},{12,8},{9,1... | collective-permute-start | bytes 1572872 | tf_op jit(solution)/shard_map/ppermute | solution.py:270
  37.8 5.6 %collective-permute-start.3 = (s32[1,1024]{1,0:T(1,128)S(1)}, s32[1,1024]{1,0:T(1,128)S(1)}, u32[]{:S(2)}, u32[]{:S(2)}) collective-permute-start(s32[1,1024]{1,0:T(1,128)S(1)} %copy-done.64), channel_id=1, source_target_pairs={{0,0},{4,1},{1,2},{5,3},{2,4},{6,5},{3,6},{7,7},{8,8},{12,9},{9,10... | collective-permute-start | bytes 12296 | tf_op jit(solution)/shard_map/ppermute | solution.py:942
  38.5 24.7 %copy-start.44 = (f32[5,256]{1,0:T(8,128)}, f32[5,256]{1,0:T(8,128)S(1)}, u32[]{:S(2)}) copy-start(f32[5,256]{1,0:T(8,128)S(1)} %stack.107) | copy-start | bytes 15364
  38.5 24.7 %collective-permute-start.6 = (f32[5,256]{1,0:T(8,128)S(1)}, f32[5,256]{1,0:T(8,128)S(1)}, u32[]{:S(2)}, u32[]{:S(2)}) collective-permute-start(f32[5,256]{1,0:T(8,128)S(1)} %stack.107), channel_id=1, source_target_pairs={{0,2},{2,0},{1,3},{3,1},{4,6},{6,4},{5,7},{7,5},{8,10},{10,8},{9,1... | collective-permute-start | bytes 15368 | tf_op jit(solution)/shard_map/ppermute | solution.py:270
  41.9 5.2 %collective-permute-start.9 = (f32[1216]{0:T(1024)S(1)}, f32[1216]{0:T(1024)S(1)}, u32[]{:S(2)}, u32[]{:S(2)}) collective-permute-start(f32[1216]{0:T(1024)S(1)} %pad_maximum_fusion.15), channel_id=1, source_target_pairs={{0,1},{1,0},{2,3},{3,2},{4,5},{5,4},{6,7},{7,6},{8,9},{9,8},{10,11... | collective-permute-start | bytes 14600 | tf_op jit(solution)/shard_map/ppermute | solution.py:270
  49.1 39.0 %collective-permute-start.5 = (bf16[512,768]{1,0:T(8,128)(2,1)}, bf16[512,768]{1,0:T(8,128)(2,1)S(1)}, u32[]{:S(2)}, u32[]{:S(2)}) collective-permute-start(bf16[512,768]{1,0:T(8,128)(2,1)} %pad_maximum_fusion.7), channel_id=1, source_target_pairs={{0,5},{5,0},{1,4},{4,1},{2,7},{7,2},{3,6},{6,3},{8,13},{13,8},{9,1... | collective-permute-start | bytes 2359304 | tf_op jit(solution)/shard_map/ppermute | solution.py:856
  62.8 7.0 %collective-permute-start.2 = (bf16[1024,256]{1,0:T(8,128)(2,1)S(1)}, bf16[1024,256]{1,0:T(8,128)(2,1)S(1)}, u32[]{:S(2)}, u32[]{:S(2)}) collective-permute-start(bf16[1024,256]{1,0:T(8,128)(2,1)S(1)} %collective-permute-done.1.x2), channel_id=1, source_target_pairs={{0,2},{2,0},{1,3},{3,1},{4,6},{6,4},{5,7},{7,5},{8,10},{10,8},{9,1... | collective-permute-start | bytes 1572872 | tf_op jit(solution)/shard_map/ppermute | solution.py:270
  63.9 24.2 %copy-start.41 = (bf16[512,256]{1,0:T(8,128)(2,1)S(1)}, bf16[512,256]{1,0:T(8,128)(2,1)}, u32[]{:S(2)}) copy-start(bf16[512,256]{1,0:T(8,128)(2,1)} %param.23) | copy-start | bytes 786436
  63.9 24.3 %copy-start.6 = (bf16[2048,256]{1,0:T(8,128)(2,1)S(1)}, bf16[2048,256]{1,0:T(8,128)(2,1)}, u32[]{:S(2)}) copy-start(bf16[2048,256]{1,0:T(8,128)(2,1)} %param.33) | copy-start | bytes 3145732
  63.9 5.3 %collective-permute-start.7 = (f32[5,512]{1,0:T(8,128)S(1)}, f32[5,512]{1,0:T(8,128)S(1)}, u32[]{:S(2)}, u32[]{:S(2)}) collective-permute-start(f32[5,512]{1,0:T(8,128)S(1)} %pad_maximum_fusion.12), channel_id=1, source_target_pairs={{0,4},{4,0},{1,5},{5,1},{2,6},{6,2},{3,7},{7,3},{8,12},{12,8},{9,1... | collective-permute-start | bytes 30728 | tf_op jit(solution)/shard_map/ppermute | solution.py:270
  69.2 20.4 %copy-start.48 = (f32[5,512]{1,0:T(8,128)}, f32[5,512]{1,0:T(8,128)S(1)}, u32[]{:S(2)}) copy-start(f32[5,512]{1,0:T(8,128)S(1)} %collective-permute-done.7) | copy-start | bytes 30724
  69.8 19.9 %copy-start.3 = (bf16[1024,256]{1,0:T(8,128)(2,1)}, bf16[1024,256]{1,0:T(8,128)(2,1)S(1)}, u32[]{:S(2)}) copy-start(bf16[1024,256]{1,0:T(8,128)(2,1)S(1)} %collective-permute-done.x1) | copy-start | bytes 1572868
  69.8 19.9 %copy-start.5 = (bf16[1024,256]{1,0:T(8,128)(2,1)}, bf16[1024,256]{1,0:T(8,128)(2,1)S(1)}, u32[]{:S(2)}) copy-start(bf16[1024,256]{1,0:T(8,128)(2,1)S(1)} %collective-permute-done.2.x3) | copy-start | bytes 1572868
  88.1 8.3 %collective-permute-start.13 = (bf16[256,256]{1,0:T(8,128)(2,1)S(1)}, bf16[256,256]{1,0:T(8,128)(2,1)S(1)}, u32[]{:S(2)}, u32[]{:S(2)}) collective-permute-start(bf16[256,256]{1,0:T(8,128)(2,1)S(1)} %get-tuple-element.211), channel_id=1, source_target_pairs={{0,2},{2,0},{1,3},{3,1},{4,6},{6,4},{5,7},{7,5},{8,10},{10,8},{9,1... | collective-permute-start | bytes 393224 | tf_op jit(solution)/shard_map/ppermute | solution.py:270
  89.1 36.9 %collective-permute-start.17 = (bf16[1024,256]{1,0:T(8,128)(2,1)}, bf16[1024,256]{1,0:T(8,128)(2,1)}, u32[]{:S(2)}, u32[]{:S(2)}) collective-permute-start(bf16[1024,256]{1,0:T(8,128)(2,1)} %get-tuple-element.203), channel_id=1, source_target_pairs={{0,4},{4,0},{1,5},{5,1},{2,6},{6,2},{3,7},{7,3},{8,12},{12,8},{9,1... | collective-permute-start | bytes 1572872 | tf_op jit(solution)/shard_map/ppermute | solution.py:270
  89.6 52.7 %collective-permute-start.18 = (bf16[1024,256]{1,0:T(8,128)(2,1)S(1)}, bf16[1024,256]{1,0:T(8,128)(2,1)}, u32[]{:S(2)}, u32[]{:S(2)}) collective-permute-start(bf16[1024,256]{1,0:T(8,128)(2,1)S(1)} %get-tuple-element.202), channel_id=1, source_target_pairs={{0,2},{2,0},{1,3},{3,1},{4,6},{6,4},{5,7},{7,5},{8,10},{10,8},{9,1... | collective-permute-start | bytes 1572872 | tf_op jit(solution)/shard_map/ppermute | solution.py:270
  98.1 20.7 %collective-permute-start.15 = (bf16[256,512]{1,0:T(8,128)(2,1)S(1)}, bf16[256,512]{1,0:T(8,128)(2,1)}, u32[]{:S(2)}, u32[]{:S(2)}) collective-permute-start(bf16[256,512]{1,0:T(8,128)(2,1)S(1)} %pad_maximum_fusion.11), channel_id=1, source_target_pairs={{0,1},{1,0},{2,3},{3,2},{4,5},{5,4},{6,7},{7,6},{8,9},{9,8},{10,11... | collective-permute-start | bytes 786440 | tf_op jit(solution)/shard_map/ppermute | solution.py:270
  98.6 26.4 %collective-permute-start.16 = (bf16[256,512]{1,0:T(8,128)(2,1)S(1)}, bf16[256,512]{1,0:T(8,128)(2,1)}, u32[]{:S(2)}, u32[]{:S(2)}) collective-permute-start(bf16[256,512]{1,0:T(8,128)(2,1)S(1)} %pad_maximum_fusion.11), channel_id=1, source_target_pairs={{0,5},{5,0},{1,4},{4,1},{2,7},{7,2},{3,6},{6,3},{8,13},{13,8},{9,1... | collective-permute-start | bytes 786440 | tf_op jit(solution)/shard_map/ppermute | solution.py:856
  105.3 20.7 %collective-permute-start.14 = (bf16[256,512]{1,0:T(8,128)(2,1)S(1)}, bf16[256,512]{1,0:T(8,128)(2,1)}, u32[]{:S(2)}, u32[]{:S(2)}) collective-permute-start(bf16[256,512]{1,0:T(8,128)(2,1)S(1)} %pad_maximum_fusion.11), channel_id=1, source_target_pairs={{0,4},{4,0},{1,5},{5,1},{2,6},{6,2},{3,7},{7,3},{8,12},{12,8},{9,1... | collective-permute-start | bytes 786440 | tf_op jit(solution)/shard_map/ppermute | solution.py:270
  106.0 20.2 %copy-start.27 = (bf16[512,768]{1,0:T(8,128)(2,1)S(1)}, bf16[512,768]{1,0:T(8,128)(2,1)}, u32[]{:S(2)}) copy-start(bf16[512,768]{1,0:T(8,128)(2,1)} %copy-done.26) | copy-start | bytes 2359300
  126.0 17.4 %collective-permute-start.19 = (bf16[1024,256]{1,0:T(8,128)(2,1)}, bf16[1024,256]{1,0:T(8,128)(2,1)}, u32[]{:S(2)}, u32[]{:S(2)}) collective-permute-start(bf16[1024,256]{1,0:T(8,128)(2,1)} %collective-permute-done.17), channel_id=1, source_target_pairs={{0,2},{2,0},{1,3},{3,1},{4,6},{6,4},{5,7},{7,5},{8,10},{10,8},{9,1... | collective-permute-start | bytes 1572872 | tf_op jit(solution)/shard_map/ppermute | solution.py:270
  152.8 4.5 collective-permute-start.20
  201.2 128.6 %reduce-scatter.7.cloned.1.call-start = ((), (), s32[]{:S(2)}) async-start(), calls=%async_computation.3 | async-start | bytes 5242880
  202.8 10.9 %collective-permute-start.21 = (bf16[1024,1024]{1,0:T(8,128)(2,1)S(1)}, bf16[1024,1024]{1,0:T(8,128)(2,1)}, u32[]{:S(2)}, u32[]{:S(2)}) collective-permute-start(bf16[1024,1024]{1,0:T(8,128)(2,1)S(1)} %copy-done.7), channel_id=1, source_target_pairs={{0,2},{2,0},{1,3},{3,1},{4,6},{6,4},{5,7},{7,5},{8,10},{10,8},{9,1... | collective-permute-start | bytes 6291464 | tf_op jit(solution)/shard_map/ppermute | solution.py:270
  263.8 45.2 %collective-permute-start.22 = (bf16[512,256]{1,0:T(8,128)(2,1)}, bf16[512,256]{1,0:T(8,128)(2,1)}, u32[]{:S(2)}, u32[]{:S(2)}) collective-permute-start(bf16[512,256]{1,0:T(8,128)(2,1)} %convolution_convert_fusion.9), channel_id=1, source_target_pairs={{0,4},{4,0},{1,5},{5,1},{2,6},{6,2},{3,7},{7,3},{8,12},{12,8},{9,1... | collective-permute-start | bytes 786440 | tf_op jit(solution)/shard_map/ppermute | solution.py:270
  266.3 16.1 %collective-permute-start.25 = (bf16[512,512]{1,0:T(8,128)(2,1)S(1)}, bf16[512,512]{1,0:T(8,128)(2,1)S(1)}, u32[]{:S(2)}, u32[]{:S(2)}) collective-permute-start(bf16[512,512]{1,0:T(8,128)(2,1)S(1)} %dynamic-slice_bitcast_fusion.1), channel_id=1, source_target_pairs={{0,8},{8,0},{16,24},{24,16},{1,9},{9,1},{17,25},{25,17},{2,10},{10... | collective-permute-start | bytes 1572872 | tf_op jit(solution)/shard_map/ppermute | solution.py:881
  272.4 36.7 %collective-permute-start.23 = (bf16[512,256]{1,0:T(8,128)(2,1)S(1)}, bf16[512,256]{1,0:T(8,128)(2,1)S(1)}, u32[]{:S(2)}, u32[]{:S(2)}) collective-permute-start(bf16[512,256]{1,0:T(8,128)(2,1)S(1)} %convolution_convert_fusion.8), channel_id=1, source_target_pairs={{0,1},{1,0},{2,3},{3,2},{4,5},{5,4},{6,7},{7,6},{8,9},{9,8},{10,11... | collective-permute-start | bytes 786440 | tf_op jit(solution)/shard_map/ppermute | solution.py:270
  273.0 36.1 %collective-permute-start.24 = (bf16[512,256]{1,0:T(8,128)(2,1)S(1)}, bf16[512,256]{1,0:T(8,128)(2,1)S(1)}, u32[]{:S(2)}, u32[]{:S(2)}) collective-permute-start(bf16[512,256]{1,0:T(8,128)(2,1)S(1)} %convolution_convert_fusion.7), channel_id=1, source_target_pairs={{0,5},{5,0},{1,4},{4,1},{2,7},{7,2},{3,6},{6,3},{8,13},{13,8},{9,1... | collective-permute-start | bytes 786440 | tf_op jit(solution)/shard_map/ppermute | solution.py:856
  282.6 25.4 %collective-permute-start.26 = (bf16[512,512]{1,0:T(8,128)(2,1)S(1)}, bf16[512,512]{1,0:T(8,128)(2,1)S(1)}, u32[]{:S(2)}, u32[]{:S(2)}) collective-permute-start(bf16[512,512]{1,0:T(8,128)(2,1)S(1)} %fusion.44), channel_id=1, source_target_pairs={{0,16},{16,0},{8,24},{24,8},{1,17},{17,1},{9,25},{25,9},{2,18},{18... | collective-permute-start | bytes 1572872 | tf_op jit(solution)/shard_map/ppermute | solution.py:885
  287.4 27.2 %copy-start.11 = (bf16[1024,1024]{1,0:T(8,128)(2,1)}, bf16[1024,1024]{1,0:T(8,128)(2,1)S(1)}, u32[]{:S(2)}) copy-start(bf16[1024,1024]{1,0:T(8,128)(2,1)S(1)} %fusion.20.part_ref) | copy-start | bytes 6291460
  309.1 4.2 collective-permute-start.27
  322.2 3.8 collective-permute-start.28
  326.0 3.8 collective-permute-start.29
  330.9 11.8 %collective-permute-start.30 = (bf16[512,512]{1,0:T(8,128)(2,1)S(1)}, bf16[512,512]{1,0:T(8,128)(2,1)S(1)}, u32[]{:S(2)}, u32[]{:S(2)}) collective-permute-start(bf16[512,512]{1,0:T(8,128)(2,1)S(1)} %dynamic-slice_bitcast_fusion), channel_id=1, source_target_pairs={{0,8},{8,0},{16,24},{24,16},{1,9},{9,1},{17,25},{25,17},{2,10},{10... | collective-permute-start | bytes 1572872 | tf_op jit(solution)/shard_map/ppermute | solution.py:881
  333.6 35.9 %collective-permute-start.39 = (bf16[512,768]{1,0:T(8,128)(2,1)}, bf16[512,768]{1,0:T(8,128)(2,1)}, u32[]{:S(2)}, u32[]{:S(2)}) collective-permute-start(bf16[512,768]{1,0:T(8,128)(2,1)} %convolution_convert_fusion.2), channel_id=1, source_target_pairs={{0,5},{5,0},{1,4},{4,1},{2,7},{7,2},{3,6},{6,3},{8,13},{13,8},{9,1... | collective-permute-start | bytes 2359304 | tf_op jit(solution)/shard_map/ppermute | solution.py:856
  334.5 35.5 %collective-permute-start.38 = (bf16[512,768]{1,0:T(8,128)(2,1)}, bf16[512,768]{1,0:T(8,128)(2,1)}, u32[]{:S(2)}, u32[]{:S(2)}) collective-permute-start(bf16[512,768]{1,0:T(8,128)(2,1)} %convolution_convert_fusion.3), channel_id=1, source_target_pairs={{0,1},{1,0},{2,3},{3,2},{4,5},{5,4},{6,7},{7,6},{8,9},{9,8},{10,11... | collective-permute-start | bytes 2359304 | tf_op jit(solution)/shard_map/ppermute | solution.py:270
  335.7 34.4 %collective-permute-start.37 = (bf16[512,768]{1,0:T(8,128)(2,1)}, bf16[512,768]{1,0:T(8,128)(2,1)}, u32[]{:S(2)}, u32[]{:S(2)}) collective-permute-start(bf16[512,768]{1,0:T(8,128)(2,1)} %convolution_convert_fusion.4), channel_id=1, source_target_pairs={{0,4},{4,0},{1,5},{5,1},{2,6},{6,2},{3,7},{7,3},{8,12},{12,8},{9,1... | collective-permute-start | bytes 2359304 | tf_op jit(solution)/shard_map/ppermute | solution.py:270
  342.9 4.2 collective-permute-start.35
  345.3 26.9 %collective-permute-start.33 = (bf16[512,512]{1,0:T(8,128)(2,1)S(1)}, bf16[512,512]{1,0:T(8,128)(2,1)}, u32[]{:S(2)}, u32[]{:S(2)}) collective-permute-start(bf16[512,512]{1,0:T(8,128)(2,1)S(1)} %fusion.43), channel_id=1, source_target_pairs={{0,16},{16,0},{8,24},{24,8},{1,17},{17,1},{9,25},{25,9},{2,18},{18... | collective-permute-start | bytes 1572872 | tf_op jit(solution)/shard_map/ppermute | solution.py:885
  347.1 22.9 %copy-start.30 = (bf16[512,768]{1,0:T(8,128)(2,1)S(1)}, bf16[512,768]{1,0:T(8,128)(2,1)}, u32[]{:S(2)}) copy-start(bf16[512,768]{1,0:T(8,128)(2,1)} %convolution_convert_fusion.5) | copy-start | bytes 2359300
  347.1 21.8 %collective-permute-start.36 = (f32[2304]{0:T(1024)S(1)}, f32[2304]{0:T(1024)S(1)}, u32[]{:S(2)}, u32[]{:S(2)}) collective-permute-start(f32[2304]{0:T(1024)S(1)} %add.237), channel_id=1, source_target_pairs={{0,16},{16,0},{8,24},{24,8},{1,17},{17,1},{9,25},{25,9},{2,18},{18... | collective-permute-start | bytes 27656 | tf_op jit(solution)/shard_map/ppermute | solution.py:1016
  368.9 13.7 %collective-permute-start.31 = (bf16[1024,512]{1,0:T(8,128)(2,1)}, bf16[1024,512]{1,0:T(8,128)(2,1)}, u32[]{:S(2)}, u32[]{:S(2)}) collective-permute-start(bf16[1024,512]{1,0:T(8,128)(2,1)} %get-tuple-element.101), channel_id=1, source_target_pairs={{0,2},{2,0},{1,3},{3,1},{4,6},{6,4},{5,7},{7,5},{8,10},{10,8},{9,1... | collective-permute-start | bytes 3145736 | tf_op jit(solution)/shard_map/ppermute | solution.py:270
  369.4 7.8 %collective-permute-start.46 = (f32[1024]{0:T(1024)S(1)}, f32[1024]{0:T(1024)S(1)}, u32[]{:S(2)}, u32[]{:S(2)}) collective-permute-start(f32[1024]{0:T(1024)S(1)} %slice.249), channel_id=1, source_target_pairs={{0,2},{2,0},{1,3},{3,1},{4,6},{6,4},{5,7},{7,5},{8,10},{10,8},{9,1... | collective-permute-start | bytes 12296 | tf_op jit(solution)/shard_map/ppermute | solution.py:270
  376.5 15.1 %collective-permute-start.40 = (bf16[256,1024]{0,1:T(8,128)(2,1)}, bf16[256,1024]{0,1:T(8,128)(2,1)}, u32[]{:S(2)}, u32[]{:S(2)}) collective-permute-start(bf16[256,1024]{0,1:T(8,128)(2,1)} %bitcast.164), channel_id=1, source_target_pairs={{0,8},{8,0},{16,24},{24,16},{1,9},{9,1},{17,25},{25,17},{2,10},{10... | collective-permute-start | bytes 1572872 | tf_op jit(solution)/shard_map/ppermute | solution.py:881
  377.9 36.2 %collective-permute-start.44 = (bf16[512,512]{1,0:T(8,128)(2,1)S(1)}, bf16[512,512]{1,0:T(8,128)(2,1)}, u32[]{:S(2)}, u32[]{:S(2)}) collective-permute-start(bf16[512,512]{1,0:T(8,128)(2,1)S(1)} %add_convert_fusion.2), channel_id=1, source_target_pairs={{0,8},{8,0},{16,24},{24,16},{1,9},{9,1},{17,25},{25,17},{2,10},{10... | collective-permute-start | bytes 1572872 | tf_op jit(solution)/shard_map/ppermute | solution.py:889
  379.1 15.1 %collective-permute-start.34 = (bf16[1024,256]{1,0:T(8,128)(2,1)}, bf16[1024,256]{1,0:T(8,128)(2,1)}, u32[]{:S(2)}, u32[]{:S(2)}) collective-permute-start(bf16[1024,256]{1,0:T(8,128)(2,1)} %get-tuple-element.104), channel_id=1, source_target_pairs={{0,4},{4,0},{1,5},{5,1},{2,6},{6,2},{3,7},{7,3},{8,12},{12,8},{9,1... | collective-permute-start | bytes 1572872 | tf_op jit(solution)/shard_map/ppermute | solution.py:270
  381.5 42.8 %collective-permute-start.47 = (bf16[512,512]{1,0:T(8,128)(2,1)S(1)}, bf16[512,512]{1,0:T(8,128)(2,1)S(1)}, u32[]{:S(2)}, u32[]{:S(2)}) collective-permute-start(bf16[512,512]{1,0:T(8,128)(2,1)S(1)} %copy-done.8), channel_id=1, source_target_pairs={{0,8},{8,0},{16,24},{24,16},{1,9},{9,1},{17,25},{25,17},{2,10},{10... | collective-permute-start | bytes 1572872 | tf_op jit(solution)/shard_map/ppermute | solution.py:889
  385.0 43.4 %collective-permute-start.32 = (bf16[1024,256]{1,0:T(8,128)(2,1)S(1)}, bf16[1024,256]{1,0:T(8,128)(2,1)S(1)}, u32[]{:S(2)}, u32[]{:S(2)}) collective-permute-start(bf16[1024,256]{1,0:T(8,128)(2,1)S(1)} %slice.234), channel_id=1, source_target_pairs={{0,4},{4,0},{1,5},{5,1},{2,6},{6,2},{3,7},{7,3},{8,12},{12,8},{9,1... | collective-permute-start | bytes 1572872 | tf_op jit(solution)/shard_map/ppermute | solution.py:270
  394.3 34.0 %collective-permute-start.41 = (bf16[256,1024]{0,1:T(8,128)(2,1)S(1)}, bf16[256,1024]{0,1:T(8,128)(2,1)S(1)}, u32[]{:S(2)}, u32[]{:S(2)}) collective-permute-start(bf16[256,1024]{0,1:T(8,128)(2,1)S(1)} %fusion.42), channel_id=1, source_target_pairs={{0,16},{16,0},{8,24},{24,8},{1,17},{17,1},{9,25},{25,9},{2,18},{18... | collective-permute-start | bytes 1572872 | tf_op jit(solution)/shard_map/ppermute | solution.py:885
  415.3 14.4 %collective-permute-start.45 = (bf16[256,1024]{1,0:T(8,128)(2,1)S(1)}, bf16[256,1024]{1,0:T(8,128)(2,1)S(1)}, u32[]{:S(2)}, u32[]{:S(2)}) collective-permute-start(bf16[256,1024]{1,0:T(8,128)(2,1)S(1)} %pad_maximum_fusion.8), channel_id=1, source_target_pairs={{0,2},{2,0},{1,3},{3,1},{4,6},{6,4},{5,7},{7,5},{8,10},{10,8},{9,1... | collective-permute-start | bytes 1572872 | tf_op jit(solution)/shard_map/ppermute | solution.py:270
  424.5 17.5 %collective-permute-start.48 = (bf16[1024,256]{1,0:T(8,128)(2,1)S(1)}, bf16[1024,256]{1,0:T(8,128)(2,1)S(1)}, u32[]{:S(2)}, u32[]{:S(2)}) collective-permute-start(bf16[1024,256]{1,0:T(8,128)(2,1)S(1)} %slice.251), channel_id=1, source_target_pairs={{0,2},{2,0},{1,3},{3,1},{4,6},{6,4},{5,7},{7,5},{8,10},{10,8},{9,1... | collective-permute-start | bytes 1572872 | tf_op jit(solution)/shard_map/ppermute | solution.py:270
  428.4 13.4 %collective-permute-start.42 = (bf16[256,1024]{0,1:T(8,128)(2,1)S(1)}, bf16[256,1024]{0,1:T(8,128)(2,1)S(1)}, u32[]{:S(2)}, u32[]{:S(2)}) collective-permute-start(bf16[256,1024]{0,1:T(8,128)(2,1)S(1)} %add_convert_fusion.1), channel_id=1, source_target_pairs={{0,8},{8,0},{16,24},{24,16},{1,9},{9,1},{17,25},{25,17},{2,10},{10... | collective-permute-start | bytes 1572872 | tf_op jit(solution)/shard_map/ppermute | solution.py:889
  441.9 2.0 collective-permute-start.43
  (59 other events, 456.5 us)
Sparse Core Ops, SparseCore 0:
  35.8 124.2 all-gather.2
  201.4 51.6 reduce-scatter.8
  256.1 63.8 reduce-scatter.6

commit v7 on v6

--- a/solution.py
+++ b/solution.py
@@ -1004,7 +1004,7 @@
     theirs = swap(after(theirs, up_far), "y")
     grad_inputs = ordered(mine, theirs.astype(FULL), y_at).reshape(2 * length, n)
     ends_own, ends_other = layer_end(at, after(hiddens, up_part), ffn)
-    down_total = depth_join(after(down_part, up_far), odd)
+    down_total = depth_join(after(down_part, ends_own), odd)
     kept_two = jnp.concatenate((residual[:, :n], residual[:, 2 * n : 3 * n]), axis=1)
     bias_two = jnp.concatenate((bias_low[:, :n], bias_low[:, 2 * n : 3 * n]), axis=1)
     ends = (kept_two + ends_own + swap(ends_other, "core").astype(FULL) + bias_two).astype(LOW)

time: 461 us -> 469 us (1.017)
  starting transfers between devices: 53.2 us -> 58.6 us
    ppermute x3, waiting for transfers between devices: 38.6 us -> 11.2 us  [depth_join(): lax.ppermute(part, 'dp', PAIRS)]
    ppermute x3, waiting for transfers between devices: 20.6 us -> 38.2 us  [depth_far(): return add_low(part, lax.ppermute(part, 'dp', FAR))]
    ppermute x3, waiting for transfers between devices: 18.6 us -> 28.8 us  [depth_pair(): lax.ppermute(pick(halves, 1 - odd), 'dp', PAIRS)]
    ppermute x33, starting transfers between devices: 23 us -> 29.6 us  [swap(): return lax.ppermute(array, axis, SWAP)]
where the time goes in v7:
time: 469 us; the launch traced here: 463 us
  waiting for transfers between devices  147 us (31%)
  Pallas kernels  141 us (30%)
  starting transfers between devices  58.6 us (12%)
  other arithmetic  36.1 us (8%)
  local copies, waits for them, and re-layouts  35 us (7%)
  matrix products  29.9 us (6%)
  between operations  15.3 us (3%)
    ppermute x3, waiting for transfers between devices, depth_far(): return add_low(part, lax.ppermute(part, 'dp', FAR))  38.2 us
    ppermute x33, waiting for transfers between devices, swap(): return lax.ppermute(array, axis, SWAP)  35.4 us
    ppermute x33, starting transfers between devices, swap(): return lax.ppermute(array, axis, SWAP)  29.6 us
    ppermute x3, waiting for transfers between devices, depth_pair(): lax.ppermute(pick(halves, 1 - odd), 'dp', PAIRS)  28.8 us
    pallas_call x2, Pallas kernels, attend_backward(): pl.pallas_call(attend_backward_kernel, out_shape=jax.ShapeDtypeStruct((le...  27.6 us
    pallas_call x1, Pallas kernels, feed_forward(): pl.pallas_call(feed_forward_kernel, out_shape=(jax.ShapeDtypeStruct((leng...  27.1 us
    pallas_call x2, Pallas kernels, attend_forward(): pl.pallas_call(attend_forward_kernel, out_shape=(jax.ShapeDtypeStruct((le...  25.9 us
    ppermute x4, waiting for transfers between devices, swap_across(): return lax.ppermute(array, ('y', 'col'), [(0, 3), (3, 0), (1, 2), (2, 1)])  23.3 us
  transfers between devices with their start and end apart: 52, of which 21 were waited for; matrix products, arithmetic and copies ran while one was open for 18% of the time, Pallas kernels for 23%

profile of v7, /device:TPU:0, one launch (start us, length us, event | category | flops | bytes accessed | tf_op | source)
XLA Modules:
  0.0 463.0 jit_solution(7168115740861532029)
XLA Ops:
  13.3 2.9 collective-permute-start.8
  16.1 1.5 collective-permute-start.10
  17.7 1.5 fusion.16
  19.3 15.0 %collective-permute-done.8 = bf16[512,768]{1,0:T(8,128)(2,1)} collective-permute-done((bf16[512,768]{1,0:T(8,128)(2,1)}, bf16[512,768]{1,0:T(8,128)(2,1)}, u32[]{:S(2)}, u32[]{:S(2)}) %collective-permute-start.8) | collective-permute-done | bytes 786464 | tf_op jit(solution)/shard_map/ppermute | solution.py:270
  38.5 3.1 collective-permute-start.6
  49.1 13.3 %collective-permute-start.5 = (bf16[512,768]{1,0:T(8,128)(2,1)}, bf16[512,768]{1,0:T(8,128)(2,1)S(1)}, u32[]{:S(2)}, u32[]{:S(2)}) collective-permute-start(bf16[512,768]{1,0:T(8,128)(2,1)} %pad_maximum_fusion.7), channel_id=1, source_target_pairs={{0,5},{5,0},{1,4},{4,1},{2,7},{7,2},{3,6},{6,3},{8,13},{13,8},{9,1... | collective-permute-start | bytes 2359304 | tf_op jit(solution)/shard_map/ppermute | solution.py:856
  63.9 2.5 collective-permute-start.7
  66.4 1.6 pad_maximum_fusion.3
  69.8 18.2 %collective-permute-done.5 = bf16[512,768]{1,0:T(8,128)(2,1)S(1)} collective-permute-done((bf16[512,768]{1,0:T(8,128)(2,1)}, bf16[512,768]{1,0:T(8,128)(2,1)S(1)}, u32[]{:S(2)}, u32[]{:S(2)}) %collective-permute-start.5) | collective-permute-done | bytes 786464 | tf_op jit(solution)/shard_map/ppermute | solution.py:856
  89.7 5.0 %first_norm.1 = (bf16[1024,512]{1,0:T(8,128)(2,1)}, bf16[1024,512]{1,0:T(8,128)(2,1)}) custom-call(bf16[1024,256]{1,0:T(8,128)(2,1)} %copy-done.2, bf16[1024,256]{1,0:T(8,128)(2,1)} %copy-done.3, bf16[1024,256]{1,0:T(8,128)(2,1)} %copy-done.4, bf16[1024,256]{1,0:T(8,128)(2,1)} %copy-done.5, f32[1,1024]{1,0:T(1,128)} %get-tuple-element.223.gain_ref, ...), custom_call_target="tpu_custom_call" | custom-call | flops 5242880 | bytes 4194304 | tf_op jit(solution)/shard_map/first_norm/pallas_call | solution.py:536
  94.7 1.5 constant_dynamic-update-slice_fusion.1
  98.6 2.6 collective-permute-start.16
  101.2 4.1 convolution_convert_fusion.1.q_ref.k_ref.v_ref
  106.0 12.8 %attend_forward.2 = (bf16[1024,256]{1,0:T(8,128)(2,1)}, bf16[4,1024,128]{2,1,0:T(8,128)(2,1)}) custom-call(s32[2,4]{1,0:T(2,128)} %pad_add_fusion.1.where_ref, bf16[1024,768]{1,0:T(8,128)(2,1)} %convolution_convert_fusion.1.q_ref.k_ref.v_ref, bf16[1024,768]{1,0:T(8,128)(2,1)} %convolution_convert_fusion.1.q_ref.k_ref.v_ref, ...), custom_call_target="tpu_custom_call" | custom-call | flops 1073741824 | bytes 12582912 | tf_op jit(solution)/shard_map/attend_forward/pallas_call | solution.py:377
  120.0 5.1 %collective-permute-done.16 = bf16[256,512]{1,0:T(8,128)(2,1)} collective-permute-done((bf16[256,512]{1,0:T(8,128)(2,1)S(1)}, bf16[256,512]{1,0:T(8,128)(2,1)}, u32[]{:S(2)}, u32[]{:S(2)}) %collective-permute-start.16) | collective-permute-done | bytes 262176 | tf_op jit(solution)/shard_map/ppermute | solution.py:856
  126.3 2.9 convolution_convert_fusion.q_ref.k_ref.v_ref
  129.2 13.0 %attend_forward.3 = (bf16[1024,256]{1,0:T(8,128)(2,1)}, bf16[4,1024,128]{2,1,0:T(8,128)(2,1)}) custom-call(s32[2,4]{1,0:T(2,128)} %pad_add_fusion.1.where_ref, bf16[1024,768]{1,0:T(8,128)(2,1)} %convolution_convert_fusion.q_ref.k_ref.v_ref, bf16[1024,768]{1,0:T(8,128)(2,1)} %convolution_convert_fusion.q_ref.k_ref.v_ref, ...), custom_call_target="tpu_custom_call" | custom-call | flops 1073741824 | bytes 12582912 | tf_op jit(solution)/shard_map/attend_forward/pallas_call | solution.py:377
  144.7 1.5 pad_maximum_fusion.1.c_ref.cots_ref
  148.0 4.8 %mix_heads.1.part_ref = bf16[1024,1024]{1,0:T(8,128)(2,1)} custom-call(bf16[1024,256]{1,0:T(8,128)(2,1)} %get-tuple-element.70.h0.heads_ref, bf16[1024,256]{1,0:T(8,128)(2,1)} %get-tuple-element.76.h1.heads_ref, bf16[256,1024]{1,0:T(8,128)(2,1)} %copy-done.17, bf16[256,1024]{1,0:T(8,128)(2,1)} %copy-done.15), custom_call_target="tpu_custom_call" | custom-call | flops 1073741824 | bytes 5242880 | tf_op jit(solution)/shard_map/mix_heads/pallas_call | solution.py:657
  154.5 2.8 collective-permute-done.20.got_ref
  158.6 6.3 %second_norm.1 = (f32[1024,1024]{1,0:T(8,128)}, bf16[2,1024,512]{2,1,0:T(8,128)(2,1)}) custom-call(bf16[1024,256]{1,0:T(8,128)(2,1)} %copy-done.2, bf16[1024,256]{1,0:T(8,128)(2,1)} %copy-done.3, bf16[1024,256]{1,0:T(8,128)(2,1)} %copy-done.4, bf16[1024,256]{1,0:T(8,128)(2,1)} %copy-done.5, bf16[1024,1024]{1,0:T(8,128)(2,1)} %mix_heads.1.part_ref, ...), custom_call_target="tpu_custom_call" | custom-call | flops 7864320 | bytes 12582912 | tf_op jit(solution)/shard_map/second_norm/pallas_call | solution.py:563
  164.9 27.1 %feed_forward.1 = (bf16[1024,1024]{1,0:T(8,128)(2,1)}, bf16[2,1024,1024]{2,1,0:T(8,128)(2,1)}, bf16[2,1024,1024]{2,1,0:T(8,128)(2,1)}, f32[8,8,256]{2,1,0:T(8,128)}) custom-call(s32[2]{0:T(128)} %pad_add_fusion.2.at_ref, bf16[2,1024,512]{2,1,0:T(8,128)(2,1)} %get-tuple-element.79.s_ref, bf16[2,1024,512]{2,1,0:T(8,128)(2,1)} %pad_maximum_fusion.1.c_ref.cots_ref, ...), custom_call_target="tpu_custom_call" | custom-call | flops 12884901888 | bytes 29360128 | tf_op jit(solution)/shard_map/feed_forward/pallas_call | solution.py:728
  192.0 9.2 %down_grads.1 = bf16[2,2,1024,512]{3,2,1,0:T(8,128)(2,1)} custom-call(s32[2]{0:T(128)} %pad_add_fusion.2.at_ref, bf16[2,1024,1024]{2,1,0:T(8,128)(2,1)} %get-tuple-element.99.hidden_ref.h0.h1, bf16[2,1024,512]{2,1,0:T(8,128)(2,1)} %pad_maximum_fusion.1.c_ref.cots_ref), custom_call_target="tpu_custom_call" | custom-call | flops 4294967296 | bytes 8388608 | tf_op jit(solution)/shard_map/down_grads/pallas_call | solution.py:792
  201.3 1.5 copy-done.7
  203.2 10.5 %up_grads.1 = bf16[4,1024,512]{2,1,0:T(8,128)(2,1)} custom-call(s32[2]{0:T(128)} %pad_add_fusion.2.at_ref, bf16[2,1024,512]{2,1,0:T(8,128)(2,1)} %get-tuple-element.79.s_ref, bf16[2,1024,1024]{2,1,0:T(8,128)(2,1)} %get-tuple-element.83.grad_ref), custom_call_target="tpu_custom_call" | custom-call | flops 4294967296 | bytes 8388608 | tf_op jit(solution)/shard_map/up_grads/pallas_call | solution.py:765
  213.7 8.0 %second_norm_back.1 = (f32[1024,256]{1,0:T(8,128)}, f32[1024,256]{1,0:T(8,128)}, bf16[1024,1024]{1,0:T(8,128)(2,1)}, f32[8,512]{1,0:T(8,128)}) custom-call(f32[1024,1024]{1,0:T(8,128)} %get-tuple-element.78.residual_ref, bf16[1024,1024]{1,0:T(8,128)(2,1)} %get-tuple-element.85.part_ref, bf16[1024,1024]{1,0:T(8,128)(2,1)} %collective-permute-done.21.got_ref, ...), custom_call_target="tpu_custom_call" | custom-call | flops 15728640 | bytes 16777216 | tf_op jit(solution)/shard_map/second_norm_back/pallas_call | solution.py:611
  221.7 4.0 select_convert_fusion.1.grads_ref
  225.7 13.7 %attend_backward.2 = bf16[1024,768]{1,0:T(8,128)(2,1)} custom-call(s32[2,4]{1,0:T(2,128)} %pad_add_fusion.1.where_ref, bf16[4,1024,128]{2,1,0:T(8,128)(2,1)} %get-tuple-element.84.kept_ref, bf16[1024,768]{1,0:T(8,128)(2,1)} %convolution_convert_fusion.1.q_ref.k_ref.v_ref, bf16[1024,768]{1,0:T(8,128)(2,1)} %convolution_convert_fusion.1.q_ref.k_ref.v_ref, ...), custom_call_target="tpu_custom_call" | custom-call | flops 2684354560 | bytes 15728640 | tf_op jit(solution)/shard_map/attend_backward/pallas_call | solution.py:467
  239.4 13.9 %attend_backward.3 = bf16[1024,768]{1,0:T(8,128)(2,1)} custom-call(s32[2,4]{1,0:T(2,128)} %pad_add_fusion.1.where_ref, bf16[4,1024,128]{2,1,0:T(8,128)(2,1)} %get-tuple-element.88.kept_ref, bf16[1024,768]{1,0:T(8,128)(2,1)} %convolution_convert_fusion.q_ref.k_ref.v_ref, bf16[1024,768]{1,0:T(8,128)(2,1)} %convolution_convert_fusion.q_ref.k_ref.v_ref, ...), custom_call_target="tpu_custom_call" | custom-call | flops 2684354560 | bytes 15728640 | tf_op jit(solution)/shard_map/attend_backward/pallas_call | solution.py:467
  253.4 3.5 convolution_convert_fusion.5
  256.9 1.9 convolution_convert_fusion.4
  258.8 1.9 convolution_convert_fusion.3
  260.7 1.9 convolution_convert_fusion.2
  266.4 1.5 collective-permute-start.25
  267.9 1.9 convolution_convert_fusion.8
  269.8 2.7 collective-permute-start.23
  273.0 6.9 %collective-permute-done.25 = bf16[512,512]{1,0:T(8,128)(2,1)S(1)} collective-permute-done((bf16[512,512]{1,0:T(8,128)(2,1)S(1)}, bf16[512,512]{1,0:T(8,128)(2,1)S(1)}, u32[]{:S(2)}, u32[]{:S(2)}) %collective-permute-start.25) | collective-permute-done | bytes 524320 | tf_op jit(solution)/shard_map/ppermute | solution.py:881
  280.1 2.5 collective-permute-start.26
  282.6 4.7 %fusion.20.part_ref = bf16[1024,1024]{1,0:T(8,128)(2,1)S(1)} fusion(bf16[1024,768]{1,0:T(8,128)(2,1)S(1)} %copy-done.38, bf16[512,768]{1,0:T(8,128)(2,1)} %collective-permute-done.8, bf16[256,768]{1,0:T(8,128)(2,1)S(1)} %copy-done.41, bf16[256,256]{1,0:T(8,128)(2,1)S(1)} %get-tuple-element.218, bf16[256,256]{1,0:T(8,128)(2,1)S(1)} %get-tuple-element.244, ...), kind=kOutput, calls=%fused_computation.30 | convolution fusion | flops 3247439872 | bytes 8388608 | tf_op jit(solution)/shard_map/dot_general | solution.py:278
  287.3 17.8 %collective-permute-done.26 = bf16[512,512]{1,0:T(8,128)(2,1)S(1)} collective-permute-done((bf16[512,512]{1,0:T(8,128)(2,1)S(1)}, bf16[512,512]{1,0:T(8,128)(2,1)S(1)}, u32[]{:S(2)}, u32[]{:S(2)}) %collective-permute-start.26) | collective-permute-done | bytes 524320 | tf_op jit(solution)/shard_map/ppermute | solution.py:885
  308.0 2.3 collective-permute-done.27.got_ref
  311.7 6.8 %first_norm_back.1 = (f32[1024,256]{1,0:T(8,128)}, bf16[1024,256]{1,0:T(8,128)(2,1)}, f32[8,512]{1,0:T(8,128)}) custom-call(bf16[1024,256]{1,0:T(8,128)(2,1)} %copy-done.2, bf16[1024,256]{1,0:T(8,128)(2,1)} %copy-done.3, bf16[1024,256]{1,0:T(8,128)(2,1)} %copy-done.4, bf16[1024,256]{1,0:T(8,128)(2,1)} %copy-done.5, bf16[1024,1024]{1,0:T(8,128)(2,1)} %copy-done.13, ...), custom_call_target="tpu_custom_call" | custom-call | flops 15728640 | bytes 10485760 | tf_op jit(solution)/shard_map/first_norm_back/pallas_call | solution.py:634
  320.3 2.7 collective-permute-done.28
  323.0 4.4 collective-permute-start.29
  327.4 1.7 collective-permute-done.29
  331.0 1.8 fusion.76
  332.9 9.3 %collective-permute-done.30 = bf16[512,512]{1,0:T(8,128)(2,1)S(1)} collective-permute-done((bf16[512,512]{1,0:T(8,128)(2,1)S(1)}, bf16[512,512]{1,0:T(8,128)(2,1)S(1)}, u32[]{:S(2)}, u32[]{:S(2)}) %collective-permute-start.30) | collective-permute-done | bytes 524320 | tf_op jit(solution)/shard_map/ppermute | solution.py:881
  344.2 1.7 collective-permute-start.39
  346.1 1.6 collective-permute-start.37
  347.7 2.4 collective-permute-start.33
  350.7 9.6 %layer_end.1 = (f32[1024,512]{1,0:T(8,128)}, bf16[1024,512]{1,0:T(8,128)(2,1)}) custom-call(s32[2]{0:T(128)} %pad_add_fusion.2.at_ref, bf16[2,1024,1024]{2,1,0:T(8,128)(2,1)} %get-tuple-element.99.hidden_ref.h0.h1, bf16[2,1024,1024]{2,1,0:T(8,128)(2,1)} %get-tuple-element.99.hidden_ref.h0.h1, bf16[4,2048,512]{2,1,0:T(8,128)(2,1)} %bitcast.144, ...), custom_call_target="tpu_custom_call" | custom-call | flops 4294967296 | bytes 10485760 | tf_op jit(solution)/shard_map/layer_end/pallas_call | solution.py:828
  360.3 10.3 %collective-permute-done.36 = f32[2304]{0:T(1024)S(1)} collective-permute-done((f32[2304]{0:T(1024)S(1)}, f32[2304]{0:T(1024)S(1)}, u32[]{:S(2)}, u32[]{:S(2)}) %collective-permute-start.36) | collective-permute-done | bytes 9248 | tf_op jit(solution)/shard_map/ppermute | solution.py:1016
  372.8 5.3 %collective-permute-done.38 = bf16[512,768]{1,0:T(8,128)(2,1)} collective-permute-done((bf16[512,768]{1,0:T(8,128)(2,1)}, bf16[512,768]{1,0:T(8,128)(2,1)}, u32[]{:S(2)}, u32[]{:S(2)}) %collective-permute-start.38) | collective-permute-done | bytes 786464 | tf_op jit(solution)/shard_map/ppermute | solution.py:270
  379.0 2.2 add_convert_fusion
  382.6 1.5 collective-permute-start.44
  385.7 2.0 copy.63
  388.4 2.1 select_bitcast_fusion.1
  393.6 1.8 fusion.19
  395.4 1.5 collective-permute-start.32
  396.9 12.6 %collective-permute-done.40 = bf16[256,1024]{0,1:T(8,128)(2,1)} collective-permute-done((bf16[256,1024]{0,1:T(8,128)(2,1)}, bf16[256,1024]{0,1:T(8,128)(2,1)}, u32[]{:S(2)}, u32[]{:S(2)}) %collective-permute-start.40) | collective-permute-done | bytes 524320 | tf_op jit(solution)/shard_map/ppermute | solution.py:881
  414.2 1.5 maximum_convert_fusion.1
  415.7 20.4 %collective-permute-done.41 = bf16[256,1024]{0,1:T(8,128)(2,1)S(1)} collective-permute-done((bf16[256,1024]{0,1:T(8,128)(2,1)S(1)}, bf16[256,1024]{0,1:T(8,128)(2,1)S(1)}, u32[]{:S(2)}, u32[]{:S(2)}) %collective-permute-start.41) | collective-permute-done | bytes 524320 | tf_op jit(solution)/shard_map/ppermute | solution.py:885
  439.0 11.2 %collective-permute-done.42 = bf16[256,1024]{0,1:T(8,128)(2,1)S(1)} collective-permute-done((bf16[256,1024]{0,1:T(8,128)(2,1)S(1)}, bf16[256,1024]{0,1:T(8,128)(2,1)S(1)}, u32[]{:S(2)}, u32[]{:S(2)}) %collective-permute-start.42) | collective-permute-done | bytes 524320 | tf_op jit(solution)/shard_map/ppermute | solution.py:889
  450.6 1.6 maximum_convert_fusion
  (338 shorter events, 72.4 us)
Async XLA Ops:
  7.2 34.4 %copy-start = (s32[8,16,3]{1,0,2:T(8,128)S(1)}, s32[8,16,3]{1,0,2:T(8,128)}, u32[]{:S(2)}) copy-start(s32[8,16,3]{1,0,2:T(8,128)} %param.31) | copy-start | bytes 4612
  7.2 157.7 %all-gather.3.cloned.1.call-start = ((), (), s32[]{:S(2)}) async-start(), calls=%async_computation.2 | async-start | bytes 10485760 | tf_op jit(solution)/shard_map/all_gather | solution.py:923
  9.5 1.9 collective-permute-start.4
  12.5 5.1 %collective-permute-start.11 = (bf16[256,1024]{1,0:T(8,128)(2,1)S(1)}, bf16[256,1024]{1,0:T(8,128)(2,1)S(1)}, u32[]{:S(2)}, u32[]{:S(2)}) collective-permute-start(bf16[256,1024]{1,0:T(8,128)(2,1)S(1)} %get-tuple-element.207), channel_id=1, source_target_pairs={{0,2},{2,0},{1,3},{3,1},{4,6},{6,4},{5,7},{7,5},{8,10},{10,8},{9,1... | collective-permute-start | bytes 1572872 | tf_op jit(solution)/shard_map/ppermute | solution.py:270
  13.1 4.6 collective-permute-start.12
  13.3 21.0 %collective-permute-start.8 = (bf16[512,768]{1,0:T(8,128)(2,1)}, bf16[512,768]{1,0:T(8,128)(2,1)}, u32[]{:S(2)}, u32[]{:S(2)}) collective-permute-start(bf16[512,768]{1,0:T(8,128)(2,1)} %pad_maximum_fusion.7), channel_id=1, source_target_pairs={{0,4},{4,0},{1,5},{5,1},{2,6},{6,2},{3,7},{7,3},{8,12},{12,8},{9,1... | collective-permute-start | bytes 2359304 | tf_op jit(solution)/shard_map/ppermute | solution.py:270
  16.1 19.5 %collective-permute-start.10 = (bf16[512,768]{1,0:T(8,128)(2,1)}, bf16[512,768]{1,0:T(8,128)(2,1)S(1)}, u32[]{:S(2)}, u32[]{:S(2)}) collective-permute-start(bf16[512,768]{1,0:T(8,128)(2,1)} %pad_maximum_fusion.7), channel_id=1, source_target_pairs={{0,1},{1,0},{2,3},{3,2},{4,5},{5,4},{6,7},{7,6},{8,9},{9,8},{10,11... | collective-permute-start | bytes 2359304 | tf_op jit(solution)/shard_map/ppermute | solution.py:270
  19.2 22.6 %copy-start.52 = (f32[2048]{0:T(1024)S(1)}, f32[2048]{0:T(1024)}, u32[]{:S(2)}) copy-start(f32[2048]{0:T(1024)} %param.27) | copy-start | bytes 24580
  19.2 24.1 %copy-start.65 = (s32[2]{0:T(128)S(1)}, s32[2]{0:T(128)}, u32[]{:S(2)}) copy-start(s32[2]{0:T(128)} %param.32) | copy-start | bytes 28
  35.7 229.5 %reduce-scatter.9.cloned.1.call-start = ((), (), s32[]{:S(2)}) async-start(), calls=%async_computation.4 | async-start | bytes 5242880
  37.4 32.4 %collective-permute-start = (bf16[1024,256]{1,0:T(8,128)(2,1)S(1)}, bf16[1024,256]{1,0:T(8,128)(2,1)S(1)}, u32[]{:S(2)}, u32[]{:S(2)}) collective-permute-start(bf16[1024,256]{1,0:T(8,128)(2,1)S(1)} %get-tuple-element.64.x0), channel_id=1, source_target_pairs={{0,2},{2,0},{1,3},{3,1},{4,6},{6,4},{5,7},{7,5},{8,10},{10,8},{9,1... | collective-permute-start | bytes 1572872 | tf_op jit(solution)/shard_map/ppermute | solution.py:270
  37.4 25.4 %collective-permute-start.1 = (bf16[1024,256]{1,0:T(8,128)(2,1)}, bf16[1024,256]{1,0:T(8,128)(2,1)S(1)}, u32[]{:S(2)}, u32[]{:S(2)}) collective-permute-start(bf16[1024,256]{1,0:T(8,128)(2,1)} %get-tuple-element.208), channel_id=1, source_target_pairs={{0,4},{4,0},{1,5},{5,1},{2,6},{6,2},{3,7},{7,3},{8,12},{12,8},{9,1... | collective-permute-start | bytes 1572872 | tf_op jit(solution)/shard_map/ppermute | solution.py:270
  37.8 5.6 %collective-permute-start.3 = (s32[1,1024]{1,0:T(1,128)S(1)}, s32[1,1024]{1,0:T(1,128)S(1)}, u32[]{:S(2)}, u32[]{:S(2)}) collective-permute-start(s32[1,1024]{1,0:T(1,128)S(1)} %copy-done.64), channel_id=1, source_target_pairs={{0,0},{4,1},{1,2},{5,3},{2,4},{6,5},{3,6},{7,7},{8,8},{12,9},{9,10... | collective-permute-start | bytes 12296 | tf_op jit(solution)/shard_map/ppermute | solution.py:942
  38.5 24.7 %copy-start.44 = (f32[5,256]{1,0:T(8,128)}, f32[5,256]{1,0:T(8,128)S(1)}, u32[]{:S(2)}) copy-start(f32[5,256]{1,0:T(8,128)S(1)} %stack.107) | copy-start | bytes 15364
  38.5 24.7 %collective-permute-start.6 = (f32[5,256]{1,0:T(8,128)S(1)}, f32[5,256]{1,0:T(8,128)S(1)}, u32[]{:S(2)}, u32[]{:S(2)}) collective-permute-start(f32[5,256]{1,0:T(8,128)S(1)} %stack.107), channel_id=1, source_target_pairs={{0,2},{2,0},{1,3},{3,1},{4,6},{6,4},{5,7},{7,5},{8,10},{10,8},{9,1... | collective-permute-start | bytes 15368 | tf_op jit(solution)/shard_map/ppermute | solution.py:270
  41.9 5.2 %collective-permute-start.9 = (f32[1216]{0:T(1024)S(1)}, f32[1216]{0:T(1024)S(1)}, u32[]{:S(2)}, u32[]{:S(2)}) collective-permute-start(f32[1216]{0:T(1024)S(1)} %pad_maximum_fusion.15), channel_id=1, source_target_pairs={{0,1},{1,0},{2,3},{3,2},{4,5},{5,4},{6,7},{7,6},{8,9},{9,8},{10,11... | collective-permute-start | bytes 14600 | tf_op jit(solution)/shard_map/ppermute | solution.py:270
  49.1 39.0 %collective-permute-start.5 = (bf16[512,768]{1,0:T(8,128)(2,1)}, bf16[512,768]{1,0:T(8,128)(2,1)S(1)}, u32[]{:S(2)}, u32[]{:S(2)}) collective-permute-start(bf16[512,768]{1,0:T(8,128)(2,1)} %pad_maximum_fusion.7), channel_id=1, source_target_pairs={{0,5},{5,0},{1,4},{4,1},{2,7},{7,2},{3,6},{6,3},{8,13},{13,8},{9,1... | collective-permute-start | bytes 2359304 | tf_op jit(solution)/shard_map/ppermute | solution.py:856
  62.8 7.0 %collective-permute-start.2 = (bf16[1024,256]{1,0:T(8,128)(2,1)S(1)}, bf16[1024,256]{1,0:T(8,128)(2,1)S(1)}, u32[]{:S(2)}, u32[]{:S(2)}) collective-permute-start(bf16[1024,256]{1,0:T(8,128)(2,1)S(1)} %collective-permute-done.1.x2), channel_id=1, source_target_pairs={{0,2},{2,0},{1,3},{3,1},{4,6},{6,4},{5,7},{7,5},{8,10},{10,8},{9,1... | collective-permute-start | bytes 1572872 | tf_op jit(solution)/shard_map/ppermute | solution.py:270
  63.9 24.2 %copy-start.42 = (bf16[512,256]{1,0:T(8,128)(2,1)S(1)}, bf16[512,256]{1,0:T(8,128)(2,1)}, u32[]{:S(2)}) copy-start(bf16[512,256]{1,0:T(8,128)(2,1)} %param.23) | copy-start | bytes 786436
  63.9 24.3 %copy-start.6 = (bf16[2048,256]{1,0:T(8,128)(2,1)S(1)}, bf16[2048,256]{1,0:T(8,128)(2,1)}, u32[]{:S(2)}) copy-start(bf16[2048,256]{1,0:T(8,128)(2,1)} %param.33) | copy-start | bytes 3145732
  63.9 5.3 %collective-permute-start.7 = (f32[5,512]{1,0:T(8,128)S(1)}, f32[5,512]{1,0:T(8,128)S(1)}, u32[]{:S(2)}, u32[]{:S(2)}) collective-permute-start(f32[5,512]{1,0:T(8,128)S(1)} %pad_maximum_fusion.12), channel_id=1, source_target_pairs={{0,4},{4,0},{1,5},{5,1},{2,6},{6,2},{3,7},{7,3},{8,12},{12,8},{9,1... | collective-permute-start | bytes 30728 | tf_op jit(solution)/shard_map/ppermute | solution.py:270
  69.2 20.4 %copy-start.48 = (f32[5,512]{1,0:T(8,128)}, f32[5,512]{1,0:T(8,128)S(1)}, u32[]{:S(2)}) copy-start(f32[5,512]{1,0:T(8,128)S(1)} %collective-permute-done.7) | copy-start | bytes 30724
  69.8 19.9 %copy-start.3 = (bf16[1024,256]{1,0:T(8,128)(2,1)}, bf16[1024,256]{1,0:T(8,128)(2,1)S(1)}, u32[]{:S(2)}) copy-start(bf16[1024,256]{1,0:T(8,128)(2,1)S(1)} %collective-permute-done.x1) | copy-start | bytes 1572868
  69.8 19.9 %copy-start.5 = (bf16[1024,256]{1,0:T(8,128)(2,1)}, bf16[1024,256]{1,0:T(8,128)(2,1)S(1)}, u32[]{:S(2)}) copy-start(bf16[1024,256]{1,0:T(8,128)(2,1)S(1)} %collective-permute-done.2.x3) | copy-start | bytes 1572868
  88.1 8.3 %collective-permute-start.13 = (bf16[256,256]{1,0:T(8,128)(2,1)S(1)}, bf16[256,256]{1,0:T(8,128)(2,1)S(1)}, u32[]{:S(2)}, u32[]{:S(2)}) collective-permute-start(bf16[256,256]{1,0:T(8,128)(2,1)S(1)} %get-tuple-element.211), channel_id=1, source_target_pairs={{0,2},{2,0},{1,3},{3,1},{4,6},{6,4},{5,7},{7,5},{8,10},{10,8},{9,1... | collective-permute-start | bytes 393224 | tf_op jit(solution)/shard_map/ppermute | solution.py:270
  89.1 36.9 %collective-permute-start.17 = (bf16[1024,256]{1,0:T(8,128)(2,1)}, bf16[1024,256]{1,0:T(8,128)(2,1)}, u32[]{:S(2)}, u32[]{:S(2)}) collective-permute-start(bf16[1024,256]{1,0:T(8,128)(2,1)} %get-tuple-element.203), channel_id=1, source_target_pairs={{0,4},{4,0},{1,5},{5,1},{2,6},{6,2},{3,7},{7,3},{8,12},{12,8},{9,1... | collective-permute-start | bytes 1572872 | tf_op jit(solution)/shard_map/ppermute | solution.py:270
  89.6 52.7 %collective-permute-start.18 = (bf16[1024,256]{1,0:T(8,128)(2,1)S(1)}, bf16[1024,256]{1,0:T(8,128)(2,1)}, u32[]{:S(2)}, u32[]{:S(2)}) collective-permute-start(bf16[1024,256]{1,0:T(8,128)(2,1)S(1)} %get-tuple-element.202), channel_id=1, source_target_pairs={{0,2},{2,0},{1,3},{3,1},{4,6},{6,4},{5,7},{7,5},{8,10},{10,8},{9,1... | collective-permute-start | bytes 1572872 | tf_op jit(solution)/shard_map/ppermute | solution.py:270
  98.1 20.7 %collective-permute-start.15 = (bf16[256,512]{1,0:T(8,128)(2,1)S(1)}, bf16[256,512]{1,0:T(8,128)(2,1)}, u32[]{:S(2)}, u32[]{:S(2)}) collective-permute-start(bf16[256,512]{1,0:T(8,128)(2,1)S(1)} %pad_maximum_fusion.11), channel_id=1, source_target_pairs={{0,1},{1,0},{2,3},{3,2},{4,5},{5,4},{6,7},{7,6},{8,9},{9,8},{10,11... | collective-permute-start | bytes 786440 | tf_op jit(solution)/shard_map/ppermute | solution.py:270
  98.6 26.4 %collective-permute-start.16 = (bf16[256,512]{1,0:T(8,128)(2,1)S(1)}, bf16[256,512]{1,0:T(8,128)(2,1)}, u32[]{:S(2)}, u32[]{:S(2)}) collective-permute-start(bf16[256,512]{1,0:T(8,128)(2,1)S(1)} %pad_maximum_fusion.11), channel_id=1, source_target_pairs={{0,5},{5,0},{1,4},{4,1},{2,7},{7,2},{3,6},{6,3},{8,13},{13,8},{9,1... | collective-permute-start | bytes 786440 | tf_op jit(solution)/shard_map/ppermute | solution.py:856
  105.3 20.7 %collective-permute-start.14 = (bf16[256,512]{1,0:T(8,128)(2,1)S(1)}, bf16[256,512]{1,0:T(8,128)(2,1)}, u32[]{:S(2)}, u32[]{:S(2)}) collective-permute-start(bf16[256,512]{1,0:T(8,128)(2,1)S(1)} %pad_maximum_fusion.11), channel_id=1, source_target_pairs={{0,4},{4,0},{1,5},{5,1},{2,6},{6,2},{3,7},{7,3},{8,12},{12,8},{9,1... | collective-permute-start | bytes 786440 | tf_op jit(solution)/shard_map/ppermute | solution.py:270
  106.0 20.2 %copy-start.29 = (bf16[512,768]{1,0:T(8,128)(2,1)S(1)}, bf16[512,768]{1,0:T(8,128)(2,1)}, u32[]{:S(2)}) copy-start(bf16[512,768]{1,0:T(8,128)(2,1)} %copy-done.28) | copy-start | bytes 2359300
  126.0 17.4 %collective-permute-start.19 = (bf16[1024,256]{1,0:T(8,128)(2,1)}, bf16[1024,256]{1,0:T(8,128)(2,1)}, u32[]{:S(2)}, u32[]{:S(2)}) collective-permute-start(bf16[1024,256]{1,0:T(8,128)(2,1)} %collective-permute-done.17), channel_id=1, source_target_pairs={{0,2},{2,0},{1,3},{3,1},{4,6},{6,4},{5,7},{7,5},{8,10},{10,8},{9,1... | collective-permute-start | bytes 1572872 | tf_op jit(solution)/shard_map/ppermute | solution.py:270
  152.8 4.5 collective-permute-start.20
  201.2 127.8 %reduce-scatter.7.cloned.1.call-start = ((), (), s32[]{:S(2)}) async-start(), calls=%async_computation.3 | async-start | bytes 5242880
  202.8 10.9 %collective-permute-start.21 = (bf16[1024,1024]{1,0:T(8,128)(2,1)S(1)}, bf16[1024,1024]{1,0:T(8,128)(2,1)}, u32[]{:S(2)}, u32[]{:S(2)}) collective-permute-start(bf16[1024,1024]{1,0:T(8,128)(2,1)S(1)} %copy-done.7), channel_id=1, source_target_pairs={{0,2},{2,0},{1,3},{3,1},{4,6},{6,4},{5,7},{7,5},{8,10},{10,8},{9,1... | collective-permute-start | bytes 6291464 | tf_op jit(solution)/shard_map/ppermute | solution.py:270
  263.8 42.3 %collective-permute-start.22 = (bf16[512,256]{1,0:T(8,128)(2,1)}, bf16[512,256]{1,0:T(8,128)(2,1)}, u32[]{:S(2)}, u32[]{:S(2)}) collective-permute-start(bf16[512,256]{1,0:T(8,128)(2,1)} %convolution_convert_fusion.9), channel_id=1, source_target_pairs={{0,4},{4,0},{1,5},{5,1},{2,6},{6,2},{3,7},{7,3},{8,12},{12,8},{9,1... | collective-permute-start | bytes 786440 | tf_op jit(solution)/shard_map/ppermute | solution.py:270
  266.4 13.6 %collective-permute-start.25 = (bf16[512,512]{1,0:T(8,128)(2,1)S(1)}, bf16[512,512]{1,0:T(8,128)(2,1)S(1)}, u32[]{:S(2)}, u32[]{:S(2)}) collective-permute-start(bf16[512,512]{1,0:T(8,128)(2,1)S(1)} %dynamic-slice_bitcast_fusion.1), channel_id=1, source_target_pairs={{0,8},{8,0},{16,24},{24,16},{1,9},{9,1},{17,25},{25,17},{2,10},{10... | collective-permute-start | bytes 1572872 | tf_op jit(solution)/shard_map/ppermute | solution.py:881
  269.8 36.3 %collective-permute-start.23 = (bf16[512,256]{1,0:T(8,128)(2,1)S(1)}, bf16[512,256]{1,0:T(8,128)(2,1)S(1)}, u32[]{:S(2)}, u32[]{:S(2)}) collective-permute-start(bf16[512,256]{1,0:T(8,128)(2,1)S(1)} %convolution_convert_fusion.8), channel_id=1, source_target_pairs={{0,1},{1,0},{2,3},{3,2},{4,5},{5,4},{6,7},{7,6},{8,9},{9,8},{10,11... | collective-permute-start | bytes 786440 | tf_op jit(solution)/shard_map/ppermute | solution.py:270
  272.9 33.1 %collective-permute-start.24 = (bf16[512,256]{1,0:T(8,128)(2,1)S(1)}, bf16[512,256]{1,0:T(8,128)(2,1)S(1)}, u32[]{:S(2)}, u32[]{:S(2)}) collective-permute-start(bf16[512,256]{1,0:T(8,128)(2,1)S(1)} %convolution_convert_fusion.7), channel_id=1, source_target_pairs={{0,5},{5,0},{1,4},{4,1},{2,7},{7,2},{3,6},{6,3},{8,13},{13,8},{9,1... | collective-permute-start | bytes 786440 | tf_op jit(solution)/shard_map/ppermute | solution.py:856
  280.1 25.0 %collective-permute-start.26 = (bf16[512,512]{1,0:T(8,128)(2,1)S(1)}, bf16[512,512]{1,0:T(8,128)(2,1)S(1)}, u32[]{:S(2)}, u32[]{:S(2)}) collective-permute-start(bf16[512,512]{1,0:T(8,128)(2,1)S(1)} %fusion.44), channel_id=1, source_target_pairs={{0,16},{16,0},{8,24},{24,8},{1,17},{17,1},{9,25},{25,9},{2,18},{18... | collective-permute-start | bytes 1572872 | tf_op jit(solution)/shard_map/ppermute | solution.py:885
  287.3 24.4 %copy-start.13 = (bf16[1024,1024]{1,0:T(8,128)(2,1)}, bf16[1024,1024]{1,0:T(8,128)(2,1)S(1)}, u32[]{:S(2)}) copy-start(bf16[1024,1024]{1,0:T(8,128)(2,1)S(1)} %fusion.20.part_ref) | copy-start | bytes 6291460
  306.1 4.2 collective-permute-start.27
  319.2 3.8 collective-permute-start.28
  323.0 6.0 %collective-permute-start.29 = (f32[2304]{0:T(1024)S(1)}, f32[2304]{0:T(1024)S(1)}, u32[]{:S(2)}, u32[]{:S(2)}) collective-permute-start(f32[2304]{0:T(1024)S(1)} %fusion.65), channel_id=1, source_target_pairs={{0,1},{1,0},{2,3},{3,2},{4,5},{5,4},{6,7},{7,6},{8,9},{9,8},{10,11... | collective-permute-start | bytes 27656 | tf_op jit(solution)/shard_map/ppermute | solution.py:270
  330.2 12.0 %collective-permute-start.30 = (bf16[512,512]{1,0:T(8,128)(2,1)S(1)}, bf16[512,512]{1,0:T(8,128)(2,1)S(1)}, u32[]{:S(2)}, u32[]{:S(2)}) collective-permute-start(bf16[512,512]{1,0:T(8,128)(2,1)S(1)} %dynamic-slice_bitcast_fusion), channel_id=1, source_target_pairs={{0,8},{8,0},{16,24},{24,16},{1,9},{9,1},{17,25},{25,17},{2,10},{10... | collective-permute-start | bytes 1572872 | tf_op jit(solution)/shard_map/ppermute | solution.py:881
  342.3 7.8 %collective-permute-start.35 = (f32[2304]{0:T(1024)S(1)}, f32[2304]{0:T(1024)S(1)}, u32[]{:S(2)}, u32[]{:S(2)}) collective-permute-start(f32[2304]{0:T(1024)S(1)} %maximum_add_fusion.1), channel_id=1, source_target_pairs={{0,8},{8,0},{16,24},{24,16},{1,9},{9,1},{17,25},{25,17},{2,10},{10... | collective-permute-start | bytes 27656 | tf_op jit(solution)/shard_map/ppermute | solution.py:1015
  344.2 28.5 %collective-permute-start.39 = (bf16[512,768]{1,0:T(8,128)(2,1)}, bf16[512,768]{1,0:T(8,128)(2,1)}, u32[]{:S(2)}, u32[]{:S(2)}) collective-permute-start(bf16[512,768]{1,0:T(8,128)(2,1)} %convolution_convert_fusion.2), channel_id=1, source_target_pairs={{0,5},{5,0},{1,4},{4,1},{2,7},{7,2},{3,6},{6,3},{8,13},{13,8},{9,1... | collective-permute-start | bytes 2359304 | tf_op jit(solution)/shard_map/ppermute | solution.py:856
  345.8 32.2 %collective-permute-start.38 = (bf16[512,768]{1,0:T(8,128)(2,1)}, bf16[512,768]{1,0:T(8,128)(2,1)}, u32[]{:S(2)}, u32[]{:S(2)}) collective-permute-start(bf16[512,768]{1,0:T(8,128)(2,1)} %convolution_convert_fusion.3), channel_id=1, source_target_pairs={{0,1},{1,0},{2,3},{3,2},{4,5},{5,4},{6,7},{7,6},{8,9},{9,8},{10,11... | collective-permute-start | bytes 2359304 | tf_op jit(solution)/shard_map/ppermute | solution.py:270
  346.1 32.9 %collective-permute-start.37 = (bf16[512,768]{1,0:T(8,128)(2,1)}, bf16[512,768]{1,0:T(8,128)(2,1)}, u32[]{:S(2)}, u32[]{:S(2)}) collective-permute-start(bf16[512,768]{1,0:T(8,128)(2,1)} %convolution_convert_fusion.4), channel_id=1, source_target_pairs={{0,4},{4,0},{1,5},{5,1},{2,6},{6,2},{3,7},{7,3},{8,12},{12,8},{9,1... | collective-permute-start | bytes 2359304 | tf_op jit(solution)/shard_map/ppermute | solution.py:270
  347.7 33.7 %collective-permute-start.33 = (bf16[512,512]{1,0:T(8,128)(2,1)S(1)}, bf16[512,512]{1,0:T(8,128)(2,1)}, u32[]{:S(2)}, u32[]{:S(2)}) collective-permute-start(bf16[512,512]{1,0:T(8,128)(2,1)S(1)} %fusion.43), channel_id=1, source_target_pairs={{0,16},{16,0},{8,24},{24,8},{1,17},{17,1},{9,25},{25,9},{2,18},{18... | collective-permute-start | bytes 1572872 | tf_op jit(solution)/shard_map/ppermute | solution.py:885
  350.2 22.5 %copy-start.8 = (bf16[512,512]{1,0:T(8,128)(2,1)S(1)}, bf16[512,512]{1,0:T(8,128)(2,1)}, u32[]{:S(2)}) copy-start(bf16[512,512]{1,0:T(8,128)(2,1)} %add_convert_fusion.3) | copy-start | bytes 1572868
  350.2 20.5 %collective-permute-start.36 = (f32[2304]{0:T(1024)S(1)}, f32[2304]{0:T(1024)S(1)}, u32[]{:S(2)}, u32[]{:S(2)}) collective-permute-start(f32[2304]{0:T(1024)S(1)} %add.237), channel_id=1, source_target_pairs={{0,16},{16,0},{8,24},{24,8},{1,17},{17,1},{9,25},{25,9},{2,18},{18... | collective-permute-start | bytes 27656 | tf_op jit(solution)/shard_map/ppermute | solution.py:1016
  370.7 1.2 collective-permute-start.46
  371.9 21.4 %collective-permute-start.31 = (bf16[1024,512]{1,0:T(8,128)(2,1)}, bf16[1024,512]{1,0:T(8,128)(2,1)}, u32[]{:S(2)}, u32[]{:S(2)}) collective-permute-start(bf16[1024,512]{1,0:T(8,128)(2,1)} %get-tuple-element.101), channel_id=1, source_target_pairs={{0,2},{2,0},{1,3},{3,1},{4,6},{6,4},{5,7},{7,5},{8,10},{10,8},{9,1... | collective-permute-start | bytes 3145736 | tf_op jit(solution)/shard_map/ppermute | solution.py:270
  372.7 15.7 %collective-permute-start.47 = (bf16[512,512]{1,0:T(8,128)(2,1)S(1)}, bf16[512,512]{1,0:T(8,128)(2,1)}, u32[]{:S(2)}, u32[]{:S(2)}) collective-permute-start(bf16[512,512]{1,0:T(8,128)(2,1)S(1)} %copy-done.8), channel_id=1, source_target_pairs={{0,8},{8,0},{16,24},{24,16},{1,9},{9,1},{17,25},{25,17},{2,10},{10... | collective-permute-start | bytes 1572872 | tf_op jit(solution)/shard_map/ppermute | solution.py:889
  382.6 29.1 %collective-permute-start.44 = (bf16[512,512]{1,0:T(8,128)(2,1)S(1)}, bf16[512,512]{1,0:T(8,128)(2,1)}, u32[]{:S(2)}, u32[]{:S(2)}) collective-permute-start(bf16[512,512]{1,0:T(8,128)(2,1)S(1)} %add_convert_fusion.2), channel_id=1, source_target_pairs={{0,8},{8,0},{16,24},{24,16},{1,9},{9,1},{17,25},{25,17},{2,10},{10... | collective-permute-start | bytes 1572872 | tf_op jit(solution)/shard_map/ppermute | solution.py:889
  384.1 26.6 %collective-permute-start.34 = (bf16[1024,256]{1,0:T(8,128)(2,1)}, bf16[1024,256]{1,0:T(8,128)(2,1)}, u32[]{:S(2)}, u32[]{:S(2)}) collective-permute-start(bf16[1024,256]{1,0:T(8,128)(2,1)} %get-tuple-element.104), channel_id=1, source_target_pairs={{0,4},{4,0},{1,5},{5,1},{2,6},{6,2},{3,7},{7,3},{8,12},{12,8},{9,1... | collective-permute-start | bytes 1572872 | tf_op jit(solution)/shard_map/ppermute | solution.py:270
  387.8 21.7 %collective-permute-start.40 = (bf16[256,1024]{0,1:T(8,128)(2,1)}, bf16[256,1024]{0,1:T(8,128)(2,1)}, u32[]{:S(2)}, u32[]{:S(2)}) collective-permute-start(bf16[256,1024]{0,1:T(8,128)(2,1)} %bitcast.164), channel_id=1, source_target_pairs={{0,8},{8,0},{16,24},{24,16},{1,9},{9,1},{17,25},{25,17},{2,10},{10... | collective-permute-start | bytes 1572872 | tf_op jit(solution)/shard_map/ppermute | solution.py:881
  393.2 21.0 %collective-permute-start.48 = (bf16[1024,256]{1,0:T(8,128)(2,1)S(1)}, bf16[1024,256]{1,0:T(8,128)(2,1)S(1)}, u32[]{:S(2)}, u32[]{:S(2)}) collective-permute-start(bf16[1024,256]{1,0:T(8,128)(2,1)S(1)} %slice.251), channel_id=1, source_target_pairs={{0,2},{2,0},{1,3},{3,1},{4,6},{6,4},{5,7},{7,5},{8,10},{10,8},{9,1... | collective-permute-start | bytes 1572872 | tf_op jit(solution)/shard_map/ppermute | solution.py:270
  395.4 40.8 %collective-permute-start.32 = (bf16[1024,256]{1,0:T(8,128)(2,1)S(1)}, bf16[1024,256]{1,0:T(8,128)(2,1)S(1)}, u32[]{:S(2)}, u32[]{:S(2)}) collective-permute-start(bf16[1024,256]{1,0:T(8,128)(2,1)S(1)} %slice.234), channel_id=1, source_target_pairs={{0,4},{4,0},{1,5},{5,1},{2,6},{6,2},{3,7},{7,3},{8,12},{12,8},{9,1... | collective-permute-start | bytes 1572872 | tf_op jit(solution)/shard_map/ppermute | solution.py:270
  410.7 25.4 %collective-permute-start.41 = (bf16[256,1024]{0,1:T(8,128)(2,1)S(1)}, bf16[256,1024]{0,1:T(8,128)(2,1)S(1)}, u32[]{:S(2)}, u32[]{:S(2)}) collective-permute-start(bf16[256,1024]{0,1:T(8,128)(2,1)S(1)} %fusion.42), channel_id=1, source_target_pairs={{0,16},{16,0},{8,24},{24,8},{1,17},{17,1},{9,25},{25,9},{2,18},{18... | collective-permute-start | bytes 1572872 | tf_op jit(solution)/shard_map/ppermute | solution.py:885
  412.8 37.5 %collective-permute-start.45 = (bf16[256,1024]{1,0:T(8,128)(2,1)S(1)}, bf16[256,1024]{1,0:T(8,128)(2,1)S(1)}, u32[]{:S(2)}, u32[]{:S(2)}) collective-permute-start(bf16[256,1024]{1,0:T(8,128)(2,1)S(1)} %pad_maximum_fusion.8), channel_id=1, source_target_pairs={{0,2},{2,0},{1,3},{3,1},{4,6},{6,4},{5,7},{7,5},{8,10},{10,8},{9,1... | collective-permute-start | bytes 1572872 | tf_op jit(solution)/shard_map/ppermute | solution.py:270
  436.3 13.9 %collective-permute-start.42 = (bf16[256,1024]{0,1:T(8,128)(2,1)S(1)}, bf16[256,1024]{0,1:T(8,128)(2,1)S(1)}, u32[]{:S(2)}, u32[]{:S(2)}) collective-permute-start(bf16[256,1024]{0,1:T(8,128)(2,1)S(1)} %add_convert_fusion.1), channel_id=1, source_target_pairs={{0,8},{8,0},{16,24},{24,16},{1,9},{9,1},{17,25},{25,17},{2,10},{10... | collective-permute-start | bytes 1572872 | tf_op jit(solution)/shard_map/ppermute | solution.py:889
  450.3 2.0 collective-permute-start.43
  (59 other events, 465.7 us)
Sparse Core Ops, SparseCore 0:
  35.8 124.2 all-gather.2
  201.4 51.7 reduce-scatter.8
  256.1 63.8 reduce-scatter.6
